TPU v7x, 32 devices: a whole 2x2x4 slice. The times are simulated.
32 devices in a mesh: chan: 8 (over y, x, core), tm: 4 (over z).
Axes of the slice: x: 2, y: 2, z: 4, core: 2. Of those that a mesh axis runs over, the one named last changes fastest.
Arguments:
- voltages: bfloat16 [2, 8, 2048, 512], P(None, None, 'chan', 'tm'), may hold values from -0.25 to 0.25
- assignment: int32 [1024, 1], replicated, may hold values from 0 to 7; in each aligned block of 1024 rows (0 to 1023, 1024 to 2047, ...) at most 192 rows name the same one
- slot_subarray_index: int32 [8], replicated, may hold values from 0 to 7, each once
Outputs:
- visibilities: float32 [8, 8, 2, 384, 384], P('tm', 'chan')
Inputs may be any that keep to these rules, and one draw needn't show every extreme that they name: `assignment`: no subarray holds more than 192 antennas; one holds exactly 192. `slot_subarray_index`: each subarray appears once.
All inputs are finite; a program needn't handle non-finite values.
Results may differ from a plain program's by a relative error of at most 0.008.
Values may be sent and summed in bfloat16 or wider, within the bound.
No kernel may reach another device: no remote copies, remote signals or barrier semaphores. Data moves between devices by JAX's collectives and lax.ppermute only.
A program may use at most 64 MiB of HBM per device.

v0:
```python
import jax
import jax.numpy as jnp
from jax import lax
from jax.sharding import PartitionSpec as P

SLOT = 384


def result_slot_lookup(assignment, slot_subarray_index, subarrays, slots, inputs):
    owner = jnp.repeat(assignment[:, 0], 2)
    onehot = (owner[:, None] == jnp.arange(subarrays, dtype=jnp.int32)[None, :]).astype(jnp.int32)
    ranks = jnp.sum((jnp.cumsum(onehot, axis=0) - onehot) * onehot, axis=1)
    table = jnp.full((subarrays, slots), inputs, jnp.int32)
    table = table.at[owner, ranks].set(jnp.arange(inputs, dtype=jnp.int32))
    return table[slot_subarray_index].reshape(-1)


def compact(block, rows, subarrays, slots):
    parts, chans, inputs, samples = block.shape
    padded_voltages = jnp.concatenate(
        [block, jnp.zeros((parts, chans, 1, samples), block.dtype)], axis=2
    )
    picked = jnp.take(padded_voltages, rows, axis=2)
    picked = picked.reshape(parts, chans, subarrays, slots, samples)
    picked = jnp.transpose(picked, (2, 1, 0, 3, 4))
    return picked.reshape(subarrays, chans, 2 * slots, samples)


def gram(stacked):
    full = jnp.einsum("...pt,...qt->...pq", stacked, stacked, preferred_element_type=jnp.float32)
    half = stacked.shape[-2] // 2
    real = full[..., :half, :half] + full[..., half:, half:]
    imag = full[..., half:, :half] - full[..., :half, half:]
    return jnp.stack([real, imag], axis=-3)


def shards(voltages, assignment, slot_subarray_index):
    subarrays = slot_subarray_index.shape[0]
    slots = SLOT
    inputs = 2 * assignment.shape[0]
    rows = result_slot_lookup(assignment, slot_subarray_index, subarrays, slots, inputs)
    local_samples = voltages.shape[3]
    time_groups = lax.axis_size("tm")
    stacked = compact(
        lax.all_to_all(voltages, "chan", split_axis=1, concat_axis=2, tiled=True),
        rows,
        subarrays,
        slots,
    )
    received = lax.all_to_all(stacked, "tm", split_axis=0, concat_axis=3, tiled=True)
    total = None
    for block_index in range(time_groups):
        piece = received[..., block_index * local_samples : (block_index + 1) * local_samples]
        rounded = gram(piece).astype(jnp.bfloat16).astype(jnp.float32)
        total = rounded if total is None else total + rounded
    return total


def solution(mesh):
    placed = (P(None, None, "chan", "tm"), P(), P())
    return jax.shard_map(
        shards,
        mesh=mesh,
        in_specs=placed,
        out_specs=P("tm", "chan", None, None, None),
        check_vma=False,
    )
```

profile of v0, /device:TPU:0, one launch (start us, length us, event | category | flops | bytes accessed | tf_op | source)
XLA Modules:
  0.0 84.1 jit_solution(1011175587574448796)
XLA Ops:
  0.0 2.3 %copy.13 = bf16[2,8,256,128]{3,2,0,1:T(8,128)(2,1)} copy(bf16[2,8,256,128]{3,2,1,0:T(8,128)(2,1)} %param.3) | data formatting | bytes 2097152 | tf_op args[0]
  2.3 0.0 copy-start
  2.3 0.0 copy-start.3
  2.3 5.3 %all-to-all-start = ((bf16[2,8,256,128]{3,2,0,1:T(8,128)(2,1)}), bf16[2,8,256,128]{3,2,0,1:T(8,128)(2,1)S(1)}, u32[]{:S(2)}, u32[]{:S(2)}) async-start(bf16[2,8,256,128]{3,2,0,1:T(8,128)(2,1)} %copy.13), calls=%async_computation | async-start | bytes 2097152 | tf_op jit(solution)/shard_map/all_to_all | solution.py:45
  7.6 0.0 copy-start.2
  7.6 0.0 copy-start.1
  7.6 0.0 copy-done
  7.7 0.2 broadcast_in_dim.30
  7.9 0.3 eq.23
  8.1 0.3 reshape.321
  8.4 0.0 copy-done.3
  8.5 0.6 broadcast.137
  9.1 0.7 reduce.9
  9.8 0.1 broadcast_in_dim.31
  9.9 0.1 copy.11
  10.0 0.1 copy.12
  10.0 2.3 %reduce-window.6 = s32[8,16,128]{2,1,0:T(8,128)S(1)} reduce-window(s32[8,16,128]{2,1,0:T(8,128)S(1)} %fusion.19, s32[]{:T(128)} %constant.11.clone.1), window={size=1x1x128 pad=0_0x0_0x127_0}, to_apply=%region_0.0 | reduce-window | flops 2080768 | bytes 131076 | tf_op jit(solution)/shard_map/reduce-window
  12.3 0.3 slice_reduce_fusion
  12.6 0.2 reduce-window.9
  12.8 0.1 add_bitcast_fusion
  13.0 0.0 copy-done.2
  13.0 0.1 and_reduce_fusion
  13.1 0.0 copy-done.1
  13.1 0.1 multiply_reduce_fusion
  13.2 8.1 %scatter_custom_fusion = s32[3072]{0:T(1024)S(1)} fusion(s32[2048]{0:T(1024)S(1)} %broadcast_select_fusion, s32[2048]{0:T(1024)S(1)} %iota.11, s32[]{:T(128)} %constant.10.clone.1), kind=kCustom, calls=%fused_computation.57 | custom fusion | bytes 12292
  21.3 0.6 gather_fusion
  21.9 1.1 %all-to-all-done = bf16[2,8,256,128]{3,2,0,1:T(8,128)(2,1)S(1)} async-done(((bf16[2,8,256,128]{3,2,0,1:T(8,128)(2,1)}), bf16[2,8,256,128]{3,2,0,1:T(8,128)(2,1)S(1)}, u32[]{:S(2)}, u32[]{:S(2)}) %all-to-all-start) | async-done | bytes 1048608 | tf_op jit(solution)/shard_map/all_to_all | solution.py:45
  23.0 1.1 %copy.14 = bf16[2,8,256,128]{3,0,2,1:T(2,128)(2,1)S(1)} copy(bf16[2,8,256,128]{3,2,0,1:T(8,128)(2,1)S(1)} %all-to-all-done) | data formatting | bytes 2097152 | tf_op jit(solution)/shard_map/all_to_all | solution.py:45
  24.1 1.0 %pad_bitcast_fusion = bf16[2,2049,128]{2,0,1:T(2,128)(2,1)S(1)} fusion(bf16[2,1,2048,128]{3,0,2,1:T(2,128)(2,1)S(1)} %bitcast.90), kind=kLoop, calls=%fused_computation.26 | loop fusion | bytes 2097664 | tf_op jit(solution)/shard_map/concatenate | solution.py:20
  25.1 10.4 %gather_fusion.1 = bf16[3072,2,128]{2,1,0:T(2,128)(2,1)S(1)} fusion(bf16[2,2049,128]{2,0,1:T(2,128)(2,1)S(1)} %pad_bitcast_fusion, s32[3072]{0:T(1024)S(1)} %broadcast_clamp_fusion), kind=kCustom, calls=%fused_computation.1 | custom fusion | bytes 3158016 | tf_op jit(solution)/shard_map/jit(_take)/gather | solution.py:23
  35.5 0.8 copy_select_fusion
  36.3 41.2 %all_to_all.30 = bf16[8,1,768,128]{3,2,1,0:T(8,128)(2,1)S(1)} all-to-all(bf16[8,1,768,128]{3,2,1,0:T(8,128)(2,1)S(1)} %bitcast.88), channel_id=1, replica_groups=mesh['chan'=8,'tm'=4] {'tm'}, dimensions={0} | all-to-all | bytes 3145728 | tf_op jit(solution)/shard_map/all_to_all | solution.py:50
  77.5 0.3 copy.25
  77.8 0.8 convolution_bitcast_fusion
  78.6 0.8 convolution_bitcast_fusion.1
  79.3 0.8 convolution_bitcast_fusion.2
  80.1 0.8 convolution_bitcast_fusion.3
  80.9 0.3 fusion.14
  81.2 0.3 fusion.12
  81.4 0.3 fusion.10
  81.7 0.3 fusion.8
  82.0 0.5 convert_add_fusion
  82.5 1.6 %copy.18 = f32[2,1,2,384,384]{4,3,2,1,0:T(8,128)} copy(f32[2,1,2,384,384]{4,3,0,2,1:T(8,128)S(1)} %convert_add_fusion) | data formatting | bytes 4718592 | tf_op jit(solution)/shard_map/add | solution.py:55
  (13 shorter events, 0.2 us)
Async XLA Ops:
  2.3 5.4 %copy-start = (s32[1024,1]{0,1:T(1,128)S(1)}, s32[1024,1]{0,1:T(1,128)}, u32[]{:S(2)}) copy-start(s32[1024,1]{0,1:T(1,128)} %param.4) | copy-start | bytes 12292
  2.3 6.1 %copy-start.3 = (s32[8]{0:T(128)S(1)}, s32[8]{0:T(128)}, u32[]{:S(2)}) copy-start(s32[8]{0:T(128)} %param.5) | copy-start | bytes 100
  2.3 20.7 %all-to-all-start = ((bf16[2,8,256,128]{3,2,0,1:T(8,128)(2,1)}), bf16[2,8,256,128]{3,2,0,1:T(8,128)(2,1)S(1)}, u32[]{:S(2)}, u32[]{:S(2)}) async-start(bf16[2,8,256,128]{3,2,0,1:T(8,128)(2,1)} %copy.13), calls=%async_computation | async-start | bytes 2097152 | tf_op jit(solution)/shard_map/all_to_all | solution.py:45
  7.6 5.3 %copy-start.2 = (s32[2]{0:T(128)S(1)}, s32[2]{0:T(128)}, u32[]{:S(2)}) copy-start(s32[2]{0:T(128)} %constant.36) | copy-start | bytes 28
  7.6 5.4 %copy-start.1 = (s32[2]{0:T(128)S(1)}, s32[2]{0:T(128)}, u32[]{:S(2)}) copy-start(s32[2]{0:T(128)} %constant.33) | copy-start | bytes 28
where the time goes:
time: 84.3 us; the launch traced here: 84.1 us
  blocking collectives  41.2 us (49%)
  local copies, waits for them, and re-layouts  27.2 us (32%)
  other arithmetic  5.91 us (7%)
  starting transfers between devices  5.33 us (6%)
  matrix products  3.09 us (4%)
  waiting for transfers between devices  1.08 us (1%)
    all_to_all x1, blocking collectives, shards(): lax.all_to_all(stacked, 'tm', split_axis=0, concat_axis=3, tiled=True)  41.2 us
    unnamed x12, local copies, waits for them, and re-layouts  11 us
    gather x1, local copies, waits for them, and re-layouts, compact(): picked = jnp.take(padded_voltages, rows, axis=2)  10.4 us
    all_to_all x1, starting transfers between devices, shards(): lax.all_to_all(voltages, 'chan', split_axis=1, concat_axis=2, tiled=True)  5.33 us
    dot_general x4, matrix products, gram(): jnp.einsum('...pt,...qt->...pq', stacked, stacked, preferred_element_type...  3.09 us
    another operation x2, other arithmetic  2.45 us
  transfers between devices with their start and end apart: 1, of which 1 were waited for; matrix products, arithmetic and copies ran while one was open for 17% of the time, Pallas kernels for 0%

commit v1 on v0

v1 whole, which is shorter than its diff:
```python
import functools

import jax
import jax.numpy as jnp
from jax import lax
from jax.experimental import pallas as pl
from jax.experimental.pallas import tpu as pltpu
from jax.sharding import PartitionSpec as P

SLOT = 384
LANES = 128

VMEM = pl.BlockSpec(memory_space=pltpu.VMEM)
SMEM = pl.BlockSpec(memory_space=pltpu.SMEM)
PARAMS = pltpu.CompilerParams(vmem_limit_bytes=20 * 1024 * 1024)


def partner(index, step, count):
    if count & (count - 1):
        return lax.rem(index + step, count) if not isinstance(index, int) else (index + step) % count
    return index ^ step


def relative(owner, me, count):
    if count & (count - 1):
        return lax.rem(owner - me + count, count)
    return owner ^ me


def plan_kernel(groups, half, slot_ref, owner_ref, select_ref):
    subarrays = slot_ref.shape[0]
    blocks = owner_ref.shape[0]
    per = subarrays // groups
    me = lax.axis_index("tm")
    shape = (subarrays, LANES)
    place = lax.broadcasted_iota(jnp.int32, shape, 0)
    name = jnp.zeros(shape, jnp.int32)
    for s in range(subarrays):
        name = jnp.where(place == s, slot_ref[s], name)
    base = jnp.zeros(shape, jnp.int32)
    for s in range(subarrays):
        chunk = relative(jnp.int32(s // per), me, groups) * per + s % per
        base = jnp.where(place == s, chunk * half, base)
    base = base.astype(jnp.float32)
    earlier = lax.broadcasted_iota(jnp.int32, (LANES, LANES), 0)
    later = lax.broadcasted_iota(jnp.int32, (LANES, LANES), 1)
    before = jnp.where(earlier < later, 1.0, 0.0).astype(jnp.bfloat16)
    held = [jnp.where(owner_ref[b : b + 1, :] == name, 1.0, 0.0) for b in range(blocks)]
    within = jnp.dot(
        jnp.concatenate(held, axis=0).astype(jnp.bfloat16), before, preferred_element_type=jnp.float32
    )
    run = base
    height = 256
    row = lax.broadcasted_iota(jnp.int32, (height, LANES), 0).astype(jnp.float32)
    for b in range(blocks):
        rank = within[b * subarrays : (b + 1) * subarrays] + run
        target = jnp.sum(held[b] * rank, axis=0, keepdims=True)
        run = run + jnp.sum(held[b], axis=1, keepdims=True)
        for top in range(0, select_ref.shape[0], height):
            hit = row == (target - top)
            select_ref[top : top + height, b * LANES : (b + 1) * LANES] = jnp.where(hit, 1.0, 0.0).astype(
                jnp.bfloat16
            )


def plan(assignment, slot_subarray_index, groups, half):
    antennas = assignment.shape[0]
    subarrays = slot_subarray_index.shape[0]
    return pl.pallas_call(
        functools.partial(plan_kernel, groups, half),
        out_shape=jax.ShapeDtypeStruct((subarrays * half, antennas), jnp.bfloat16),
        in_specs=[SMEM, VMEM],
        out_specs=VMEM,
        compiler_params=PARAMS,
        cost_estimate=pl.CostEstimate(flops=4_000_000_000, bytes_accessed=3_000_000, transcendentals=0),
    )(slot_subarray_index, assignment.reshape(antennas // LANES, LANES))


def gather_kernel(select_ref, x_ref, *rest):
    *outs, wide, pair, tall = rest
    inputs = x_ref.shape[0]
    antennas = inputs // 2
    wide[...] = x_ref[...].astype(jnp.float32)
    for pol in range(2):
        pair[:, pol * LANES : (pol + 1) * LANES] = wide[pl.ds(pol, antennas, stride=2), :].astype(jnp.bfloat16)
    picked = jnp.dot(select_ref[...], pair[...], preferred_element_type=jnp.float32)
    rows = select_ref.shape[0]
    for pol in range(2):
        tall[pl.ds(pol, rows, stride=2), :] = picked[:, pol * LANES : (pol + 1) * LANES]
    per, slots, _ = outs[0].shape
    for g, out in enumerate(outs):
        for s in range(per):
            top = (g * per + s) * slots
            out[s] = tall[top : top + slots, :].astype(jnp.bfloat16)


def gather(select, x, groups, per, slots):
    inputs, samples = x.shape
    rows, antennas = select.shape
    return pl.pallas_call(
        gather_kernel,
        out_shape=[jax.ShapeDtypeStruct((per, slots, samples), jnp.bfloat16)] * groups,
        in_specs=[VMEM, VMEM],
        out_specs=[VMEM] * groups,
        scratch_shapes=[
            pltpu.VMEM((inputs, samples), jnp.float32),
            pltpu.VMEM((antennas, 2 * samples), jnp.bfloat16),
            pltpu.VMEM((2 * rows, samples), jnp.float32),
        ],
        compiler_params=PARAMS,
        cost_estimate=pl.CostEstimate(
            flops=2 * rows * antennas * 2 * samples, bytes_accessed=4_000_000, transcendentals=0
        ),
    )(select, x)


def gram_kernel(*refs):
    *parts, out = refs
    count = len(parts) // 2
    for s in range(parts[0].shape[0]):
        for part in range(2):
            total = None
            for e in range(count):
                real, imag = parts[e][s], parts[count + e][s]
                right = jnp.concatenate([real, imag], axis=1)
                left = right if part == 0 else jnp.concatenate([imag, -real], axis=1)
                term = lax.dot_general(
                    left, right, (((1,), (1,)), ((), ())), preferred_element_type=jnp.float32
                )
                total = term if total is None else total + term
            out[s, 0, part] = total


def gram(real, imag):
    per, slots, _ = real[0].shape
    return pl.pallas_call(
        gram_kernel,
        out_shape=jax.ShapeDtypeStruct((per, 1, 2, slots, slots), jnp.float32),
        in_specs=[VMEM] * (2 * len(real)),
        out_specs=VMEM,
        compiler_params=PARAMS,
        cost_estimate=pl.CostEstimate(flops=1_200_000_000, bytes_accessed=4_000_000, transcendentals=0),
    )(*real, *imag)


def shards(voltages, assignment, slot_subarray_index):
    groups = lax.axis_size("tm")
    subarrays = slot_subarray_index.shape[0]
    per = subarrays // groups
    select = plan(assignment, slot_subarray_index, groups, SLOT // 2)
    order = sorted(range(1, groups), reverse=True)
    received = []
    for k in range(2):
        x = lax.all_to_all(voltages[k], "chan", split_axis=0, concat_axis=1, tiled=True)
        x = x.reshape(x.shape[1], x.shape[2])
        chunks = gather(select, x, groups, per, SLOT)
        got = [chunks[0]] + [None] * (groups - 1)
        for step in order:
            pairs = [(j, partner(j, step, groups)) for j in range(groups)]
            got[step] = lax.ppermute(chunks[step], "tm", pairs)
        received.append(got)
    return gram(received[0], received[1])


def solution(mesh):
    placed = (P(None, None, "chan", "tm"), P(), P())
    return jax.shard_map(
        shards,
        mesh=mesh,
        in_specs=placed,
        out_specs=P("tm", "chan", None, None, None),
        check_vma=False,
    )
```

time: 84.3 us -> 66.5 us (0.79); the launches traced: 84.1 us -> 65.2 us
  blocking collectives: 41.2 us -> 14.8 us
  local copies, waits for them, and re-layouts: 27.2 us -> 2.12 us
  waiting for transfers between devices: 1.08 us -> 22.4 us
  Pallas kernels: 0 us -> 10.6 us
  starting transfers between devices: 5.33 us -> 15.2 us
  other arithmetic: 5.91 us -> 0 us
  matrix products: 3.09 us -> 0 us
    all_to_all x1, blocking collectives: 41.2 us -> 14.8 us  [shards(): lax.all_to_all(voltages[k], 'chan', split_axis=0, concat_axis=1, tiled=True)]
    ppermute x0 -> x6, waiting for transfers between devices: none -> 21.2 us  [shards(): got[step] = lax.ppermute(chunks[step], 'tm', pairs)]
    ppermute x0 -> x6, starting transfers between devices: none -> 11.1 us  [shards(): got[step] = lax.ppermute(chunks[step], 'tm', pairs)]
    unnamed x12 -> x6, local copies, waits for them, and re-layouts: 11 us -> 0.01 us
    gather x2 -> x0, local copies, waits for them, and re-layouts: 11 us -> none  [the longest x1 10.4 us: compact(): picked = jnp.take(padded_voltages, rows, axis=2)]
    pallas_call x0 -> x4, Pallas kernels: none -> 10.6 us  [the longest x2 4.28 us: gather(): pl.pallas_call(gather_kernel, out_shape=[jax.ShapeDtypeStruct((per, slots...]
    another operation x6 -> x0, other arithmetic: 3.49 us -> none
    dot_general x4 -> x0, matrix products: 3.09 us -> none  [gram(): jnp.einsum('...pt,...qt->...pq', stacked, stacked, preferred_element_type...]
  transfers between devices with their start and end apart: 1 -> 7, of which waited for: 1 -> 4; matrix products, arithmetic and copies ran while one was open for 17% -> 0% of each run, Pallas kernels for 0% -> 10%
where the time goes in v1:
time: 66.5 us; the launch traced here: 65.2 us
  waiting for transfers between devices  22.4 us (34%)
  starting transfers between devices  15.2 us (23%)
  blocking collectives  14.8 us (22%)
  Pallas kernels  10.6 us (16%)
  local copies, waits for them, and re-layouts  2.12 us (3%)
    ppermute x6, waiting for transfers between devices, shards(): got[step] = lax.ppermute(chunks[step], 'tm', pairs)  21.2 us
    all_to_all x1, blocking collectives, shards(): lax.all_to_all(voltages[k], 'chan', split_axis=0, concat_axis=1, tiled=True)  14.8 us
    ppermute x6, starting transfers between devices, shards(): got[step] = lax.ppermute(chunks[step], 'tm', pairs)  11.1 us
    pallas_call x2, Pallas kernels, gather(): pl.pallas_call(gather_kernel, out_shape=[jax.ShapeDtypeStruct((per, slots...  4.28 us
    pallas_call x1, Pallas kernels, gram(): pl.pallas_call(gram_kernel, out_shape=jax.ShapeDtypeStruct((per, 1, 2, sl...  4.22 us
    all_to_all x1, starting transfers between devices, shards(): lax.all_to_all(voltages[k], 'chan', split_axis=0, concat_axis=1, tiled=True)  4.15 us
    squeeze x1, local copies, waits for them, and re-layouts, shards(): voltages[k]  2.11 us
    pallas_call x1, Pallas kernels, plan(): pl.pallas_call(functools.partial(plan_kernel, groups, half), out_shape=ja...  2.05 us
  transfers between devices with their start and end apart: 7, of which 4 were waited for; matrix products, arithmetic and copies ran while one was open for 0% of the time, Pallas kernels for 10%

profile of v1, /device:TPU:0, one launch (start us, length us, event | category | flops | bytes accessed | tf_op | source)
XLA Modules:
  0.0 65.2 jit_solution(13199429431172216413)
XLA Ops:
  0.0 0.0 copy-start.2
  0.0 0.0 copy-start.1
  0.0 2.1 %slice_bitcast_fusion = (bf16[8,256,128]{2,1,0:T(8,128)(2,1)}, bf16[8,256,128]{2,1,0:T(8,128)(2,1)S(1)}) fusion(bf16[2,8,256,128]{3,2,1,0:T(8,128)(2,1)} %param.3), kind=kLoop, calls=%fused_computation | loop fusion | bytes 2097152 | tf_op jit(solution)/shard_map/squeeze | solution.py:154
  2.1 14.8 %all_to_all.8 = bf16[8,256,128]{2,1,0:T(8,128)(2,1)} all-to-all(bf16[8,256,128]{2,1,0:T(8,128)(2,1)S(1)} %get-tuple-element.22), channel_id=1, replica_groups=mesh['chan'=8,'tm'=4] {'chan'}, dimensions={0} | all-to-all | bytes 1048576 | tf_op jit(solution)/shard_map/all_to_all | solution.py:154
  16.9 4.1 %all-to-all-start.1 = ((bf16[8,256,128]{2,1,0:T(8,128)(2,1)}), bf16[8,256,128]{2,1,0:T(8,128)(2,1)}, u32[]{:S(2)}, u32[]{:S(2)}) async-start(bf16[8,256,128]{2,1,0:T(8,128)(2,1)} %get-tuple-element.21), calls=%async_computation.1 | async-start | bytes 1048576 | tf_op jit(solution)/shard_map/all_to_all | solution.py:154
  21.1 0.0 copy-done.2
  21.1 0.0 copy-done.1
  21.1 0.0 copy-start
  21.1 2.1 %shard_map.37.select_ref = bf16[1536,1024]{1,0:T(8,128)(2,1)S(1)} custom-call(s32[8]{0:T(128)S(1)} %copy-done.2, s32[8,128]{1,0:T(8,128)S(1)} %bitcast.8), custom_call_target="tpu_custom_call" | custom-call | flops 4000000000 | bytes 3000000 | tf_op jit(solution)/shard_map/pallas_call | solution.py:69
  23.2 0.0 copy-done
  23.2 2.0 %shard_map.38 = (bf16[2,384,128]{2,1,0:T(8,128)(2,1)S(1)}, bf16[2,384,128]{2,1,0:T(8,128)(2,1)}, bf16[2,384,128]{2,1,0:T(8,128)(2,1)}, bf16[2,384,128]{2,1,0:T(8,128)(2,1)}) custom-call(bf16[1536,1024]{1,0:T(8,128)(2,1)S(1)} %shard_map.37.select_ref, bf16[2048,128]{1,0:T(8,128)(2,1)S(1)} %bitcast.7), custom_call_target="tpu_custom_call" | custom-call | flops 805306368 | bytes 4000000 | tf_op jit(solution)/shard_map/pallas_call | solution.py:100
  25.1 1.6 %collective-permute-start = (bf16[2,384,128]{2,1,0:T(8,128)(2,1)}, bf16[2,384,128]{2,1,0:T(8,128)(2,1)S(1)}, u32[]{:S(2)}, u32[]{:S(2)}) collective-permute-start(bf16[2,384,128]{2,1,0:T(8,128)(2,1)} %get-tuple-element.14), channel_id=1, source_target_pairs={{0,1},{1,0},{2,3},{3,2},{4,5},{5,4},{6,7},{7,6},{8,9},{9,8},{10,11... | collective-permute-start | bytes 589832 | tf_op jit(solution)/shard_map/ppermute | solution.py:160
  26.7 2.6 %collective-permute-start.1 = (bf16[2,384,128]{2,1,0:T(8,128)(2,1)}, bf16[2,384,128]{2,1,0:T(8,128)(2,1)}, u32[]{:S(2)}, u32[]{:S(2)}) collective-permute-start(bf16[2,384,128]{2,1,0:T(8,128)(2,1)} %get-tuple-element.15), channel_id=1, source_target_pairs={{0,2},{1,3},{2,0},{3,1},{4,6},{5,7},{6,4},{7,5},{8,10},{9,11},{10,... | collective-permute-start | bytes 589832 | tf_op jit(solution)/shard_map/ppermute | solution.py:160
  29.3 0.2 collective-permute-start.2
  29.5 1.3 %all-to-all-done.1 = bf16[8,256,128]{2,1,0:T(8,128)(2,1)} async-done(((bf16[8,256,128]{2,1,0:T(8,128)(2,1)}), bf16[8,256,128]{2,1,0:T(8,128)(2,1)}, u32[]{:S(2)}, u32[]{:S(2)}) %all-to-all-start.1) | async-done | bytes 524320 | tf_op jit(solution)/shard_map/all_to_all | solution.py:154
  30.8 2.3 %shard_map.39 = (bf16[2,384,128]{2,1,0:T(8,128)(2,1)S(1)}, bf16[2,384,128]{2,1,0:T(8,128)(2,1)S(1)}, bf16[2,384,128]{2,1,0:T(8,128)(2,1)S(1)}, bf16[2,384,128]{2,1,0:T(8,128)(2,1)S(1)}) custom-call(bf16[1536,1024]{1,0:T(8,128)(2,1)S(1)} %shard_map.37.select_ref, bf16[2048,128]{1,0:T(8,128)(2,1)} %bitcast.4.x_ref), custom_call_target="tpu_custom_call" | custom-call | flops 805306368 | bytes 4000000 | tf_op jit(solution)/shard_map/pallas_call | solution.py:100
  33.1 1.6 %collective-permute-start.3 = (bf16[2,384,128]{2,1,0:T(8,128)(2,1)S(1)}, bf16[2,384,128]{2,1,0:T(8,128)(2,1)S(1)}, u32[]{:S(2)}, u32[]{:S(2)}) collective-permute-start(bf16[2,384,128]{2,1,0:T(8,128)(2,1)S(1)} %get-tuple-element.18), channel_id=1, source_target_pairs={{0,1},{1,0},{2,3},{3,2},{4,5},{5,4},{6,7},{7,6},{8,9},{9,8},{10,11... | collective-permute-start | bytes 589832 | tf_op jit(solution)/shard_map/ppermute | solution.py:160
  34.8 2.6 %collective-permute-start.4 = (bf16[2,384,128]{2,1,0:T(8,128)(2,1)S(1)}, bf16[2,384,128]{2,1,0:T(8,128)(2,1)S(1)}, u32[]{:S(2)}, u32[]{:S(2)}) collective-permute-start(bf16[2,384,128]{2,1,0:T(8,128)(2,1)S(1)} %get-tuple-element.19), channel_id=1, source_target_pairs={{0,2},{1,3},{2,0},{3,1},{4,6},{5,7},{6,4},{7,5},{8,10},{9,11},{10,... | collective-permute-start | bytes 589832 | tf_op jit(solution)/shard_map/ppermute | solution.py:160
  37.3 0.0 collective-permute-done.refs_1_
  37.4 2.5 %collective-permute-start.5 = (bf16[2,384,128]{2,1,0:T(8,128)(2,1)S(1)}, bf16[2,384,128]{2,1,0:T(8,128)(2,1)S(1)}, u32[]{:S(2)}, u32[]{:S(2)}) collective-permute-start(bf16[2,384,128]{2,1,0:T(8,128)(2,1)S(1)} %get-tuple-element.20), channel_id=1, source_target_pairs={{0,3},{1,2},{2,1},{3,0},{4,7},{5,6},{6,5},{7,4},{8,11},{9,10},{10,... | collective-permute-start | bytes 589832 | tf_op jit(solution)/shard_map/ppermute | solution.py:160
  39.8 4.4 %collective-permute-done.1.refs_2_ = bf16[2,384,128]{2,1,0:T(8,128)(2,1)} collective-permute-done((bf16[2,384,128]{2,1,0:T(8,128)(2,1)}, bf16[2,384,128]{2,1,0:T(8,128)(2,1)}, u32[]{:S(2)}, u32[]{:S(2)}) %collective-permute-start.1) | collective-permute-done | bytes 196640 | tf_op jit(solution)/shard_map/ppermute | solution.py:160
  44.2 0.0 collective-permute-done.2.refs_3_
  44.2 0.9 %collective-permute-done.3.refs_5_ = bf16[2,384,128]{2,1,0:T(8,128)(2,1)S(1)} collective-permute-done((bf16[2,384,128]{2,1,0:T(8,128)(2,1)S(1)}, bf16[2,384,128]{2,1,0:T(8,128)(2,1)S(1)}, u32[]{:S(2)}, u32[]{:S(2)}) %collective-permute-start.3) | collective-permute-done | bytes 196640 | tf_op jit(solution)/shard_map/ppermute | solution.py:160
  45.2 15.8 %collective-permute-done.4.refs_6_ = bf16[2,384,128]{2,1,0:T(8,128)(2,1)S(1)} collective-permute-done((bf16[2,384,128]{2,1,0:T(8,128)(2,1)S(1)}, bf16[2,384,128]{2,1,0:T(8,128)(2,1)S(1)}, u32[]{:S(2)}, u32[]{:S(2)}) %collective-permute-start.4) | collective-permute-done | bytes 196640 | tf_op jit(solution)/shard_map/ppermute | solution.py:160
  61.0 0.0 collective-permute-done.5.refs_7_
  61.0 4.2 %shard_map.40 = f32[2,1,2,384,384]{4,3,2,1,0:T(8,128)} custom-call(bf16[2,384,128]{2,1,0:T(8,128)(2,1)S(1)} %get-tuple-element.13.refs_0_, bf16[2,384,128]{2,1,0:T(8,128)(2,1)S(1)} %collective-permute-done.refs_1_, bf16[2,384,128]{2,1,0:T(8,128)(2,1)} %collective-permute-done.1.refs_2_, bf16[2,384,128]{2,1,0:T(8,128)(2,1)} %collective-permute-done.2.refs_3_, ...), custom_call_target="tpu_custom_call" | custom-call | flops 1200000000 | bytes 4000000 | tf_op jit(solution)/shard_map/pallas_call | solution.py:136
Async XLA Ops:
  0.0 21.1 %copy-start.2 = (s32[8]{0:T(128)S(1)}, s32[8]{0:T(128)}, u32[]{:S(2)}) copy-start(s32[8]{0:T(128)} %slot_ref.1) | copy-start | bytes 100
  0.0 21.1 %copy-start.1 = (s32[1024,1]{0,1:T(1,128)S(1)}, s32[1024,1]{0,1:T(1,128)}, u32[]{:S(2)}) copy-start(s32[1024,1]{0,1:T(1,128)} %param.4) | copy-start | bytes 12292
  16.9 13.9 %all-to-all-start.1 = ((bf16[8,256,128]{2,1,0:T(8,128)(2,1)}), bf16[8,256,128]{2,1,0:T(8,128)(2,1)}, u32[]{:S(2)}, u32[]{:S(2)}) async-start(bf16[8,256,128]{2,1,0:T(8,128)(2,1)} %get-tuple-element.21), calls=%async_computation.1 | async-start | bytes 1048576 | tf_op jit(solution)/shard_map/all_to_all | solution.py:154
  21.1 2.1 %copy-start = (bf16[8,256,128]{2,1,0:T(8,128)(2,1)S(1)}, bf16[8,256,128]{2,1,0:T(8,128)(2,1)}, u32[]{:S(2)}) copy-start(bf16[8,256,128]{2,1,0:T(8,128)(2,1)} %all_to_all.8) | copy-start | bytes 1572868
  25.1 12.2 %collective-permute-start = (bf16[2,384,128]{2,1,0:T(8,128)(2,1)}, bf16[2,384,128]{2,1,0:T(8,128)(2,1)S(1)}, u32[]{:S(2)}, u32[]{:S(2)}) collective-permute-start(bf16[2,384,128]{2,1,0:T(8,128)(2,1)} %get-tuple-element.14), channel_id=1, source_target_pairs={{0,1},{1,0},{2,3},{3,2},{4,5},{5,4},{6,7},{7,6},{8,9},{9,8},{10,11... | collective-permute-start | bytes 589832 | tf_op jit(solution)/shard_map/ppermute | solution.py:160
  26.7 17.5 %collective-permute-start.1 = (bf16[2,384,128]{2,1,0:T(8,128)(2,1)}, bf16[2,384,128]{2,1,0:T(8,128)(2,1)}, u32[]{:S(2)}, u32[]{:S(2)}) collective-permute-start(bf16[2,384,128]{2,1,0:T(8,128)(2,1)} %get-tuple-element.15), channel_id=1, source_target_pairs={{0,2},{1,3},{2,0},{3,1},{4,6},{5,7},{6,4},{7,5},{8,10},{9,11},{10,... | collective-permute-start | bytes 589832 | tf_op jit(solution)/shard_map/ppermute | solution.py:160
  29.3 14.9 %collective-permute-start.2 = (bf16[2,384,128]{2,1,0:T(8,128)(2,1)}, bf16[2,384,128]{2,1,0:T(8,128)(2,1)}, u32[]{:S(2)}, u32[]{:S(2)}) collective-permute-start(bf16[2,384,128]{2,1,0:T(8,128)(2,1)} %get-tuple-element.16), channel_id=1, source_target_pairs={{0,3},{1,2},{2,1},{3,0},{4,7},{5,6},{6,5},{7,4},{8,11},{9,10},{10,... | collective-permute-start | bytes 589832 | tf_op jit(solution)/shard_map/ppermute | solution.py:160
  33.1 12.1 %collective-permute-start.3 = (bf16[2,384,128]{2,1,0:T(8,128)(2,1)S(1)}, bf16[2,384,128]{2,1,0:T(8,128)(2,1)S(1)}, u32[]{:S(2)}, u32[]{:S(2)}) collective-permute-start(bf16[2,384,128]{2,1,0:T(8,128)(2,1)S(1)} %get-tuple-element.18), channel_id=1, source_target_pairs={{0,1},{1,0},{2,3},{3,2},{4,5},{5,4},{6,7},{7,6},{8,9},{9,8},{10,11... | collective-permute-start | bytes 589832 | tf_op jit(solution)/shard_map/ppermute | solution.py:160
  34.8 26.2 %collective-permute-start.4 = (bf16[2,384,128]{2,1,0:T(8,128)(2,1)S(1)}, bf16[2,384,128]{2,1,0:T(8,128)(2,1)S(1)}, u32[]{:S(2)}, u32[]{:S(2)}) collective-permute-start(bf16[2,384,128]{2,1,0:T(8,128)(2,1)S(1)} %get-tuple-element.19), channel_id=1, source_target_pairs={{0,2},{1,3},{2,0},{3,1},{4,6},{5,7},{6,4},{7,5},{8,10},{9,11},{10,... | collective-permute-start | bytes 589832 | tf_op jit(solution)/shard_map/ppermute | solution.py:160
  37.4 23.6 %collective-permute-start.5 = (bf16[2,384,128]{2,1,0:T(8,128)(2,1)S(1)}, bf16[2,384,128]{2,1,0:T(8,128)(2,1)S(1)}, u32[]{:S(2)}, u32[]{:S(2)}) collective-permute-start(bf16[2,384,128]{2,1,0:T(8,128)(2,1)S(1)} %get-tuple-element.20), channel_id=1, source_target_pairs={{0,3},{1,2},{2,1},{3,0},{4,7},{5,6},{6,5},{7,4},{8,11},{9,10},{10,... | collective-permute-start | bytes 589832 | tf_op jit(solution)/shard_map/ppermute | solution.py:160

commit v2 on v1

--- a/solution.py
+++ b/solution.py
@@ -6,6 +6,7 @@
 from jax.experimental import pallas as pl
 from jax.experimental.pallas import tpu as pltpu
 from jax.sharding import PartitionSpec as P
+
 
 SLOT = 384
 LANES = 128
@@ -76,13 +77,51 @@
     )(slot_subarray_index, assignment.reshape(antennas // LANES, LANES))
 
 
-def gather_kernel(select_ref, x_ref, *rest):
-    *outs, wide, pair, tall = rest
-    inputs = x_ref.shape[0]
+def split_kernel(steps, x_ref, *rest):
+    *outs, sem = rest
+    chunks, other = outs[:-1], outs[-1]
+    me = lax.axis_index("chan")
+    copies = [
+        pltpu.make_async_copy(x_ref.at[0, partner(me, step, len(steps))], chunk, sem.at[i])
+        for i, (step, chunk) in enumerate(zip(steps, chunks))
+    ]
+    copies.append(pltpu.make_async_copy(x_ref.at[1], other, sem.at[len(steps)]))
+    for copy in copies:
+        copy.start()
+    for copy in copies:
+        copy.wait()
+
+
+def split(voltages, steps):
+    _, chans, inputs, samples = voltages.shape
+    piece = jax.ShapeDtypeStruct((inputs, samples), voltages.dtype)
+    return pl.pallas_call(
+        functools.partial(split_kernel, steps),
+        out_shape=[piece] * len(steps) + [jax.ShapeDtypeStruct((chans, inputs, samples), voltages.dtype)],
+        in_specs=[pl.BlockSpec(memory_space=pltpu.HBM)],
+        out_specs=[VMEM] * (len(steps) + 1),
+        scratch_shapes=[pltpu.SemaphoreType.DMA((len(steps) + 1,))],
+        compiler_params=PARAMS,
+        cost_estimate=pl.CostEstimate(flops=1_000_000, bytes_accessed=2_000_000, transcendentals=0),
+    )(voltages)
+
+
+def gather_kernel(steps, outputs, select_ref, *rest):
+    xs, outs = rest[: len(steps)], rest[len(steps) : len(steps) + outputs]
+    wide, pair, tall = rest[len(steps) + outputs :]
+    inputs = xs[0].shape[0]
     antennas = inputs // 2
-    wide[...] = x_ref[...].astype(jnp.float32)
-    for pol in range(2):
-        pair[:, pol * LANES : (pol + 1) * LANES] = wide[pl.ds(pol, antennas, stride=2), :].astype(jnp.bfloat16)
+    me = lax.axis_index("chan")
+    for i, (step, x) in enumerate(zip(steps, xs)):
+        wide[i * inputs : (i + 1) * inputs] = x[...].astype(jnp.float32)
+        if len(steps) == 1:
+            top = 0
+        else:
+            top = pl.multiple_of(partner(me, step, len(steps)) * antennas, antennas)
+        for pol in range(2):
+            pair[pl.ds(top, antennas), pol * LANES : (pol + 1) * LANES] = wide[
+                pl.ds(i * inputs + pol, antennas, stride=2), :
+            ].astype(jnp.bfloat16)
     picked = jnp.dot(select_ref[...], pair[...], preferred_element_type=jnp.float32)
     rows = select_ref.shape[0]
     for pol in range(2):
@@ -94,16 +133,16 @@
             out[s] = tall[top : top + slots, :].astype(jnp.bfloat16)
 
 
-def gather(select, x, groups, per, slots):
-    inputs, samples = x.shape
+def gather(select, xs, steps, groups, per, slots):
+    _, samples = xs[0].shape
     rows, antennas = select.shape
     return pl.pallas_call(
-        gather_kernel,
+        functools.partial(gather_kernel, steps, groups),
         out_shape=[jax.ShapeDtypeStruct((per, slots, samples), jnp.bfloat16)] * groups,
-        in_specs=[VMEM, VMEM],
+        in_specs=[VMEM] * (1 + len(xs)),
         out_specs=[VMEM] * groups,
         scratch_shapes=[
-            pltpu.VMEM((inputs, samples), jnp.float32),
+            pltpu.VMEM((2 * antennas, samples), jnp.float32),
             pltpu.VMEM((antennas, 2 * samples), jnp.bfloat16),
             pltpu.VMEM((2 * rows, samples), jnp.float32),
         ],
@@ -111,61 +150,107 @@
         cost_estimate=pl.CostEstimate(
             flops=2 * rows * antennas * 2 * samples, bytes_accessed=4_000_000, transcendentals=0
         ),
-    )(select, x)
-
-
-def gram_kernel(*refs):
+    )(select, *xs)
+
+
+def products(real, imag, part):
+    right = jnp.concatenate([real, imag], axis=1)
+    left = right if part == 0 else jnp.concatenate([imag, -real], axis=1)
+    return lax.dot_general(left, right, (((1,), (1,)), ((), ())), preferred_element_type=jnp.float32)
+
+
+def early_kernel(*refs):
     *parts, out = refs
     count = len(parts) // 2
     for s in range(parts[0].shape[0]):
         for part in range(2):
             total = None
             for e in range(count):
-                real, imag = parts[e][s], parts[count + e][s]
-                right = jnp.concatenate([real, imag], axis=1)
-                left = right if part == 0 else jnp.concatenate([imag, -real], axis=1)
-                term = lax.dot_general(
-                    left, right, (((1,), (1,)), ((), ())), preferred_element_type=jnp.float32
-                )
+                term = products(parts[e][s], parts[count + e][s], part)
                 total = term if total is None else total + term
-            out[s, 0, part] = total
-
-
-def gram(real, imag):
-    per, slots, _ = real[0].shape
-    return pl.pallas_call(
-        gram_kernel,
+            out[s, part] = total
+
+
+def late_kernel(real, imag, so_far, out, stage, sem):
+    copies = []
+    for s in range(real.shape[0]):
+        for part in range(2):
+            stage[s, part] = so_far[s, part] + products(real[s], imag[s], part)
+            copy = pltpu.make_async_copy(stage.at[s, part], out.at[s, 0, part], sem.at[s, part])
+            copy.start()
+            copies.append(copy)
+    for copy in copies:
+        copy.wait()
+
+
+def gram(real, imag, last):
+    per, slots, samples = real[0].shape
+    early = [e for e in range(len(real)) if e != last]
+    flops = 2 * per * 2 * slots * slots * 2 * samples
+    so_far = pl.pallas_call(
+        early_kernel,
+        out_shape=jax.ShapeDtypeStruct((per, 2, slots, slots), jnp.float32),
+        in_specs=[VMEM] * (2 * len(early)),
+        out_specs=VMEM,
+        compiler_params=PARAMS,
+        cost_estimate=pl.CostEstimate(flops=flops * len(early), bytes_accessed=3_000_000, transcendentals=0),
+    )(*[real[e] for e in early], *[imag[e] for e in early])
+    return pl.pallas_call(
+        late_kernel,
         out_shape=jax.ShapeDtypeStruct((per, 1, 2, slots, slots), jnp.float32),
-        in_specs=[VMEM] * (2 * len(real)),
-        out_specs=VMEM,
-        compiler_params=PARAMS,
-        cost_estimate=pl.CostEstimate(flops=1_200_000_000, bytes_accessed=4_000_000, transcendentals=0),
-    )(*real, *imag)
-
-
-def shards(voltages, assignment, slot_subarray_index):
+        in_specs=[VMEM] * 3,
+        out_specs=pl.BlockSpec(memory_space=pl.ANY),
+        scratch_shapes=[
+            pltpu.VMEM((per, 2, slots, slots), jnp.float32),
+            pltpu.SemaphoreType.DMA((per, 2)),
+        ],
+        compiler_params=PARAMS,
+        cost_estimate=pl.CostEstimate(flops=flops, bytes_accessed=3_000_000, transcendentals=0),
+    )(real[last], imag[last], so_far)
+
+
+def exchange(chunks, order, groups):
+    got = list(chunks)
+    for step in order:
+        pairs = [(j, partner(j, step, groups)) for j in range(groups)]
+        got[step] = lax.ppermute(chunks[step], "tm", pairs)
+    return got
+
+
+def across(x):
+    x = lax.all_to_all(x, "chan", split_axis=0, concat_axis=1, tiled=True)
+    return x.reshape(x.shape[1], x.shape[2])
+
+
+def steps_of(voltages, assignment, slot_subarray_index):
     groups = lax.axis_size("tm")
+    chans = lax.axis_size("chan")
     subarrays = slot_subarray_index.shape[0]
     per = subarrays // groups
+    order = sorted(range(1, groups), reverse=True)
+    last = order[0]
+    if chans <= 8 and chans & (chans - 1) == 0:
+        steps = tuple(range(chans))
+        *chunks, imag = split(voltages, steps)
+        reals = list(chunks)
+        for step in (6, 7, 2, 3, 4, 5, 1):
+            if step < chans:
+                pairs = [(j, j ^ step) for j in range(chans)]
+                reals[step] = lax.ppermute(chunks[step], "chan", pairs)
+    else:
+        steps, imag = (0,), voltages[1]
+        reals = [across(voltages[0])]
     select = plan(assignment, slot_subarray_index, groups, SLOT // 2)
-    order = sorted(range(1, groups), reverse=True)
-    received = []
-    for k in range(2):
-        x = lax.all_to_all(voltages[k], "chan", split_axis=0, concat_axis=1, tiled=True)
-        x = x.reshape(x.shape[1], x.shape[2])
-        chunks = gather(select, x, groups, per, SLOT)
-        got = [chunks[0]] + [None] * (groups - 1)
-        for step in order:
-            pairs = [(j, partner(j, step, groups)) for j in range(groups)]
-            got[step] = lax.ppermute(chunks[step], "tm", pairs)
-        received.append(got)
-    return gram(received[0], received[1])
+    real = exchange(gather(select, reals, steps, groups, per, SLOT), order, groups)
+    imag = across(imag)
+    imag = exchange(gather(select, [imag], (0,), groups, per, SLOT), order[1:] + order[:1], groups)
+    return gram(real, imag, last)
 
 
 def solution(mesh):
     placed = (P(None, None, "chan", "tm"), P(), P())
     return jax.shard_map(
-        shards,
+        steps_of,
         mesh=mesh,
         in_specs=placed,
         out_specs=P("tm", "chan", None, None, None),

time: 66.5 us -> 65.4 us (0.983)
  the two profiles are of different devices: /device:TPU:0 before, /device:TPU:10 now
where the time goes in v2:
time: 65.4 us; the launch traced here: 65.1 us
  waiting for transfers between devices  30.9 us (47%)
  starting transfers between devices  18.9 us (29%)
  Pallas kernels  11.9 us (18%)
  local copies, waits for them, and re-layouts  3.24 us (5%)
    ppermute x6, waiting for transfers between devices, exchange(): got[step] = lax.ppermute(chunks[step], 'tm', pairs)  25 us
    ppermute x6, starting transfers between devices, exchange(): got[step] = lax.ppermute(chunks[step], 'tm', pairs)  8.21 us
    ppermute x7, waiting for transfers between devices, steps_of(): reals[step] = lax.ppermute(chunks[step], 'chan', pairs)  5.93 us
    all_to_all x1, starting transfers between devices, across(): x = lax.all_to_all(x, 'chan', split_axis=0, concat_axis=1, tiled=True)  5.52 us
    ppermute x7, starting transfers between devices, steps_of(): reals[step] = lax.ppermute(chunks[step], 'chan', pairs)  5.17 us
    pallas_call x2, Pallas kernels, gather(): pl.pallas_call(functools.partial(gather_kernel, steps, groups), out_shape...  4.23 us
    unnamed x10, local copies, waits for them, and re-layouts  3.24 us
    pallas_call x1, Pallas kernels, gram(): pl.pallas_call(early_kernel, out_shape=jax.ShapeDtypeStruct((per, 2, slot...  2.32 us
  transfers between devices with their start and end apart: 14, of which 9 were waited for; matrix products, arithmetic and copies ran while one was open for 0% of the time, Pallas kernels for 13%

profile of v2, /device:TPU:10, one launch (start us, length us, event | category | flops | bytes accessed | tf_op | source)
XLA Modules:
  0.0 65.1 jit_solution(2560319122250680164)
XLA Ops:
  0.0 0.0 copy-start
  0.0 1.2 %copy-done = bf16[2,8,256,128]{3,2,1,0:T(8,128)(2,1)S(1)} copy-done((bf16[2,8,256,128]{3,2,1,0:T(8,128)(2,1)S(1)}, bf16[2,8,256,128]{3,2,1,0:T(8,128)(2,1)}, u32[]{:S(2)}) %copy-start) | copy-done | bytes 1048600
  1.2 1.6 %shard_map.38 = (bf16[256,128]{1,0:T(8,128)(2,1)S(1)}, bf16[256,128]{1,0:T(8,128)(2,1)S(1)}, bf16[256,128]{1,0:T(8,128)(2,1)S(1)}, bf16[256,128]{1,0:T(8,128)(2,...) custom-call(bf16[2,8,256,128]{3,2,1,0:T(8,128)(2,1)S(1)} %copy-done), custom_call_target="tpu_custom_call" | custom-call | flops 1000000 | bytes 2000000 | tf_op jit(solution)/shard_map/pallas_call | solution.py:98
  2.8 0.1 collective-permute-start
  2.9 0.6 collective-permute-start.1
  3.5 5.5 %all-to-all-start = ((bf16[8,256,128]{2,1,0:T(8,128)(2,1)}), bf16[8,256,128]{2,1,0:T(8,128)(2,1)}, u32[]{:S(2)}, u32[]{:S(2)}) async-start(bf16[8,256,128]{2,1,0:T(8,128)(2,1)} %get-tuple-element.31), calls=%async_computation | async-start | bytes 1048576 | tf_op jit(solution)/shard_map/all_to_all | solution.py:221
  9.0 0.1 collective-permute-start.2
  9.2 1.7 %collective-permute-start.3 = (bf16[256,128]{1,0:T(8,128)(2,1)}, bf16[256,128]{1,0:T(8,128)(2,1)S(1)}, u32[]{:S(2)}, u32[]{:S(2)}) collective-permute-start(bf16[256,128]{1,0:T(8,128)(2,1)} %get-tuple-element.26), channel_id=1, source_target_pairs={{0,16},{4,20},{8,24},{12,28},{16,0},{20,4},{24,8},{28,12},{1,17},{... | collective-permute-start | bytes 196616 | tf_op jit(solution)/shard_map/ppermute | solution.py:239
  10.8 0.0 collective-permute-start.4
  10.8 0.0 collective-permute-done.rest_1_
  10.8 2.6 %collective-permute-start.5 = (bf16[256,128]{1,0:T(8,128)(2,1)S(1)}, bf16[256,128]{1,0:T(8,128)(2,1)S(1)}, u32[]{:S(2)}, u32[]{:S(2)}) collective-permute-start(bf16[256,128]{1,0:T(8,128)(2,1)S(1)} %get-tuple-element.28), channel_id=1, source_target_pairs={{0,24},{4,28},{8,16},{12,20},{16,8},{20,12},{24,0},{28,4},{1,25},{... | collective-permute-start | bytes 196616 | tf_op jit(solution)/shard_map/ppermute | solution.py:239
  13.5 0.0 collective-permute-done.1.rest_2_
  13.5 0.1 collective-permute-start.6
  13.6 0.0 copy-start.3
  13.6 0.7 %copy-done.3 = s32[1024,1]{0,1:T(1,128)S(1)} copy-done((s32[1024,1]{0,1:T(1,128)S(1)}, s32[1024,1]{0,1:T(1,128)}, u32[]{:S(2)}) %copy-start.3) | copy-done | bytes 4120
  14.2 0.0 copy-start.4
  14.2 0.7 %copy-done.4 = s32[8]{0:T(128)S(1)} copy-done((s32[8]{0:T(128)S(1)}, s32[8]{0:T(128)}, u32[]{:S(2)}) %copy-start.4) | copy-done | bytes 56
  14.9 2.1 %shard_map.37.select_ref = bf16[1536,1024]{1,0:T(8,128)(2,1)S(1)} custom-call(s32[8]{0:T(128)S(1)} %copy-done.4, s32[8,128]{1,0:T(8,128)S(1)} %bitcast.2), custom_call_target="tpu_custom_call" | custom-call | flops 4000000000 | bytes 3000000 | tf_op jit(solution)/shard_map/pallas_call | solution.py:70
  17.0 0.5 collective-permute-done.2.rest_3_
  17.5 1.9 %collective-permute-done.3.rest_4_ = bf16[256,128]{1,0:T(8,128)(2,1)S(1)} collective-permute-done((bf16[256,128]{1,0:T(8,128)(2,1)}, bf16[256,128]{1,0:T(8,128)(2,1)S(1)}, u32[]{:S(2)}, u32[]{:S(2)}) %collective-permute-start.3) | collective-permute-done | bytes 65568 | tf_op jit(solution)/shard_map/ppermute | solution.py:239
  19.3 3.5 %collective-permute-done.4.rest_5_ = bf16[256,128]{1,0:T(8,128)(2,1)S(1)} collective-permute-done((bf16[256,128]{1,0:T(8,128)(2,1)S(1)}, bf16[256,128]{1,0:T(8,128)(2,1)S(1)}, u32[]{:S(2)}, u32[]{:S(2)}) %collective-permute-start.4) | collective-permute-done | bytes 65568 | tf_op jit(solution)/shard_map/ppermute | solution.py:239
  22.9 0.0 collective-permute-done.5.rest_6_
  22.9 0.0 collective-permute-done.6.rest_7_
  22.9 1.9 %shard_map.39 = (bf16[2,384,128]{2,1,0:T(8,128)(2,1)S(1)}, bf16[2,384,128]{2,1,0:T(8,128)(2,1)}, bf16[2,384,128]{2,1,0:T(8,128)(2,1)}, bf16[2,384,128]{2,1,0:T(8,128)(2,1)S(1)}) custom-call(bf16[1536,1024]{1,0:T(8,128)(2,1)S(1)} %shard_map.37.select_ref, bf16[256,128]{1,0:T(8,128)(2,1)S(1)} %get-tuple-element.22.rest_0_, ...), custom_call_target="tpu_custom_call" | custom-call | flops 805306368 | bytes 4000000 | tf_op jit(solution)/shard_map/pallas_call | solution.py:139
  24.8 0.0 copy-start.1
  24.8 0.7 %copy-done.1 = bf16[2,384,128]{2,1,0:T(8,128)(2,1)} copy-done((bf16[2,384,128]{2,1,0:T(8,128)(2,1)}, bf16[2,384,128]{2,1,0:T(8,128)(2,1)S(1)}, u32[]{:S(2)}) %copy-start.1) | copy-done | bytes 196632
  25.4 0.4 collective-permute-start.9
  25.9 2.6 %collective-permute-start.10 = (bf16[2,384,128]{2,1,0:T(8,128)(2,1)}, bf16[2,384,128]{2,1,0:T(8,128)(2,1)}, u32[]{:S(2)}, u32[]{:S(2)}) collective-permute-start(bf16[2,384,128]{2,1,0:T(8,128)(2,1)} %get-tuple-element.35), channel_id=1, source_target_pairs={{0,2},{1,3},{2,0},{3,1},{4,6},{5,7},{6,4},{7,5},{8,10},{9,11},{10,... | collective-permute-start | bytes 589832 | tf_op jit(solution)/shard_map/ppermute | solution.py:216
  28.5 0.0 all-to-all-done
  28.5 0.0 copy-start.2
  28.5 2.3 %shard_map.40 = (bf16[2,384,128]{2,1,0:T(8,128)(2,1)S(1)}, bf16[2,384,128]{2,1,0:T(8,128)(2,1)S(1)}, bf16[2,384,128]{2,1,0:T(8,128)(2,1)S(1)}, bf16[2,384,128]{2,1,0:T(8,128)(2,1)S(1)}) custom-call(bf16[1536,1024]{1,0:T(8,128)(2,1)S(1)} %shard_map.37.select_ref, bf16[2048,128]{1,0:T(8,128)(2,1)} %bitcast.1.rest_0_), custom_call_target="tpu_custom_call" | custom-call | flops 805306368 | bytes 4000000 | tf_op jit(solution)/shard_map/pallas_call | solution.py:139
  30.8 1.6 %collective-permute-start.11 = (bf16[2,384,128]{2,1,0:T(8,128)(2,1)S(1)}, bf16[2,384,128]{2,1,0:T(8,128)(2,1)S(1)}, u32[]{:S(2)}, u32[]{:S(2)}) collective-permute-start(bf16[2,384,128]{2,1,0:T(8,128)(2,1)S(1)} %get-tuple-element.37), channel_id=1, source_target_pairs={{0,1},{1,0},{2,3},{3,2},{4,5},{5,4},{6,7},{7,6},{8,9},{9,8},{10,11... | collective-permute-start | bytes 589832 | tf_op jit(solution)/shard_map/ppermute | solution.py:216
  32.5 0.3 collective-permute-start.12
  32.8 0.0 copy-done.2
  32.8 1.6 %collective-permute-start.7 = (bf16[2,384,128]{2,1,0:T(8,128)(2,1)S(1)}, bf16[2,384,128]{2,1,0:T(8,128)(2,1)S(1)}, u32[]{:S(2)}, u32[]{:S(2)}) collective-permute-start(bf16[2,384,128]{2,1,0:T(8,128)(2,1)S(1)} %copy-done.2), channel_id=1, source_target_pairs={{0,3},{1,2},{2,1},{3,0},{4,7},{5,6},{6,5},{7,4},{8,11},{9,10},{10,... | collective-permute-start | bytes 589832 | tf_op jit(solution)/shard_map/ppermute | solution.py:216
  34.4 1.2 %collective-permute-done.9.refs_1_ = bf16[2,384,128]{2,1,0:T(8,128)(2,1)S(1)} collective-permute-done((bf16[2,384,128]{2,1,0:T(8,128)(2,1)}, bf16[2,384,128]{2,1,0:T(8,128)(2,1)S(1)}, u32[]{:S(2)}, u32[]{:S(2)}) %collective-permute-start.9) | collective-permute-done | bytes 196640 | tf_op jit(solution)/shard_map/ppermute | solution.py:216
  35.6 1.6 %collective-permute-start.8 = (bf16[2,384,128]{2,1,0:T(8,128)(2,1)S(1)}, bf16[2,384,128]{2,1,0:T(8,128)(2,1)S(1)}, u32[]{:S(2)}, u32[]{:S(2)}) collective-permute-start(bf16[2,384,128]{2,1,0:T(8,128)(2,1)S(1)} %get-tuple-element.32), channel_id=1, source_target_pairs={{0,3},{1,2},{2,1},{3,0},{4,7},{5,6},{6,5},{7,4},{8,11},{9,10},{10,... | collective-permute-start | bytes 589832 | tf_op jit(solution)/shard_map/ppermute | solution.py:216
  37.2 1.6 %collective-permute-done.10.refs_2_ = bf16[2,384,128]{2,1,0:T(8,128)(2,1)} collective-permute-done((bf16[2,384,128]{2,1,0:T(8,128)(2,1)}, bf16[2,384,128]{2,1,0:T(8,128)(2,1)}, u32[]{:S(2)}, u32[]{:S(2)}) %collective-permute-start.10) | collective-permute-done | bytes 196640 | tf_op jit(solution)/shard_map/ppermute | solution.py:216
  38.8 4.2 %collective-permute-done.11.refs_4_ = bf16[2,384,128]{2,1,0:T(8,128)(2,1)S(1)} collective-permute-done((bf16[2,384,128]{2,1,0:T(8,128)(2,1)S(1)}, bf16[2,384,128]{2,1,0:T(8,128)(2,1)S(1)}, u32[]{:S(2)}, u32[]{:S(2)}) %collective-permute-start.11) | collective-permute-done | bytes 196640 | tf_op jit(solution)/shard_map/ppermute | solution.py:216
  43.0 12.1 %collective-permute-done.12.refs_5_ = bf16[2,384,128]{2,1,0:T(8,128)(2,1)S(1)} collective-permute-done((bf16[2,384,128]{2,1,0:T(8,128)(2,1)S(1)}, bf16[2,384,128]{2,1,0:T(8,128)(2,1)S(1)}, u32[]{:S(2)}, u32[]{:S(2)}) %collective-permute-start.12) | collective-permute-done | bytes 196640 | tf_op jit(solution)/shard_map/ppermute | solution.py:216
  55.1 2.3 %shard_map.41.so_far = f32[2,2,384,384]{3,2,1,0:T(8,128)S(1)} custom-call(bf16[2,384,128]{2,1,0:T(8,128)(2,1)S(1)} %get-tuple-element.33.refs_0_, bf16[2,384,128]{2,1,0:T(8,128)(2,1)S(1)} %collective-permute-done.9.refs_1_, bf16[2,384,128]{2,1,0:T(8,128)(2,1)} %collective-permute-done.10.refs_2_, bf16[2,384,128]{2,1,0:T(8,128)(2,1)S(1)} %get-tuple-element.36.refs_3_, ...), custom_call_target="tpu_custom_call" | custom-call | flops 905969664 | bytes 3000000 | tf_op jit(solution)/shard_map/pallas_call | solution.py:190
  57.4 2.0 %collective-permute-done.7.real = bf16[2,384,128]{2,1,0:T(8,128)(2,1)S(1)} collective-permute-done((bf16[2,384,128]{2,1,0:T(8,128)(2,1)S(1)}, bf16[2,384,128]{2,1,0:T(8,128)(2,1)S(1)}, u32[]{:S(2)}, u32[]{:S(2)}) %collective-permute-start.7) | collective-permute-done | bytes 196640 | tf_op jit(solution)/shard_map/ppermute | solution.py:216
  59.4 3.9 %collective-permute-done.8.imag = bf16[2,384,128]{2,1,0:T(8,128)(2,1)S(1)} collective-permute-done((bf16[2,384,128]{2,1,0:T(8,128)(2,1)S(1)}, bf16[2,384,128]{2,1,0:T(8,128)(2,1)S(1)}, u32[]{:S(2)}, u32[]{:S(2)}) %collective-permute-start.8) | collective-permute-done | bytes 196640 | tf_op jit(solution)/shard_map/ppermute | solution.py:216
  63.3 1.7 %shard_map.42 = f32[2,1,2,384,384]{4,3,2,1,0:T(8,128)} custom-call(bf16[2,384,128]{2,1,0:T(8,128)(2,1)S(1)} %collective-permute-done.7.real, bf16[2,384,128]{2,1,0:T(8,128)(2,1)S(1)} %collective-permute-done.8.imag, f32[2,2,384,384]{3,2,1,0:T(8,128)S(1)} %shard_map.41.so_far), custom_call_target="tpu_custom_call" | custom-call | flops 301989888 | bytes 3000000 | tf_op jit(solution)/shard_map/pallas_call | solution.py:198
Async XLA Ops:
  0.0 1.2 %copy-start = (bf16[2,8,256,128]{3,2,1,0:T(8,128)(2,1)S(1)}, bf16[2,8,256,128]{3,2,1,0:T(8,128)(2,1)}, u32[]{:S(2)}) copy-start(bf16[2,8,256,128]{3,2,1,0:T(8,128)(2,1)} %x_ref.1) | copy-start | bytes 3145732
  2.8 8.0 %collective-permute-start = (bf16[256,128]{1,0:T(8,128)(2,1)S(1)}, bf16[256,128]{1,0:T(8,128)(2,1)S(1)}, u32[]{:S(2)}, u32[]{:S(2)}) collective-permute-start(bf16[256,128]{1,0:T(8,128)(2,1)S(1)} %get-tuple-element.23), channel_id=1, source_target_pairs={{0,4},{4,0},{8,12},{12,8},{16,20},{20,16},{24,28},{28,24},{1,5},{5... | collective-permute-start | bytes 196616 | tf_op jit(solution)/shard_map/ppermute | solution.py:239
  2.9 10.5 %collective-permute-start.1 = (bf16[256,128]{1,0:T(8,128)(2,1)S(1)}, bf16[256,128]{1,0:T(8,128)(2,1)S(1)}, u32[]{:S(2)}, u32[]{:S(2)}) collective-permute-start(bf16[256,128]{1,0:T(8,128)(2,1)S(1)} %get-tuple-element.24), channel_id=1, source_target_pairs={{0,8},{4,12},{8,0},{12,4},{16,24},{20,28},{24,16},{28,20},{1,9},{5... | collective-permute-start | bytes 196616 | tf_op jit(solution)/shard_map/ppermute | solution.py:239
  3.5 25.0 %all-to-all-start = ((bf16[8,256,128]{2,1,0:T(8,128)(2,1)}), bf16[8,256,128]{2,1,0:T(8,128)(2,1)}, u32[]{:S(2)}, u32[]{:S(2)}) async-start(bf16[8,256,128]{2,1,0:T(8,128)(2,1)} %get-tuple-element.31), calls=%async_computation | async-start | bytes 1048576 | tf_op jit(solution)/shard_map/all_to_all | solution.py:221
  9.0 8.4 %collective-permute-start.2 = (bf16[256,128]{1,0:T(8,128)(2,1)}, bf16[256,128]{1,0:T(8,128)(2,1)S(1)}, u32[]{:S(2)}, u32[]{:S(2)}) collective-permute-start(bf16[256,128]{1,0:T(8,128)(2,1)} %get-tuple-element.25), channel_id=1, source_target_pairs={{0,12},{4,8},{8,4},{12,0},{16,28},{20,24},{24,20},{28,16},{1,13},{... | collective-permute-start | bytes 196616 | tf_op jit(solution)/shard_map/ppermute | solution.py:239
  9.2 10.2 %collective-permute-start.3 = (bf16[256,128]{1,0:T(8,128)(2,1)}, bf16[256,128]{1,0:T(8,128)(2,1)S(1)}, u32[]{:S(2)}, u32[]{:S(2)}) collective-permute-start(bf16[256,128]{1,0:T(8,128)(2,1)} %get-tuple-element.26), channel_id=1, source_target_pairs={{0,16},{4,20},{8,24},{12,28},{16,0},{20,4},{24,8},{28,12},{1,17},{... | collective-permute-start | bytes 196616 | tf_op jit(solution)/shard_map/ppermute | solution.py:239
  10.8 12.1 %collective-permute-start.4 = (bf16[256,128]{1,0:T(8,128)(2,1)S(1)}, bf16[256,128]{1,0:T(8,128)(2,1)S(1)}, u32[]{:S(2)}, u32[]{:S(2)}) collective-permute-start(bf16[256,128]{1,0:T(8,128)(2,1)S(1)} %get-tuple-element.27), channel_id=1, source_target_pairs={{0,20},{4,16},{8,28},{12,24},{16,4},{20,0},{24,12},{28,8},{1,21},{... | collective-permute-start | bytes 196616 | tf_op jit(solution)/shard_map/ppermute | solution.py:239
  10.8 12.1 %collective-permute-start.5 = (bf16[256,128]{1,0:T(8,128)(2,1)S(1)}, bf16[256,128]{1,0:T(8,128)(2,1)S(1)}, u32[]{:S(2)}, u32[]{:S(2)}) collective-permute-start(bf16[256,128]{1,0:T(8,128)(2,1)S(1)} %get-tuple-element.28), channel_id=1, source_target_pairs={{0,24},{4,28},{8,16},{12,20},{16,8},{20,12},{24,0},{28,4},{1,25},{... | collective-permute-start | bytes 196616 | tf_op jit(solution)/shard_map/ppermute | solution.py:239
  13.5 9.4 %collective-permute-start.6 = (bf16[256,128]{1,0:T(8,128)(2,1)S(1)}, bf16[256,128]{1,0:T(8,128)(2,1)S(1)}, u32[]{:S(2)}, u32[]{:S(2)}) collective-permute-start(bf16[256,128]{1,0:T(8,128)(2,1)S(1)} %get-tuple-element.29), channel_id=1, source_target_pairs={{0,28},{4,24},{8,20},{12,16},{16,12},{20,8},{24,4},{28,0},{1,29},{... | collective-permute-start | bytes 196616 | tf_op jit(solution)/shard_map/ppermute | solution.py:239
  13.6 0.7 %copy-start.3 = (s32[1024,1]{0,1:T(1,128)S(1)}, s32[1024,1]{0,1:T(1,128)}, u32[]{:S(2)}) copy-start(s32[1024,1]{0,1:T(1,128)} %param.4) | copy-start | bytes 12292
  14.2 0.7 %copy-start.4 = (s32[8]{0:T(128)S(1)}, s32[8]{0:T(128)}, u32[]{:S(2)}) copy-start(s32[8]{0:T(128)} %slot_ref.1) | copy-start | bytes 100
  24.8 0.7 %copy-start.1 = (bf16[2,384,128]{2,1,0:T(8,128)(2,1)}, bf16[2,384,128]{2,1,0:T(8,128)(2,1)S(1)}, u32[]{:S(2)}) copy-start(bf16[2,384,128]{2,1,0:T(8,128)(2,1)S(1)} %get-tuple-element.30) | copy-start | bytes 589828
  25.4 10.2 %collective-permute-start.9 = (bf16[2,384,128]{2,1,0:T(8,128)(2,1)}, bf16[2,384,128]{2,1,0:T(8,128)(2,1)S(1)}, u32[]{:S(2)}, u32[]{:S(2)}) collective-permute-start(bf16[2,384,128]{2,1,0:T(8,128)(2,1)} %get-tuple-element.34), channel_id=1, source_target_pairs={{0,1},{1,0},{2,3},{3,2},{4,5},{5,4},{6,7},{7,6},{8,9},{9,8},{10,11... | collective-permute-start | bytes 589832 | tf_op jit(solution)/shard_map/ppermute | solution.py:216
  25.9 12.9 %collective-permute-start.10 = (bf16[2,384,128]{2,1,0:T(8,128)(2,1)}, bf16[2,384,128]{2,1,0:T(8,128)(2,1)}, u32[]{:S(2)}, u32[]{:S(2)}) collective-permute-start(bf16[2,384,128]{2,1,0:T(8,128)(2,1)} %get-tuple-element.35), channel_id=1, source_target_pairs={{0,2},{1,3},{2,0},{3,1},{4,6},{5,7},{6,4},{7,5},{8,10},{9,11},{10,... | collective-permute-start | bytes 589832 | tf_op jit(solution)/shard_map/ppermute | solution.py:216
  28.5 4.3 %copy-start.2 = (bf16[2,384,128]{2,1,0:T(8,128)(2,1)S(1)}, bf16[2,384,128]{2,1,0:T(8,128)(2,1)}, u32[]{:S(2)}) copy-start(bf16[2,384,128]{2,1,0:T(8,128)(2,1)} %copy-done.1) | copy-start | bytes 589828
  30.8 12.1 %collective-permute-start.11 = (bf16[2,384,128]{2,1,0:T(8,128)(2,1)S(1)}, bf16[2,384,128]{2,1,0:T(8,128)(2,1)S(1)}, u32[]{:S(2)}, u32[]{:S(2)}) collective-permute-start(bf16[2,384,128]{2,1,0:T(8,128)(2,1)S(1)} %get-tuple-element.37), channel_id=1, source_target_pairs={{0,1},{1,0},{2,3},{3,2},{4,5},{5,4},{6,7},{7,6},{8,9},{9,8},{10,11... | collective-permute-start | bytes 589832 | tf_op jit(solution)/shard_map/ppermute | solution.py:216
  32.5 22.6 %collective-permute-start.12 = (bf16[2,384,128]{2,1,0:T(8,128)(2,1)S(1)}, bf16[2,384,128]{2,1,0:T(8,128)(2,1)S(1)}, u32[]{:S(2)}, u32[]{:S(2)}) collective-permute-start(bf16[2,384,128]{2,1,0:T(8,128)(2,1)S(1)} %get-tuple-element.38), channel_id=1, source_target_pairs={{0,2},{1,3},{2,0},{3,1},{4,6},{5,7},{6,4},{7,5},{8,10},{9,11},{10,... | collective-permute-start | bytes 589832 | tf_op jit(solution)/shard_map/ppermute | solution.py:216
  32.8 26.6 %collective-permute-start.7 = (bf16[2,384,128]{2,1,0:T(8,128)(2,1)S(1)}, bf16[2,384,128]{2,1,0:T(8,128)(2,1)S(1)}, u32[]{:S(2)}, u32[]{:S(2)}) collective-permute-start(bf16[2,384,128]{2,1,0:T(8,128)(2,1)S(1)} %copy-done.2), channel_id=1, source_target_pairs={{0,3},{1,2},{2,1},{3,0},{4,7},{5,6},{6,5},{7,4},{8,11},{9,10},{10,... | collective-permute-start | bytes 589832 | tf_op jit(solution)/shard_map/ppermute | solution.py:216
  35.6 27.7 %collective-permute-start.8 = (bf16[2,384,128]{2,1,0:T(8,128)(2,1)S(1)}, bf16[2,384,128]{2,1,0:T(8,128)(2,1)S(1)}, u32[]{:S(2)}, u32[]{:S(2)}) collective-permute-start(bf16[2,384,128]{2,1,0:T(8,128)(2,1)S(1)} %get-tuple-element.32), channel_id=1, source_target_pairs={{0,3},{1,2},{2,1},{3,0},{4,7},{5,6},{6,5},{7,4},{8,11},{9,10},{10,... | collective-permute-start | bytes 589832 | tf_op jit(solution)/shard_map/ppermute | solution.py:216

commit v3 on v2

--- a/solution.py
+++ b/solution.py
@@ -10,6 +10,7 @@
 
 SLOT = 384
 LANES = 128
+
 
 VMEM = pl.BlockSpec(memory_space=pltpu.VMEM)
 SMEM = pl.BlockSpec(memory_space=pltpu.SMEM)
@@ -77,38 +78,54 @@
     )(slot_subarray_index, assignment.reshape(antennas // LANES, LANES))
 
 
-def split_kernel(steps, x_ref, *rest):
+def split_kernel(chans, x_ref, *rest):
     *outs, sem = rest
-    chunks, other = outs[:-1], outs[-1]
     me = lax.axis_index("chan")
-    copies = [
-        pltpu.make_async_copy(x_ref.at[0, partner(me, step, len(steps))], chunk, sem.at[i])
-        for i, (step, chunk) in enumerate(zip(steps, chunks))
-    ]
-    copies.append(pltpu.make_async_copy(x_ref.at[1], other, sem.at[len(steps)]))
+    early = chans // 2
+    wanted = [(x_ref.at[1, me ^ (2 * r + (me & 1))], outs[0].at[r]) for r in range(early)]
+    for k in range(2):
+        wanted += [(x_ref.at[k, me ^ s], outs[1 + k * chans + s]) for s in range(chans)]
+    copies = [pltpu.make_async_copy(a, b, sem.at[i]) for i, (a, b) in enumerate(wanted)]
     for copy in copies:
         copy.start()
     for copy in copies:
         copy.wait()
 
 
-def split(voltages, steps):
+def split(voltages):
     _, chans, inputs, samples = voltages.shape
     piece = jax.ShapeDtypeStruct((inputs, samples), voltages.dtype)
-    return pl.pallas_call(
-        functools.partial(split_kernel, steps),
-        out_shape=[piece] * len(steps) + [jax.ShapeDtypeStruct((chans, inputs, samples), voltages.dtype)],
+    raw = jax.ShapeDtypeStruct((chans // 2, inputs, samples), voltages.dtype)
+    out = pl.pallas_call(
+        functools.partial(split_kernel, chans),
+        out_shape=[raw] + [piece] * (2 * chans),
         in_specs=[pl.BlockSpec(memory_space=pltpu.HBM)],
-        out_specs=[VMEM] * (len(steps) + 1),
-        scratch_shapes=[pltpu.SemaphoreType.DMA((len(steps) + 1,))],
+        out_specs=[VMEM] * (2 * chans + 1),
+        scratch_shapes=[pltpu.SemaphoreType.DMA((2 * chans + chans // 2,))],
         compiler_params=PARAMS,
         cost_estimate=pl.CostEstimate(flops=1_000_000, bytes_accessed=2_000_000, transcendentals=0),
     )(voltages)
-
-
-def gather_kernel(steps, outputs, select_ref, *rest):
-    xs, outs = rest[: len(steps)], rest[len(steps) : len(steps) + outputs]
-    wide, pair, tall = rest[len(steps) + outputs :]
+    return out[0], out[1 : 1 + chans], out[1 + chans :]
+
+
+def unstack_kernel(x_ref, *outs):
+    for r, out in enumerate(outs):
+        out[...] = x_ref[r]
+
+
+def unstack(x):
+    count, inputs, samples = x.shape
+    return pl.pallas_call(
+        unstack_kernel,
+        out_shape=[jax.ShapeDtypeStruct((inputs, samples), x.dtype)] * count,
+        in_specs=[VMEM],
+        out_specs=[VMEM] * count,
+        compiler_params=PARAMS,
+        cost_estimate=pl.CostEstimate(flops=1_000_000, bytes_accessed=500_000, transcendentals=0),
+    )(x)
+
+
+def load_pair(steps, xs, wide, pair):
     inputs = xs[0].shape[0]
     antennas = inputs // 2
     me = lax.axis_index("chan")
@@ -122,8 +139,10 @@
             pair[pl.ds(top, antennas), pol * LANES : (pol + 1) * LANES] = wide[
                 pl.ds(i * inputs + pol, antennas, stride=2), :
             ].astype(jnp.bfloat16)
-    picked = jnp.dot(select_ref[...], pair[...], preferred_element_type=jnp.float32)
-    rows = select_ref.shape[0]
+
+
+def store_rows(picked, tall, outs):
+    rows = picked.shape[0]
     for pol in range(2):
         tall[pl.ds(pol, rows, stride=2), :] = picked[:, pol * LANES : (pol + 1) * LANES]
     per, slots, _ = outs[0].shape
@@ -131,6 +150,50 @@
         for s in range(per):
             top = (g * per + s) * slots
             out[s] = tall[top : top + slots, :].astype(jnp.bfloat16)
+
+
+def gather_kernel(steps, outputs, select_ref, *rest):
+    xs, outs = rest[: len(steps)], rest[len(steps) : len(steps) + outputs]
+    wide, pair, tall = rest[len(steps) + outputs :]
+    load_pair(steps, xs, wide, pair)
+    picked = jnp.dot(select_ref[...], pair[...], preferred_element_type=jnp.float32)
+    store_rows(picked, tall, outs)
+
+
+def twin_kernel(steps, select_ref, *rest):
+    count = len(steps)
+    own, other = rest[:count], rest[count : 2 * count]
+    outs = rest[2 * count : 2 * count + 4]
+    wide, pair, tall = rest[2 * count + 4 :]
+    odd = lax.axis_index("chan") & 1
+    rows = select_ref.shape[0] // 2
+    load_pair(steps, own, wide.at[0], pair.at[0])
+    picked = jnp.dot(select_ref[:rows], pair[0], preferred_element_type=jnp.float32)
+    store_rows(picked, tall.at[0], outs[:2])
+    load_pair(steps, other, wide.at[1], pair.at[1])
+    top = pl.multiple_of(odd * rows, rows)
+    picked = jnp.dot(select_ref[pl.ds(top, rows)], pair[1 - odd], preferred_element_type=jnp.float32)
+    store_rows(picked, tall.at[1], outs[2:])
+
+
+def twin(select, own, other, steps, per, slots):
+    _, samples = own[0].shape
+    rows, antennas = select.shape
+    return pl.pallas_call(
+        functools.partial(twin_kernel, steps),
+        out_shape=[jax.ShapeDtypeStruct((per, slots, samples), jnp.bfloat16)] * 4,
+        in_specs=[VMEM] * (1 + 2 * len(own)),
+        out_specs=[VMEM] * 4,
+        scratch_shapes=[
+            pltpu.VMEM((2, 2 * antennas, samples), jnp.float32),
+            pltpu.VMEM((2, antennas, 2 * samples), jnp.bfloat16),
+            pltpu.VMEM((2, rows, samples), jnp.float32),
+        ],
+        compiler_params=PARAMS,
+        cost_estimate=pl.CostEstimate(
+            flops=2 * rows * antennas * 2 * samples, bytes_accessed=4_000_000, transcendentals=0
+        ),
+    )(select, *own, *other)
 
 
 def gather(select, xs, steps, groups, per, slots):
@@ -171,11 +234,18 @@
             out[s, part] = total
 
 
-def late_kernel(real, imag, so_far, out, stage, sem):
+def late_kernel(real, *rest):
+    *imags, so_far, out, stage, sem = rest
+    slots, samples = real.shape[1:]
+    odd = lax.axis_index("chan") & 1
     copies = []
     for s in range(real.shape[0]):
+        imag = imags[0][s]
+        if len(imags) == 2:
+            imag = jnp.where(jnp.full((slots, samples), odd) == 1, imags[1][s].astype(jnp.float32), imag.astype(jnp.float32))
+            imag = imag.astype(jnp.bfloat16)
         for part in range(2):
-            stage[s, part] = so_far[s, part] + products(real[s], imag[s], part)
+            stage[s, part] = so_far[s, part] + products(real[s], imag, part)
             copy = pltpu.make_async_copy(stage.at[s, part], out.at[s, 0, part], sem.at[s, part])
             copy.start()
             copies.append(copy)
@@ -186,6 +256,7 @@
 def gram(real, imag, last):
     per, slots, samples = real[0].shape
     early = [e for e in range(len(real)) if e != last]
+    ends = imag[last] if isinstance(imag[last], tuple) else (imag[last],)
     flops = 2 * per * 2 * slots * slots * 2 * samples
     so_far = pl.pallas_call(
         early_kernel,
@@ -198,7 +269,7 @@
     return pl.pallas_call(
         late_kernel,
         out_shape=jax.ShapeDtypeStruct((per, 1, 2, slots, slots), jnp.float32),
-        in_specs=[VMEM] * 3,
+        in_specs=[VMEM] * (2 + len(ends)),
         out_specs=pl.BlockSpec(memory_space=pl.ANY),
         scratch_shapes=[
             pltpu.VMEM((per, 2, slots, slots), jnp.float32),
@@ -206,7 +277,7 @@
         ],
         compiler_params=PARAMS,
         cost_estimate=pl.CostEstimate(flops=flops, bytes_accessed=3_000_000, transcendentals=0),
-    )(real[last], imag[last], so_far)
+    )(real[last], *ends, so_far)
 
 
 def exchange(chunks, order, groups):
@@ -222,29 +293,59 @@
     return x.reshape(x.shape[1], x.shape[2])
 
 
+CHAN_ORDER = (6, 7, 2, 3, 4, 5, 1)
+
+
+def cross(chunks, chans):
+    got = list(chunks)
+    for step in CHAN_ORDER:
+        if step < chans:
+            got[step] = lax.ppermute(chunks[step], "chan", [(i, i ^ step) for i in range(chans)])
+    return got
+
+
+def paired(chans, groups):
+    return groups == 4 and chans in (2, 4, 8)
+
+
 def steps_of(voltages, assignment, slot_subarray_index):
     groups = lax.axis_size("tm")
     chans = lax.axis_size("chan")
     subarrays = slot_subarray_index.shape[0]
     per = subarrays // groups
     order = sorted(range(1, groups), reverse=True)
-    last = order[0]
-    if chans <= 8 and chans & (chans - 1) == 0:
-        steps = tuple(range(chans))
-        *chunks, imag = split(voltages, steps)
-        reals = list(chunks)
-        for step in (6, 7, 2, 3, 4, 5, 1):
-            if step < chans:
-                pairs = [(j, j ^ step) for j in range(chans)]
-                reals[step] = lax.ppermute(chunks[step], "chan", pairs)
-    else:
-        steps, imag = (0,), voltages[1]
-        reals = [across(voltages[0])]
+    last = 2 if groups == 4 else order[0]
+    first = [step for step in order if step != last]
+    if not paired(chans, groups):
+        select = plan(assignment, slot_subarray_index, groups, SLOT // 2)
+        real = across(voltages[0])
+        real = exchange(gather(select, [real], (0,), groups, per, SLOT), order, groups)
+        imag = across(voltages[1])
+        imag = exchange(gather(select, [imag], (0,), groups, per, SLOT), first + [last], groups)
+        return gram(real, imag, last)
+
+    steps = tuple(range(chans))
+    device = [(i, j, i * groups + j) for i in range(chans) for j in range(groups)]
+    raw, reals, imags = split(voltages)
+    raw = lax.ppermute(raw, "tm", [(j, j ^ 2) for j in range(groups)])
+    reals = cross(reals, chans)
     select = plan(assignment, slot_subarray_index, groups, SLOT // 2)
     real = exchange(gather(select, reals, steps, groups, per, SLOT), order, groups)
-    imag = across(imag)
-    imag = exchange(gather(select, [imag], (0,), groups, per, SLOT), order[1:] + order[:1], groups)
-    return gram(real, imag, last)
+
+    imags = cross(imags, chans)
+    pieces = unstack(raw)
+    far = [pieces[s // 2] for s in steps]
+    for step in CHAN_ORDER:
+        if step < chans:
+            pairs = [(i, i ^ step) for i in range(chans) if (i ^ step) % 2 == 0]
+            far[step] = lax.ppermute(far[step], "chan", pairs)
+    mine, near, third, fourth = twin(select, imags, far, steps, per, SLOT)
+    pairs = [(n, i * groups + (j ^ (3 if i % 2 else 1))) for i, j, n in device]
+    fourth = lax.ppermute(fourth, ("chan", "tm"), pairs)
+    pairs = [(n, i * groups + (j ^ 2)) for i, j, n in device if i % 2]
+    there = lax.ppermute(third, ("chan", "tm"), pairs)
+    near = lax.ppermute(near, "tm", [(j, j ^ 1) for j in range(groups)])
+    return gram(real, [mine, near, (third, there), fourth], last)
 
 
 def solution(mesh):

time: 65.4 us -> 74 us (1.13)
  the two profiles are of different devices: /device:TPU:10 before, /device:TPU:1 now
where the time goes in v3:
time: 74 us; the launch traced here: 73.7 us
  starting transfers between devices  42.8 us (58%)
  waiting for transfers between devices  18 us (24%)
  Pallas kernels  10.1 us (14%)
  local copies, waits for them, and re-layouts  2.56 us (3%)
    ppermute x14, starting transfers between devices, cross(): lax.ppermute(chunks[step], 'chan', [(i, i ^ step) for i in range(chans)])  17 us
    ppermute x7, starting transfers between devices, steps_of(): far[step] = lax.ppermute(far[step], 'chan', pairs)  13.6 us
    ppermute x3, waiting for transfers between devices, exchange(): got[step] = lax.ppermute(chunks[step], 'tm', pairs)  7.6 us
    ppermute x3, starting transfers between devices, exchange(): got[step] = lax.ppermute(chunks[step], 'tm', pairs)  4.66 us
    ppermute x1, waiting for transfers between devices, steps_of(): near = lax.ppermute(near, 'tm', [(j, j ^ 1) for j in range(groups)])  4.44 us
    ppermute x1, waiting for transfers between devices, steps_of(): fourth = lax.ppermute(fourth, ('chan', 'tm'), pairs)  3.69 us
    ppermute x1, starting transfers between devices, steps_of(): raw = lax.ppermute(raw, 'tm', [(j, j ^ 2) for j in range(groups)])  3.19 us
    ppermute x1, starting transfers between devices, steps_of(): there = lax.ppermute(third, ('chan', 'tm'), pairs)  3.01 us
  transfers between devices with their start and end apart: 28, of which 6 were waited for; matrix products, arithmetic and copies ran while one was open for 0% of the time, Pallas kernels for 8%

profile of v3, /device:TPU:1, one launch (start us, length us, event | category | flops | bytes accessed | tf_op | source)
XLA Modules:
  0.0 73.7 jit_solution(12774157212061013476)
XLA Ops:
  0.0 1.2 %copy-done = bf16[2,8,256,128]{3,2,1,0:T(8,128)(2,1)S(1)} copy-done((bf16[2,8,256,128]{3,2,1,0:T(8,128)(2,1)S(1)}, bf16[2,8,256,128]{3,2,1,0:T(8,128)(2,1)}, u32[]{:S(2)}) %copy-start) | copy-done | bytes 1048600
  1.2 2.1 %shard_map.38 = (bf16[4,256,128]{2,1,0:T(8,128)(2,1)S(1)}, bf16[256,128]{1,0:T(8,128)(2,1)S(1)}, bf16[256,128]{1,0:T(8,128)(2,1)S(1)}, bf16[256,128]{1,0:T(8,128...) custom-call(bf16[2,8,256,128]{3,2,1,0:T(8,128)(2,1)S(1)} %copy-done), custom_call_target="tpu_custom_call" | custom-call | flops 1000000 | bytes 2000000 | tf_op jit(solution)/shard_map/pallas_call | solution.py:99
  3.3 3.2 %collective-permute-start.15 = (bf16[4,256,128]{2,1,0:T(8,128)(2,1)S(1)}, bf16[4,256,128]{2,1,0:T(8,128)(2,1)S(1)}, u32[]{:S(2)}, u32[]{:S(2)}) collective-permute-start(bf16[4,256,128]{2,1,0:T(8,128)(2,1)S(1)} %get-tuple-element.51), channel_id=1, source_target_pairs={{0,2},{1,3},{2,0},{3,1},{4,6},{5,7},{6,4},{7,5},{8,10},{9,11},{10,... | collective-permute-start | bytes 786440 | tf_op jit(solution)/shard_map/ppermute | solution.py:330
  6.5 1.0 %collective-permute-start = (bf16[256,128]{1,0:T(8,128)(2,1)S(1)}, bf16[256,128]{1,0:T(8,128)(2,1)S(1)}, u32[]{:S(2)}, u32[]{:S(2)}) collective-permute-start(bf16[256,128]{1,0:T(8,128)(2,1)S(1)} %get-tuple-element.35), channel_id=1, source_target_pairs={{0,4},{4,0},{8,12},{12,8},{16,20},{20,16},{24,28},{28,24},{1,5},{5... | collective-permute-start | bytes 196616 | tf_op jit(solution)/shard_map/ppermute | solution.py:303
  7.5 1.2 %collective-permute-start.1 = (bf16[256,128]{1,0:T(8,128)(2,1)S(1)}, bf16[256,128]{1,0:T(8,128)(2,1)S(1)}, u32[]{:S(2)}, u32[]{:S(2)}) collective-permute-start(bf16[256,128]{1,0:T(8,128)(2,1)S(1)} %get-tuple-element.36), channel_id=1, source_target_pairs={{0,8},{4,12},{8,0},{12,4},{16,24},{20,28},{24,16},{28,20},{1,9},{5... | collective-permute-start | bytes 196616 | tf_op jit(solution)/shard_map/ppermute | solution.py:303
  8.7 0.4 collective-permute-start.2
  9.1 1.2 %collective-permute-start.3 = (bf16[256,128]{1,0:T(8,128)(2,1)S(1)}, bf16[256,128]{1,0:T(8,128)(2,1)S(1)}, u32[]{:S(2)}, u32[]{:S(2)}) collective-permute-start(bf16[256,128]{1,0:T(8,128)(2,1)S(1)} %get-tuple-element.38), channel_id=1, source_target_pairs={{0,16},{4,20},{8,24},{12,28},{16,0},{20,4},{24,8},{28,12},{1,17},{... | collective-permute-start | bytes 196616 | tf_op jit(solution)/shard_map/ppermute | solution.py:303
  10.4 0.0 collective-permute-done.rest_1_
  10.4 0.6 collective-permute-start.4
  11.0 0.1 collective-permute-done.1.rest_2_
  11.1 2.2 %collective-permute-start.5 = (bf16[256,128]{1,0:T(8,128)(2,1)S(1)}, bf16[256,128]{1,0:T(8,128)(2,1)S(1)}, u32[]{:S(2)}, u32[]{:S(2)}) collective-permute-start(bf16[256,128]{1,0:T(8,128)(2,1)S(1)} %get-tuple-element.40), channel_id=1, source_target_pairs={{0,24},{4,28},{8,16},{12,20},{16,8},{20,12},{24,0},{28,4},{1,25},{... | collective-permute-start | bytes 196616 | tf_op jit(solution)/shard_map/ppermute | solution.py:303
  13.3 0.0 collective-permute-done.2.rest_3_
  13.3 1.7 %collective-permute-start.6 = (bf16[256,128]{1,0:T(8,128)(2,1)S(1)}, bf16[256,128]{1,0:T(8,128)(2,1)S(1)}, u32[]{:S(2)}, u32[]{:S(2)}) collective-permute-start(bf16[256,128]{1,0:T(8,128)(2,1)S(1)} %get-tuple-element.41), channel_id=1, source_target_pairs={{0,28},{4,24},{8,20},{12,16},{16,12},{20,8},{24,4},{28,0},{1,29},{... | collective-permute-start | bytes 196616 | tf_op jit(solution)/shard_map/ppermute | solution.py:303
  15.0 0.0 collective-permute-done.3.rest_4_
  15.0 0.6 collective-permute-start.8
  15.6 0.0 collective-permute-done.4.rest_5_
  15.6 1.2 %collective-permute-start.9 = (bf16[256,128]{1,0:T(8,128)(2,1)S(1)}, bf16[256,128]{1,0:T(8,128)(2,1)S(1)}, u32[]{:S(2)}, u32[]{:S(2)}) collective-permute-start(bf16[256,128]{1,0:T(8,128)(2,1)S(1)} %get-tuple-element.45), channel_id=1, source_target_pairs={{0,8},{4,12},{8,0},{12,4},{16,24},{20,28},{24,16},{28,20},{1,9},{5... | collective-permute-start | bytes 196616 | tf_op jit(solution)/shard_map/ppermute | solution.py:303
  16.8 0.0 collective-permute-done.5.rest_6_
  16.8 2.1 %collective-permute-start.10 = (bf16[256,128]{1,0:T(8,128)(2,1)S(1)}, bf16[256,128]{1,0:T(8,128)(2,1)S(1)}, u32[]{:S(2)}, u32[]{:S(2)}) collective-permute-start(bf16[256,128]{1,0:T(8,128)(2,1)S(1)} %get-tuple-element.46), channel_id=1, source_target_pairs={{0,12},{4,8},{8,4},{12,0},{16,28},{20,24},{24,20},{28,16},{1,13},{... | collective-permute-start | bytes 196616 | tf_op jit(solution)/shard_map/ppermute | solution.py:303
  18.9 0.0 collective-permute-done.15.x_ref
  18.9 1.6 %collective-permute-start.11 = (bf16[256,128]{1,0:T(8,128)(2,1)S(1)}, bf16[256,128]{1,0:T(8,128)(2,1)S(1)}, u32[]{:S(2)}, u32[]{:S(2)}) collective-permute-start(bf16[256,128]{1,0:T(8,128)(2,1)S(1)} %get-tuple-element.47), channel_id=1, source_target_pairs={{0,16},{4,20},{8,24},{12,28},{16,0},{20,4},{24,8},{28,12},{1,17},{... | collective-permute-start | bytes 196616 | tf_op jit(solution)/shard_map/ppermute | solution.py:303
  20.6 0.0 collective-permute-done.6.rest_7_
  20.6 0.5 collective-permute-start.12
  21.1 0.0 collective-permute-done.8.rest_1_
  21.1 2.2 %collective-permute-start.13 = (bf16[256,128]{1,0:T(8,128)(2,1)S(1)}, bf16[256,128]{1,0:T(8,128)(2,1)S(1)}, u32[]{:S(2)}, u32[]{:S(2)}) collective-permute-start(bf16[256,128]{1,0:T(8,128)(2,1)S(1)} %get-tuple-element.49), channel_id=1, source_target_pairs={{0,24},{4,28},{8,16},{12,20},{16,8},{20,12},{24,0},{28,4},{1,25},{... | collective-permute-start | bytes 196616 | tf_op jit(solution)/shard_map/ppermute | solution.py:303
  23.4 0.0 collective-permute-done.9.rest_2_
  23.4 0.3 collective-permute-start.14
  23.7 0.0 collective-permute-done.10.rest_3_
  23.7 2.1 %collective-permute-start.16 = (bf16[256,128]{1,0:T(8,128)(2,1)S(1)}, bf16[256,128]{1,0:T(8,128)(2,1)S(1)}, u32[]{:S(2)}, u32[]{:S(2)}) collective-permute-start(bf16[256,128]{1,0:T(8,128)(2,1)S(1)} %get-tuple-element.52.rest_8_), channel_id=1, source_target_pairs={{4,0},{12,8},{20,16},{28,24},{5,1},{13,9},{21,17},{29,25},{6,2},{1... | collective-permute-start | bytes 196616 | tf_op jit(solution)/shard_map/ppermute | solution.py:341
  25.8 0.0 collective-permute-done.11.rest_4_
  25.8 2.4 %collective-permute-start.18 = (bf16[256,128]{1,0:T(8,128)(2,1)S(1)}, bf16[256,128]{1,0:T(8,128)(2,1)S(1)}, u32[]{:S(2)}, u32[]{:S(2)}) collective-permute-start(bf16[256,128]{1,0:T(8,128)(2,1)S(1)} %get-tuple-element.53), channel_id=1, source_target_pairs={{4,8},{12,0},{20,24},{28,16},{5,9},{13,1},{21,25},{29,17},{6,10},{... | collective-permute-start | bytes 196616 | tf_op jit(solution)/shard_map/ppermute | solution.py:341
  28.3 0.0 copy-start.1
  28.3 0.7 copy-done.1
  29.0 0.7 copy-done.2
  29.6 2.1 %shard_map.37.select_ref = bf16[1536,1024]{1,0:T(8,128)(2,1)S(1)} custom-call(s32[8]{0:T(128)S(1)} %copy-done.2, s32[8,128]{1,0:T(8,128)S(1)} %bitcast.1), custom_call_target="tpu_custom_call" | custom-call | flops 4000000000 | bytes 3000000 | tf_op jit(solution)/shard_map/pallas_call | solution.py:71
  31.7 0.0 collective-permute-done.12.rest_5_
  31.7 0.7 collective-permute-start.17
  32.4 0.0 collective-permute-done.13.rest_6_
  32.4 4.1 %collective-permute-start.20 = (bf16[256,128]{1,0:T(8,128)(2,1)S(1)}, bf16[256,128]{1,0:T(8,128)(2,1)S(1)}, u32[]{:S(2)}, u32[]{:S(2)}) collective-permute-start(bf16[256,128]{1,0:T(8,128)(2,1)S(1)} %get-tuple-element.54), channel_id=1, source_target_pairs={{4,16},{12,24},{20,0},{28,8},{5,17},{13,25},{21,1},{29,9},{6,18},{... | collective-permute-start | bytes 196616 | tf_op jit(solution)/shard_map/ppermute | solution.py:341
  36.4 0.0 collective-permute-done.14.rest_7_
  36.4 0.7 collective-permute-start.19
  37.1 3.0 %collective-permute-start.22 = (bf16[256,128]{1,0:T(8,128)(2,1)S(1)}, bf16[256,128]{1,0:T(8,128)(2,1)S(1)}, u32[]{:S(2)}, u32[]{:S(2)}) collective-permute-start(bf16[256,128]{1,0:T(8,128)(2,1)S(1)} %get-tuple-element.55), channel_id=1, source_target_pairs={{4,24},{12,16},{20,8},{28,0},{5,25},{13,17},{21,9},{29,1},{6,26},{... | collective-permute-start | bytes 196616 | tf_op jit(solution)/shard_map/ppermute | solution.py:341
  40.1 0.7 collective-permute-start.21
  40.8 1.3 %shard_map.39 = (bf16[2,384,128]{2,1,0:T(8,128)(2,1)S(1)}, bf16[2,384,128]{2,1,0:T(8,128)(2,1)S(1)}, bf16[2,384,128]{2,1,0:T(8,128)(2,1)S(1)}, bf16[2,384,128]{2,1,0:T(8,128)(2,1)S(1)}) custom-call(bf16[1536,1024]{1,0:T(8,128)(2,1)S(1)} %shard_map.37.select_ref, bf16[256,128]{1,0:T(8,128)(2,1)S(1)} %get-tuple-element.34.rest_0_, ...), custom_call_target="tpu_custom_call" | custom-call | flops 805306368 | bytes 4000000 | tf_op jit(solution)/shard_map/pallas_call | solution.py:202
  42.1 0.0 collective-permute-done.17.rest_10_
  42.1 1.0 %collective-permute-start.24 = (bf16[2,384,128]{2,1,0:T(8,128)(2,1)S(1)}, bf16[2,384,128]{2,1,0:T(8,128)(2,1)S(1)}, u32[]{:S(2)}, u32[]{:S(2)}) collective-permute-start(bf16[2,384,128]{2,1,0:T(8,128)(2,1)S(1)} %get-tuple-element.58), channel_id=1, source_target_pairs={{0,1},{1,0},{2,3},{3,2},{4,5},{5,4},{6,7},{7,6},{8,9},{9,8},{10,11... | collective-permute-start | bytes 589832 | tf_op jit(solution)/shard_map/ppermute | solution.py:287
  43.1 0.0 collective-permute-done.20.rest_13_
  43.1 2.4 %collective-permute-start.25 = (bf16[2,384,128]{2,1,0:T(8,128)(2,1)S(1)}, bf16[2,384,128]{2,1,0:T(8,128)(2,1)S(1)}, u32[]{:S(2)}, u32[]{:S(2)}) collective-permute-start(bf16[2,384,128]{2,1,0:T(8,128)(2,1)S(1)} %get-tuple-element.59), channel_id=1, source_target_pairs={{0,3},{1,2},{2,1},{3,0},{4,7},{5,6},{6,5},{7,4},{8,11},{9,10},{10,... | collective-permute-start | bytes 589832 | tf_op jit(solution)/shard_map/ppermute | solution.py:287
  45.5 0.0 collective-permute-done.19.rest_12_
  45.5 0.0 collective-permute-done.22.rest_15_
  45.5 0.0 collective-permute-done.21.rest_14_
  45.5 1.4 %shard_map.41 = (bf16[2,384,128]{2,1,0:T(8,128)(2,1)S(1)}, bf16[2,384,128]{2,1,0:T(8,128)(2,1)S(1)}, bf16[2,384,128]{2,1,0:T(8,128)(2,1)S(1)}, bf16[2,384,128]{2,1,0:T(8,128)(2,1)S(1)}) custom-call(bf16[1536,1024]{1,0:T(8,128)(2,1)S(1)} %shard_map.37.select_ref, bf16[256,128]{1,0:T(8,128)(2,1)S(1)} %get-tuple-element.43.rest_0_, ...), custom_call_target="tpu_custom_call" | custom-call | flops 805306368 | bytes 4000000 | tf_op jit(solution)/shard_map/pallas_call | solution.py:182
  47.0 0.5 collective-permute-start.26
  47.5 0.9 %collective-permute-start.27 = (bf16[2,384,128]{2,1,0:T(8,128)(2,1)S(1)}, bf16[2,384,128]{2,1,0:T(8,128)(2,1)S(1)}, u32[]{:S(2)}, u32[]{:S(2)}) collective-permute-start(bf16[2,384,128]{2,1,0:T(8,128)(2,1)S(1)} %get-tuple-element.62), channel_id=1, source_target_pairs={{0,1},{1,0},{2,3},{3,2},{4,7},{5,6},{6,5},{7,4},{8,9},{9,8},{10,11... | collective-permute-start | bytes 589832 | tf_op jit(solution)/shard_map/ppermute | solution.py:344
  48.5 1.3 %collective-permute-start.7 = (bf16[2,384,128]{2,1,0:T(8,128)(2,1)S(1)}, bf16[2,384,128]{2,1,0:T(8,128)(2,1)S(1)}, u32[]{:S(2)}, u32[]{:S(2)}) collective-permute-start(bf16[2,384,128]{2,1,0:T(8,128)(2,1)S(1)} %get-tuple-element.42), channel_id=1, source_target_pairs={{0,2},{1,3},{2,0},{3,1},{4,6},{5,7},{6,4},{7,5},{8,10},{9,11},{10,... | collective-permute-start | bytes 589832 | tf_op jit(solution)/shard_map/ppermute | solution.py:287
  49.7 0.0 collective-permute-done.24.refs_1_
  49.7 3.0 %collective-permute-start.23 = (bf16[2,384,128]{2,1,0:T(8,128)(2,1)S(1)}, bf16[2,384,128]{2,1,0:T(8,128)(2,1)S(1)}, u32[]{:S(2)}, u32[]{:S(2)}) collective-permute-start(bf16[2,384,128]{2,1,0:T(8,128)(2,1)S(1)} %get-tuple-element.56.rest_0_), channel_id=1, source_target_pairs={{4,6},{5,7},{6,4},{7,5},{12,14},{13,15},{14,12},{15,13},{20,22},{2... | collective-permute-start | bytes 589832 | tf_op jit(solution)/shard_map/ppermute | solution.py:346
  52.7 1.2 %collective-permute-done.25.refs_2_ = bf16[2,384,128]{2,1,0:T(8,128)(2,1)S(1)} collective-permute-done((bf16[2,384,128]{2,1,0:T(8,128)(2,1)S(1)}, bf16[2,384,128]{2,1,0:T(8,128)(2,1)S(1)}, u32[]{:S(2)}, u32[]{:S(2)}) %collective-permute-start.25) | collective-permute-done | bytes 196640 | tf_op jit(solution)/shard_map/ppermute | solution.py:287
  54.0 4.4 %collective-permute-done.26.refs_4_ = bf16[2,384,128]{2,1,0:T(8,128)(2,1)S(1)} collective-permute-done((bf16[2,384,128]{2,1,0:T(8,128)(2,1)S(1)}, bf16[2,384,128]{2,1,0:T(8,128)(2,1)S(1)}, u32[]{:S(2)}, u32[]{:S(2)}) %collective-permute-start.26) | collective-permute-done | bytes 196640 | tf_op jit(solution)/shard_map/ppermute | solution.py:347
  58.4 3.7 %collective-permute-done.27.refs_5_ = bf16[2,384,128]{2,1,0:T(8,128)(2,1)S(1)} collective-permute-done((bf16[2,384,128]{2,1,0:T(8,128)(2,1)S(1)}, bf16[2,384,128]{2,1,0:T(8,128)(2,1)S(1)}, u32[]{:S(2)}, u32[]{:S(2)}) %collective-permute-start.27) | collective-permute-done | bytes 196640 | tf_op jit(solution)/shard_map/ppermute | solution.py:344
  62.1 1.4 %shard_map.42.rest_2_ = f32[2,2,384,384]{3,2,1,0:T(8,128)S(1)} custom-call(bf16[2,384,128]{2,1,0:T(8,128)(2,1)S(1)} %get-tuple-element.57.refs_0_, bf16[2,384,128]{2,1,0:T(8,128)(2,1)S(1)} %collective-permute-done.24.refs_1_, bf16[2,384,128]{2,1,0:T(8,128)(2,1)S(1)} %collective-permute-done.25.refs_2_, bf16[2,384,128]{2,1,0:T(8,128)(2,1)S(1)} %get-tuple-element.60.refs_3_, ...), custom_call_target="tpu_custom_call" | custom-call | flops 905969664 | bytes 3000000 | tf_op jit(solution)/shard_map/pallas_call | solution.py:261
  63.5 6.4 %collective-permute-done.7.real = bf16[2,384,128]{2,1,0:T(8,128)(2,1)S(1)} collective-permute-done((bf16[2,384,128]{2,1,0:T(8,128)(2,1)S(1)}, bf16[2,384,128]{2,1,0:T(8,128)(2,1)S(1)}, u32[]{:S(2)}, u32[]{:S(2)}) %collective-permute-start.7) | collective-permute-done | bytes 196640 | tf_op jit(solution)/shard_map/ppermute | solution.py:287
  69.9 2.1 %collective-permute-done.23.rest_1_ = bf16[2,384,128]{2,1,0:T(8,128)(2,1)S(1)} collective-permute-done((bf16[2,384,128]{2,1,0:T(8,128)(2,1)S(1)}, bf16[2,384,128]{2,1,0:T(8,128)(2,1)S(1)}, u32[]{:S(2)}, u32[]{:S(2)}) %collective-permute-start.23) | collective-permute-done | bytes 196640 | tf_op jit(solution)/shard_map/ppermute | solution.py:346
  72.0 1.7 %shard_map.43 = f32[2,1,2,384,384]{4,3,2,1,0:T(8,128)} custom-call(bf16[2,384,128]{2,1,0:T(8,128)(2,1)S(1)} %collective-permute-done.7.real, bf16[2,384,128]{2,1,0:T(8,128)(2,1)S(1)} %get-tuple-element.56.rest_0_, bf16[2,384,128]{2,1,0:T(8,128)(2,1)S(1)} %collective-permute-done.23.rest_1_, f32[2,2,384,384]{3,2,1,0:T(8,128)S(1)} %shard_map.42.rest_2_), custom_call_target="tpu_custom_call" | custom-call | flops 301989888 | bytes 3000000 | tf_op jit(solution)/shard_map/pallas_call | solution.py:269
  (5 shorter events, 0.0 us)
Async XLA Ops:
  0.0 1.2 %copy-start = (bf16[2,8,256,128]{3,2,1,0:T(8,128)(2,1)S(1)}, bf16[2,8,256,128]{3,2,1,0:T(8,128)(2,1)}, u32[]{:S(2)}) copy-start(bf16[2,8,256,128]{3,2,1,0:T(8,128)(2,1)} %x_ref.1) | copy-start | bytes 3145732
  3.3 15.6 %collective-permute-start.15 = (bf16[4,256,128]{2,1,0:T(8,128)(2,1)S(1)}, bf16[4,256,128]{2,1,0:T(8,128)(2,1)S(1)}, u32[]{:S(2)}, u32[]{:S(2)}) collective-permute-start(bf16[4,256,128]{2,1,0:T(8,128)(2,1)S(1)} %get-tuple-element.51), channel_id=1, source_target_pairs={{0,2},{1,3},{2,0},{3,1},{4,6},{5,7},{6,4},{7,5},{8,10},{9,11},{10,... | collective-permute-start | bytes 786440 | tf_op jit(solution)/shard_map/ppermute | solution.py:330
  6.5 3.8 %collective-permute-start = (bf16[256,128]{1,0:T(8,128)(2,1)S(1)}, bf16[256,128]{1,0:T(8,128)(2,1)S(1)}, u32[]{:S(2)}, u32[]{:S(2)}) collective-permute-start(bf16[256,128]{1,0:T(8,128)(2,1)S(1)} %get-tuple-element.35), channel_id=1, source_target_pairs={{0,4},{4,0},{8,12},{12,8},{16,20},{20,16},{24,28},{28,24},{1,5},{5... | collective-permute-start | bytes 196616 | tf_op jit(solution)/shard_map/ppermute | solution.py:303
  7.5 3.6 %collective-permute-start.1 = (bf16[256,128]{1,0:T(8,128)(2,1)S(1)}, bf16[256,128]{1,0:T(8,128)(2,1)S(1)}, u32[]{:S(2)}, u32[]{:S(2)}) collective-permute-start(bf16[256,128]{1,0:T(8,128)(2,1)S(1)} %get-tuple-element.36), channel_id=1, source_target_pairs={{0,8},{4,12},{8,0},{12,4},{16,24},{20,28},{24,16},{28,20},{1,9},{5... | collective-permute-start | bytes 196616 | tf_op jit(solution)/shard_map/ppermute | solution.py:303
  8.7 4.6 %collective-permute-start.2 = (bf16[256,128]{1,0:T(8,128)(2,1)S(1)}, bf16[256,128]{1,0:T(8,128)(2,1)S(1)}, u32[]{:S(2)}, u32[]{:S(2)}) collective-permute-start(bf16[256,128]{1,0:T(8,128)(2,1)S(1)} %get-tuple-element.37), channel_id=1, source_target_pairs={{0,12},{4,8},{8,4},{12,0},{16,28},{20,24},{24,20},{28,16},{1,13},{... | collective-permute-start | bytes 196616 | tf_op jit(solution)/shard_map/ppermute | solution.py:303
  9.1 5.9 %collective-permute-start.3 = (bf16[256,128]{1,0:T(8,128)(2,1)S(1)}, bf16[256,128]{1,0:T(8,128)(2,1)S(1)}, u32[]{:S(2)}, u32[]{:S(2)}) collective-permute-start(bf16[256,128]{1,0:T(8,128)(2,1)S(1)} %get-tuple-element.38), channel_id=1, source_target_pairs={{0,16},{4,20},{8,24},{12,28},{16,0},{20,4},{24,8},{28,12},{1,17},{... | collective-permute-start | bytes 196616 | tf_op jit(solution)/shard_map/ppermute | solution.py:303
  10.4 5.2 %collective-permute-start.4 = (bf16[256,128]{1,0:T(8,128)(2,1)S(1)}, bf16[256,128]{1,0:T(8,128)(2,1)S(1)}, u32[]{:S(2)}, u32[]{:S(2)}) collective-permute-start(bf16[256,128]{1,0:T(8,128)(2,1)S(1)} %get-tuple-element.39), channel_id=1, source_target_pairs={{0,20},{4,16},{8,28},{12,24},{16,4},{20,0},{24,12},{28,8},{1,21},{... | collective-permute-start | bytes 196616 | tf_op jit(solution)/shard_map/ppermute | solution.py:303
  11.1 5.7 %collective-permute-start.5 = (bf16[256,128]{1,0:T(8,128)(2,1)S(1)}, bf16[256,128]{1,0:T(8,128)(2,1)S(1)}, u32[]{:S(2)}, u32[]{:S(2)}) collective-permute-start(bf16[256,128]{1,0:T(8,128)(2,1)S(1)} %get-tuple-element.40), channel_id=1, source_target_pairs={{0,24},{4,28},{8,16},{12,20},{16,8},{20,12},{24,0},{28,4},{1,25},{... | collective-permute-start | bytes 196616 | tf_op jit(solution)/shard_map/ppermute | solution.py:303
  13.3 7.3 %collective-permute-start.6 = (bf16[256,128]{1,0:T(8,128)(2,1)S(1)}, bf16[256,128]{1,0:T(8,128)(2,1)S(1)}, u32[]{:S(2)}, u32[]{:S(2)}) collective-permute-start(bf16[256,128]{1,0:T(8,128)(2,1)S(1)} %get-tuple-element.41), channel_id=1, source_target_pairs={{0,28},{4,24},{8,20},{12,16},{16,12},{20,8},{24,4},{28,0},{1,29},{... | collective-permute-start | bytes 196616 | tf_op jit(solution)/shard_map/ppermute | solution.py:303
  15.0 6.2 %collective-permute-start.8 = (bf16[256,128]{1,0:T(8,128)(2,1)S(1)}, bf16[256,128]{1,0:T(8,128)(2,1)S(1)}, u32[]{:S(2)}, u32[]{:S(2)}) collective-permute-start(bf16[256,128]{1,0:T(8,128)(2,1)S(1)} %get-tuple-element.44), channel_id=1, source_target_pairs={{0,4},{4,0},{8,12},{12,8},{16,20},{20,16},{24,28},{28,24},{1,5},{5... | collective-permute-start | bytes 196616 | tf_op jit(solution)/shard_map/ppermute | solution.py:303
  15.6 7.8 %collective-permute-start.9 = (bf16[256,128]{1,0:T(8,128)(2,1)S(1)}, bf16[256,128]{1,0:T(8,128)(2,1)S(1)}, u32[]{:S(2)}, u32[]{:S(2)}) collective-permute-start(bf16[256,128]{1,0:T(8,128)(2,1)S(1)} %get-tuple-element.45), channel_id=1, source_target_pairs={{0,8},{4,12},{8,0},{12,4},{16,24},{20,28},{24,16},{28,20},{1,9},{5... | collective-permute-start | bytes 196616 | tf_op jit(solution)/shard_map/ppermute | solution.py:303
  16.8 6.9 %collective-permute-start.10 = (bf16[256,128]{1,0:T(8,128)(2,1)S(1)}, bf16[256,128]{1,0:T(8,128)(2,1)S(1)}, u32[]{:S(2)}, u32[]{:S(2)}) collective-permute-start(bf16[256,128]{1,0:T(8,128)(2,1)S(1)} %get-tuple-element.46), channel_id=1, source_target_pairs={{0,12},{4,8},{8,4},{12,0},{16,28},{20,24},{24,20},{28,16},{1,13},{... | collective-permute-start | bytes 196616 | tf_op jit(solution)/shard_map/ppermute | solution.py:303
  18.9 6.9 %collective-permute-start.11 = (bf16[256,128]{1,0:T(8,128)(2,1)S(1)}, bf16[256,128]{1,0:T(8,128)(2,1)S(1)}, u32[]{:S(2)}, u32[]{:S(2)}) collective-permute-start(bf16[256,128]{1,0:T(8,128)(2,1)S(1)} %get-tuple-element.47), channel_id=1, source_target_pairs={{0,16},{4,20},{8,24},{12,28},{16,0},{20,4},{24,8},{28,12},{1,17},{... | collective-permute-start | bytes 196616 | tf_op jit(solution)/shard_map/ppermute | solution.py:303
  20.6 11.1 %collective-permute-start.12 = (bf16[256,128]{1,0:T(8,128)(2,1)S(1)}, bf16[256,128]{1,0:T(8,128)(2,1)S(1)}, u32[]{:S(2)}, u32[]{:S(2)}) collective-permute-start(bf16[256,128]{1,0:T(8,128)(2,1)S(1)} %get-tuple-element.48), channel_id=1, source_target_pairs={{0,20},{4,16},{8,28},{12,24},{16,4},{20,0},{24,12},{28,8},{1,21},{... | collective-permute-start | bytes 196616 | tf_op jit(solution)/shard_map/ppermute | solution.py:303
  21.1 11.2 %collective-permute-start.13 = (bf16[256,128]{1,0:T(8,128)(2,1)S(1)}, bf16[256,128]{1,0:T(8,128)(2,1)S(1)}, u32[]{:S(2)}, u32[]{:S(2)}) collective-permute-start(bf16[256,128]{1,0:T(8,128)(2,1)S(1)} %get-tuple-element.49), channel_id=1, source_target_pairs={{0,24},{4,28},{8,16},{12,20},{16,8},{20,12},{24,0},{28,4},{1,25},{... | collective-permute-start | bytes 196616 | tf_op jit(solution)/shard_map/ppermute | solution.py:303
  23.4 13.1 %collective-permute-start.14 = (bf16[256,128]{1,0:T(8,128)(2,1)S(1)}, bf16[256,128]{1,0:T(8,128)(2,1)S(1)}, u32[]{:S(2)}, u32[]{:S(2)}) collective-permute-start(bf16[256,128]{1,0:T(8,128)(2,1)S(1)} %get-tuple-element.50), channel_id=1, source_target_pairs={{0,28},{4,24},{8,20},{12,16},{16,12},{20,8},{24,4},{28,0},{1,29},{... | collective-permute-start | bytes 196616 | tf_op jit(solution)/shard_map/ppermute | solution.py:303
  23.7 13.4 %collective-permute-start.16 = (bf16[256,128]{1,0:T(8,128)(2,1)S(1)}, bf16[256,128]{1,0:T(8,128)(2,1)S(1)}, u32[]{:S(2)}, u32[]{:S(2)}) collective-permute-start(bf16[256,128]{1,0:T(8,128)(2,1)S(1)} %get-tuple-element.52.rest_8_), channel_id=1, source_target_pairs={{4,0},{12,8},{20,16},{28,24},{5,1},{13,9},{21,17},{29,25},{6,2},{1... | collective-permute-start | bytes 196616 | tf_op jit(solution)/shard_map/ppermute | solution.py:341
  25.8 14.3 %collective-permute-start.18 = (bf16[256,128]{1,0:T(8,128)(2,1)S(1)}, bf16[256,128]{1,0:T(8,128)(2,1)S(1)}, u32[]{:S(2)}, u32[]{:S(2)}) collective-permute-start(bf16[256,128]{1,0:T(8,128)(2,1)S(1)} %get-tuple-element.53), channel_id=1, source_target_pairs={{4,8},{12,0},{20,24},{28,16},{5,9},{13,1},{21,25},{29,17},{6,10},{... | collective-permute-start | bytes 196616 | tf_op jit(solution)/shard_map/ppermute | solution.py:341
  28.3 0.7 copy-start.1
  29.0 0.7 copy-start.2
  31.7 10.4 %collective-permute-start.17 = (bf16[256,128]{1,0:T(8,128)(2,1)S(1)}, bf16[256,128]{1,0:T(8,128)(2,1)S(1)}, u32[]{:S(2)}, u32[]{:S(2)}) collective-permute-start(bf16[256,128]{1,0:T(8,128)(2,1)S(1)} %get-tuple-element.53), channel_id=1, source_target_pairs={{0,8},{8,0},{16,24},{24,16},{1,9},{9,1},{17,25},{25,17},{2,10},{10... | collective-permute-start | bytes 196616 | tf_op jit(solution)/shard_map/ppermute | solution.py:341
  32.4 10.7 %collective-permute-start.20 = (bf16[256,128]{1,0:T(8,128)(2,1)S(1)}, bf16[256,128]{1,0:T(8,128)(2,1)S(1)}, u32[]{:S(2)}, u32[]{:S(2)}) collective-permute-start(bf16[256,128]{1,0:T(8,128)(2,1)S(1)} %get-tuple-element.54), channel_id=1, source_target_pairs={{4,16},{12,24},{20,0},{28,8},{5,17},{13,25},{21,1},{29,9},{6,18},{... | collective-permute-start | bytes 196616 | tf_op jit(solution)/shard_map/ppermute | solution.py:341
  36.4 9.1 %collective-permute-start.19 = (bf16[256,128]{1,0:T(8,128)(2,1)S(1)}, bf16[256,128]{1,0:T(8,128)(2,1)S(1)}, u32[]{:S(2)}, u32[]{:S(2)}) collective-permute-start(bf16[256,128]{1,0:T(8,128)(2,1)S(1)} %get-tuple-element.54), channel_id=1, source_target_pairs={{0,16},{8,24},{16,0},{24,8},{1,17},{9,25},{17,1},{25,9},{2,18},{10... | collective-permute-start | bytes 196616 | tf_op jit(solution)/shard_map/ppermute | solution.py:341
  37.1 8.4 %collective-permute-start.22 = (bf16[256,128]{1,0:T(8,128)(2,1)S(1)}, bf16[256,128]{1,0:T(8,128)(2,1)S(1)}, u32[]{:S(2)}, u32[]{:S(2)}) collective-permute-start(bf16[256,128]{1,0:T(8,128)(2,1)S(1)} %get-tuple-element.55), channel_id=1, source_target_pairs={{4,24},{12,16},{20,8},{28,0},{5,25},{13,17},{21,9},{29,1},{6,26},{... | collective-permute-start | bytes 196616 | tf_op jit(solution)/shard_map/ppermute | solution.py:341
  40.1 5.4 %collective-permute-start.21 = (bf16[256,128]{1,0:T(8,128)(2,1)S(1)}, bf16[256,128]{1,0:T(8,128)(2,1)S(1)}, u32[]{:S(2)}, u32[]{:S(2)}) collective-permute-start(bf16[256,128]{1,0:T(8,128)(2,1)S(1)} %get-tuple-element.55), channel_id=1, source_target_pairs={{0,24},{8,16},{16,8},{24,0},{1,25},{9,17},{17,9},{25,1},{2,26},{10... | collective-permute-start | bytes 196616 | tf_op jit(solution)/shard_map/ppermute | solution.py:341
  42.1 7.6 %collective-permute-start.24 = (bf16[2,384,128]{2,1,0:T(8,128)(2,1)S(1)}, bf16[2,384,128]{2,1,0:T(8,128)(2,1)S(1)}, u32[]{:S(2)}, u32[]{:S(2)}) collective-permute-start(bf16[2,384,128]{2,1,0:T(8,128)(2,1)S(1)} %get-tuple-element.58), channel_id=1, source_target_pairs={{0,1},{1,0},{2,3},{3,2},{4,5},{5,4},{6,7},{7,6},{8,9},{9,8},{10,11... | collective-permute-start | bytes 589832 | tf_op jit(solution)/shard_map/ppermute | solution.py:287
  43.1 10.9 %collective-permute-start.25 = (bf16[2,384,128]{2,1,0:T(8,128)(2,1)S(1)}, bf16[2,384,128]{2,1,0:T(8,128)(2,1)S(1)}, u32[]{:S(2)}, u32[]{:S(2)}) collective-permute-start(bf16[2,384,128]{2,1,0:T(8,128)(2,1)S(1)} %get-tuple-element.59), channel_id=1, source_target_pairs={{0,3},{1,2},{2,1},{3,0},{4,7},{5,6},{6,5},{7,4},{8,11},{9,10},{10,... | collective-permute-start | bytes 589832 | tf_op jit(solution)/shard_map/ppermute | solution.py:287
  47.0 11.4 %collective-permute-start.26 = (bf16[2,384,128]{2,1,0:T(8,128)(2,1)S(1)}, bf16[2,384,128]{2,1,0:T(8,128)(2,1)S(1)}, u32[]{:S(2)}, u32[]{:S(2)}) collective-permute-start(bf16[2,384,128]{2,1,0:T(8,128)(2,1)S(1)} %get-tuple-element.61), channel_id=1, source_target_pairs={{0,1},{1,0},{2,3},{3,2},{4,5},{5,4},{6,7},{7,6},{8,9},{9,8},{10,11... | collective-permute-start | bytes 589832 | tf_op jit(solution)/shard_map/ppermute | solution.py:347
  47.5 14.5 %collective-permute-start.27 = (bf16[2,384,128]{2,1,0:T(8,128)(2,1)S(1)}, bf16[2,384,128]{2,1,0:T(8,128)(2,1)S(1)}, u32[]{:S(2)}, u32[]{:S(2)}) collective-permute-start(bf16[2,384,128]{2,1,0:T(8,128)(2,1)S(1)} %get-tuple-element.62), channel_id=1, source_target_pairs={{0,1},{1,0},{2,3},{3,2},{4,7},{5,6},{6,5},{7,4},{8,9},{9,8},{10,11... | collective-permute-start | bytes 589832 | tf_op jit(solution)/shard_map/ppermute | solution.py:344
  48.5 21.4 %collective-permute-start.7 = (bf16[2,384,128]{2,1,0:T(8,128)(2,1)S(1)}, bf16[2,384,128]{2,1,0:T(8,128)(2,1)S(1)}, u32[]{:S(2)}, u32[]{:S(2)}) collective-permute-start(bf16[2,384,128]{2,1,0:T(8,128)(2,1)S(1)} %get-tuple-element.42), channel_id=1, source_target_pairs={{0,2},{1,3},{2,0},{3,1},{4,6},{5,7},{6,4},{7,5},{8,10},{9,11},{10,... | collective-permute-start | bytes 589832 | tf_op jit(solution)/shard_map/ppermute | solution.py:287
  49.7 22.2 %collective-permute-start.23 = (bf16[2,384,128]{2,1,0:T(8,128)(2,1)S(1)}, bf16[2,384,128]{2,1,0:T(8,128)(2,1)S(1)}, u32[]{:S(2)}, u32[]{:S(2)}) collective-permute-start(bf16[2,384,128]{2,1,0:T(8,128)(2,1)S(1)} %get-tuple-element.56.rest_0_), channel_id=1, source_target_pairs={{4,6},{5,7},{6,4},{7,5},{12,14},{13,15},{14,12},{15,13},{20,22},{2... | collective-permute-start | bytes 589832 | tf_op jit(solution)/shard_map/ppermute | solution.py:346

commit v4 on v3

--- a/solution.py
+++ b/solution.py
@@ -78,34 +78,55 @@
     )(slot_subarray_index, assignment.reshape(antennas // LANES, LANES))
 
 
-def split_kernel(chans, x_ref, *rest):
-    *outs, sem = rest
+def give_kernel(chips, x_ref, out):
     me = lax.axis_index("chan")
-    early = chans // 2
-    wanted = [(x_ref.at[1, me ^ (2 * r + (me & 1))], outs[0].at[r]) for r in range(early)]
     for k in range(2):
-        wanted += [(x_ref.at[k, me ^ s], outs[1 + k * chans + s]) for s in range(chans)]
-    copies = [pltpu.make_async_copy(a, b, sem.at[i]) for i, (a, b) in enumerate(wanted)]
-    for copy in copies:
-        copy.start()
-    for copy in copies:
-        copy.wait()
-
-
-def split(voltages):
-    _, chans, inputs, samples = voltages.shape
-    piece = jax.ShapeDtypeStruct((inputs, samples), voltages.dtype)
-    raw = jax.ShapeDtypeStruct((chans // 2, inputs, samples), voltages.dtype)
+        for t in range(chips):
+            out[k, t] = x_ref[k, (me ^ (2 * t)) ^ 1]
+
+
+def give(voltages):
+    parts, chans, inputs, samples = voltages.shape
+    return pl.pallas_call(
+        functools.partial(give_kernel, chans // 2),
+        out_shape=jax.ShapeDtypeStruct((parts, chans // 2, inputs, samples), voltages.dtype),
+        in_specs=[VMEM],
+        out_specs=VMEM,
+        compiler_params=PARAMS,
+        cost_estimate=pl.CostEstimate(flops=1_000_000, bytes_accessed=1_000_000, transcendentals=0),
+    )(voltages)
+
+
+def merge_kernel(chips, x_ref, given_ref, raw, *outs):
+    me = lax.axis_index("chan")
+    inputs = x_ref.shape[2]
+    mine = pl.multiple_of((me & 1) * inputs, inputs)
+    theirs = pl.multiple_of(inputs - (me & 1) * inputs, inputs)
+    for k in range(2):
+        for t in range(chips):
+            out = outs[k * chips + t]
+            piece, other = x_ref[k, me ^ (2 * t)], given_ref[k, t]
+            out[pl.ds(mine, inputs)] = piece
+            out[pl.ds(theirs, inputs)] = other
+            if k:
+                raw[t, pl.ds(mine, inputs)] = piece
+                raw[t, pl.ds(theirs, inputs)] = other
+
+
+def merge(voltages, given):
+    parts, chans, inputs, samples = voltages.shape
+    chips = chans // 2
+    piece = jax.ShapeDtypeStruct((2 * inputs, samples), voltages.dtype)
+    raw = jax.ShapeDtypeStruct((chips, 2 * inputs, samples), voltages.dtype)
     out = pl.pallas_call(
-        functools.partial(split_kernel, chans),
-        out_shape=[raw] + [piece] * (2 * chans),
-        in_specs=[pl.BlockSpec(memory_space=pltpu.HBM)],
-        out_specs=[VMEM] * (2 * chans + 1),
-        scratch_shapes=[pltpu.SemaphoreType.DMA((2 * chans + chans // 2,))],
+        functools.partial(merge_kernel, chips),
+        out_shape=[raw] + [piece] * (parts * chips),
+        in_specs=[VMEM] * 2,
+        out_specs=[VMEM] * (1 + parts * chips),
         compiler_params=PARAMS,
         cost_estimate=pl.CostEstimate(flops=1_000_000, bytes_accessed=2_000_000, transcendentals=0),
-    )(voltages)
-    return out[0], out[1 : 1 + chans], out[1 + chans :]
+    )(voltages, given)
+    return out[0], out[1 : 1 + chips], out[1 + chips :]
 
 
 def unstack_kernel(x_ref, *outs):
@@ -128,13 +149,13 @@
 def load_pair(steps, xs, wide, pair):
     inputs = xs[0].shape[0]
     antennas = inputs // 2
-    me = lax.axis_index("chan")
+    chip = lax.axis_index("chan") // 2
     for i, (step, x) in enumerate(zip(steps, xs)):
         wide[i * inputs : (i + 1) * inputs] = x[...].astype(jnp.float32)
         if len(steps) == 1:
             top = 0
         else:
-            top = pl.multiple_of(partner(me, step, len(steps)) * antennas, antennas)
+            top = pl.multiple_of((chip ^ step) * antennas, antennas)
         for pol in range(2):
             pair[pl.ds(top, antennas), pol * LANES : (pol + 1) * LANES] = wide[
                 pl.ds(i * inputs + pol, antennas, stride=2), :
@@ -293,14 +314,14 @@
     return x.reshape(x.shape[1], x.shape[2])
 
 
-CHAN_ORDER = (6, 7, 2, 3, 4, 5, 1)
-
-
-def cross(chunks, chans):
+CHIP_ORDER = (3, 1, 2)
+
+
+def cross(chunks, chans, starts):
     got = list(chunks)
-    for step in CHAN_ORDER:
-        if step < chans:
-            got[step] = lax.ppermute(chunks[step], "chan", [(i, i ^ step) for i in range(chans)])
+    for step in CHIP_ORDER:
+        if 2 * step < chans:
+            got[step] = lax.ppermute(chunks[step], "chan", [(i, i ^ (2 * step)) for i in starts])
     return got
 
 
@@ -324,21 +345,18 @@
         imag = exchange(gather(select, [imag], (0,), groups, per, SLOT), first + [last], groups)
         return gram(real, imag, last)
 
-    steps = tuple(range(chans))
+    steps = tuple(range(chans // 2))
     device = [(i, j, i * groups + j) for i in range(chans) for j in range(groups)]
-    raw, reals, imags = split(voltages)
-    raw = lax.ppermute(raw, "tm", [(j, j ^ 2) for j in range(groups)])
-    reals = cross(reals, chans)
+    given = lax.ppermute(give(voltages), "chan", [(i, i ^ 1) for i in range(chans)])
+    raw, reals, imags = merge(voltages, given)
+    pairs = [(n, i * groups + (j ^ 2)) for i, j, n in device if i % 2 == 0]
+    raw = lax.ppermute(raw, ("chan", "tm"), pairs)
+    reals = cross(reals, chans, range(chans))
     select = plan(assignment, slot_subarray_index, groups, SLOT // 2)
     real = exchange(gather(select, reals, steps, groups, per, SLOT), order, groups)
 
-    imags = cross(imags, chans)
-    pieces = unstack(raw)
-    far = [pieces[s // 2] for s in steps]
-    for step in CHAN_ORDER:
-        if step < chans:
-            pairs = [(i, i ^ step) for i in range(chans) if (i ^ step) % 2 == 0]
-            far[step] = lax.ppermute(far[step], "chan", pairs)
+    imags = cross(imags, chans, range(chans))
+    far = cross(unstack(raw), chans, range(0, chans, 2))
     mine, near, third, fourth = twin(select, imags, far, steps, per, SLOT)
     pairs = [(n, i * groups + (j ^ (3 if i % 2 else 1))) for i, j, n in device]
     fourth = lax.ppermute(fourth, ("chan", "tm"), pairs)

time: 74 us -> 57.4 us (0.78)
  the two profiles are of different devices: /device:TPU:1 before, /device:TPU:0 now
where the time goes in v4:
time: 57.4 us; the launch traced here: 57.1 us
  starting transfers between devices  30.9 us (54%)
  waiting for transfers between devices  16.7 us (29%)
  Pallas kernels  8.16 us (14%)
  local copies, waits for them, and re-layouts  1.23 us (2%)
    ppermute x9, starting transfers between devices, cross(): lax.ppermute(chunks[step], 'chan', [(i, i ^ 2 * step) for i in starts])  17.6 us
    ppermute x1, waiting for transfers between devices, steps_of(): raw = lax.ppermute(raw, ('chan', 'tm'), pairs)  7.81 us
    ppermute x1, starting transfers between devices, steps_of(): raw = lax.ppermute(raw, ('chan', 'tm'), pairs)  5.85 us
    ppermute x3, starting transfers between devices, exchange(): got[step] = lax.ppermute(chunks[step], 'tm', pairs)  4.14 us
    ppermute x1, waiting for transfers between devices, steps_of(): fourth = lax.ppermute(fourth, ('chan', 'tm'), pairs)  4.1 us
    pallas_call x1, Pallas kernels, plan(): pl.pallas_call(functools.partial(plan_kernel, groups, half), out_shape=ja...  2.06 us
    ppermute x1, waiting for transfers between devices, steps_of(): near = lax.ppermute(near, 'tm', [(j, j ^ 1) for j in range(groups)])  2.03 us
    pallas_call x1, Pallas kernels, gram(): pl.pallas_call(late_kernel, out_shape=jax.ShapeDtypeStruct((per, 1, 2, sl...  1.73 us
  transfers between devices with their start and end apart: 17, of which 5 were waited for; matrix products, arithmetic and copies ran while one was open for 0% of the time, Pallas kernels for 11%

profile of v4, /device:TPU:0, one launch (start us, length us, event | category | flops | bytes accessed | tf_op | source)
XLA Modules:
  0.0 57.1 jit_solution(2003879515707180795)
XLA Ops:
  0.0 0.0 copy-start
  0.0 1.2 %copy-done = bf16[2,8,256,128]{3,2,1,0:T(8,128)(2,1)S(1)} copy-done((bf16[2,8,256,128]{3,2,1,0:T(8,128)(2,1)S(1)}, bf16[2,8,256,128]{3,2,1,0:T(8,128)(2,1)}, u32[]{:S(2)}) %copy-start) | copy-done | bytes 1048600
  1.2 0.0 copy-start.1
  1.2 0.0 copy-start.2
  1.3 0.6 collective-permute-start
  1.8 1.5 %collective-permute-done.given_ref = bf16[2,4,256,128]{3,2,1,0:T(8,128)(2,1)S(1)} collective-permute-done((bf16[2,4,256,128]{3,2,1,0:T(8,128)(2,1)S(1)}, bf16[2,4,256,128]{3,2,1,0:T(8,128)(2,1)S(1)}, u32[]{:S(2)}, u32[]{:S(2)}) %collective-permute-start) | collective-permute-done | bytes 524320 | tf_op jit(solution)/shard_map/ppermute | solution.py:350
  3.4 0.2 shard_map.39
  3.5 5.9 %collective-permute-start.8 = (bf16[4,512,128]{2,1,0:T(8,128)(2,1)S(1)}, bf16[4,512,128]{2,1,0:T(8,128)(2,1)S(1)}, u32[]{:S(2)}, u32[]{:S(2)}) collective-permute-start(bf16[4,512,128]{2,1,0:T(8,128)(2,1)S(1)} %get-tuple-element.35), channel_id=1, source_target_pairs={{0,2},{1,3},{2,0},{3,1},{8,10},{9,11},{10,8},{11,9},{16,18},{17,19... | collective-permute-start | bytes 1572872 | tf_op jit(solution)/shard_map/ppermute | solution.py:353
  9.4 1.6 %collective-permute-start.1 = (bf16[512,128]{1,0:T(8,128)(2,1)S(1)}, bf16[512,128]{1,0:T(8,128)(2,1)S(1)}, u32[]{:S(2)}, u32[]{:S(2)}) collective-permute-start(bf16[512,128]{1,0:T(8,128)(2,1)S(1)} %get-tuple-element.27), channel_id=1, source_target_pairs={{0,8},{4,12},{8,0},{12,4},{16,24},{20,28},{24,16},{28,20},{1,9},{5... | collective-permute-start | bytes 393224 | tf_op jit(solution)/shard_map/ppermute | solution.py:324
  11.0 1.5 %collective-permute-start.2 = (bf16[512,128]{1,0:T(8,128)(2,1)S(1)}, bf16[512,128]{1,0:T(8,128)(2,1)S(1)}, u32[]{:S(2)}, u32[]{:S(2)}) collective-permute-start(bf16[512,128]{1,0:T(8,128)(2,1)S(1)} %get-tuple-element.28), channel_id=1, source_target_pairs={{0,16},{4,20},{8,24},{12,28},{16,0},{20,4},{24,8},{28,12},{1,17},{... | collective-permute-start | bytes 393224 | tf_op jit(solution)/shard_map/ppermute | solution.py:324
  12.5 0.5 collective-permute-start.3
  13.0 1.5 %collective-permute-start.5 = (bf16[512,128]{1,0:T(8,128)(2,1)S(1)}, bf16[512,128]{1,0:T(8,128)(2,1)S(1)}, u32[]{:S(2)}, u32[]{:S(2)}) collective-permute-start(bf16[512,128]{1,0:T(8,128)(2,1)S(1)} %get-tuple-element.32), channel_id=1, source_target_pairs={{0,8},{4,12},{8,0},{12,4},{16,24},{20,28},{24,16},{28,20},{1,9},{5... | collective-permute-start | bytes 393224 | tf_op jit(solution)/shard_map/ppermute | solution.py:324
  14.5 7.8 %collective-permute-done.8.x_ref = bf16[4,512,128]{2,1,0:T(8,128)(2,1)S(1)} collective-permute-done((bf16[4,512,128]{2,1,0:T(8,128)(2,1)S(1)}, bf16[4,512,128]{2,1,0:T(8,128)(2,1)S(1)}, u32[]{:S(2)}, u32[]{:S(2)}) %collective-permute-start.8) | collective-permute-done | bytes 524320 | tf_op jit(solution)/shard_map/ppermute | solution.py:353
  22.3 1.8 %collective-permute-start.6 = (bf16[512,128]{1,0:T(8,128)(2,1)S(1)}, bf16[512,128]{1,0:T(8,128)(2,1)S(1)}, u32[]{:S(2)}, u32[]{:S(2)}) collective-permute-start(bf16[512,128]{1,0:T(8,128)(2,1)S(1)} %get-tuple-element.33), channel_id=1, source_target_pairs={{0,16},{4,20},{8,24},{12,28},{16,0},{20,4},{24,8},{28,12},{1,17},{... | collective-permute-start | bytes 393224 | tf_op jit(solution)/shard_map/ppermute | solution.py:324
  24.1 0.0 collective-permute-done.1.rest_1_
  24.2 1.5 %collective-permute-start.7 = (bf16[512,128]{1,0:T(8,128)(2,1)S(1)}, bf16[512,128]{1,0:T(8,128)(2,1)S(1)}, u32[]{:S(2)}, u32[]{:S(2)}) collective-permute-start(bf16[512,128]{1,0:T(8,128)(2,1)S(1)} %get-tuple-element.34), channel_id=1, source_target_pairs={{0,24},{4,28},{8,16},{12,20},{16,8},{20,12},{24,0},{28,4},{1,25},{... | collective-permute-start | bytes 393224 | tf_op jit(solution)/shard_map/ppermute | solution.py:324
  25.7 0.0 collective-permute-done.2.rest_2_
  25.7 2.1 %collective-permute-start.9 = (bf16[512,128]{1,0:T(8,128)(2,1)S(1)}, bf16[512,128]{1,0:T(8,128)(2,1)S(1)}, u32[]{:S(2)}, u32[]{:S(2)}) collective-permute-start(bf16[512,128]{1,0:T(8,128)(2,1)S(1)} %get-tuple-element.37), channel_id=1, source_target_pairs={{0,8},{8,0},{16,24},{24,16},{1,9},{9,1},{17,25},{25,17},{2,10},{10... | collective-permute-start | bytes 393224 | tf_op jit(solution)/shard_map/ppermute | solution.py:324
  27.8 0.0 collective-permute-done.3.rest_3_
  27.8 3.8 %collective-permute-start.10 = (bf16[512,128]{1,0:T(8,128)(2,1)S(1)}, bf16[512,128]{1,0:T(8,128)(2,1)S(1)}, u32[]{:S(2)}, u32[]{:S(2)}) collective-permute-start(bf16[512,128]{1,0:T(8,128)(2,1)S(1)} %get-tuple-element.38), channel_id=1, source_target_pairs={{0,16},{8,24},{16,0},{24,8},{1,17},{9,25},{17,1},{25,9},{2,18},{10... | collective-permute-start | bytes 393224 | tf_op jit(solution)/shard_map/ppermute | solution.py:324
  31.6 0.0 collective-permute-done.5.rest_1_
  31.6 3.3 %collective-permute-start.11 = (bf16[512,128]{1,0:T(8,128)(2,1)S(1)}, bf16[512,128]{1,0:T(8,128)(2,1)S(1)}, u32[]{:S(2)}, u32[]{:S(2)}) collective-permute-start(bf16[512,128]{1,0:T(8,128)(2,1)S(1)} %get-tuple-element.39), channel_id=1, source_target_pairs={{0,24},{8,16},{16,8},{24,0},{1,25},{9,17},{17,9},{25,1},{2,26},{10... | collective-permute-start | bytes 393224 | tf_op jit(solution)/shard_map/ppermute | solution.py:324
  34.9 0.0 copy-done.1
  34.9 0.0 copy-done.2
  34.9 2.1 %shard_map.37.select_ref = bf16[1536,1024]{1,0:T(8,128)(2,1)S(1)} custom-call(s32[8]{0:T(128)S(1)} %copy-done.2, s32[8,128]{1,0:T(8,128)S(1)} %bitcast.1), custom_call_target="tpu_custom_call" | custom-call | flops 4000000000 | bytes 3000000 | tf_op jit(solution)/shard_map/pallas_call | solution.py:71
  37.0 1.3 %shard_map.40 = (bf16[2,384,128]{2,1,0:T(8,128)(2,1)S(1)}, bf16[2,384,128]{2,1,0:T(8,128)(2,1)S(1)}, bf16[2,384,128]{2,1,0:T(8,128)(2,1)S(1)}, bf16[2,384,128]{2,1,0:T(8,128)(2,1)S(1)}) custom-call(bf16[1536,1024]{1,0:T(8,128)(2,1)S(1)} %shard_map.37.select_ref, bf16[512,128]{1,0:T(8,128)(2,1)S(1)} %get-tuple-element.26.rest_0_, ...), custom_call_target="tpu_custom_call" | custom-call | flops 805306368 | bytes 4000000 | tf_op jit(solution)/shard_map/pallas_call | solution.py:223
  38.3 0.0 collective-permute-done.6.rest_2_
  38.3 0.6 %collective-permute-start.13 = (bf16[2,384,128]{2,1,0:T(8,128)(2,1)S(1)}, bf16[2,384,128]{2,1,0:T(8,128)(2,1)S(1)}, u32[]{:S(2)}, u32[]{:S(2)}) collective-permute-start(bf16[2,384,128]{2,1,0:T(8,128)(2,1)S(1)} %get-tuple-element.42), channel_id=1, source_target_pairs={{0,1},{1,0},{2,3},{3,2},{4,5},{5,4},{6,7},{7,6},{8,9},{9,8},{10,11... | collective-permute-start | bytes 589832 | tf_op jit(solution)/shard_map/ppermute | solution.py:308
  39.0 0.0 collective-permute-done.7.rest_3_
  39.0 3.0 %collective-permute-start.14 = (bf16[2,384,128]{2,1,0:T(8,128)(2,1)S(1)}, bf16[2,384,128]{2,1,0:T(8,128)(2,1)S(1)}, u32[]{:S(2)}, u32[]{:S(2)}) collective-permute-start(bf16[2,384,128]{2,1,0:T(8,128)(2,1)S(1)} %get-tuple-element.43), channel_id=1, source_target_pairs={{0,3},{1,2},{2,1},{3,0},{4,7},{5,6},{6,5},{7,4},{8,11},{9,10},{10,... | collective-permute-start | bytes 589832 | tf_op jit(solution)/shard_map/ppermute | solution.py:308
  42.0 0.0 collective-permute-done.9.rest_5_
  42.0 0.0 collective-permute-done.10.rest_6_
  42.0 0.0 collective-permute-done.11.rest_7_
  42.0 1.4 %shard_map.42 = (bf16[2,384,128]{2,1,0:T(8,128)(2,1)S(1)}, bf16[2,384,128]{2,1,0:T(8,128)(2,1)S(1)}, bf16[2,384,128]{2,1,0:T(8,128)(2,1)S(1)}, bf16[2,384,128]{2,1,0:T(8,128)(2,1)S(1)}) custom-call(bf16[1536,1024]{1,0:T(8,128)(2,1)S(1)} %shard_map.37.select_ref, bf16[512,128]{1,0:T(8,128)(2,1)S(1)} %get-tuple-element.31.rest_0_, ...), custom_call_target="tpu_custom_call" | custom-call | flops 805306368 | bytes 4000000 | tf_op jit(solution)/shard_map/pallas_call | solution.py:203
  43.4 1.1 %collective-permute-start.15 = (bf16[2,384,128]{2,1,0:T(8,128)(2,1)S(1)}, bf16[2,384,128]{2,1,0:T(8,128)(2,1)S(1)}, u32[]{:S(2)}, u32[]{:S(2)}) collective-permute-start(bf16[2,384,128]{2,1,0:T(8,128)(2,1)S(1)} %get-tuple-element.45), channel_id=1, source_target_pairs={{0,1},{1,0},{2,3},{3,2},{4,5},{5,4},{6,7},{7,6},{8,9},{9,8},{10,11... | collective-permute-start | bytes 589832 | tf_op jit(solution)/shard_map/ppermute | solution.py:365
  44.5 1.0 %collective-permute-start.16 = (bf16[2,384,128]{2,1,0:T(8,128)(2,1)S(1)}, bf16[2,384,128]{2,1,0:T(8,128)(2,1)S(1)}, u32[]{:S(2)}, u32[]{:S(2)}) collective-permute-start(bf16[2,384,128]{2,1,0:T(8,128)(2,1)S(1)} %get-tuple-element.46), channel_id=1, source_target_pairs={{0,1},{1,0},{2,3},{3,2},{4,7},{5,6},{6,5},{7,4},{8,9},{9,8},{10,11... | collective-permute-start | bytes 589832 | tf_op jit(solution)/shard_map/ppermute | solution.py:362
  45.5 0.5 collective-permute-start.4
  46.0 0.0 collective-permute-done.13.refs_1_
  46.0 0.7 %collective-permute-start.12 = (bf16[2,384,128]{2,1,0:T(8,128)(2,1)S(1)}, bf16[2,384,128]{2,1,0:T(8,128)(2,1)S(1)}, u32[]{:S(2)}, u32[]{:S(2)}) collective-permute-start(bf16[2,384,128]{2,1,0:T(8,128)(2,1)S(1)} %get-tuple-element.40.rest_0_), channel_id=1, source_target_pairs={{4,6},{5,7},{6,4},{7,5},{12,14},{13,15},{14,12},{15,13},{20,22},{2... | collective-permute-start | bytes 589832 | tf_op jit(solution)/shard_map/ppermute | solution.py:364
  46.7 1.1 %collective-permute-done.14.refs_2_ = bf16[2,384,128]{2,1,0:T(8,128)(2,1)S(1)} collective-permute-done((bf16[2,384,128]{2,1,0:T(8,128)(2,1)S(1)}, bf16[2,384,128]{2,1,0:T(8,128)(2,1)S(1)}, u32[]{:S(2)}, u32[]{:S(2)}) %collective-permute-start.14) | collective-permute-done | bytes 196640 | tf_op jit(solution)/shard_map/ppermute | solution.py:308
  47.8 2.0 %collective-permute-done.15.refs_4_ = bf16[2,384,128]{2,1,0:T(8,128)(2,1)S(1)} collective-permute-done((bf16[2,384,128]{2,1,0:T(8,128)(2,1)S(1)}, bf16[2,384,128]{2,1,0:T(8,128)(2,1)S(1)}, u32[]{:S(2)}, u32[]{:S(2)}) %collective-permute-start.15) | collective-permute-done | bytes 196640 | tf_op jit(solution)/shard_map/ppermute | solution.py:365
  49.8 4.1 %collective-permute-done.16.refs_5_ = bf16[2,384,128]{2,1,0:T(8,128)(2,1)S(1)} collective-permute-done((bf16[2,384,128]{2,1,0:T(8,128)(2,1)S(1)}, bf16[2,384,128]{2,1,0:T(8,128)(2,1)S(1)}, u32[]{:S(2)}, u32[]{:S(2)}) %collective-permute-start.16) | collective-permute-done | bytes 196640 | tf_op jit(solution)/shard_map/ppermute | solution.py:362
  53.9 1.4 %shard_map.43.rest_2_ = f32[2,2,384,384]{3,2,1,0:T(8,128)S(1)} custom-call(bf16[2,384,128]{2,1,0:T(8,128)(2,1)S(1)} %get-tuple-element.41.refs_0_, bf16[2,384,128]{2,1,0:T(8,128)(2,1)S(1)} %collective-permute-done.13.refs_1_, bf16[2,384,128]{2,1,0:T(8,128)(2,1)S(1)} %collective-permute-done.14.refs_2_, bf16[2,384,128]{2,1,0:T(8,128)(2,1)S(1)} %get-tuple-element.44.refs_3_, ...), custom_call_target="tpu_custom_call" | custom-call | flops 905969664 | bytes 3000000 | tf_op jit(solution)/shard_map/pallas_call | solution.py:282
  55.3 0.0 collective-permute-done.4.real
  55.4 0.0 collective-permute-done.12.rest_1_
  55.4 1.7 %shard_map.44 = f32[2,1,2,384,384]{4,3,2,1,0:T(8,128)} custom-call(bf16[2,384,128]{2,1,0:T(8,128)(2,1)S(1)} %collective-permute-done.4.real, bf16[2,384,128]{2,1,0:T(8,128)(2,1)S(1)} %get-tuple-element.40.rest_0_, bf16[2,384,128]{2,1,0:T(8,128)(2,1)S(1)} %collective-permute-done.12.rest_1_, f32[2,2,384,384]{3,2,1,0:T(8,128)S(1)} %shard_map.43.rest_2_), custom_call_target="tpu_custom_call" | custom-call | flops 301989888 | bytes 3000000 | tf_op jit(solution)/shard_map/pallas_call | solution.py:290
  (2 shorter events, 0.1 us)
Async XLA Ops:
  0.0 1.2 %copy-start = (bf16[2,8,256,128]{3,2,1,0:T(8,128)(2,1)S(1)}, bf16[2,8,256,128]{3,2,1,0:T(8,128)(2,1)}, u32[]{:S(2)}) copy-start(bf16[2,8,256,128]{3,2,1,0:T(8,128)(2,1)} %x_ref.3) | copy-start | bytes 3145732
  1.2 33.7 %copy-start.1 = (s32[1024,1]{0,1:T(1,128)S(1)}, s32[1024,1]{0,1:T(1,128)}, u32[]{:S(2)}) copy-start(s32[1024,1]{0,1:T(1,128)} %param.4) | copy-start | bytes 12292
  1.2 33.7 %copy-start.2 = (s32[8]{0:T(128)S(1)}, s32[8]{0:T(128)}, u32[]{:S(2)}) copy-start(s32[8]{0:T(128)} %slot_ref.1) | copy-start | bytes 100
  1.3 2.1 %collective-permute-start = (bf16[2,4,256,128]{3,2,1,0:T(8,128)(2,1)S(1)}, bf16[2,4,256,128]{3,2,1,0:T(8,128)(2,1)S(1)}, u32[]{:S(2)}, u32[]{:S(2)}) collective-permute-start(bf16[2,4,256,128]{3,2,1,0:T(8,128)(2,1)S(1)} %shard_map.38), channel_id=1, source_target_pairs={{0,4},{4,0},{8,12},{12,8},{16,20},{20,16},{24,28},{28,24},{1,5},{5... | collective-permute-start | bytes 1572872 | tf_op jit(solution)/shard_map/ppermute | solution.py:350
  3.5 18.7 %collective-permute-start.8 = (bf16[4,512,128]{2,1,0:T(8,128)(2,1)S(1)}, bf16[4,512,128]{2,1,0:T(8,128)(2,1)S(1)}, u32[]{:S(2)}, u32[]{:S(2)}) collective-permute-start(bf16[4,512,128]{2,1,0:T(8,128)(2,1)S(1)} %get-tuple-element.35), channel_id=1, source_target_pairs={{0,2},{1,3},{2,0},{3,1},{8,10},{9,11},{10,8},{11,9},{16,18},{17,19... | collective-permute-start | bytes 1572872 | tf_op jit(solution)/shard_map/ppermute | solution.py:353
  9.4 14.7 %collective-permute-start.1 = (bf16[512,128]{1,0:T(8,128)(2,1)S(1)}, bf16[512,128]{1,0:T(8,128)(2,1)S(1)}, u32[]{:S(2)}, u32[]{:S(2)}) collective-permute-start(bf16[512,128]{1,0:T(8,128)(2,1)S(1)} %get-tuple-element.27), channel_id=1, source_target_pairs={{0,8},{4,12},{8,0},{12,4},{16,24},{20,28},{24,16},{28,20},{1,9},{5... | collective-permute-start | bytes 393224 | tf_op jit(solution)/shard_map/ppermute | solution.py:324
  11.0 14.7 %collective-permute-start.2 = (bf16[512,128]{1,0:T(8,128)(2,1)S(1)}, bf16[512,128]{1,0:T(8,128)(2,1)S(1)}, u32[]{:S(2)}, u32[]{:S(2)}) collective-permute-start(bf16[512,128]{1,0:T(8,128)(2,1)S(1)} %get-tuple-element.28), channel_id=1, source_target_pairs={{0,16},{4,20},{8,24},{12,28},{16,0},{20,4},{24,8},{28,12},{1,17},{... | collective-permute-start | bytes 393224 | tf_op jit(solution)/shard_map/ppermute | solution.py:324
  12.5 15.3 %collective-permute-start.3 = (bf16[512,128]{1,0:T(8,128)(2,1)S(1)}, bf16[512,128]{1,0:T(8,128)(2,1)S(1)}, u32[]{:S(2)}, u32[]{:S(2)}) collective-permute-start(bf16[512,128]{1,0:T(8,128)(2,1)S(1)} %get-tuple-element.29), channel_id=1, source_target_pairs={{0,24},{4,28},{8,16},{12,20},{16,8},{20,12},{24,0},{28,4},{1,25},{... | collective-permute-start | bytes 393224 | tf_op jit(solution)/shard_map/ppermute | solution.py:324
  13.0 18.6 %collective-permute-start.5 = (bf16[512,128]{1,0:T(8,128)(2,1)S(1)}, bf16[512,128]{1,0:T(8,128)(2,1)S(1)}, u32[]{:S(2)}, u32[]{:S(2)}) collective-permute-start(bf16[512,128]{1,0:T(8,128)(2,1)S(1)} %get-tuple-element.32), channel_id=1, source_target_pairs={{0,8},{4,12},{8,0},{12,4},{16,24},{20,28},{24,16},{28,20},{1,9},{5... | collective-permute-start | bytes 393224 | tf_op jit(solution)/shard_map/ppermute | solution.py:324
  22.3 16.1 %collective-permute-start.6 = (bf16[512,128]{1,0:T(8,128)(2,1)S(1)}, bf16[512,128]{1,0:T(8,128)(2,1)S(1)}, u32[]{:S(2)}, u32[]{:S(2)}) collective-permute-start(bf16[512,128]{1,0:T(8,128)(2,1)S(1)} %get-tuple-element.33), channel_id=1, source_target_pairs={{0,16},{4,20},{8,24},{12,28},{16,0},{20,4},{24,8},{28,12},{1,17},{... | collective-permute-start | bytes 393224 | tf_op jit(solution)/shard_map/ppermute | solution.py:324
  24.2 14.8 %collective-permute-start.7 = (bf16[512,128]{1,0:T(8,128)(2,1)S(1)}, bf16[512,128]{1,0:T(8,128)(2,1)S(1)}, u32[]{:S(2)}, u32[]{:S(2)}) collective-permute-start(bf16[512,128]{1,0:T(8,128)(2,1)S(1)} %get-tuple-element.34), channel_id=1, source_target_pairs={{0,24},{4,28},{8,16},{12,20},{16,8},{20,12},{24,0},{28,4},{1,25},{... | collective-permute-start | bytes 393224 | tf_op jit(solution)/shard_map/ppermute | solution.py:324
  25.7 16.3 %collective-permute-start.9 = (bf16[512,128]{1,0:T(8,128)(2,1)S(1)}, bf16[512,128]{1,0:T(8,128)(2,1)S(1)}, u32[]{:S(2)}, u32[]{:S(2)}) collective-permute-start(bf16[512,128]{1,0:T(8,128)(2,1)S(1)} %get-tuple-element.37), channel_id=1, source_target_pairs={{0,8},{8,0},{16,24},{24,16},{1,9},{9,1},{17,25},{25,17},{2,10},{10... | collective-permute-start | bytes 393224 | tf_op jit(solution)/shard_map/ppermute | solution.py:324
  27.8 14.2 %collective-permute-start.10 = (bf16[512,128]{1,0:T(8,128)(2,1)S(1)}, bf16[512,128]{1,0:T(8,128)(2,1)S(1)}, u32[]{:S(2)}, u32[]{:S(2)}) collective-permute-start(bf16[512,128]{1,0:T(8,128)(2,1)S(1)} %get-tuple-element.38), channel_id=1, source_target_pairs={{0,16},{8,24},{16,0},{24,8},{1,17},{9,25},{17,1},{25,9},{2,18},{10... | collective-permute-start | bytes 393224 | tf_op jit(solution)/shard_map/ppermute | solution.py:324
  31.6 10.4 %collective-permute-start.11 = (bf16[512,128]{1,0:T(8,128)(2,1)S(1)}, bf16[512,128]{1,0:T(8,128)(2,1)S(1)}, u32[]{:S(2)}, u32[]{:S(2)}) collective-permute-start(bf16[512,128]{1,0:T(8,128)(2,1)S(1)} %get-tuple-element.39), channel_id=1, source_target_pairs={{0,24},{8,16},{16,8},{24,0},{1,25},{9,17},{17,9},{25,1},{2,26},{10... | collective-permute-start | bytes 393224 | tf_op jit(solution)/shard_map/ppermute | solution.py:324
  38.3 7.7 %collective-permute-start.13 = (bf16[2,384,128]{2,1,0:T(8,128)(2,1)S(1)}, bf16[2,384,128]{2,1,0:T(8,128)(2,1)S(1)}, u32[]{:S(2)}, u32[]{:S(2)}) collective-permute-start(bf16[2,384,128]{2,1,0:T(8,128)(2,1)S(1)} %get-tuple-element.42), channel_id=1, source_target_pairs={{0,1},{1,0},{2,3},{3,2},{4,5},{5,4},{6,7},{7,6},{8,9},{9,8},{10,11... | collective-permute-start | bytes 589832 | tf_op jit(solution)/shard_map/ppermute | solution.py:308
  39.0 8.8 %collective-permute-start.14 = (bf16[2,384,128]{2,1,0:T(8,128)(2,1)S(1)}, bf16[2,384,128]{2,1,0:T(8,128)(2,1)S(1)}, u32[]{:S(2)}, u32[]{:S(2)}) collective-permute-start(bf16[2,384,128]{2,1,0:T(8,128)(2,1)S(1)} %get-tuple-element.43), channel_id=1, source_target_pairs={{0,3},{1,2},{2,1},{3,0},{4,7},{5,6},{6,5},{7,4},{8,11},{9,10},{10,... | collective-permute-start | bytes 589832 | tf_op jit(solution)/shard_map/ppermute | solution.py:308
  43.4 6.4 %collective-permute-start.15 = (bf16[2,384,128]{2,1,0:T(8,128)(2,1)S(1)}, bf16[2,384,128]{2,1,0:T(8,128)(2,1)S(1)}, u32[]{:S(2)}, u32[]{:S(2)}) collective-permute-start(bf16[2,384,128]{2,1,0:T(8,128)(2,1)S(1)} %get-tuple-element.45), channel_id=1, source_target_pairs={{0,1},{1,0},{2,3},{3,2},{4,5},{5,4},{6,7},{7,6},{8,9},{9,8},{10,11... | collective-permute-start | bytes 589832 | tf_op jit(solution)/shard_map/ppermute | solution.py:365
  44.5 9.4 %collective-permute-start.16 = (bf16[2,384,128]{2,1,0:T(8,128)(2,1)S(1)}, bf16[2,384,128]{2,1,0:T(8,128)(2,1)S(1)}, u32[]{:S(2)}, u32[]{:S(2)}) collective-permute-start(bf16[2,384,128]{2,1,0:T(8,128)(2,1)S(1)} %get-tuple-element.46), channel_id=1, source_target_pairs={{0,1},{1,0},{2,3},{3,2},{4,7},{5,6},{6,5},{7,4},{8,9},{9,8},{10,11... | collective-permute-start | bytes 589832 | tf_op jit(solution)/shard_map/ppermute | solution.py:362
  45.5 9.8 %collective-permute-start.4 = (bf16[2,384,128]{2,1,0:T(8,128)(2,1)S(1)}, bf16[2,384,128]{2,1,0:T(8,128)(2,1)S(1)}, u32[]{:S(2)}, u32[]{:S(2)}) collective-permute-start(bf16[2,384,128]{2,1,0:T(8,128)(2,1)S(1)} %get-tuple-element.30), channel_id=1, source_target_pairs={{0,2},{1,3},{2,0},{3,1},{4,6},{5,7},{6,4},{7,5},{8,10},{9,11},{10,... | collective-permute-start | bytes 589832 | tf_op jit(solution)/shard_map/ppermute | solution.py:308
  46.0 9.4 %collective-permute-start.12 = (bf16[2,384,128]{2,1,0:T(8,128)(2,1)S(1)}, bf16[2,384,128]{2,1,0:T(8,128)(2,1)S(1)}, u32[]{:S(2)}, u32[]{:S(2)}) collective-permute-start(bf16[2,384,128]{2,1,0:T(8,128)(2,1)S(1)} %get-tuple-element.40.rest_0_), channel_id=1, source_target_pairs={{4,6},{5,7},{6,4},{7,5},{12,14},{13,15},{14,12},{15,13},{20,22},{2... | collective-permute-start | bytes 589832 | tf_op jit(solution)/shard_map/ppermute | solution.py:364

commit v5 on v2

--- a/solution.py
+++ b/solution.py
@@ -10,6 +10,7 @@
 
 SLOT = 384
 LANES = 128
+
 
 VMEM = pl.BlockSpec(memory_space=pltpu.VMEM)
 SMEM = pl.BlockSpec(memory_space=pltpu.SMEM)
@@ -77,53 +78,71 @@
     )(slot_subarray_index, assignment.reshape(antennas // LANES, LANES))
 
 
-def split_kernel(steps, x_ref, *rest):
-    *outs, sem = rest
-    chunks, other = outs[:-1], outs[-1]
+def give_kernel(chips, x_ref, out):
     me = lax.axis_index("chan")
-    copies = [
-        pltpu.make_async_copy(x_ref.at[0, partner(me, step, len(steps))], chunk, sem.at[i])
-        for i, (step, chunk) in enumerate(zip(steps, chunks))
-    ]
-    copies.append(pltpu.make_async_copy(x_ref.at[1], other, sem.at[len(steps)]))
-    for copy in copies:
-        copy.start()
-    for copy in copies:
-        copy.wait()
-
-
-def split(voltages, steps):
-    _, chans, inputs, samples = voltages.shape
-    piece = jax.ShapeDtypeStruct((inputs, samples), voltages.dtype)
+    for k in range(2):
+        for t in range(chips):
+            out[k, t] = x_ref[k, (me ^ (2 * t)) ^ 1]
+
+
+def give(voltages):
+    parts, chans, inputs, samples = voltages.shape
     return pl.pallas_call(
-        functools.partial(split_kernel, steps),
-        out_shape=[piece] * len(steps) + [jax.ShapeDtypeStruct((chans, inputs, samples), voltages.dtype)],
-        in_specs=[pl.BlockSpec(memory_space=pltpu.HBM)],
-        out_specs=[VMEM] * (len(steps) + 1),
-        scratch_shapes=[pltpu.SemaphoreType.DMA((len(steps) + 1,))],
+        functools.partial(give_kernel, chans // 2),
+        out_shape=jax.ShapeDtypeStruct((parts, chans // 2, inputs, samples), voltages.dtype),
+        in_specs=[VMEM],
+        out_specs=VMEM,
+        compiler_params=PARAMS,
+        cost_estimate=pl.CostEstimate(flops=1_000_000, bytes_accessed=1_000_000, transcendentals=0),
+    )(voltages)
+
+
+def merge_kernel(chips, x_ref, given_ref, *outs):
+    me = lax.axis_index("chan")
+    inputs = x_ref.shape[2]
+    mine = pl.multiple_of((me & 1) * inputs, inputs)
+    theirs = pl.multiple_of(inputs - (me & 1) * inputs, inputs)
+    for k in range(2):
+        for t in range(chips):
+            out = outs[k * chips + t]
+            piece, other = x_ref[k, me ^ (2 * t)], given_ref[k, t]
+            out[pl.ds(mine, inputs)] = piece
+            out[pl.ds(theirs, inputs)] = other
+
+
+def merge(voltages, given):
+    parts, chans, inputs, samples = voltages.shape
+    chips = chans // 2
+    piece = jax.ShapeDtypeStruct((2 * inputs, samples), voltages.dtype)
+    out = pl.pallas_call(
+        functools.partial(merge_kernel, chips),
+        out_shape=[piece] * (parts * chips),
+        in_specs=[VMEM] * 2,
+        out_specs=[VMEM] * (parts * chips),
         compiler_params=PARAMS,
         cost_estimate=pl.CostEstimate(flops=1_000_000, bytes_accessed=2_000_000, transcendentals=0),
-    )(voltages)
-
-
-def gather_kernel(steps, outputs, select_ref, *rest):
-    xs, outs = rest[: len(steps)], rest[len(steps) : len(steps) + outputs]
-    wide, pair, tall = rest[len(steps) + outputs :]
+    )(voltages, given)
+    return out[:chips], out[chips:]
+
+
+def load_pair(steps, xs, wide, pair):
     inputs = xs[0].shape[0]
     antennas = inputs // 2
-    me = lax.axis_index("chan")
+    chip = lax.axis_index("chan") // 2
     for i, (step, x) in enumerate(zip(steps, xs)):
         wide[i * inputs : (i + 1) * inputs] = x[...].astype(jnp.float32)
         if len(steps) == 1:
             top = 0
         else:
-            top = pl.multiple_of(partner(me, step, len(steps)) * antennas, antennas)
+            top = pl.multiple_of((chip ^ step) * antennas, antennas)
         for pol in range(2):
             pair[pl.ds(top, antennas), pol * LANES : (pol + 1) * LANES] = wide[
                 pl.ds(i * inputs + pol, antennas, stride=2), :
             ].astype(jnp.bfloat16)
-    picked = jnp.dot(select_ref[...], pair[...], preferred_element_type=jnp.float32)
-    rows = select_ref.shape[0]
+
+
+def store_rows(picked, tall, outs):
+    rows = picked.shape[0]
     for pol in range(2):
         tall[pl.ds(pol, rows, stride=2), :] = picked[:, pol * LANES : (pol + 1) * LANES]
     per, slots, _ = outs[0].shape
@@ -131,6 +150,14 @@
         for s in range(per):
             top = (g * per + s) * slots
             out[s] = tall[top : top + slots, :].astype(jnp.bfloat16)
+
+
+def gather_kernel(steps, outputs, select_ref, *rest):
+    xs, outs = rest[: len(steps)], rest[len(steps) : len(steps) + outputs]
+    wide, pair, tall = rest[len(steps) + outputs :]
+    load_pair(steps, xs, wide, pair)
+    picked = jnp.dot(select_ref[...], pair[...], preferred_element_type=jnp.float32)
+    store_rows(picked, tall, outs)
 
 
 def gather(select, xs, steps, groups, per, slots):
@@ -222,28 +249,46 @@
     return x.reshape(x.shape[1], x.shape[2])
 
 
+CHIP_ORDER = (3, 1, 2)
+
+
+def cross(chunks, chans, starts):
+    got = list(chunks)
+    for step in CHIP_ORDER:
+        if 2 * step < chans:
+            got[step] = lax.ppermute(chunks[step], "chan", [(i, i ^ (2 * step)) for i in starts])
+    return got
+
+
+def by_chip(chans):
+    return chans in (2, 4, 8)
+
+
+def orders(groups):
+    last = 2 if groups == 4 else groups - 1
+    rest = [step for step in range(groups - 1, 0, -1) if step != last]
+    return rest[:1] + [last] + rest[1:], rest + [last], last
+
+
 def steps_of(voltages, assignment, slot_subarray_index):
     groups = lax.axis_size("tm")
     chans = lax.axis_size("chan")
     subarrays = slot_subarray_index.shape[0]
     per = subarrays // groups
-    order = sorted(range(1, groups), reverse=True)
-    last = order[0]
-    if chans <= 8 and chans & (chans - 1) == 0:
-        steps = tuple(range(chans))
-        *chunks, imag = split(voltages, steps)
-        reals = list(chunks)
-        for step in (6, 7, 2, 3, 4, 5, 1):
-            if step < chans:
-                pairs = [(j, j ^ step) for j in range(chans)]
-                reals[step] = lax.ppermute(chunks[step], "chan", pairs)
+    first, second, last = orders(groups)
+    if by_chip(chans):
+        steps = tuple(range(chans // 2))
+        given = lax.ppermute(give(voltages), "chan", [(i, i ^ 1) for i in range(chans)])
+        reals, imags = merge(voltages, given)
+        reals = cross(reals, chans, range(chans))
+        imags = cross(imags, chans, range(chans))
     else:
-        steps, imag = (0,), voltages[1]
+        steps = (0,)
         reals = [across(voltages[0])]
+        imags = [across(voltages[1])]
     select = plan(assignment, slot_subarray_index, groups, SLOT // 2)
-    real = exchange(gather(select, reals, steps, groups, per, SLOT), order, groups)
-    imag = across(imag)
-    imag = exchange(gather(select, [imag], (0,), groups, per, SLOT), order[1:] + order[:1], groups)
+    real = exchange(gather(select, reals, steps, groups, per, SLOT), first, groups)
+    imag = exchange(gather(select, imags, steps, groups, per, SLOT), second, groups)
     return gram(real, imag, last)
 
 

time: 65.4 us -> 60.8 us (0.930)
  the two profiles are of different devices: /device:TPU:10 before, /device:TPU:0 now
where the time goes in v5:
time: 60.8 us; the launch traced here: 60.7 us
  waiting for transfers between devices  29.2 us (48%)
  starting transfers between devices  22.3 us (37%)
  Pallas kernels  7.92 us (13%)
  local copies, waits for them, and re-layouts  1.23 us (2%)
    ppermute x6, waiting for transfers between devices, exchange(): got[step] = lax.ppermute(chunks[step], 'tm', pairs)  23 us
    ppermute x6, starting transfers between devices, exchange(): got[step] = lax.ppermute(chunks[step], 'tm', pairs)  11.5 us
    ppermute x6, starting transfers between devices, cross(): lax.ppermute(chunks[step], 'chan', [(i, i ^ 2 * step) for i in starts])  10.2 us
    ppermute x6, waiting for transfers between devices, cross(): lax.ppermute(chunks[step], 'chan', [(i, i ^ 2 * step) for i in starts])  4.66 us
    pallas_call x2, Pallas kernels, gather(): pl.pallas_call(functools.partial(gather_kernel, steps, groups), out_shape...  2.64 us
    pallas_call x1, Pallas kernels, plan(): pl.pallas_call(functools.partial(plan_kernel, groups, half), out_shape=ja...  2.06 us
    pallas_call x1, Pallas kernels, gram(): pl.pallas_call(late_kernel, out_shape=jax.ShapeDtypeStruct((per, 1, 2, sl...  1.72 us
    ppermute x1, waiting for transfers between devices, steps_of(): lax.ppermute(give(voltages), 'chan', [(i, i ^ 1) for i in range(chans)])  1.54 us
  transfers between devices with their start and end apart: 13, of which 7 were waited for; matrix products, arithmetic and copies ran while one was open for 0% of the time, Pallas kernels for 10%

profile of v5, /device:TPU:0, one launch (start us, length us, event | category | flops | bytes accessed | tf_op | source)
XLA Modules:
  0.0 60.7 jit_solution(11868446257518779093)
XLA Ops:
  0.0 0.0 copy-start
  0.0 1.2 %copy-done = bf16[2,8,256,128]{3,2,1,0:T(8,128)(2,1)S(1)} copy-done((bf16[2,8,256,128]{3,2,1,0:T(8,128)(2,1)S(1)}, bf16[2,8,256,128]{3,2,1,0:T(8,128)(2,1)}, u32[]{:S(2)}) %copy-start) | copy-done | bytes 1048600
  1.2 0.0 copy-start.1
  1.2 0.0 copy-start.2
  1.3 0.6 collective-permute-start
  1.8 1.5 %collective-permute-done.given_ref = bf16[2,4,256,128]{3,2,1,0:T(8,128)(2,1)S(1)} collective-permute-done((bf16[2,4,256,128]{3,2,1,0:T(8,128)(2,1)S(1)}, bf16[2,4,256,128]{3,2,1,0:T(8,128)(2,1)S(1)}, u32[]{:S(2)}, u32[]{:S(2)}) %collective-permute-start) | collective-permute-done | bytes 524320 | tf_op jit(solution)/shard_map/ppermute | solution.py:281
  3.4 0.1 shard_map.39
  3.4 2.9 %collective-permute-start.5 = (bf16[512,128]{1,0:T(8,128)(2,1)S(1)}, bf16[512,128]{1,0:T(8,128)(2,1)S(1)}, u32[]{:S(2)}, u32[]{:S(2)}) collective-permute-start(bf16[512,128]{1,0:T(8,128)(2,1)S(1)} %get-tuple-element.27), channel_id=1, source_target_pairs={{0,8},{4,12},{8,0},{12,4},{16,24},{20,28},{24,16},{28,20},{1,9},{5... | collective-permute-start | bytes 393224 | tf_op jit(solution)/shard_map/ppermute | solution.py:259
  6.4 0.1 collective-permute-start.1
  6.4 2.0 %collective-permute-start.2 = (bf16[512,128]{1,0:T(8,128)(2,1)S(1)}, bf16[512,128]{1,0:T(8,128)(2,1)S(1)}, u32[]{:S(2)}, u32[]{:S(2)}) collective-permute-start(bf16[512,128]{1,0:T(8,128)(2,1)S(1)} %get-tuple-element.23), channel_id=1, source_target_pairs={{0,16},{4,20},{8,24},{12,28},{16,0},{20,4},{24,8},{28,12},{1,17},{... | collective-permute-start | bytes 393224 | tf_op jit(solution)/shard_map/ppermute | solution.py:259
  8.4 1.4 %collective-permute-start.3 = (bf16[512,128]{1,0:T(8,128)(2,1)S(1)}, bf16[512,128]{1,0:T(8,128)(2,1)S(1)}, u32[]{:S(2)}, u32[]{:S(2)}) collective-permute-start(bf16[512,128]{1,0:T(8,128)(2,1)S(1)} %get-tuple-element.24), channel_id=1, source_target_pairs={{0,24},{4,28},{8,16},{12,20},{16,8},{20,12},{24,0},{28,4},{1,25},{... | collective-permute-start | bytes 393224 | tf_op jit(solution)/shard_map/ppermute | solution.py:259
  9.8 1.5 %collective-permute-start.6 = (bf16[512,128]{1,0:T(8,128)(2,1)S(1)}, bf16[512,128]{1,0:T(8,128)(2,1)S(1)}, u32[]{:S(2)}, u32[]{:S(2)}) collective-permute-start(bf16[512,128]{1,0:T(8,128)(2,1)S(1)} %get-tuple-element.28), channel_id=1, source_target_pairs={{0,16},{4,20},{8,24},{12,28},{16,0},{20,4},{24,8},{28,12},{1,17},{... | collective-permute-start | bytes 393224 | tf_op jit(solution)/shard_map/ppermute | solution.py:259
  11.4 0.0 collective-permute-done.5.rest_1_
  11.4 2.3 %collective-permute-start.7 = (bf16[512,128]{1,0:T(8,128)(2,1)S(1)}, bf16[512,128]{1,0:T(8,128)(2,1)S(1)}, u32[]{:S(2)}, u32[]{:S(2)}) collective-permute-start(bf16[512,128]{1,0:T(8,128)(2,1)S(1)} %get-tuple-element.29), channel_id=1, source_target_pairs={{0,24},{4,28},{8,16},{12,20},{16,8},{20,12},{24,0},{28,4},{1,25},{... | collective-permute-start | bytes 393224 | tf_op jit(solution)/shard_map/ppermute | solution.py:259
  13.7 0.0 copy-done.1
  13.7 0.0 copy-done.2
  13.7 2.1 %shard_map.37.select_ref = bf16[1536,1024]{1,0:T(8,128)(2,1)S(1)} custom-call(s32[8]{0:T(128)S(1)} %copy-done.2, s32[8,128]{1,0:T(8,128)S(1)} %bitcast.1), custom_call_target="tpu_custom_call" | custom-call | flops 4000000000 | bytes 3000000 | tf_op jit(solution)/shard_map/pallas_call | solution.py:71
  15.7 4.6 %collective-permute-done.6.rest_2_ = bf16[512,128]{1,0:T(8,128)(2,1)S(1)} collective-permute-done((bf16[512,128]{1,0:T(8,128)(2,1)S(1)}, bf16[512,128]{1,0:T(8,128)(2,1)S(1)}, u32[]{:S(2)}, u32[]{:S(2)}) %collective-permute-start.6) | collective-permute-done | bytes 131104 | tf_op jit(solution)/shard_map/ppermute | solution.py:259
  20.4 0.0 collective-permute-done.7.rest_3_
  20.4 1.3 %shard_map.41 = (bf16[2,384,128]{2,1,0:T(8,128)(2,1)S(1)}, bf16[2,384,128]{2,1,0:T(8,128)(2,1)S(1)}, bf16[2,384,128]{2,1,0:T(8,128)(2,1)S(1)}, bf16[2,384,128]{2,1,0:T(8,128)(2,1)S(1)}) custom-call(bf16[1536,1024]{1,0:T(8,128)(2,1)S(1)} %shard_map.37.select_ref, bf16[512,128]{1,0:T(8,128)(2,1)S(1)} %get-tuple-element.26.rest_0_, ...), custom_call_target="tpu_custom_call" | custom-call | flops 805306368 | bytes 4000000 | tf_op jit(solution)/shard_map/pallas_call | solution.py:166
  21.7 1.6 %collective-permute-start.11 = (bf16[2,384,128]{2,1,0:T(8,128)(2,1)S(1)}, bf16[2,384,128]{2,1,0:T(8,128)(2,1)S(1)}, u32[]{:S(2)}, u32[]{:S(2)}) collective-permute-start(bf16[2,384,128]{2,1,0:T(8,128)(2,1)S(1)} %get-tuple-element.35), channel_id=1, source_target_pairs={{0,1},{1,0},{2,3},{3,2},{4,5},{5,4},{6,7},{7,6},{8,9},{9,8},{10,11... | collective-permute-start | bytes 589832 | tf_op jit(solution)/shard_map/ppermute | solution.py:243
  23.4 2.5 %collective-permute-start.12 = (bf16[2,384,128]{2,1,0:T(8,128)(2,1)S(1)}, bf16[2,384,128]{2,1,0:T(8,128)(2,1)S(1)}, u32[]{:S(2)}, u32[]{:S(2)}) collective-permute-start(bf16[2,384,128]{2,1,0:T(8,128)(2,1)S(1)} %get-tuple-element.36), channel_id=1, source_target_pairs={{0,3},{1,2},{2,1},{3,0},{4,7},{5,6},{6,5},{7,4},{8,11},{9,10},{10,... | collective-permute-start | bytes 589832 | tf_op jit(solution)/shard_map/ppermute | solution.py:243
  25.8 0.0 collective-permute-done.1.rest_1_
  25.8 0.0 collective-permute-done.2.rest_2_
  25.8 0.0 collective-permute-done.3.rest_3_
  25.9 1.3 %shard_map.40 = (bf16[2,384,128]{2,1,0:T(8,128)(2,1)S(1)}, bf16[2,384,128]{2,1,0:T(8,128)(2,1)S(1)}, bf16[2,384,128]{2,1,0:T(8,128)(2,1)S(1)}, bf16[2,384,128]{2,1,0:T(8,128)(2,1)S(1)}) custom-call(bf16[1536,1024]{1,0:T(8,128)(2,1)S(1)} %shard_map.37.select_ref, bf16[512,128]{1,0:T(8,128)(2,1)S(1)} %get-tuple-element.21.rest_0_, ...), custom_call_target="tpu_custom_call" | custom-call | flops 805306368 | bytes 4000000 | tf_op jit(solution)/shard_map/pallas_call | solution.py:166
  27.2 0.7 %collective-permute-start.9 = (bf16[2,384,128]{2,1,0:T(8,128)(2,1)S(1)}, bf16[2,384,128]{2,1,0:T(8,128)(2,1)S(1)}, u32[]{:S(2)}, u32[]{:S(2)}) collective-permute-start(bf16[2,384,128]{2,1,0:T(8,128)(2,1)S(1)} %get-tuple-element.32), channel_id=1, source_target_pairs={{0,1},{1,0},{2,3},{3,2},{4,5},{5,4},{6,7},{7,6},{8,9},{9,8},{10,11... | collective-permute-start | bytes 589832 | tf_op jit(solution)/shard_map/ppermute | solution.py:243
  27.9 0.9 %collective-permute-start.10 = (bf16[2,384,128]{2,1,0:T(8,128)(2,1)S(1)}, bf16[2,384,128]{2,1,0:T(8,128)(2,1)S(1)}, u32[]{:S(2)}, u32[]{:S(2)}) collective-permute-start(bf16[2,384,128]{2,1,0:T(8,128)(2,1)S(1)} %get-tuple-element.33), channel_id=1, source_target_pairs={{0,3},{1,2},{2,1},{3,0},{4,7},{5,6},{6,5},{7,4},{8,11},{9,10},{10,... | collective-permute-start | bytes 589832 | tf_op jit(solution)/shard_map/ppermute | solution.py:243
  28.8 1.9 %collective-permute-start.8 = (bf16[2,384,128]{2,1,0:T(8,128)(2,1)S(1)}, bf16[2,384,128]{2,1,0:T(8,128)(2,1)S(1)}, u32[]{:S(2)}, u32[]{:S(2)}) collective-permute-start(bf16[2,384,128]{2,1,0:T(8,128)(2,1)S(1)} %get-tuple-element.30), channel_id=1, source_target_pairs={{0,2},{1,3},{2,0},{3,1},{4,6},{5,7},{6,4},{7,5},{8,10},{9,11},{10,... | collective-permute-start | bytes 589832 | tf_op jit(solution)/shard_map/ppermute | solution.py:243
  30.7 0.0 collective-permute-done.11.refs_4_
  30.7 3.8 %collective-permute-start.4 = (bf16[2,384,128]{2,1,0:T(8,128)(2,1)S(1)}, bf16[2,384,128]{2,1,0:T(8,128)(2,1)S(1)}, u32[]{:S(2)}, u32[]{:S(2)}) collective-permute-start(bf16[2,384,128]{2,1,0:T(8,128)(2,1)S(1)} %get-tuple-element.25), channel_id=1, source_target_pairs={{0,2},{1,3},{2,0},{3,1},{4,6},{5,7},{6,4},{7,5},{8,10},{9,11},{10,... | collective-permute-start | bytes 589832 | tf_op jit(solution)/shard_map/ppermute | solution.py:243
  34.5 1.3 %collective-permute-done.12.refs_5_ = bf16[2,384,128]{2,1,0:T(8,128)(2,1)S(1)} collective-permute-done((bf16[2,384,128]{2,1,0:T(8,128)(2,1)S(1)}, bf16[2,384,128]{2,1,0:T(8,128)(2,1)S(1)}, u32[]{:S(2)}, u32[]{:S(2)}) %collective-permute-start.12) | collective-permute-done | bytes 196640 | tf_op jit(solution)/shard_map/ppermute | solution.py:243
  35.8 1.3 %collective-permute-done.9.refs_1_ = bf16[2,384,128]{2,1,0:T(8,128)(2,1)S(1)} collective-permute-done((bf16[2,384,128]{2,1,0:T(8,128)(2,1)S(1)}, bf16[2,384,128]{2,1,0:T(8,128)(2,1)S(1)}, u32[]{:S(2)}, u32[]{:S(2)}) %collective-permute-start.9) | collective-permute-done | bytes 196640 | tf_op jit(solution)/shard_map/ppermute | solution.py:243
  37.1 7.1 %collective-permute-done.10.refs_2_ = bf16[2,384,128]{2,1,0:T(8,128)(2,1)S(1)} collective-permute-done((bf16[2,384,128]{2,1,0:T(8,128)(2,1)S(1)}, bf16[2,384,128]{2,1,0:T(8,128)(2,1)S(1)}, u32[]{:S(2)}, u32[]{:S(2)}) %collective-permute-start.10) | collective-permute-done | bytes 196640 | tf_op jit(solution)/shard_map/ppermute | solution.py:243
  44.2 1.4 %shard_map.42.so_far = f32[2,2,384,384]{3,2,1,0:T(8,128)S(1)} custom-call(bf16[2,384,128]{2,1,0:T(8,128)(2,1)S(1)} %get-tuple-element.31.refs_0_, bf16[2,384,128]{2,1,0:T(8,128)(2,1)S(1)} %collective-permute-done.9.refs_1_, bf16[2,384,128]{2,1,0:T(8,128)(2,1)S(1)} %collective-permute-done.10.refs_2_, bf16[2,384,128]{2,1,0:T(8,128)(2,1)S(1)} %get-tuple-element.34.refs_3_, ...), custom_call_target="tpu_custom_call" | custom-call | flops 905969664 | bytes 3000000 | tf_op jit(solution)/shard_map/pallas_call | solution.py:217
  45.6 10.4 %collective-permute-done.8.imag = bf16[2,384,128]{2,1,0:T(8,128)(2,1)S(1)} collective-permute-done((bf16[2,384,128]{2,1,0:T(8,128)(2,1)S(1)}, bf16[2,384,128]{2,1,0:T(8,128)(2,1)S(1)}, u32[]{:S(2)}, u32[]{:S(2)}) %collective-permute-start.8) | collective-permute-done | bytes 196640 | tf_op jit(solution)/shard_map/ppermute | solution.py:243
  56.1 2.9 %collective-permute-done.4.real = bf16[2,384,128]{2,1,0:T(8,128)(2,1)S(1)} collective-permute-done((bf16[2,384,128]{2,1,0:T(8,128)(2,1)S(1)}, bf16[2,384,128]{2,1,0:T(8,128)(2,1)S(1)}, u32[]{:S(2)}, u32[]{:S(2)}) %collective-permute-start.4) | collective-permute-done | bytes 196640 | tf_op jit(solution)/shard_map/ppermute | solution.py:243
  58.9 1.7 %shard_map.43 = f32[2,1,2,384,384]{4,3,2,1,0:T(8,128)} custom-call(bf16[2,384,128]{2,1,0:T(8,128)(2,1)S(1)} %collective-permute-done.4.real, bf16[2,384,128]{2,1,0:T(8,128)(2,1)S(1)} %collective-permute-done.8.imag, f32[2,2,384,384]{3,2,1,0:T(8,128)S(1)} %shard_map.42.so_far), custom_call_target="tpu_custom_call" | custom-call | flops 301989888 | bytes 3000000 | tf_op jit(solution)/shard_map/pallas_call | solution.py:225
  (1 shorter events, 0.0 us)
Async XLA Ops:
  0.0 1.2 %copy-start = (bf16[2,8,256,128]{3,2,1,0:T(8,128)(2,1)S(1)}, bf16[2,8,256,128]{3,2,1,0:T(8,128)(2,1)}, u32[]{:S(2)}) copy-start(bf16[2,8,256,128]{3,2,1,0:T(8,128)(2,1)} %x_ref.3) | copy-start | bytes 3145732
  1.2 12.5 %copy-start.1 = (s32[1024,1]{0,1:T(1,128)S(1)}, s32[1024,1]{0,1:T(1,128)}, u32[]{:S(2)}) copy-start(s32[1024,1]{0,1:T(1,128)} %param.4) | copy-start | bytes 12292
  1.2 12.5 %copy-start.2 = (s32[8]{0:T(128)S(1)}, s32[8]{0:T(128)}, u32[]{:S(2)}) copy-start(s32[8]{0:T(128)} %slot_ref.1) | copy-start | bytes 100
  1.3 2.1 %collective-permute-start = (bf16[2,4,256,128]{3,2,1,0:T(8,128)(2,1)S(1)}, bf16[2,4,256,128]{3,2,1,0:T(8,128)(2,1)S(1)}, u32[]{:S(2)}, u32[]{:S(2)}) collective-permute-start(bf16[2,4,256,128]{3,2,1,0:T(8,128)(2,1)S(1)} %shard_map.38), channel_id=1, source_target_pairs={{0,4},{4,0},{8,12},{12,8},{16,20},{20,16},{24,28},{28,24},{1,5},{5... | collective-permute-start | bytes 1572872 | tf_op jit(solution)/shard_map/ppermute | solution.py:281
  3.4 7.9 %collective-permute-start.5 = (bf16[512,128]{1,0:T(8,128)(2,1)S(1)}, bf16[512,128]{1,0:T(8,128)(2,1)S(1)}, u32[]{:S(2)}, u32[]{:S(2)}) collective-permute-start(bf16[512,128]{1,0:T(8,128)(2,1)S(1)} %get-tuple-element.27), channel_id=1, source_target_pairs={{0,8},{4,12},{8,0},{12,4},{16,24},{20,28},{24,16},{28,20},{1,9},{5... | collective-permute-start | bytes 393224 | tf_op jit(solution)/shard_map/ppermute | solution.py:259
  6.4 19.5 %collective-permute-start.1 = (bf16[512,128]{1,0:T(8,128)(2,1)S(1)}, bf16[512,128]{1,0:T(8,128)(2,1)S(1)}, u32[]{:S(2)}, u32[]{:S(2)}) collective-permute-start(bf16[512,128]{1,0:T(8,128)(2,1)S(1)} %get-tuple-element.22), channel_id=1, source_target_pairs={{0,8},{4,12},{8,0},{12,4},{16,24},{20,28},{24,16},{28,20},{1,9},{5... | collective-permute-start | bytes 393224 | tf_op jit(solution)/shard_map/ppermute | solution.py:259
  6.4 19.4 %collective-permute-start.2 = (bf16[512,128]{1,0:T(8,128)(2,1)S(1)}, bf16[512,128]{1,0:T(8,128)(2,1)S(1)}, u32[]{:S(2)}, u32[]{:S(2)}) collective-permute-start(bf16[512,128]{1,0:T(8,128)(2,1)S(1)} %get-tuple-element.23), channel_id=1, source_target_pairs={{0,16},{4,20},{8,24},{12,28},{16,0},{20,4},{24,8},{28,12},{1,17},{... | collective-permute-start | bytes 393224 | tf_op jit(solution)/shard_map/ppermute | solution.py:259
  8.4 17.4 %collective-permute-start.3 = (bf16[512,128]{1,0:T(8,128)(2,1)S(1)}, bf16[512,128]{1,0:T(8,128)(2,1)S(1)}, u32[]{:S(2)}, u32[]{:S(2)}) collective-permute-start(bf16[512,128]{1,0:T(8,128)(2,1)S(1)} %get-tuple-element.24), channel_id=1, source_target_pairs={{0,24},{4,28},{8,16},{12,20},{16,8},{20,12},{24,0},{28,4},{1,25},{... | collective-permute-start | bytes 393224 | tf_op jit(solution)/shard_map/ppermute | solution.py:259
  9.8 10.5 %collective-permute-start.6 = (bf16[512,128]{1,0:T(8,128)(2,1)S(1)}, bf16[512,128]{1,0:T(8,128)(2,1)S(1)}, u32[]{:S(2)}, u32[]{:S(2)}) collective-permute-start(bf16[512,128]{1,0:T(8,128)(2,1)S(1)} %get-tuple-element.28), channel_id=1, source_target_pairs={{0,16},{4,20},{8,24},{12,28},{16,0},{20,4},{24,8},{28,12},{1,17},{... | collective-permute-start | bytes 393224 | tf_op jit(solution)/shard_map/ppermute | solution.py:259
  11.4 9.0 %collective-permute-start.7 = (bf16[512,128]{1,0:T(8,128)(2,1)S(1)}, bf16[512,128]{1,0:T(8,128)(2,1)S(1)}, u32[]{:S(2)}, u32[]{:S(2)}) collective-permute-start(bf16[512,128]{1,0:T(8,128)(2,1)S(1)} %get-tuple-element.29), channel_id=1, source_target_pairs={{0,24},{4,28},{8,16},{12,20},{16,8},{20,12},{24,0},{28,4},{1,25},{... | collective-permute-start | bytes 393224 | tf_op jit(solution)/shard_map/ppermute | solution.py:259
  21.7 9.0 %collective-permute-start.11 = (bf16[2,384,128]{2,1,0:T(8,128)(2,1)S(1)}, bf16[2,384,128]{2,1,0:T(8,128)(2,1)S(1)}, u32[]{:S(2)}, u32[]{:S(2)}) collective-permute-start(bf16[2,384,128]{2,1,0:T(8,128)(2,1)S(1)} %get-tuple-element.35), channel_id=1, source_target_pairs={{0,1},{1,0},{2,3},{3,2},{4,5},{5,4},{6,7},{7,6},{8,9},{9,8},{10,11... | collective-permute-start | bytes 589832 | tf_op jit(solution)/shard_map/ppermute | solution.py:243
  23.4 12.4 %collective-permute-start.12 = (bf16[2,384,128]{2,1,0:T(8,128)(2,1)S(1)}, bf16[2,384,128]{2,1,0:T(8,128)(2,1)S(1)}, u32[]{:S(2)}, u32[]{:S(2)}) collective-permute-start(bf16[2,384,128]{2,1,0:T(8,128)(2,1)S(1)} %get-tuple-element.36), channel_id=1, source_target_pairs={{0,3},{1,2},{2,1},{3,0},{4,7},{5,6},{6,5},{7,4},{8,11},{9,10},{10,... | collective-permute-start | bytes 589832 | tf_op jit(solution)/shard_map/ppermute | solution.py:243
  27.2 9.9 %collective-permute-start.9 = (bf16[2,384,128]{2,1,0:T(8,128)(2,1)S(1)}, bf16[2,384,128]{2,1,0:T(8,128)(2,1)S(1)}, u32[]{:S(2)}, u32[]{:S(2)}) collective-permute-start(bf16[2,384,128]{2,1,0:T(8,128)(2,1)S(1)} %get-tuple-element.32), channel_id=1, source_target_pairs={{0,1},{1,0},{2,3},{3,2},{4,5},{5,4},{6,7},{7,6},{8,9},{9,8},{10,11... | collective-permute-start | bytes 589832 | tf_op jit(solution)/shard_map/ppermute | solution.py:243
  27.9 16.3 %collective-permute-start.10 = (bf16[2,384,128]{2,1,0:T(8,128)(2,1)S(1)}, bf16[2,384,128]{2,1,0:T(8,128)(2,1)S(1)}, u32[]{:S(2)}, u32[]{:S(2)}) collective-permute-start(bf16[2,384,128]{2,1,0:T(8,128)(2,1)S(1)} %get-tuple-element.33), channel_id=1, source_target_pairs={{0,3},{1,2},{2,1},{3,0},{4,7},{5,6},{6,5},{7,4},{8,11},{9,10},{10,... | collective-permute-start | bytes 589832 | tf_op jit(solution)/shard_map/ppermute | solution.py:243
  28.8 27.2 %collective-permute-start.8 = (bf16[2,384,128]{2,1,0:T(8,128)(2,1)S(1)}, bf16[2,384,128]{2,1,0:T(8,128)(2,1)S(1)}, u32[]{:S(2)}, u32[]{:S(2)}) collective-permute-start(bf16[2,384,128]{2,1,0:T(8,128)(2,1)S(1)} %get-tuple-element.30), channel_id=1, source_target_pairs={{0,2},{1,3},{2,0},{3,1},{4,6},{5,7},{6,4},{7,5},{8,10},{9,11},{10,... | collective-permute-start | bytes 589832 | tf_op jit(solution)/shard_map/ppermute | solution.py:243
  30.7 28.2 %collective-permute-start.4 = (bf16[2,384,128]{2,1,0:T(8,128)(2,1)S(1)}, bf16[2,384,128]{2,1,0:T(8,128)(2,1)S(1)}, u32[]{:S(2)}, u32[]{:S(2)}) collective-permute-start(bf16[2,384,128]{2,1,0:T(8,128)(2,1)S(1)} %get-tuple-element.25), channel_id=1, source_target_pairs={{0,2},{1,3},{2,0},{3,1},{4,6},{5,7},{6,4},{7,5},{8,10},{9,11},{10,... | collective-permute-start | bytes 589832 | tf_op jit(solution)/shard_map/ppermute | solution.py:243

commit v6 on v5

--- a/solution.py
+++ b/solution.py
@@ -29,52 +29,92 @@
     return owner ^ me
 
 
-def plan_kernel(groups, half, slot_ref, owner_ref, select_ref):
+GRAIN = 32
+
+
+def sizes(inputs, subarrays, groups):
+    total = subarrays // groups * SLOT
+    base = min(total, -(-inputs // (groups * GRAIN)) * GRAIN)
+    return total, base, list(range(GRAIN, total - base + 1, GRAIN))
+
+
+def plan_kernel(groups, base_rows, slot_ref, owner_ref, select_ref, place_ref, class_ref):
     subarrays = slot_ref.shape[0]
     blocks = owner_ref.shape[0]
     per = subarrays // groups
+    half = SLOT // 2
     me = lax.axis_index("tm")
     shape = (subarrays, LANES)
     place = lax.broadcasted_iota(jnp.int32, shape, 0)
     name = jnp.zeros(shape, jnp.int32)
     for s in range(subarrays):
         name = jnp.where(place == s, slot_ref[s], name)
-    base = jnp.zeros(shape, jnp.int32)
+    held = [jnp.where(owner_ref[b : b + 1, :] == name, 1.0, 0.0) for b in range(blocks)]
+    counts = [jnp.sum(one, axis=1, keepdims=True) for one in held]
+    count = jnp.broadcast_to(sum(counts), shape)
+    ahead = jnp.zeros(shape, jnp.float32)
+    full = jnp.zeros(shape, jnp.float32)
     for s in range(subarrays):
-        chunk = relative(jnp.int32(s // per), me, groups) * per + s % per
-        base = jnp.where(place == s, chunk * half, base)
-    base = base.astype(jnp.float32)
+        mates = jnp.logical_and(place >= s // per * per, place < (s // per + 1) * per)
+        row = jnp.broadcast_to(count[s : s + 1, :], shape)
+        full = full + jnp.where(mates, row, 0.0)
+        ahead = ahead + jnp.where(jnp.logical_and(mates, place > s), row, 0.0)
+    rest = 2 * jnp.max(full).astype(jnp.int32) - base_rows
+    class_ref[0] = jnp.maximum((rest + GRAIN - 1) // GRAIN - 1, 0)
+
+    start = jnp.zeros(shape, jnp.float32)
+    for s in range(subarrays):
+        chunk = relative(jnp.int32(s // per), me, groups)
+        top = (chunk * (per * half)).astype(jnp.float32)
+        mine = jnp.where(chunk == 0, 1.0, 0.0)
+        inside = mine * (s % per * half) + (1.0 - mine) * ahead
+        start = jnp.where(place == s, top + inside, start)
     earlier = lax.broadcasted_iota(jnp.int32, (LANES, LANES), 0)
     later = lax.broadcasted_iota(jnp.int32, (LANES, LANES), 1)
     before = jnp.where(earlier < later, 1.0, 0.0).astype(jnp.bfloat16)
-    held = [jnp.where(owner_ref[b : b + 1, :] == name, 1.0, 0.0) for b in range(blocks)]
     within = jnp.dot(
         jnp.concatenate(held, axis=0).astype(jnp.bfloat16), before, preferred_element_type=jnp.float32
     )
-    run = base
+    run = start
     height = 256
     row = lax.broadcasted_iota(jnp.int32, (height, LANES), 0).astype(jnp.float32)
     for b in range(blocks):
         rank = within[b * subarrays : (b + 1) * subarrays] + run
         target = jnp.sum(held[b] * rank, axis=0, keepdims=True)
-        run = run + jnp.sum(held[b], axis=1, keepdims=True)
+        run = run + counts[b]
         for top in range(0, select_ref.shape[0], height):
             hit = row == (target - top)
             select_ref[top : top + height, b * LANES : (b + 1) * LANES] = jnp.where(hit, 1.0, 0.0).astype(
                 jnp.bfloat16
             )
-
-
-def plan(assignment, slot_subarray_index, groups, half):
+    rank = lax.broadcasted_iota(jnp.int32, (SLOT, LANES), 0).astype(jnp.float32)
+    column = lax.broadcasted_iota(jnp.int32, (SLOT, LANES), 1).astype(jnp.float32)
+    for s in range(per):
+        own = place == me * per + s
+        held_here = 2 * jnp.sum(jnp.where(own, count, 0.0), axis=0, keepdims=True)
+        offset = 2 * jnp.sum(jnp.where(own, ahead, 0.0), axis=0, keepdims=True)
+        target = jnp.where(rank < held_here, rank + offset, -1.0)
+        for left in range(0, place_ref.shape[1], LANES):
+            place_ref[s * SLOT : (s + 1) * SLOT, left : left + LANES] = jnp.where(
+                column == target - left, 1.0, 0.0
+            ).astype(jnp.bfloat16)
+
+
+def plan(assignment, slot_subarray_index, groups, base):
     antennas = assignment.shape[0]
     subarrays = slot_subarray_index.shape[0]
+    total = subarrays // groups * SLOT
     return pl.pallas_call(
-        functools.partial(plan_kernel, groups, half),
-        out_shape=jax.ShapeDtypeStruct((subarrays * half, antennas), jnp.bfloat16),
+        functools.partial(plan_kernel, groups, base),
+        out_shape=[
+            jax.ShapeDtypeStruct((subarrays * SLOT // 2, antennas), jnp.bfloat16),
+            jax.ShapeDtypeStruct((total, total), jnp.bfloat16),
+            jax.ShapeDtypeStruct((1,), jnp.int32),
+        ],
         in_specs=[SMEM, VMEM],
-        out_specs=VMEM,
-        compiler_params=PARAMS,
-        cost_estimate=pl.CostEstimate(flops=4_000_000_000, bytes_accessed=3_000_000, transcendentals=0),
+        out_specs=[VMEM, VMEM, SMEM],
+        compiler_params=PARAMS,
+        cost_estimate=pl.CostEstimate(flops=4_000_000_000, bytes_accessed=4_000_000, transcendentals=0),
     )(slot_subarray_index, assignment.reshape(antennas // LANES, LANES))
 
 
@@ -141,33 +181,43 @@
             ].astype(jnp.bfloat16)
 
 
-def store_rows(picked, tall, outs):
+def gather_kernel(steps, groups, after, select_ref, *rest):
+    xs, rest = rest[: len(steps)], rest[len(steps) :]
+    if after:
+        reals, rest = rest[: groups - 1], rest[groups - 1 :]
+    own, bases, rests = rest[0], rest[1:groups], rest[groups : 2 * groups - 1]
+    wide, pair, tall = rest[2 * groups - 1 :]
+    load_pair(steps, xs, wide, pair)
+    picked = jnp.dot(select_ref[...], pair[...], preferred_element_type=jnp.float32)
     rows = picked.shape[0]
     for pol in range(2):
         tall[pl.ds(pol, rows, stride=2), :] = picked[:, pol * LANES : (pol + 1) * LANES]
-    per, slots, _ = outs[0].shape
-    for g, out in enumerate(outs):
-        for s in range(per):
-            top = (g * per + s) * slots
-            out[s] = tall[top : top + slots, :].astype(jnp.bfloat16)
-
-
-def gather_kernel(steps, outputs, select_ref, *rest):
-    xs, outs = rest[: len(steps)], rest[len(steps) : len(steps) + outputs]
-    wide, pair, tall = rest[len(steps) + outputs :]
-    load_pair(steps, xs, wide, pair)
-    picked = jnp.dot(select_ref[...], pair[...], preferred_element_type=jnp.float32)
-    store_rows(picked, tall, outs)
-
-
-def gather(select, xs, steps, groups, per, slots):
+    per, slots, _ = own.shape
+    for s in range(per):
+        own[s] = tall[s * slots : (s + 1) * slots, :].astype(jnp.bfloat16)
+    for i in range(groups - 1):
+        top = (i + 1) * per * slots
+        middle = top + bases[i].shape[0]
+        bases[i][...] = tall[top:middle, :].astype(jnp.bfloat16)
+        end = top + per * slots
+        if after:
+            rests[i][:, :LANES] = reals[i][...]
+            rests[i][:, LANES:] = tall[middle:end, :].astype(jnp.bfloat16)
+        else:
+            rests[i][...] = tall[middle:end, :].astype(jnp.bfloat16)
+
+
+def gather(select, xs, steps, groups, per, base, reals=()):
     _, samples = xs[0].shape
     rows, antennas = select.shape
-    return pl.pallas_call(
-        functools.partial(gather_kernel, steps, groups),
-        out_shape=[jax.ShapeDtypeStruct((per, slots, samples), jnp.bfloat16)] * groups,
-        in_specs=[VMEM] * (1 + len(xs)),
-        out_specs=[VMEM] * groups,
+    rest = per * SLOT - base
+    out = pl.pallas_call(
+        functools.partial(gather_kernel, steps, groups, bool(reals)),
+        out_shape=[jax.ShapeDtypeStruct((per, SLOT, samples), jnp.bfloat16)]
+        + [jax.ShapeDtypeStruct((base, samples), jnp.bfloat16)] * (groups - 1)
+        + [jax.ShapeDtypeStruct((rest, (2 if reals else 1) * samples), jnp.bfloat16)] * (groups - 1),
+        in_specs=[VMEM] * (1 + len(xs) + len(reals)),
+        out_specs=[VMEM] * (2 * groups - 1),
         scratch_shapes=[
             pltpu.VMEM((2 * antennas, samples), jnp.float32),
             pltpu.VMEM((antennas, 2 * samples), jnp.bfloat16),
@@ -177,32 +227,43 @@
         cost_estimate=pl.CostEstimate(
             flops=2 * rows * antennas * 2 * samples, bytes_accessed=4_000_000, transcendentals=0
         ),
-    )(select, *xs)
-
-
-def products(real, imag, part):
-    right = jnp.concatenate([real, imag], axis=1)
-    left = right if part == 0 else jnp.concatenate([imag, -real], axis=1)
-    return lax.dot_general(left, right, (((1,), (1,)), ((), ())), preferred_element_type=jnp.float32)
-
-
-def early_kernel(*refs):
-    *parts, out = refs
-    count = len(parts) // 2
-    for s in range(parts[0].shape[0]):
+    )(select, *xs, *reals)
+    return out[0], [None] + list(out[1:groups]), list(out[groups:])
+
+
+def products(both, part):
+    samples = both.shape[1] // 2
+    left = both
+    if part:
+        left = jnp.concatenate([both[:, samples:], -both[:, :samples]], axis=1)
+    return lax.dot_general(left, both, (((1,), (1,)), ((), ())), preferred_element_type=jnp.float32)
+
+
+def unpack(place_ref, real, imag, rest, packed):
+    base, samples = real.shape
+    packed[:base, :samples] = real[...]
+    packed[:base, samples:] = imag[...]
+    packed[base:, :] = rest[...]
+    return jnp.dot(place_ref[...], packed[...], preferred_element_type=jnp.float32).astype(jnp.bfloat16)
+
+
+def early_kernel(place_ref, own_real, own_imag, *refs):
+    *parts, out, packed = refs
+    count = len(parts) // 3
+    blocks = [unpack(place_ref, *parts[3 * e : 3 * e + 3], packed.at[e]) for e in range(count)]
+    for s in range(own_real.shape[0]):
+        both = [jnp.concatenate([own_real[s], own_imag[s]], axis=1)]
+        both += [block[s * SLOT : (s + 1) * SLOT] for block in blocks]
         for part in range(2):
-            total = None
-            for e in range(count):
-                term = products(parts[e][s], parts[count + e][s], part)
-                total = term if total is None else total + term
-            out[s, part] = total
-
-
-def late_kernel(real, imag, so_far, out, stage, sem):
+            out[s, part] = sum(products(one, part) for one in both)
+
+
+def late_kernel(place_ref, real, imag, rest, so_far, out, packed, stage, sem):
+    block = unpack(place_ref, real, imag, rest, packed)
     copies = []
-    for s in range(real.shape[0]):
+    for s in range(out.shape[0]):
         for part in range(2):
-            stage[s, part] = so_far[s, part] + products(real[s], imag[s], part)
+            stage[s, part] = so_far[s, part] + products(block[s * SLOT : (s + 1) * SLOT], part)
             copy = pltpu.make_async_copy(stage.at[s, part], out.at[s, 0, part], sem.at[s, part])
             copy.start()
             copies.append(copy)
@@ -210,38 +271,55 @@
         copy.wait()
 
 
-def gram(real, imag, last):
-    per, slots, samples = real[0].shape
-    early = [e for e in range(len(real)) if e != last]
+def gram(place, own, real, imag, rest, last):
+    per, slots, samples = own[0].shape
+    total = per * slots
+    early = [e for e in range(1, len(real)) if e != last]
     flops = 2 * per * 2 * slots * slots * 2 * samples
     so_far = pl.pallas_call(
         early_kernel,
         out_shape=jax.ShapeDtypeStruct((per, 2, slots, slots), jnp.float32),
-        in_specs=[VMEM] * (2 * len(early)),
+        in_specs=[VMEM] * (3 + 3 * len(early)),
         out_specs=VMEM,
-        compiler_params=PARAMS,
-        cost_estimate=pl.CostEstimate(flops=flops * len(early), bytes_accessed=3_000_000, transcendentals=0),
-    )(*[real[e] for e in early], *[imag[e] for e in early])
+        scratch_shapes=[pltpu.VMEM((len(early), total, 2 * samples), jnp.bfloat16)],
+        compiler_params=PARAMS,
+        cost_estimate=pl.CostEstimate(flops=flops * len(real), bytes_accessed=3_000_000, transcendentals=0),
+    )(place, *own, *[x for e in early for x in (real[e], imag[e], rest[e - 1])])
     return pl.pallas_call(
         late_kernel,
         out_shape=jax.ShapeDtypeStruct((per, 1, 2, slots, slots), jnp.float32),
-        in_specs=[VMEM] * 3,
+        in_specs=[VMEM] * 5,
         out_specs=pl.BlockSpec(memory_space=pl.ANY),
         scratch_shapes=[
+            pltpu.VMEM((total, 2 * samples), jnp.bfloat16),
             pltpu.VMEM((per, 2, slots, slots), jnp.float32),
             pltpu.SemaphoreType.DMA((per, 2)),
         ],
         compiler_params=PARAMS,
         cost_estimate=pl.CostEstimate(flops=flops, bytes_accessed=3_000_000, transcendentals=0),
-    )(real[last], imag[last], so_far)
+    )(place, real[last], imag[last], rest[last - 1], so_far)
+
+
+def hop(x, step, groups):
+    return lax.ppermute(x, "tm", [(j, partner(j, step, groups)) for j in range(groups)])
 
 
 def exchange(chunks, order, groups):
     got = list(chunks)
     for step in order:
-        pairs = [(j, partner(j, step, groups)) for j in range(groups)]
-        got[step] = lax.ppermute(chunks[step], "tm", pairs)
+        got[step] = hop(chunks[step], step, groups)
     return got
+
+
+def exchange_rest(chunks, size_class, rows, groups):
+    def send(count):
+        def branch(*chunks):
+            got = [hop(x[:count], i + 1, groups) for i, x in enumerate(chunks)]
+            return [jnp.pad(x, ((0, chunks[0].shape[0] - count), (0, 0))) for x in got]
+
+        return branch
+
+    return lax.switch(size_class, [send(count) for count in rows], *chunks)
 
 
 def across(x):
@@ -286,10 +364,14 @@
         steps = (0,)
         reals = [across(voltages[0])]
         imags = [across(voltages[1])]
-    select = plan(assignment, slot_subarray_index, groups, SLOT // 2)
-    real = exchange(gather(select, reals, steps, groups, per, SLOT), first, groups)
-    imag = exchange(gather(select, imags, steps, groups, per, SLOT), second, groups)
-    return gram(real, imag, last)
+    _, base, rows = sizes(2 * assignment.shape[0], subarrays, groups)
+    select, place, size_class = plan(assignment, slot_subarray_index, groups, base)
+    own_real, real, real_rest = gather(select, reals, steps, groups, per, base)
+    real = exchange(real, first, groups)
+    own_imag, imag, rest = gather(select, imags, steps, groups, per, base, real_rest)
+    imag = exchange(imag, second, groups)
+    rest = exchange_rest(rest, size_class[0], rows, groups)
+    return gram(place, (own_real, own_imag), real, imag, rest, last)
 
 
 def solution(mesh):

time: 60.8 us -> 62.4 us (1.026)
  waiting for transfers between devices: 29.2 us -> 21.2 us
  Pallas kernels: 7.92 us -> 11.8 us
  starting transfers between devices: 22.3 us -> 25.3 us
  local copies, waits for them, and re-layouts: 1.23 us -> 3.23 us
  between operations: 0.05 us -> 0.72 us
    ppermute x6 -> x9, waiting for transfers between devices: 23 us -> 17.3 us  [hop(): lax.ppermute(x, 'tm', [(j, partner(j, step, groups)) for j in range(group...]
    ppermute x6 -> x9, starting transfers between devices: 11.5 us -> 14.5 us  [hop(): lax.ppermute(x, 'tm', [(j, partner(j, step, groups)) for j in range(group...]
    ppermute x6, waiting for transfers between devices: 4.66 us -> 2.35 us  [cross(): lax.ppermute(chunks[step], 'chan', [(i, i ^ 2 * step) for i in starts])]
    pad x0 -> x3, local copies, waits for them, and re-layouts: none -> 1.98 us  [branch(): return [jnp.pad(x, ((0, chunks[0].shape[0] - count), (0, 0))) for x in got]]
    pallas_call x1, Pallas kernels: 1.39 us -> 3.03 us  [gram(): pl.pallas_call(early_kernel, out_shape=jax.ShapeDtypeStruct((per, 2, slot...]
    pallas_call x1, Pallas kernels: 1.72 us -> 3.34 us  [gram(): pl.pallas_call(late_kernel, out_shape=jax.ShapeDtypeStruct((per, 1, 2, sl...]
  transfers between devices with their start and end apart: 13 -> 16, of which waited for: 7 -> 8; matrix products, arithmetic and copies ran while one was open for 0% -> 3% of each run, Pallas kernels for 10% -> 11%
where the time goes in v6:
time: 62.4 us; the launch traced here: 62.2 us
  starting transfers between devices  25.3 us (41%)
  waiting for transfers between devices  21.2 us (34%)
  Pallas kernels  11.8 us (19%)
  local copies, waits for them, and re-layouts  3.23 us (5%)
  between operations  0.72 us (1%)
    ppermute x9, waiting for transfers between devices, hop(): lax.ppermute(x, 'tm', [(j, partner(j, step, groups)) for j in range(group...  17.3 us
    ppermute x9, starting transfers between devices, hop(): lax.ppermute(x, 'tm', [(j, partner(j, step, groups)) for j in range(group...  14.5 us
    ppermute x6, starting transfers between devices, cross(): lax.ppermute(chunks[step], 'chan', [(i, i ^ 2 * step) for i in starts])  10.2 us
    pallas_call x1, Pallas kernels, gram(): pl.pallas_call(late_kernel, out_shape=jax.ShapeDtypeStruct((per, 1, 2, sl...  3.34 us
    pallas_call x1, Pallas kernels, gram(): pl.pallas_call(early_kernel, out_shape=jax.ShapeDtypeStruct((per, 2, slot...  3.03 us
    pallas_call x1, Pallas kernels, plan(): pl.pallas_call(functools.partial(plan_kernel, groups, base), out_shape=[j...  2.65 us
    pallas_call x2, Pallas kernels, gather(): pl.pallas_call(functools.partial(gather_kernel, steps, groups, bool(reals...  2.63 us
    ppermute x6, waiting for transfers between devices, cross(): lax.ppermute(chunks[step], 'chan', [(i, i ^ 2 * step) for i in starts])  2.35 us
  transfers between devices with their start and end apart: 16, of which 8 were waited for; matrix products, arithmetic and copies ran while one was open for 3% of the time, Pallas kernels for 11%

profile of v6, /device:TPU:0, one launch (start us, length us, event | category | flops | bytes accessed | tf_op | source)
XLA Modules:
  0.0 62.2 jit_solution(7235502945168739725)
XLA Ops:
  0.0 0.0 copy-start
  0.0 1.2 %copy-done = bf16[2,8,256,128]{3,2,1,0:T(8,128)(2,1)S(1)} copy-done((bf16[2,8,256,128]{3,2,1,0:T(8,128)(2,1)S(1)}, bf16[2,8,256,128]{3,2,1,0:T(8,128)(2,1)}, u32[]{:S(2)}) %copy-start) | copy-done | bytes 1048600
  1.2 0.0 copy-start.1
  1.2 0.0 copy-start.2
  1.3 0.6 collective-permute-start.24
  1.8 1.5 %collective-permute-done.24.given_ref = bf16[2,4,256,128]{3,2,1,0:T(8,128)(2,1)S(1)} collective-permute-done((bf16[2,4,256,128]{3,2,1,0:T(8,128)(2,1)S(1)}, bf16[2,4,256,128]{3,2,1,0:T(8,128)(2,1)S(1)}, u32[]{:S(2)}, u32[]{:S(2)}) %collective-permute-start.24) | collective-permute-done | bytes 524320 | tf_op jit(solution)/shard_map/ppermute | solution.py:359
  3.4 0.1 shard_map.39
  3.4 2.9 %collective-permute-start.25 = (bf16[512,128]{1,0:T(8,128)(2,1)S(1)}, bf16[512,128]{1,0:T(8,128)(2,1)S(1)}, u32[]{:S(2)}, u32[]{:S(2)}) collective-permute-start(bf16[512,128]{1,0:T(8,128)(2,1)S(1)} %get-tuple-element.108), channel_id=1, source_target_pairs={{0,8},{4,12},{8,0},{12,4},{16,24},{20,28},{24,16},{28,20},{1,9},{5... | collective-permute-start | bytes 393224 | tf_op jit(solution)/shard_map/ppermute | solution.py:337
  6.4 1.5 %collective-permute-start.26 = (bf16[512,128]{1,0:T(8,128)(2,1)S(1)}, bf16[512,128]{1,0:T(8,128)(2,1)S(1)}, u32[]{:S(2)}, u32[]{:S(2)}) collective-permute-start(bf16[512,128]{1,0:T(8,128)(2,1)S(1)} %get-tuple-element.109), channel_id=1, source_target_pairs={{0,16},{4,20},{8,24},{12,28},{16,0},{20,4},{24,8},{28,12},{1,17},{... | collective-permute-start | bytes 393224 | tf_op jit(solution)/shard_map/ppermute | solution.py:337
  7.9 0.0 collective-permute-start.27
  7.9 1.9 %collective-permute-start.29 = (bf16[512,128]{1,0:T(8,128)(2,1)S(1)}, bf16[512,128]{1,0:T(8,128)(2,1)S(1)}, u32[]{:S(2)}, u32[]{:S(2)}) collective-permute-start(bf16[512,128]{1,0:T(8,128)(2,1)S(1)} %get-tuple-element.113), channel_id=1, source_target_pairs={{0,8},{4,12},{8,0},{12,4},{16,24},{20,28},{24,16},{28,20},{1,9},{5... | collective-permute-start | bytes 393224 | tf_op jit(solution)/shard_map/ppermute | solution.py:337
  9.8 1.5 %collective-permute-start.30 = (bf16[512,128]{1,0:T(8,128)(2,1)S(1)}, bf16[512,128]{1,0:T(8,128)(2,1)S(1)}, u32[]{:S(2)}, u32[]{:S(2)}) collective-permute-start(bf16[512,128]{1,0:T(8,128)(2,1)S(1)} %get-tuple-element.114), channel_id=1, source_target_pairs={{0,16},{4,20},{8,24},{12,28},{16,0},{20,4},{24,8},{28,12},{1,17},{... | collective-permute-start | bytes 393224 | tf_op jit(solution)/shard_map/ppermute | solution.py:337
  11.4 0.0 collective-permute-done.25.rest_1_
  11.4 2.3 %collective-permute-start.31 = (bf16[512,128]{1,0:T(8,128)(2,1)S(1)}, bf16[512,128]{1,0:T(8,128)(2,1)S(1)}, u32[]{:S(2)}, u32[]{:S(2)}) collective-permute-start(bf16[512,128]{1,0:T(8,128)(2,1)S(1)} %get-tuple-element.115), channel_id=1, source_target_pairs={{0,24},{4,28},{8,16},{12,20},{16,8},{20,12},{24,0},{28,4},{1,25},{... | collective-permute-start | bytes 393224 | tf_op jit(solution)/shard_map/ppermute | solution.py:337
  13.7 0.0 copy-done.1
  13.7 0.0 copy-done.2
  13.7 2.7 %shard_map.37 = (bf16[1536,1024]{1,0:T(8,128)(2,1)S(1)}, bf16[768,768]{1,0:T(8,128)(2,1)S(1)}, s32[1]{0:T(128)}) custom-call(s32[8]{0:T(128)S(1)} %copy-done.2, s32[8,128]{1,0:T(8,128)S(1)} %bitcast.2), custom_call_target="tpu_custom_call" | custom-call | flops 4000000000 | bytes 4000000 | tf_op jit(solution)/shard_map/pallas_call | solution.py:107
  16.3 0.0 collective-permute-done.26.rest_2_
  16.4 0.0 collective-permute-done.27.rest_3_
  16.4 1.3 %shard_map.40 = (bf16[2,384,128]{2,1,0:T(8,128)(2,1)S(1)}, bf16[512,128]{1,0:T(8,128)(2,1)S(1)}, bf16[512,128]{1,0:T(8,128)(2,1)S(1)}, bf16[512,128]{1,0:T(8,128...) custom-call(bf16[1536,1024]{1,0:T(8,128)(2,1)S(1)} %get-tuple-element.106.selec, ...), custom_call_target="tpu_custom_call" | custom-call | flops 805306368 | bytes 4000000 | tf_op jit(solution)/shard_map/pallas_call | solution.py:214
  17.7 0.0 collective-permute-done.29.rest_1_
  17.7 2.3 %collective-permute-done.30.rest_2_ = bf16[512,128]{1,0:T(8,128)(2,1)S(1)} collective-permute-done((bf16[512,128]{1,0:T(8,128)(2,1)S(1)}, bf16[512,128]{1,0:T(8,128)(2,1)S(1)}, u32[]{:S(2)}, u32[]{:S(2)}) %collective-permute-start.30) | collective-permute-done | bytes 131104 | tf_op jit(solution)/shard_map/ppermute | solution.py:337
  20.0 0.0 collective-permute-done.31.rest_3_
  20.0 1.3 %shard_map.41 = (bf16[2,384,128]{2,1,0:T(8,128)(2,1)S(1)}, bf16[512,128]{1,0:T(8,128)(2,1)S(1)}, bf16[512,128]{1,0:T(8,128)(2,1)S(1)}, bf16[512,128]{1,0:T(8,128...) custom-call(bf16[1536,1024]{1,0:T(8,128)(2,1)S(1)} %get-tuple-element.106.selec, ...), custom_call_target="tpu_custom_call" | custom-call | flops 805306368 | bytes 4000000 | tf_op jit(solution)/shard_map/pallas_call | solution.py:214
  21.4 1.6 %collective-permute-start.34 = (bf16[512,128]{1,0:T(8,128)(2,1)S(1)}, bf16[512,128]{1,0:T(8,128)(2,1)S(1)}, u32[]{:S(2)}, u32[]{:S(2)}) collective-permute-start(bf16[512,128]{1,0:T(8,128)(2,1)S(1)} %get-tuple-element.128), channel_id=1, source_target_pairs={{0,1},{1,0},{2,3},{3,2},{4,5},{5,4},{6,7},{7,6},{8,9},{9,8},{10,11... | collective-permute-start | bytes 393224 | tf_op jit(solution)/shard_map/ppermute | solution.py:304
  23.7 2.5 %collective-permute-start.36 = (bf16[512,128]{1,0:T(8,128)(2,1)S(1)}, bf16[512,128]{1,0:T(8,128)(2,1)S(1)}, u32[]{:S(2)}, u32[]{:S(2)}) collective-permute-start(bf16[512,128]{1,0:T(8,128)(2,1)S(1)} %get-tuple-element.131), channel_id=1, source_target_pairs={{0,3},{1,2},{2,1},{3,0},{4,7},{5,6},{6,5},{7,4},{8,11},{9,10},{10,... | collective-permute-start | bytes 393224 | tf_op jit(solution)/shard_map/ppermute | solution.py:304
  26.2 13.6 %conditional.1 = (bf16[256,256]{1,0:T(8,128)(2,1)}, bf16[256,256]{1,0:T(8,128)(2,1)}, bf16[256,256]{1,0:T(8,128)(2,1)}) conditional(s32[]{:T(128)} %bitcast.1, (bf16[256,256]{1,0:T(8,128)(2,1)S(1)}, bf16[256,256]{1,0:T(8,128)(2,1)S(1)}, bf16[256,256]{1,0:T(8,128)(2,1)S(1)}) %tuple.37, ...), branch_computations={%region_0.1_spmd, %region_1.2_spmd, %region_2.3_spmd, %region_3.4_... | conditional | bytes 2801814 | solution.py:322
  26.2 1.3 %collective-permute-start.14 = (bf16[160,256]{1,0:T(8,128)(2,1)S(1)}, bf16[160,256]{1,0:T(8,128)(2,1)S(1)}, u32[]{:S(2)}, u32[]{:S(2)}) collective-permute-start(bf16[160,256]{1,0:T(8,128)(2,1)S(1)} %slice.56), channel_id=1, source_target_pairs={{0,3},{1,2},{2,1},{3,0},{4,7},{5,6},{6,5},{7,4},{8,11},{9,10},{10,... | collective-permute-start | bytes 245768 | tf_op jit(solution)/shard_map/cond/branch_4_fun/ppermute | solution.py:304
  27.6 0.8 %collective-permute-start.13 = (bf16[160,256]{1,0:T(8,128)(2,1)S(1)}, bf16[160,256]{1,0:T(8,128)(2,1)S(1)}, u32[]{:S(2)}, u32[]{:S(2)}) collective-permute-start(bf16[160,256]{1,0:T(8,128)(2,1)S(1)} %slice.55), channel_id=1, source_target_pairs={{0,2},{1,3},{2,0},{3,1},{4,6},{5,7},{6,4},{7,5},{8,10},{9,11},{10,... | collective-permute-start | bytes 245768 | tf_op jit(solution)/shard_map/cond/branch_4_fun/ppermute | solution.py:304
  28.4 2.2 %collective-permute-start.12 = (bf16[160,256]{1,0:T(8,128)(2,1)S(1)}, bf16[160,256]{1,0:T(8,128)(2,1)S(1)}, u32[]{:S(2)}, u32[]{:S(2)}) collective-permute-start(bf16[160,256]{1,0:T(8,128)(2,1)S(1)} %slice.54), channel_id=1, source_target_pairs={{0,1},{1,0},{2,3},{3,2},{4,5},{5,4},{6,7},{7,6},{8,9},{9,8},{10,11... | collective-permute-start | bytes 245768 | tf_op jit(solution)/shard_map/cond/branch_4_fun/ppermute | solution.py:304
  30.6 3.8 %collective-permute-done.14 = bf16[160,256]{1,0:T(8,128)(2,1)S(1)} collective-permute-done((bf16[160,256]{1,0:T(8,128)(2,1)S(1)}, bf16[160,256]{1,0:T(8,128)(2,1)S(1)}, u32[]{:S(2)}, u32[]{:S(2)}) %collective-permute-start.14) | collective-permute-done | bytes 81952 | tf_op jit(solution)/shard_map/cond/branch_4_fun/ppermute | solution.py:304
  34.4 0.7 %pad.63 = bf16[256,256]{1,0:T(8,128)(2,1)} pad(bf16[160,256]{1,0:T(8,128)(2,1)S(1)} %collective-permute-done.14, bf16[]{:T(256)} %constant.23.clone), padding=0_96x0_0 | pad | bytes 212994 | tf_op jit(solution)/shard_map/cond/branch_4_fun/jit(_pad)/pad | solution.py:318
  35.1 3.4 %collective-permute-done.13 = bf16[160,256]{1,0:T(8,128)(2,1)S(1)} collective-permute-done((bf16[160,256]{1,0:T(8,128)(2,1)S(1)}, bf16[160,256]{1,0:T(8,128)(2,1)S(1)}, u32[]{:S(2)}, u32[]{:S(2)}) %collective-permute-start.13) | collective-permute-done | bytes 81952 | tf_op jit(solution)/shard_map/cond/branch_4_fun/ppermute | solution.py:304
  38.4 0.7 %pad.62 = bf16[256,256]{1,0:T(8,128)(2,1)} pad(bf16[160,256]{1,0:T(8,128)(2,1)S(1)} %collective-permute-done.13, bf16[]{:T(256)} %constant.23.clone), padding=0_96x0_0 | pad | bytes 212994 | tf_op jit(solution)/shard_map/cond/branch_4_fun/jit(_pad)/pad | solution.py:318
  39.1 0.0 collective-permute-done.12
  39.1 0.7 %pad.61 = bf16[256,256]{1,0:T(8,128)(2,1)} pad(bf16[160,256]{1,0:T(8,128)(2,1)S(1)} %collective-permute-done.12, bf16[]{:T(256)} %constant.23.clone), padding=0_96x0_0 | pad | bytes 212994 | tf_op jit(solution)/shard_map/cond/branch_4_fun/jit(_pad)/pad | solution.py:318
  39.8 0.4 collective-permute-start.33
  40.1 2.6 %collective-permute-start.35 = (bf16[512,128]{1,0:T(8,128)(2,1)S(1)}, bf16[512,128]{1,0:T(8,128)(2,1)S(1)}, u32[]{:S(2)}, u32[]{:S(2)}) collective-permute-start(bf16[512,128]{1,0:T(8,128)(2,1)S(1)} %get-tuple-element.130), channel_id=1, source_target_pairs={{0,3},{1,2},{2,1},{3,0},{4,7},{5,6},{6,5},{7,4},{8,11},{9,10},{10,... | collective-permute-start | bytes 393224 | tf_op jit(solution)/shard_map/ppermute | solution.py:304
  42.8 0.5 collective-permute-start.32
  43.3 0.0 collective-permute-done.34.refs_1_
  43.3 2.4 %collective-permute-start.28 = (bf16[512,128]{1,0:T(8,128)(2,1)S(1)}, bf16[512,128]{1,0:T(8,128)(2,1)S(1)}, u32[]{:S(2)}, u32[]{:S(2)}) collective-permute-start(bf16[512,128]{1,0:T(8,128)(2,1)S(1)} %get-tuple-element.111), channel_id=1, source_target_pairs={{0,2},{1,3},{2,0},{3,1},{4,6},{5,7},{6,4},{7,5},{8,10},{9,11},{10,... | collective-permute-start | bytes 393224 | tf_op jit(solution)/shard_map/ppermute | solution.py:304
  45.7 0.0 collective-permute-done.36.refs_4_
  45.7 0.6 collective-permute-done.33.refs_0_
  46.3 3.6 %collective-permute-done.35.refs_3_ = bf16[512,128]{1,0:T(8,128)(2,1)S(1)} collective-permute-done((bf16[512,128]{1,0:T(8,128)(2,1)S(1)}, bf16[512,128]{1,0:T(8,128)(2,1)S(1)}, u32[]{:S(2)}, u32[]{:S(2)}) %collective-permute-start.35) | collective-permute-done | bytes 131104 | tf_op jit(solution)/shard_map/ppermute | solution.py:304
  49.9 3.0 %shard_map.42.so_far = f32[2,2,384,384]{3,2,1,0:T(8,128)S(1)} custom-call(bf16[768,768]{1,0:T(8,128)(2,1)S(1)} %get-tuple-element.105.place_ref, bf16[2,384,128]{2,1,0:T(8,128)(2,1)S(1)} %get-tuple-element.125.own_real, bf16[2,384,128]{2,1,0:T(8,128)(2,1)S(1)} %get-tuple-element.126.own_imag, bf16[512,128]{1,0:T(8,128)(2,1)S(1)} %collective-permute-done.33.refs_0_, ...), custom_call_target="tpu_custom_call" | custom-call | flops 1207959552 | bytes 3000000 | tf_op jit(solution)/shard_map/pallas_call | solution.py:279
  52.9 4.4 %collective-permute-done.32.imag = bf16[512,128]{1,0:T(8,128)(2,1)S(1)} collective-permute-done((bf16[512,128]{1,0:T(8,128)(2,1)S(1)}, bf16[512,128]{1,0:T(8,128)(2,1)S(1)}, u32[]{:S(2)}, u32[]{:S(2)}) %collective-permute-start.32) | collective-permute-done | bytes 131104 | tf_op jit(solution)/shard_map/ppermute | solution.py:304
  57.4 1.5 %collective-permute-done.28.real = bf16[512,128]{1,0:T(8,128)(2,1)S(1)} collective-permute-done((bf16[512,128]{1,0:T(8,128)(2,1)S(1)}, bf16[512,128]{1,0:T(8,128)(2,1)S(1)}, u32[]{:S(2)}, u32[]{:S(2)}) %collective-permute-start.28) | collective-permute-done | bytes 131104 | tf_op jit(solution)/shard_map/ppermute | solution.py:304
  58.8 3.3 %shard_map.43 = f32[2,1,2,384,384]{4,3,2,1,0:T(8,128)} custom-call(bf16[768,768]{1,0:T(8,128)(2,1)S(1)} %get-tuple-element.105.place_ref, bf16[512,128]{1,0:T(8,128)(2,1)S(1)} %collective-permute-done.28.real, bf16[512,128]{1,0:T(8,128)(2,1)S(1)} %collective-permute-done.32.imag, bf16[256,256]{1,0:T(8,128)(2,1)} %get-tuple-element.124.rest, ...), custom_call_target="tpu_custom_call" | custom-call | flops 301989888 | bytes 3000000 | tf_op jit(solution)/shard_map/pallas_call | solution.py:288
  (4 shorter events, 0.1 us)
Async XLA Ops:
  0.0 1.2 %copy-start = (bf16[2,8,256,128]{3,2,1,0:T(8,128)(2,1)S(1)}, bf16[2,8,256,128]{3,2,1,0:T(8,128)(2,1)}, u32[]{:S(2)}) copy-start(bf16[2,8,256,128]{3,2,1,0:T(8,128)(2,1)} %x_ref.3) | copy-start | bytes 3145732
  1.2 12.5 %copy-start.1 = (s32[1024,1]{0,1:T(1,128)S(1)}, s32[1024,1]{0,1:T(1,128)}, u32[]{:S(2)}) copy-start(s32[1024,1]{0,1:T(1,128)} %param.12) | copy-start | bytes 12292
  1.2 12.5 %copy-start.2 = (s32[8]{0:T(128)S(1)}, s32[8]{0:T(128)}, u32[]{:S(2)}) copy-start(s32[8]{0:T(128)} %slot_ref.1) | copy-start | bytes 100
  1.3 2.1 %collective-permute-start.24 = (bf16[2,4,256,128]{3,2,1,0:T(8,128)(2,1)S(1)}, bf16[2,4,256,128]{3,2,1,0:T(8,128)(2,1)S(1)}, u32[]{:S(2)}, u32[]{:S(2)}) collective-permute-start(bf16[2,4,256,128]{3,2,1,0:T(8,128)(2,1)S(1)} %shard_map.38), channel_id=1, source_target_pairs={{0,4},{4,0},{8,12},{12,8},{16,20},{20,16},{24,28},{28,24},{1,5},{5... | collective-permute-start | bytes 1572872 | tf_op jit(solution)/shard_map/ppermute | solution.py:359
  3.4 7.9 %collective-permute-start.25 = (bf16[512,128]{1,0:T(8,128)(2,1)S(1)}, bf16[512,128]{1,0:T(8,128)(2,1)S(1)}, u32[]{:S(2)}, u32[]{:S(2)}) collective-permute-start(bf16[512,128]{1,0:T(8,128)(2,1)S(1)} %get-tuple-element.108), channel_id=1, source_target_pairs={{0,8},{4,12},{8,0},{12,4},{16,24},{20,28},{24,16},{28,20},{1,9},{5... | collective-permute-start | bytes 393224 | tf_op jit(solution)/shard_map/ppermute | solution.py:337
  6.4 10.0 %collective-permute-start.26 = (bf16[512,128]{1,0:T(8,128)(2,1)S(1)}, bf16[512,128]{1,0:T(8,128)(2,1)S(1)}, u32[]{:S(2)}, u32[]{:S(2)}) collective-permute-start(bf16[512,128]{1,0:T(8,128)(2,1)S(1)} %get-tuple-element.109), channel_id=1, source_target_pairs={{0,16},{4,20},{8,24},{12,28},{16,0},{20,4},{24,8},{28,12},{1,17},{... | collective-permute-start | bytes 393224 | tf_op jit(solution)/shard_map/ppermute | solution.py:337
  7.9 8.5 %collective-permute-start.27 = (bf16[512,128]{1,0:T(8,128)(2,1)S(1)}, bf16[512,128]{1,0:T(8,128)(2,1)S(1)}, u32[]{:S(2)}, u32[]{:S(2)}) collective-permute-start(bf16[512,128]{1,0:T(8,128)(2,1)S(1)} %get-tuple-element.110), channel_id=1, source_target_pairs={{0,24},{4,28},{8,16},{12,20},{16,8},{20,12},{24,0},{28,4},{1,25},{... | collective-permute-start | bytes 393224 | tf_op jit(solution)/shard_map/ppermute | solution.py:337
  7.9 9.8 %collective-permute-start.29 = (bf16[512,128]{1,0:T(8,128)(2,1)S(1)}, bf16[512,128]{1,0:T(8,128)(2,1)S(1)}, u32[]{:S(2)}, u32[]{:S(2)}) collective-permute-start(bf16[512,128]{1,0:T(8,128)(2,1)S(1)} %get-tuple-element.113), channel_id=1, source_target_pairs={{0,8},{4,12},{8,0},{12,4},{16,24},{20,28},{24,16},{28,20},{1,9},{5... | collective-permute-start | bytes 393224 | tf_op jit(solution)/shard_map/ppermute | solution.py:337
  9.8 10.2 %collective-permute-start.30 = (bf16[512,128]{1,0:T(8,128)(2,1)S(1)}, bf16[512,128]{1,0:T(8,128)(2,1)S(1)}, u32[]{:S(2)}, u32[]{:S(2)}) collective-permute-start(bf16[512,128]{1,0:T(8,128)(2,1)S(1)} %get-tuple-element.114), channel_id=1, source_target_pairs={{0,16},{4,20},{8,24},{12,28},{16,0},{20,4},{24,8},{28,12},{1,17},{... | collective-permute-start | bytes 393224 | tf_op jit(solution)/shard_map/ppermute | solution.py:337
  11.4 8.7 %collective-permute-start.31 = (bf16[512,128]{1,0:T(8,128)(2,1)S(1)}, bf16[512,128]{1,0:T(8,128)(2,1)S(1)}, u32[]{:S(2)}, u32[]{:S(2)}) collective-permute-start(bf16[512,128]{1,0:T(8,128)(2,1)S(1)} %get-tuple-element.115), channel_id=1, source_target_pairs={{0,24},{4,28},{8,16},{12,20},{16,8},{20,12},{24,0},{28,4},{1,25},{... | collective-permute-start | bytes 393224 | tf_op jit(solution)/shard_map/ppermute | solution.py:337
  21.4 21.9 %collective-permute-start.34 = (bf16[512,128]{1,0:T(8,128)(2,1)S(1)}, bf16[512,128]{1,0:T(8,128)(2,1)S(1)}, u32[]{:S(2)}, u32[]{:S(2)}) collective-permute-start(bf16[512,128]{1,0:T(8,128)(2,1)S(1)} %get-tuple-element.128), channel_id=1, source_target_pairs={{0,1},{1,0},{2,3},{3,2},{4,5},{5,4},{6,7},{7,6},{8,9},{9,8},{10,11... | collective-permute-start | bytes 393224 | tf_op jit(solution)/shard_map/ppermute | solution.py:304
  23.7 22.0 %collective-permute-start.36 = (bf16[512,128]{1,0:T(8,128)(2,1)S(1)}, bf16[512,128]{1,0:T(8,128)(2,1)S(1)}, u32[]{:S(2)}, u32[]{:S(2)}) collective-permute-start(bf16[512,128]{1,0:T(8,128)(2,1)S(1)} %get-tuple-element.131), channel_id=1, source_target_pairs={{0,3},{1,2},{2,1},{3,0},{4,7},{5,6},{6,5},{7,4},{8,11},{9,10},{10,... | collective-permute-start | bytes 393224 | tf_op jit(solution)/shard_map/ppermute | solution.py:304
  26.2 8.2 %collective-permute-start.14 = (bf16[160,256]{1,0:T(8,128)(2,1)S(1)}, bf16[160,256]{1,0:T(8,128)(2,1)S(1)}, u32[]{:S(2)}, u32[]{:S(2)}) collective-permute-start(bf16[160,256]{1,0:T(8,128)(2,1)S(1)} %slice.56), channel_id=1, source_target_pairs={{0,3},{1,2},{2,1},{3,0},{4,7},{5,6},{6,5},{7,4},{8,11},{9,10},{10,... | collective-permute-start | bytes 245768 | tf_op jit(solution)/shard_map/cond/branch_4_fun/ppermute | solution.py:304
  27.6 10.9 %collective-permute-start.13 = (bf16[160,256]{1,0:T(8,128)(2,1)S(1)}, bf16[160,256]{1,0:T(8,128)(2,1)S(1)}, u32[]{:S(2)}, u32[]{:S(2)}) collective-permute-start(bf16[160,256]{1,0:T(8,128)(2,1)S(1)} %slice.55), channel_id=1, source_target_pairs={{0,2},{1,3},{2,0},{3,1},{4,6},{5,7},{6,4},{7,5},{8,10},{9,11},{10,... | collective-permute-start | bytes 245768 | tf_op jit(solution)/shard_map/cond/branch_4_fun/ppermute | solution.py:304
  28.4 10.8 %collective-permute-start.12 = (bf16[160,256]{1,0:T(8,128)(2,1)S(1)}, bf16[160,256]{1,0:T(8,128)(2,1)S(1)}, u32[]{:S(2)}, u32[]{:S(2)}) collective-permute-start(bf16[160,256]{1,0:T(8,128)(2,1)S(1)} %slice.54), channel_id=1, source_target_pairs={{0,1},{1,0},{2,3},{3,2},{4,5},{5,4},{6,7},{7,6},{8,9},{9,8},{10,11... | collective-permute-start | bytes 245768 | tf_op jit(solution)/shard_map/cond/branch_4_fun/ppermute | solution.py:304
  39.8 6.5 %collective-permute-start.33 = (bf16[512,128]{1,0:T(8,128)(2,1)S(1)}, bf16[512,128]{1,0:T(8,128)(2,1)S(1)}, u32[]{:S(2)}, u32[]{:S(2)}) collective-permute-start(bf16[512,128]{1,0:T(8,128)(2,1)S(1)} %get-tuple-element.127), channel_id=1, source_target_pairs={{0,1},{1,0},{2,3},{3,2},{4,5},{5,4},{6,7},{7,6},{8,9},{9,8},{10,11... | collective-permute-start | bytes 393224 | tf_op jit(solution)/shard_map/ppermute | solution.py:304
  40.1 9.8 %collective-permute-start.35 = (bf16[512,128]{1,0:T(8,128)(2,1)S(1)}, bf16[512,128]{1,0:T(8,128)(2,1)S(1)}, u32[]{:S(2)}, u32[]{:S(2)}) collective-permute-start(bf16[512,128]{1,0:T(8,128)(2,1)S(1)} %get-tuple-element.130), channel_id=1, source_target_pairs={{0,3},{1,2},{2,1},{3,0},{4,7},{5,6},{6,5},{7,4},{8,11},{9,10},{10,... | collective-permute-start | bytes 393224 | tf_op jit(solution)/shard_map/ppermute | solution.py:304
  42.8 14.6 %collective-permute-start.32 = (bf16[512,128]{1,0:T(8,128)(2,1)S(1)}, bf16[512,128]{1,0:T(8,128)(2,1)S(1)}, u32[]{:S(2)}, u32[]{:S(2)}) collective-permute-start(bf16[512,128]{1,0:T(8,128)(2,1)S(1)} %get-tuple-element.119), channel_id=1, source_target_pairs={{0,2},{1,3},{2,0},{3,1},{4,6},{5,7},{6,4},{7,5},{8,10},{9,11},{10,... | collective-permute-start | bytes 393224 | tf_op jit(solution)/shard_map/ppermute | solution.py:304
  43.3 15.6 %collective-permute-start.28 = (bf16[512,128]{1,0:T(8,128)(2,1)S(1)}, bf16[512,128]{1,0:T(8,128)(2,1)S(1)}, u32[]{:S(2)}, u32[]{:S(2)}) collective-permute-start(bf16[512,128]{1,0:T(8,128)(2,1)S(1)} %get-tuple-element.111), channel_id=1, source_target_pairs={{0,2},{1,3},{2,0},{3,1},{4,6},{5,7},{6,4},{7,5},{8,10},{9,11},{10,... | collective-permute-start | bytes 393224 | tf_op jit(solution)/shard_map/ppermute | solution.py:304

commit v7 on v5

--- a/solution.py
+++ b/solution.py
@@ -78,23 +78,46 @@
     )(slot_subarray_index, assignment.reshape(antennas // LANES, LANES))
 
 
-def give_kernel(chips, x_ref, out):
+def give_kernel(chips, x_ref, *outs):
     me = lax.axis_index("chan")
-    for k in range(2):
+    for k, out in enumerate(outs):
         for t in range(chips):
-            out[k, t] = x_ref[k, (me ^ (2 * t)) ^ 1]
+            out[t] = x_ref[k, (me ^ (2 * t)) ^ 1]
 
 
 def give(voltages):
     parts, chans, inputs, samples = voltages.shape
     return pl.pallas_call(
         functools.partial(give_kernel, chans // 2),
-        out_shape=jax.ShapeDtypeStruct((parts, chans // 2, inputs, samples), voltages.dtype),
+        out_shape=[jax.ShapeDtypeStruct((chans // 2, inputs, samples), voltages.dtype)] * parts,
         in_specs=[VMEM],
-        out_specs=VMEM,
+        out_specs=[VMEM] * parts,
         compiler_params=PARAMS,
         cost_estimate=pl.CostEstimate(flops=1_000_000, bytes_accessed=1_000_000, transcendentals=0),
     )(voltages)
+
+
+def fold(a, b):
+    half = LANES // 2
+    left = lax.broadcasted_iota(jnp.int32, a.shape, 1) < half
+    return (
+        jnp.where(left, a, pltpu.roll(b, half, 1)),
+        jnp.where(left, pltpu.roll(a, half, 1), b),
+    )
+
+
+def merge_halves_kernel(chips, x_ref, given_ref, *outs):
+    me = lax.axis_index("chan")
+    for parity in range(2):
+
+        @pl.when((me & 1) == parity)
+        def _():
+            for t in range(chips):
+                cores = [x_ref[0, me ^ (2 * t)], given_ref[t]]
+                if parity:
+                    cores.reverse()
+                for h, half in enumerate(fold(*[core.astype(jnp.float32) for core in cores])):
+                    outs[h * chips + t][...] = half.astype(jnp.bfloat16)
 
 
 def merge_kernel(chips, x_ref, given_ref, *outs):
@@ -102,27 +125,88 @@
     inputs = x_ref.shape[2]
     mine = pl.multiple_of((me & 1) * inputs, inputs)
     theirs = pl.multiple_of(inputs - (me & 1) * inputs, inputs)
-    for k in range(2):
-        for t in range(chips):
-            out = outs[k * chips + t]
-            piece, other = x_ref[k, me ^ (2 * t)], given_ref[k, t]
-            out[pl.ds(mine, inputs)] = piece
-            out[pl.ds(theirs, inputs)] = other
-
-
-def merge(voltages, given):
-    parts, chans, inputs, samples = voltages.shape
+    for t in range(chips):
+        outs[t][pl.ds(mine, inputs)] = x_ref[1, me ^ (2 * t)]
+        outs[t][pl.ds(theirs, inputs)] = given_ref[t]
+
+
+def merge(kernel, height, voltages, given):
+    _, chans, inputs, samples = voltages.shape
     chips = chans // 2
-    piece = jax.ShapeDtypeStruct((2 * inputs, samples), voltages.dtype)
-    out = pl.pallas_call(
-        functools.partial(merge_kernel, chips),
-        out_shape=[piece] * (parts * chips),
+    count = 2 * chips // height
+    return pl.pallas_call(
+        functools.partial(kernel, chips),
+        out_shape=[jax.ShapeDtypeStruct((height * inputs, samples), voltages.dtype)] * count,
         in_specs=[VMEM] * 2,
-        out_specs=[VMEM] * (parts * chips),
+        out_specs=[VMEM] * count,
+        compiler_params=PARAMS,
+        cost_estimate=pl.CostEstimate(flops=1_000_000, bytes_accessed=1_000_000, transcendentals=0),
+    )(voltages, given)
+
+
+def gather_half_kernel(steps, groups, select_ref, *rest):
+    xs, outs = rest[: len(steps)], rest[len(steps) : len(steps) + groups]
+    wide, pair = rest[len(steps) + groups :]
+    inputs = xs[0].shape[0]
+    each = inputs // 2
+    chip = lax.axis_index("chan") // 2
+    for i, (step, x) in enumerate(zip(steps, xs)):
+        wide[i * inputs : (i + 1) * inputs] = x[...].astype(jnp.float32)
+        pols = [wide[pl.ds(i * inputs + pol, each, stride=2), :] for pol in range(2)]
+        top = (chip ^ step) * inputs
+        for core, one in enumerate(fold(*pols)):
+            pair[pl.ds(pl.multiple_of(top + core * each, each), each)] = one.astype(jnp.bfloat16)
+    picked = jnp.dot(select_ref[...], pair[...], preferred_element_type=jnp.float32)
+    per, rows, _ = outs[0].shape
+    for g, out in enumerate(outs):
+        for s in range(per):
+            top = (g * per + s) * rows
+            out[s] = picked[top : top + rows].astype(jnp.bfloat16)
+
+
+def gather_half(select, xs, steps, groups, per):
+    inputs, samples = xs[0].shape
+    rows, antennas = select.shape
+    return pl.pallas_call(
+        functools.partial(gather_half_kernel, steps, groups),
+        out_shape=[jax.ShapeDtypeStruct((per, rows // (groups * per), samples), jnp.bfloat16)] * groups,
+        in_specs=[VMEM] * (1 + len(xs)),
+        out_specs=[VMEM] * groups,
+        scratch_shapes=[
+            pltpu.VMEM((inputs * len(xs), samples), jnp.float32),
+            pltpu.VMEM((antennas, samples), jnp.bfloat16),
+        ],
+        compiler_params=PARAMS,
+        cost_estimate=pl.CostEstimate(
+            flops=2 * rows * antennas * samples, bytes_accessed=4_000_000, transcendentals=0
+        ),
+    )(select, *xs)
+
+
+def join_kernel(*refs):
+    *parts, tall = refs
+    count = len(parts) // 3
+    for e in range(count):
+        first, second, out = parts[e], parts[count + e], parts[2 * count + e]
+        per, rows, _ = first.shape
+        for s in range(per):
+            for pol, one in enumerate(fold(first[s].astype(jnp.float32), second[s].astype(jnp.float32))):
+                tall[e * per + s, pl.ds(pol, rows, stride=2), :] = one
+            out[s] = tall[e * per + s].astype(jnp.bfloat16)
+
+
+def join(first, second):
+    per, rows, samples = first[0].shape
+    count = len(first)
+    return pl.pallas_call(
+        join_kernel,
+        out_shape=[jax.ShapeDtypeStruct((per, 2 * rows, samples), jnp.bfloat16)] * count,
+        in_specs=[VMEM] * (2 * count),
+        out_specs=[VMEM] * count,
+        scratch_shapes=[pltpu.VMEM((count * per, 2 * rows, samples), jnp.float32)],
         compiler_params=PARAMS,
         cost_estimate=pl.CostEstimate(flops=1_000_000, bytes_accessed=2_000_000, transcendentals=0),
-    )(voltages, given)
-    return out[:chips], out[chips:]
+    )(*first, *second)
 
 
 def load_pair(steps, xs, wide, pair):
@@ -276,20 +360,30 @@
     subarrays = slot_subarray_index.shape[0]
     per = subarrays // groups
     first, second, last = orders(groups)
-    if by_chip(chans):
-        steps = tuple(range(chans // 2))
-        given = lax.ppermute(give(voltages), "chan", [(i, i ^ 1) for i in range(chans)])
-        reals, imags = merge(voltages, given)
-        reals = cross(reals, chans, range(chans))
-        imags = cross(imags, chans, range(chans))
-    else:
+    if not by_chip(chans):
         steps = (0,)
         reals = [across(voltages[0])]
         imags = [across(voltages[1])]
+        select = plan(assignment, slot_subarray_index, groups, SLOT // 2)
+        real = exchange(gather(select, reals, steps, groups, per, SLOT), first, groups)
+        imag = exchange(gather(select, imags, steps, groups, per, SLOT), second, groups)
+        return gram(real, imag, last)
+
+    chips = chans // 2
+    steps = tuple(range(chips))
+    swap = [(i, i ^ 1) for i in range(chans)]
+    give_real, give_imag = give(voltages)
+    given_real = lax.ppermute(give_real, "chan", swap)
+    halves = merge(merge_halves_kernel, 1, voltages, given_real)
+    given_imag = lax.ppermute(give_imag, "chan", swap)
     select = plan(assignment, slot_subarray_index, groups, SLOT // 2)
-    real = exchange(gather(select, reals, steps, groups, per, SLOT), first, groups)
+    got = []
+    for h in range(2):
+        pieces = cross(halves[h * chips : (h + 1) * chips], chans, range(chans))
+        got.append(exchange(gather_half(select, pieces, steps, groups, per), first, groups))
+    imags = cross(merge(merge_kernel, 2, voltages, given_imag), chans, range(chans))
     imag = exchange(gather(select, imags, steps, groups, per, SLOT), second, groups)
-    return gram(real, imag, last)
+    return gram(join(*got), imag, last)
 
 
 def solution(mesh):

time: 60.8 us -> 58.6 us (0.964)
  waiting for transfers between devices: 29.2 us -> 20.8 us
  starting transfers between devices: 22.3 us -> 26.8 us
  Pallas kernels: 7.92 us -> 9.43 us
    ppermute x6 -> x9, waiting for transfers between devices: 4.66 us -> 0.02 us  [cross(): lax.ppermute(chunks[step], 'chan', [(i, i ^ 2 * step) for i in starts])]
    ppermute x6 -> x9, waiting for transfers between devices: 23 us -> 19.7 us  [exchange(): got[step] = lax.ppermute(chunks[step], 'tm', pairs)]
    pallas_call x2 -> x6, Pallas kernels: 0.11 us -> 2.95 us  [the longest x2 2.26 us: gather_half(): pl.pallas_call(functools.partial(gather_half_kernel, steps, groups), out_...]
    ppermute x6 -> x9, starting transfers between devices: 10.2 us -> 12.7 us  [cross(): lax.ppermute(chunks[step], 'chan', [(i, i ^ 2 * step) for i in starts])]
    ppermute x6 -> x9, starting transfers between devices: 11.5 us -> 13.4 us  [exchange(): got[step] = lax.ppermute(chunks[step], 'tm', pairs)]
    pallas_call x2 -> x1, Pallas kernels: 2.64 us -> 1.32 us  [gather(): pl.pallas_call(functools.partial(gather_kernel, steps, groups), out_shape...]
    ppermute x1 -> x2, waiting for transfers between devices: 1.54 us -> 1.09 us  [the longest x1 1.08 us: steps_of(): given_real = lax.ppermute(give_real, 'chan', swap)]
  transfers between devices with their start and end apart: 13 -> 20, of which waited for: 7 -> 3; matrix products, arithmetic and copies ran while one was open for 0% -> 0% of each run, Pallas kernels for 10% -> 13%
where the time goes in v7:
time: 58.6 us; the launch traced here: 58.4 us
  starting transfers between devices  26.8 us (46%)
  waiting for transfers between devices  20.8 us (35%)
  Pallas kernels  9.43 us (16%)
  local copies, waits for them, and re-layouts  1.23 us (2%)
    ppermute x9, waiting for transfers between devices, exchange(): got[step] = lax.ppermute(chunks[step], 'tm', pairs)  19.7 us
    ppermute x9, starting transfers between devices, exchange(): got[step] = lax.ppermute(chunks[step], 'tm', pairs)  13.4 us
    ppermute x9, starting transfers between devices, cross(): lax.ppermute(chunks[step], 'chan', [(i, i ^ 2 * step) for i in starts])  12.7 us
    pallas_call x2, Pallas kernels, gather_half(): pl.pallas_call(functools.partial(gather_half_kernel, steps, groups), out_...  2.26 us
    pallas_call x1, Pallas kernels, plan(): pl.pallas_call(functools.partial(plan_kernel, groups, half), out_shape=ja...  2.06 us
    pallas_call x1, Pallas kernels, gram(): pl.pallas_call(late_kernel, out_shape=jax.ShapeDtypeStruct((per, 1, 2, sl...  1.72 us
    pallas_call x1, Pallas kernels, gram(): pl.pallas_call(early_kernel, out_shape=jax.ShapeDtypeStruct((per, 2, slot...  1.39 us
    pallas_call x1, Pallas kernels, gather(): pl.pallas_call(functools.partial(gather_kernel, steps, groups), out_shape...  1.32 us
  transfers between devices with their start and end apart: 20, of which 3 were waited for; matrix products, arithmetic and copies ran while one was open for 0% of the time, Pallas kernels for 13%

profile of v7, /device:TPU:0, one launch (start us, length us, event | category | flops | bytes accessed | tf_op | source)
XLA Modules:
  0.0 58.4 jit_solution(8199686850859693819)
XLA Ops:
  0.0 0.0 copy-start
  0.0 1.2 %copy-done = bf16[2,8,256,128]{3,2,1,0:T(8,128)(2,1)S(1)} copy-done((bf16[2,8,256,128]{3,2,1,0:T(8,128)(2,1)S(1)}, bf16[2,8,256,128]{3,2,1,0:T(8,128)(2,1)}, u32[]{:S(2)}) %copy-start) | copy-done | bytes 1048600
  1.2 0.0 copy-start.1
  1.2 0.0 copy-start.2
  1.3 0.6 collective-permute-start
  1.8 0.1 collective-permute-start.13
  1.9 1.1 %collective-permute-done.given_ref = bf16[4,256,128]{2,1,0:T(8,128)(2,1)S(1)} collective-permute-done((bf16[4,256,128]{2,1,0:T(8,128)(2,1)S(1)}, bf16[4,256,128]{2,1,0:T(8,128)(2,1)S(1)}, u32[]{:S(2)}, u32[]{:S(2)}) %collective-permute-start) | collective-permute-done | bytes 262176 | tf_op jit(solution)/shard_map/ppermute | solution.py:376
  3.0 0.2 shard_map.39
  3.2 2.9 %collective-permute-start.1 = (bf16[256,128]{1,0:T(8,128)(2,1)S(1)}, bf16[256,128]{1,0:T(8,128)(2,1)S(1)}, u32[]{:S(2)}, u32[]{:S(2)}) collective-permute-start(bf16[256,128]{1,0:T(8,128)(2,1)S(1)} %get-tuple-element.37), channel_id=1, source_target_pairs={{0,8},{4,12},{8,0},{12,4},{16,24},{20,28},{24,16},{28,20},{1,9},{5... | collective-permute-start | bytes 196616 | tf_op jit(solution)/shard_map/ppermute | solution.py:343
  6.1 0.1 collective-permute-start.7
  6.2 2.0 %collective-permute-start.8 = (bf16[256,128]{1,0:T(8,128)(2,1)S(1)}, bf16[256,128]{1,0:T(8,128)(2,1)S(1)}, u32[]{:S(2)}, u32[]{:S(2)}) collective-permute-start(bf16[256,128]{1,0:T(8,128)(2,1)S(1)} %get-tuple-element.46), channel_id=1, source_target_pairs={{0,16},{4,20},{8,24},{12,28},{16,0},{20,4},{24,8},{28,12},{1,17},{... | collective-permute-start | bytes 196616 | tf_op jit(solution)/shard_map/ppermute | solution.py:343
  8.2 1.4 %collective-permute-start.9 = (bf16[256,128]{1,0:T(8,128)(2,1)S(1)}, bf16[256,128]{1,0:T(8,128)(2,1)S(1)}, u32[]{:S(2)}, u32[]{:S(2)}) collective-permute-start(bf16[256,128]{1,0:T(8,128)(2,1)S(1)} %get-tuple-element.47), channel_id=1, source_target_pairs={{0,24},{4,28},{8,16},{12,20},{16,8},{20,12},{24,0},{28,4},{1,25},{... | collective-permute-start | bytes 196616 | tf_op jit(solution)/shard_map/ppermute | solution.py:343
  9.6 0.0 collective-permute-done.13.given_ref
  9.6 1.5 %collective-permute-start.2 = (bf16[256,128]{1,0:T(8,128)(2,1)S(1)}, bf16[256,128]{1,0:T(8,128)(2,1)S(1)}, u32[]{:S(2)}, u32[]{:S(2)}) collective-permute-start(bf16[256,128]{1,0:T(8,128)(2,1)S(1)} %get-tuple-element.38), channel_id=1, source_target_pairs={{0,16},{4,20},{8,24},{12,28},{16,0},{20,4},{24,8},{28,12},{1,17},{... | collective-permute-start | bytes 196616 | tf_op jit(solution)/shard_map/ppermute | solution.py:343
  11.2 0.0 collective-permute-done.1.rest_1_
  11.2 0.7 %collective-permute-start.3 = (bf16[256,128]{1,0:T(8,128)(2,1)S(1)}, bf16[256,128]{1,0:T(8,128)(2,1)S(1)}, u32[]{:S(2)}, u32[]{:S(2)}) collective-permute-start(bf16[256,128]{1,0:T(8,128)(2,1)S(1)} %get-tuple-element.39), channel_id=1, source_target_pairs={{0,24},{4,28},{8,16},{12,20},{16,8},{20,12},{24,0},{28,4},{1,25},{... | collective-permute-start | bytes 196616 | tf_op jit(solution)/shard_map/ppermute | solution.py:343
  11.9 0.0 collective-permute-done.7.rest_1_
  11.9 1.3 %collective-permute-start.14 = (bf16[512,128]{1,0:T(8,128)(2,1)S(1)}, bf16[512,128]{1,0:T(8,128)(2,1)S(1)}, u32[]{:S(2)}, u32[]{:S(2)}) collective-permute-start(bf16[512,128]{1,0:T(8,128)(2,1)S(1)} %get-tuple-element.55), channel_id=1, source_target_pairs={{0,8},{4,12},{8,0},{12,4},{16,24},{20,28},{24,16},{28,20},{1,9},{5... | collective-permute-start | bytes 393224 | tf_op jit(solution)/shard_map/ppermute | solution.py:343
  13.3 0.0 collective-permute-done.8.rest_2_
  13.3 1.5 %collective-permute-start.15 = (bf16[512,128]{1,0:T(8,128)(2,1)S(1)}, bf16[512,128]{1,0:T(8,128)(2,1)S(1)}, u32[]{:S(2)}, u32[]{:S(2)}) collective-permute-start(bf16[512,128]{1,0:T(8,128)(2,1)S(1)} %get-tuple-element.56), channel_id=1, source_target_pairs={{0,16},{4,20},{8,24},{12,28},{16,0},{20,4},{24,8},{28,12},{1,17},{... | collective-permute-start | bytes 393224 | tf_op jit(solution)/shard_map/ppermute | solution.py:343
  14.8 0.0 collective-permute-done.9.rest_3_
  14.8 1.3 %collective-permute-start.16 = (bf16[512,128]{1,0:T(8,128)(2,1)S(1)}, bf16[512,128]{1,0:T(8,128)(2,1)S(1)}, u32[]{:S(2)}, u32[]{:S(2)}) collective-permute-start(bf16[512,128]{1,0:T(8,128)(2,1)S(1)} %get-tuple-element.57), channel_id=1, source_target_pairs={{0,24},{4,28},{8,16},{12,20},{16,8},{20,12},{24,0},{28,4},{1,25},{... | collective-permute-start | bytes 393224 | tf_op jit(solution)/shard_map/ppermute | solution.py:343
  16.0 0.0 copy-done.1
  16.0 0.0 copy-done.2
  16.0 2.1 %shard_map.37.select_ref = bf16[1536,1024]{1,0:T(8,128)(2,1)S(1)} custom-call(s32[8]{0:T(128)S(1)} %copy-done.2, s32[8,128]{1,0:T(8,128)S(1)} %bitcast.1), custom_call_target="tpu_custom_call" | custom-call | flops 4000000000 | bytes 3000000 | tf_op jit(solution)/shard_map/pallas_call | solution.py:71
  18.1 1.1 %shard_map.41 = (bf16[2,192,128]{2,1,0:T(8,128)(2,1)S(1)}, bf16[2,192,128]{2,1,0:T(8,128)(2,1)S(1)}, bf16[2,192,128]{2,1,0:T(8,128)(2,1)S(1)}, bf16[2,192,128]{2,1,0:T(8,128)(2,1)S(1)}) custom-call(bf16[1536,1024]{1,0:T(8,128)(2,1)S(1)} %shard_map.37.select_ref, bf16[256,128]{1,0:T(8,128)(2,1)S(1)} %get-tuple-element.44.rest_0_, ...), custom_call_target="tpu_custom_call" | custom-call | flops 402653184 | bytes 4000000 | tf_op jit(solution)/shard_map/pallas_call | solution.py:170
  19.2 0.0 collective-permute-done.2.rest_2_
  19.3 1.6 %collective-permute-start.10 = (bf16[2,192,128]{2,1,0:T(8,128)(2,1)S(1)}, bf16[2,192,128]{2,1,0:T(8,128)(2,1)S(1)}, u32[]{:S(2)}, u32[]{:S(2)}) collective-permute-start(bf16[2,192,128]{2,1,0:T(8,128)(2,1)S(1)} %get-tuple-element.49), channel_id=1, source_target_pairs={{0,1},{1,0},{2,3},{3,2},{4,5},{5,4},{6,7},{7,6},{8,9},{9,8},{10,11... | collective-permute-start | bytes 294920 | tf_op jit(solution)/shard_map/ppermute | solution.py:327
  20.9 0.0 collective-permute-done.3.rest_3_
  20.9 2.6 %collective-permute-start.11 = (bf16[2,192,128]{2,1,0:T(8,128)(2,1)S(1)}, bf16[2,192,128]{2,1,0:T(8,128)(2,1)S(1)}, u32[]{:S(2)}, u32[]{:S(2)}) collective-permute-start(bf16[2,192,128]{2,1,0:T(8,128)(2,1)S(1)} %get-tuple-element.50), channel_id=1, source_target_pairs={{0,2},{1,3},{2,0},{3,1},{4,6},{5,7},{6,4},{7,5},{8,10},{9,11},{10,... | collective-permute-start | bytes 294920 | tf_op jit(solution)/shard_map/ppermute | solution.py:327
  23.5 1.1 %shard_map.40 = (bf16[2,192,128]{2,1,0:T(8,128)(2,1)S(1)}, bf16[2,192,128]{2,1,0:T(8,128)(2,1)S(1)}, bf16[2,192,128]{2,1,0:T(8,128)(2,1)S(1)}, bf16[2,192,128]{2,1,0:T(8,128)(2,1)S(1)}) custom-call(bf16[1536,1024]{1,0:T(8,128)(2,1)S(1)} %shard_map.37.select_ref, bf16[256,128]{1,0:T(8,128)(2,1)S(1)} %get-tuple-element.36.rest_0_, ...), custom_call_target="tpu_custom_call" | custom-call | flops 402653184 | bytes 4000000 | tf_op jit(solution)/shard_map/pallas_call | solution.py:170
  24.6 0.0 collective-permute-done.14.rest_1_
  24.6 0.3 collective-permute-start.12
  24.9 0.0 collective-permute-done.15.rest_2_
  24.9 0.7 %collective-permute-start.4 = (bf16[2,192,128]{2,1,0:T(8,128)(2,1)S(1)}, bf16[2,192,128]{2,1,0:T(8,128)(2,1)S(1)}, u32[]{:S(2)}, u32[]{:S(2)}) collective-permute-start(bf16[2,192,128]{2,1,0:T(8,128)(2,1)S(1)} %get-tuple-element.41), channel_id=1, source_target_pairs={{0,1},{1,0},{2,3},{3,2},{4,5},{5,4},{6,7},{7,6},{8,9},{9,8},{10,11... | collective-permute-start | bytes 294920 | tf_op jit(solution)/shard_map/ppermute | solution.py:327
  25.6 0.0 collective-permute-done.16.rest_3_
  25.6 1.3 %shard_map.44 = (bf16[2,384,128]{2,1,0:T(8,128)(2,1)S(1)}, bf16[2,384,128]{2,1,0:T(8,128)(2,1)S(1)}, bf16[2,384,128]{2,1,0:T(8,128)(2,1)S(1)}, bf16[2,384,128]{2,1,0:T(8,128)(2,1)S(1)}) custom-call(bf16[1536,1024]{1,0:T(8,128)(2,1)S(1)} %shard_map.37.select_ref, bf16[512,128]{1,0:T(8,128)(2,1)S(1)} %get-tuple-element.54.rest_0_, ...), custom_call_target="tpu_custom_call" | custom-call | flops 805306368 | bytes 4000000 | tf_op jit(solution)/shard_map/pallas_call | solution.py:250
  26.9 1.4 %collective-permute-start.18 = (bf16[2,384,128]{2,1,0:T(8,128)(2,1)S(1)}, bf16[2,384,128]{2,1,0:T(8,128)(2,1)S(1)}, u32[]{:S(2)}, u32[]{:S(2)}) collective-permute-start(bf16[2,384,128]{2,1,0:T(8,128)(2,1)S(1)} %get-tuple-element.63), channel_id=1, source_target_pairs={{0,1},{1,0},{2,3},{3,2},{4,5},{5,4},{6,7},{7,6},{8,9},{9,8},{10,11... | collective-permute-start | bytes 589832 | tf_op jit(solution)/shard_map/ppermute | solution.py:327
  28.4 0.0 collective-permute-done.10.refs_5_
  28.4 3.6 %collective-permute-start.19 = (bf16[2,384,128]{2,1,0:T(8,128)(2,1)S(1)}, bf16[2,384,128]{2,1,0:T(8,128)(2,1)S(1)}, u32[]{:S(2)}, u32[]{:S(2)}) collective-permute-start(bf16[2,384,128]{2,1,0:T(8,128)(2,1)S(1)} %get-tuple-element.64), channel_id=1, source_target_pairs={{0,3},{1,2},{2,1},{3,0},{4,7},{5,6},{6,5},{7,4},{8,11},{9,10},{10,... | collective-permute-start | bytes 589832 | tf_op jit(solution)/shard_map/ppermute | solution.py:327
  32.0 0.0 collective-permute-done.11.refs_6_
  32.0 0.0 collective-permute-start.17
  32.0 0.2 collective-permute-done.12.refs_7_
  32.2 2.7 %collective-permute-start.5 = (bf16[2,192,128]{2,1,0:T(8,128)(2,1)S(1)}, bf16[2,192,128]{2,1,0:T(8,128)(2,1)S(1)}, u32[]{:S(2)}, u32[]{:S(2)}) collective-permute-start(bf16[2,192,128]{2,1,0:T(8,128)(2,1)S(1)} %get-tuple-element.42), channel_id=1, source_target_pairs={{0,2},{1,3},{2,0},{3,1},{4,6},{5,7},{6,4},{7,5},{8,10},{9,11},{10,... | collective-permute-start | bytes 294920 | tf_op jit(solution)/shard_map/ppermute | solution.py:327
  34.9 0.0 collective-permute-done.4.refs_1_
  34.9 0.5 collective-permute-start.6
  35.4 19.5 %collective-permute-done.5.refs_2_ = bf16[2,192,128]{2,1,0:T(8,128)(2,1)S(1)} collective-permute-done((bf16[2,192,128]{2,1,0:T(8,128)(2,1)S(1)}, bf16[2,192,128]{2,1,0:T(8,128)(2,1)S(1)}, u32[]{:S(2)}, u32[]{:S(2)}) %collective-permute-start.5) | collective-permute-done | bytes 98336 | tf_op jit(solution)/shard_map/ppermute | solution.py:327
  54.9 0.0 collective-permute-done.6.refs_3_
  54.9 0.4 shard_map.42
  55.3 0.0 collective-permute-done.18.refs_4_
  55.3 0.0 collective-permute-done.19.refs_5_
  55.3 1.4 %shard_map.45.so_far = f32[2,2,384,384]{3,2,1,0:T(8,128)S(1)} custom-call(bf16[2,384,128]{2,1,0:T(8,128)(2,1)S(1)} %get-tuple-element.59.refs_0_, bf16[2,384,128]{2,1,0:T(8,128)(2,1)S(1)} %get-tuple-element.60.refs_1_, bf16[2,384,128]{2,1,0:T(8,128)(2,1)S(1)} %get-tuple-element.61.refs_2_, bf16[2,384,128]{2,1,0:T(8,128)(2,1)S(1)} %get-tuple-element.62.refs_3_, ...), custom_call_target="tpu_custom_call" | custom-call | flops 905969664 | bytes 3000000 | tf_op jit(solution)/shard_map/pallas_call | solution.py:301
  56.7 0.0 collective-permute-done.17.imag
  56.7 1.7 %shard_map.46 = f32[2,1,2,384,384]{4,3,2,1,0:T(8,128)} custom-call(bf16[2,384,128]{2,1,0:T(8,128)(2,1)S(1)} %get-tuple-element.52.real, bf16[2,384,128]{2,1,0:T(8,128)(2,1)S(1)} %collective-permute-done.17.imag, f32[2,2,384,384]{3,2,1,0:T(8,128)S(1)} %shard_map.45.so_far), custom_call_target="tpu_custom_call" | custom-call | flops 301989888 | bytes 3000000 | tf_op jit(solution)/shard_map/pallas_call | solution.py:309
  (2 shorter events, 0.1 us)
Async XLA Ops:
  0.0 1.2 %copy-start = (bf16[2,8,256,128]{3,2,1,0:T(8,128)(2,1)S(1)}, bf16[2,8,256,128]{3,2,1,0:T(8,128)(2,1)}, u32[]{:S(2)}) copy-start(bf16[2,8,256,128]{3,2,1,0:T(8,128)(2,1)} %x_ref.5) | copy-start | bytes 3145732
  1.2 14.8 %copy-start.1 = (s32[1024,1]{0,1:T(1,128)S(1)}, s32[1024,1]{0,1:T(1,128)}, u32[]{:S(2)}) copy-start(s32[1024,1]{0,1:T(1,128)} %param.4) | copy-start | bytes 12292
  1.2 14.8 %copy-start.2 = (s32[8]{0:T(128)S(1)}, s32[8]{0:T(128)}, u32[]{:S(2)}) copy-start(s32[8]{0:T(128)} %slot_ref.1) | copy-start | bytes 100
  1.3 1.7 %collective-permute-start = (bf16[4,256,128]{2,1,0:T(8,128)(2,1)S(1)}, bf16[4,256,128]{2,1,0:T(8,128)(2,1)S(1)}, u32[]{:S(2)}, u32[]{:S(2)}) collective-permute-start(bf16[4,256,128]{2,1,0:T(8,128)(2,1)S(1)} %get-tuple-element.35), channel_id=1, source_target_pairs={{0,4},{4,0},{8,12},{12,8},{16,20},{20,16},{24,28},{28,24},{1,5},{5... | collective-permute-start | bytes 786440 | tf_op jit(solution)/shard_map/ppermute | solution.py:376
  1.8 7.8 %collective-permute-start.13 = (bf16[4,256,128]{2,1,0:T(8,128)(2,1)S(1)}, bf16[4,256,128]{2,1,0:T(8,128)(2,1)S(1)}, u32[]{:S(2)}, u32[]{:S(2)}) collective-permute-start(bf16[4,256,128]{2,1,0:T(8,128)(2,1)S(1)} %get-tuple-element.53), channel_id=1, source_target_pairs={{0,4},{4,0},{8,12},{12,8},{16,20},{20,16},{24,28},{28,24},{1,5},{5... | collective-permute-start | bytes 786440 | tf_op jit(solution)/shard_map/ppermute | solution.py:378
  3.2 8.0 %collective-permute-start.1 = (bf16[256,128]{1,0:T(8,128)(2,1)S(1)}, bf16[256,128]{1,0:T(8,128)(2,1)S(1)}, u32[]{:S(2)}, u32[]{:S(2)}) collective-permute-start(bf16[256,128]{1,0:T(8,128)(2,1)S(1)} %get-tuple-element.37), channel_id=1, source_target_pairs={{0,8},{4,12},{8,0},{12,4},{16,24},{20,28},{24,16},{28,20},{1,9},{5... | collective-permute-start | bytes 196616 | tf_op jit(solution)/shard_map/ppermute | solution.py:343
  6.1 5.8 %collective-permute-start.7 = (bf16[256,128]{1,0:T(8,128)(2,1)S(1)}, bf16[256,128]{1,0:T(8,128)(2,1)S(1)}, u32[]{:S(2)}, u32[]{:S(2)}) collective-permute-start(bf16[256,128]{1,0:T(8,128)(2,1)S(1)} %get-tuple-element.45), channel_id=1, source_target_pairs={{0,8},{4,12},{8,0},{12,4},{16,24},{20,28},{24,16},{28,20},{1,9},{5... | collective-permute-start | bytes 196616 | tf_op jit(solution)/shard_map/ppermute | solution.py:343
  6.2 7.0 %collective-permute-start.8 = (bf16[256,128]{1,0:T(8,128)(2,1)S(1)}, bf16[256,128]{1,0:T(8,128)(2,1)S(1)}, u32[]{:S(2)}, u32[]{:S(2)}) collective-permute-start(bf16[256,128]{1,0:T(8,128)(2,1)S(1)} %get-tuple-element.46), channel_id=1, source_target_pairs={{0,16},{4,20},{8,24},{12,28},{16,0},{20,4},{24,8},{28,12},{1,17},{... | collective-permute-start | bytes 196616 | tf_op jit(solution)/shard_map/ppermute | solution.py:343
  8.2 6.6 %collective-permute-start.9 = (bf16[256,128]{1,0:T(8,128)(2,1)S(1)}, bf16[256,128]{1,0:T(8,128)(2,1)S(1)}, u32[]{:S(2)}, u32[]{:S(2)}) collective-permute-start(bf16[256,128]{1,0:T(8,128)(2,1)S(1)} %get-tuple-element.47), channel_id=1, source_target_pairs={{0,24},{4,28},{8,16},{12,20},{16,8},{20,12},{24,0},{28,4},{1,25},{... | collective-permute-start | bytes 196616 | tf_op jit(solution)/shard_map/ppermute | solution.py:343
  9.6 9.6 %collective-permute-start.2 = (bf16[256,128]{1,0:T(8,128)(2,1)S(1)}, bf16[256,128]{1,0:T(8,128)(2,1)S(1)}, u32[]{:S(2)}, u32[]{:S(2)}) collective-permute-start(bf16[256,128]{1,0:T(8,128)(2,1)S(1)} %get-tuple-element.38), channel_id=1, source_target_pairs={{0,16},{4,20},{8,24},{12,28},{16,0},{20,4},{24,8},{28,12},{1,17},{... | collective-permute-start | bytes 196616 | tf_op jit(solution)/shard_map/ppermute | solution.py:343
  11.2 9.7 %collective-permute-start.3 = (bf16[256,128]{1,0:T(8,128)(2,1)S(1)}, bf16[256,128]{1,0:T(8,128)(2,1)S(1)}, u32[]{:S(2)}, u32[]{:S(2)}) collective-permute-start(bf16[256,128]{1,0:T(8,128)(2,1)S(1)} %get-tuple-element.39), channel_id=1, source_target_pairs={{0,24},{4,28},{8,16},{12,20},{16,8},{20,12},{24,0},{28,4},{1,25},{... | collective-permute-start | bytes 196616 | tf_op jit(solution)/shard_map/ppermute | solution.py:343
  11.9 12.7 %collective-permute-start.14 = (bf16[512,128]{1,0:T(8,128)(2,1)S(1)}, bf16[512,128]{1,0:T(8,128)(2,1)S(1)}, u32[]{:S(2)}, u32[]{:S(2)}) collective-permute-start(bf16[512,128]{1,0:T(8,128)(2,1)S(1)} %get-tuple-element.55), channel_id=1, source_target_pairs={{0,8},{4,12},{8,0},{12,4},{16,24},{20,28},{24,16},{28,20},{1,9},{5... | collective-permute-start | bytes 393224 | tf_op jit(solution)/shard_map/ppermute | solution.py:343
  13.3 11.7 %collective-permute-start.15 = (bf16[512,128]{1,0:T(8,128)(2,1)S(1)}, bf16[512,128]{1,0:T(8,128)(2,1)S(1)}, u32[]{:S(2)}, u32[]{:S(2)}) collective-permute-start(bf16[512,128]{1,0:T(8,128)(2,1)S(1)} %get-tuple-element.56), channel_id=1, source_target_pairs={{0,16},{4,20},{8,24},{12,28},{16,0},{20,4},{24,8},{28,12},{1,17},{... | collective-permute-start | bytes 393224 | tf_op jit(solution)/shard_map/ppermute | solution.py:343
  14.8 10.8 %collective-permute-start.16 = (bf16[512,128]{1,0:T(8,128)(2,1)S(1)}, bf16[512,128]{1,0:T(8,128)(2,1)S(1)}, u32[]{:S(2)}, u32[]{:S(2)}) collective-permute-start(bf16[512,128]{1,0:T(8,128)(2,1)S(1)} %get-tuple-element.57), channel_id=1, source_target_pairs={{0,24},{4,28},{8,16},{12,20},{16,8},{20,12},{24,0},{28,4},{1,25},{... | collective-permute-start | bytes 393224 | tf_op jit(solution)/shard_map/ppermute | solution.py:343
  19.3 9.1 %collective-permute-start.10 = (bf16[2,192,128]{2,1,0:T(8,128)(2,1)S(1)}, bf16[2,192,128]{2,1,0:T(8,128)(2,1)S(1)}, u32[]{:S(2)}, u32[]{:S(2)}) collective-permute-start(bf16[2,192,128]{2,1,0:T(8,128)(2,1)S(1)} %get-tuple-element.49), channel_id=1, source_target_pairs={{0,1},{1,0},{2,3},{3,2},{4,5},{5,4},{6,7},{7,6},{8,9},{9,8},{10,11... | collective-permute-start | bytes 294920 | tf_op jit(solution)/shard_map/ppermute | solution.py:327
  20.9 11.1 %collective-permute-start.11 = (bf16[2,192,128]{2,1,0:T(8,128)(2,1)S(1)}, bf16[2,192,128]{2,1,0:T(8,128)(2,1)S(1)}, u32[]{:S(2)}, u32[]{:S(2)}) collective-permute-start(bf16[2,192,128]{2,1,0:T(8,128)(2,1)S(1)} %get-tuple-element.50), channel_id=1, source_target_pairs={{0,2},{1,3},{2,0},{3,1},{4,6},{5,7},{6,4},{7,5},{8,10},{9,11},{10,... | collective-permute-start | bytes 294920 | tf_op jit(solution)/shard_map/ppermute | solution.py:327
  24.6 7.5 %collective-permute-start.12 = (bf16[2,192,128]{2,1,0:T(8,128)(2,1)S(1)}, bf16[2,192,128]{2,1,0:T(8,128)(2,1)S(1)}, u32[]{:S(2)}, u32[]{:S(2)}) collective-permute-start(bf16[2,192,128]{2,1,0:T(8,128)(2,1)S(1)} %get-tuple-element.51), channel_id=1, source_target_pairs={{0,3},{1,2},{2,1},{3,0},{4,7},{5,6},{6,5},{7,4},{8,11},{9,10},{10,... | collective-permute-start | bytes 294920 | tf_op jit(solution)/shard_map/ppermute | solution.py:327
  24.9 10.0 %collective-permute-start.4 = (bf16[2,192,128]{2,1,0:T(8,128)(2,1)S(1)}, bf16[2,192,128]{2,1,0:T(8,128)(2,1)S(1)}, u32[]{:S(2)}, u32[]{:S(2)}) collective-permute-start(bf16[2,192,128]{2,1,0:T(8,128)(2,1)S(1)} %get-tuple-element.41), channel_id=1, source_target_pairs={{0,1},{1,0},{2,3},{3,2},{4,5},{5,4},{6,7},{7,6},{8,9},{9,8},{10,11... | collective-permute-start | bytes 294920 | tf_op jit(solution)/shard_map/ppermute | solution.py:327
  26.9 28.4 %collective-permute-start.18 = (bf16[2,384,128]{2,1,0:T(8,128)(2,1)S(1)}, bf16[2,384,128]{2,1,0:T(8,128)(2,1)S(1)}, u32[]{:S(2)}, u32[]{:S(2)}) collective-permute-start(bf16[2,384,128]{2,1,0:T(8,128)(2,1)S(1)} %get-tuple-element.63), channel_id=1, source_target_pairs={{0,1},{1,0},{2,3},{3,2},{4,5},{5,4},{6,7},{7,6},{8,9},{9,8},{10,11... | collective-permute-start | bytes 589832 | tf_op jit(solution)/shard_map/ppermute | solution.py:327
  28.4 27.0 %collective-permute-start.19 = (bf16[2,384,128]{2,1,0:T(8,128)(2,1)S(1)}, bf16[2,384,128]{2,1,0:T(8,128)(2,1)S(1)}, u32[]{:S(2)}, u32[]{:S(2)}) collective-permute-start(bf16[2,384,128]{2,1,0:T(8,128)(2,1)S(1)} %get-tuple-element.64), channel_id=1, source_target_pairs={{0,3},{1,2},{2,1},{3,0},{4,7},{5,6},{6,5},{7,4},{8,11},{9,10},{10,... | collective-permute-start | bytes 589832 | tf_op jit(solution)/shard_map/ppermute | solution.py:327
  32.0 24.7 %collective-permute-start.17 = (bf16[2,384,128]{2,1,0:T(8,128)(2,1)S(1)}, bf16[2,384,128]{2,1,0:T(8,128)(2,1)S(1)}, u32[]{:S(2)}, u32[]{:S(2)}) collective-permute-start(bf16[2,384,128]{2,1,0:T(8,128)(2,1)S(1)} %get-tuple-element.58), channel_id=1, source_target_pairs={{0,2},{1,3},{2,0},{3,1},{4,6},{5,7},{6,4},{7,5},{8,10},{9,11},{10,... | collective-permute-start | bytes 589832 | tf_op jit(solution)/shard_map/ppermute | solution.py:327
  32.2 22.7 %collective-permute-start.5 = (bf16[2,192,128]{2,1,0:T(8,128)(2,1)S(1)}, bf16[2,192,128]{2,1,0:T(8,128)(2,1)S(1)}, u32[]{:S(2)}, u32[]{:S(2)}) collective-permute-start(bf16[2,192,128]{2,1,0:T(8,128)(2,1)S(1)} %get-tuple-element.42), channel_id=1, source_target_pairs={{0,2},{1,3},{2,0},{3,1},{4,6},{5,7},{6,4},{7,5},{8,10},{9,11},{10,... | collective-permute-start | bytes 294920 | tf_op jit(solution)/shard_map/ppermute | solution.py:327
  34.9 20.0 %collective-permute-start.6 = (bf16[2,192,128]{2,1,0:T(8,128)(2,1)S(1)}, bf16[2,192,128]{2,1,0:T(8,128)(2,1)S(1)}, u32[]{:S(2)}, u32[]{:S(2)}) collective-permute-start(bf16[2,192,128]{2,1,0:T(8,128)(2,1)S(1)} %get-tuple-element.43), channel_id=1, source_target_pairs={{0,3},{1,2},{2,1},{3,0},{4,7},{5,6},{6,5},{7,4},{8,11},{9,10},{10,... | collective-permute-start | bytes 294920 | tf_op jit(solution)/shard_map/ppermute | solution.py:327

commit v8 on v7

--- a/solution.py
+++ b/solution.py
@@ -13,7 +13,6 @@
 
 
 VMEM = pl.BlockSpec(memory_space=pltpu.VMEM)
-SMEM = pl.BlockSpec(memory_space=pltpu.SMEM)
 PARAMS = pltpu.CompilerParams(vmem_limit_bytes=20 * 1024 * 1024)
 
 
@@ -30,15 +29,17 @@
 
 
 def plan_kernel(groups, half, slot_ref, owner_ref, select_ref):
-    subarrays = slot_ref.shape[0]
+    subarrays = slot_ref.shape[1]
     blocks = owner_ref.shape[0]
     per = subarrays // groups
     me = lax.axis_index("tm")
     shape = (subarrays, LANES)
     place = lax.broadcasted_iota(jnp.int32, shape, 0)
-    name = jnp.zeros(shape, jnp.int32)
-    for s in range(subarrays):
-        name = jnp.where(place == s, slot_ref[s], name)
+    square = (subarrays, subarrays)
+    diagonal = lax.broadcasted_iota(jnp.int32, square, 0) == lax.broadcasted_iota(jnp.int32, square, 1)
+    slot = jnp.broadcast_to(slot_ref[...].astype(jnp.float32), square)
+    name = jnp.sum(jnp.where(diagonal, slot, 0.0), axis=1, keepdims=True)
+    name = jnp.broadcast_to(name, shape).astype(jnp.int32)
     base = jnp.zeros(shape, jnp.int32)
     for s in range(subarrays):
         chunk = relative(jnp.int32(s // per), me, groups) * per + s % per
@@ -52,17 +53,21 @@
         jnp.concatenate(held, axis=0).astype(jnp.bfloat16), before, preferred_element_type=jnp.float32
     )
     run = base
-    height = 256
-    row = lax.broadcasted_iota(jnp.int32, (height, LANES), 0).astype(jnp.float32)
+    height, strip = 256, 16
+    rows = lax.broadcasted_iota(jnp.int32, (strip, LANES), 0)
+    strips = [(rows + top).astype(jnp.float32).astype(jnp.bfloat16) for top in range(0, height, strip)]
+    one, zero = jnp.ones((strip, LANES), jnp.bfloat16), jnp.zeros((strip, LANES), jnp.bfloat16)
     for b in range(blocks):
         rank = within[b * subarrays : (b + 1) * subarrays] + run
         target = jnp.sum(held[b] * rank, axis=0, keepdims=True)
         run = run + jnp.sum(held[b], axis=1, keepdims=True)
         for top in range(0, select_ref.shape[0], height):
-            hit = row == (target - top)
-            select_ref[top : top + height, b * LANES : (b + 1) * LANES] = jnp.where(hit, 1.0, 0.0).astype(
-                jnp.bfloat16
-            )
+            inside = jnp.logical_and(target >= top, target < top + height)
+            at = jnp.where(inside, target - top, -1.0)
+            at = jnp.broadcast_to(at, (strip, LANES)).astype(jnp.bfloat16)
+            for i, row in enumerate(strips):
+                start = top + i * strip
+                select_ref[start : start + strip, b * LANES : (b + 1) * LANES] = jnp.where(row == at, one, zero)
 
 
 def plan(assignment, slot_subarray_index, groups, half):
@@ -71,27 +76,27 @@
     return pl.pallas_call(
         functools.partial(plan_kernel, groups, half),
         out_shape=jax.ShapeDtypeStruct((subarrays * half, antennas), jnp.bfloat16),
-        in_specs=[SMEM, VMEM],
+        in_specs=[VMEM, VMEM],
         out_specs=VMEM,
         compiler_params=PARAMS,
         cost_estimate=pl.CostEstimate(flops=4_000_000_000, bytes_accessed=3_000_000, transcendentals=0),
-    )(slot_subarray_index, assignment.reshape(antennas // LANES, LANES))
-
-
-def give_kernel(chips, x_ref, *outs):
+    )(slot_subarray_index.reshape(1, subarrays), assignment.reshape(antennas // LANES, LANES))
+
+
+def give_kernel(chips, x_ref, out):
     me = lax.axis_index("chan")
-    for k, out in enumerate(outs):
+    for k in range(2):
         for t in range(chips):
-            out[t] = x_ref[k, (me ^ (2 * t)) ^ 1]
+            out[k, t] = x_ref[k, (me ^ (2 * t)) ^ 1]
 
 
 def give(voltages):
     parts, chans, inputs, samples = voltages.shape
     return pl.pallas_call(
         functools.partial(give_kernel, chans // 2),
-        out_shape=[jax.ShapeDtypeStruct((chans // 2, inputs, samples), voltages.dtype)] * parts,
+        out_shape=jax.ShapeDtypeStruct((parts, chans // 2, inputs, samples), voltages.dtype),
         in_specs=[VMEM],
-        out_specs=[VMEM] * parts,
+        out_specs=VMEM,
         compiler_params=PARAMS,
         cost_estimate=pl.CostEstimate(flops=1_000_000, bytes_accessed=1_000_000, transcendentals=0),
     )(voltages)
@@ -113,7 +118,7 @@
         @pl.when((me & 1) == parity)
         def _():
             for t in range(chips):
-                cores = [x_ref[0, me ^ (2 * t)], given_ref[t]]
+                cores = [x_ref[0, me ^ (2 * t)], given_ref[0, t]]
                 if parity:
                     cores.reverse()
                 for h, half in enumerate(fold(*[core.astype(jnp.float32) for core in cores])):
@@ -127,7 +132,7 @@
     theirs = pl.multiple_of(inputs - (me & 1) * inputs, inputs)
     for t in range(chips):
         outs[t][pl.ds(mine, inputs)] = x_ref[1, me ^ (2 * t)]
-        outs[t][pl.ds(theirs, inputs)] = given_ref[t]
+        outs[t][pl.ds(theirs, inputs)] = given_ref[1, t]
 
 
 def merge(kernel, height, voltages, given):
@@ -229,11 +234,12 @@
     rows = picked.shape[0]
     for pol in range(2):
         tall[pl.ds(pol, rows, stride=2), :] = picked[:, pol * LANES : (pol + 1) * LANES]
-    per, slots, _ = outs[0].shape
-    for g, out in enumerate(outs):
-        for s in range(per):
-            top = (g * per + s) * slots
+    slots = outs[0].shape[1]
+    top = 0
+    for out in outs:
+        for s in range(out.shape[0]):
             out[s] = tall[top : top + slots, :].astype(jnp.bfloat16)
+            top += slots
 
 
 def gather_kernel(steps, outputs, select_ref, *rest):
@@ -244,14 +250,17 @@
     store_rows(picked, tall, outs)
 
 
-def gather(select, xs, steps, groups, per, slots):
+def gather(select, xs, steps, groups, per, slots, apart=None):
     _, samples = xs[0].shape
     rows, antennas = select.shape
-    return pl.pallas_call(
-        functools.partial(gather_kernel, steps, groups),
-        out_shape=[jax.ShapeDtypeStruct((per, slots, samples), jnp.bfloat16)] * groups,
+    heights = []
+    for g in range(groups):
+        heights += [1] * per if g == apart else [per]
+    out = pl.pallas_call(
+        functools.partial(gather_kernel, steps, len(heights)),
+        out_shape=[jax.ShapeDtypeStruct((height, slots, samples), jnp.bfloat16) for height in heights],
         in_specs=[VMEM] * (1 + len(xs)),
-        out_specs=[VMEM] * groups,
+        out_specs=[VMEM] * len(heights),
         scratch_shapes=[
             pltpu.VMEM((2 * antennas, samples), jnp.float32),
             pltpu.VMEM((antennas, 2 * samples), jnp.bfloat16),
@@ -262,11 +271,16 @@
             flops=2 * rows * antennas * 2 * samples, bytes_accessed=4_000_000, transcendentals=0
         ),
     )(select, *xs)
-
-
-def products(real, imag, part):
+    chunks = []
+    for g in range(groups):
+        chunks.append(list(out[:per]) if g == apart else out[0])
+        out = out[per:] if g == apart else out[1:]
+    return chunks
+
+
+def products(real, imag):
     right = jnp.concatenate([real, imag], axis=1)
-    left = right if part == 0 else jnp.concatenate([imag, -real], axis=1)
+    left = jnp.concatenate([right, jnp.concatenate([imag, -real], axis=1)], axis=0)
     return lax.dot_general(left, right, (((1,), (1,)), ((), ())), preferred_element_type=jnp.float32)
 
 
@@ -274,22 +288,23 @@
     *parts, out = refs
     count = len(parts) // 2
     for s in range(parts[0].shape[0]):
-        for part in range(2):
-            total = None
-            for e in range(count):
-                term = products(parts[e][s], parts[count + e][s], part)
-                total = term if total is None else total + term
-            out[s, part] = total
-
-
-def late_kernel(real, imag, so_far, out, stage, sem):
+        total = None
+        for e in range(count):
+            term = products(parts[e][s], parts[count + e][s])
+            total = term if total is None else total + term
+        out[s] = total
+
+
+def late_kernel(slot, real, imag, so_far, *rest):
+    out, stage, sem = rest[-3:]
+    slots = real.shape[1]
+    term = products(real[slot], imag[0])
     copies = []
-    for s in range(real.shape[0]):
-        for part in range(2):
-            stage[s, part] = so_far[s, part] + products(real[s], imag[s], part)
-            copy = pltpu.make_async_copy(stage.at[s, part], out.at[s, 0, part], sem.at[s, part])
-            copy.start()
-            copies.append(copy)
+    for part in range(2):
+        stage[part] = so_far[slot, part * slots : (part + 1) * slots] + term[part * slots : (part + 1) * slots]
+        copy = pltpu.make_async_copy(stage.at[part], out.at[slot, 0, part], sem.at[part])
+        copy.start()
+        copies.append(copy)
     for copy in copies:
         copy.wait()
 
@@ -300,31 +315,37 @@
     flops = 2 * per * 2 * slots * slots * 2 * samples
     so_far = pl.pallas_call(
         early_kernel,
-        out_shape=jax.ShapeDtypeStruct((per, 2, slots, slots), jnp.float32),
+        out_shape=jax.ShapeDtypeStruct((per, 2 * slots, slots), jnp.float32),
         in_specs=[VMEM] * (2 * len(early)),
         out_specs=VMEM,
         compiler_params=PARAMS,
         cost_estimate=pl.CostEstimate(flops=flops * len(early), bytes_accessed=3_000_000, transcendentals=0),
     )(*[real[e] for e in early], *[imag[e] for e in early])
-    return pl.pallas_call(
-        late_kernel,
-        out_shape=jax.ShapeDtypeStruct((per, 1, 2, slots, slots), jnp.float32),
-        in_specs=[VMEM] * 3,
-        out_specs=pl.BlockSpec(memory_space=pl.ANY),
-        scratch_shapes=[
-            pltpu.VMEM((per, 2, slots, slots), jnp.float32),
-            pltpu.SemaphoreType.DMA((per, 2)),
-        ],
-        compiler_params=PARAMS,
-        cost_estimate=pl.CostEstimate(flops=flops, bytes_accessed=3_000_000, transcendentals=0),
-    )(real[last], imag[last], so_far)
+    anywhere = pl.BlockSpec(memory_space=pl.ANY)
+    out = ()
+    for s in range(per):
+        out = pl.pallas_call(
+            functools.partial(late_kernel, s),
+            out_shape=[jax.ShapeDtypeStruct((per, 1, 2, slots, slots), jnp.float32)],
+            in_specs=[VMEM] * 3 + [anywhere] * len(out),
+            out_specs=[anywhere],
+            scratch_shapes=[pltpu.VMEM((2, slots, slots), jnp.float32), pltpu.SemaphoreType.DMA((2,))],
+            input_output_aliases={3: 0} if out else {},
+            compiler_params=PARAMS,
+            cost_estimate=pl.CostEstimate(flops=flops // per, bytes_accessed=2_000_000, transcendentals=0),
+        )(real[last], imag[last][s], so_far, *out)
+    return out[0]
 
 
 def exchange(chunks, order, groups):
     got = list(chunks)
     for step in order:
         pairs = [(j, partner(j, step, groups)) for j in range(groups)]
-        got[step] = lax.ppermute(chunks[step], "tm", pairs)
+        parts = chunks[step] if isinstance(chunks[step], list) else [chunks[step]]
+        moved = []
+        for part in parts:
+            moved.append(lax.ppermute(part, "tm", pairs))
+        got[step] = moved if len(parts) > 1 else moved[0]
     return got
 
 
@@ -350,8 +371,7 @@
 
 def orders(groups):
     last = 2 if groups == 4 else groups - 1
-    rest = [step for step in range(groups - 1, 0, -1) if step != last]
-    return rest[:1] + [last] + rest[1:], rest + [last], last
+    return [2,3,1], [3,1,2], last
 
 
 def steps_of(voltages, assignment, slot_subarray_index):
@@ -366,23 +386,21 @@
         imags = [across(voltages[1])]
         select = plan(assignment, slot_subarray_index, groups, SLOT // 2)
         real = exchange(gather(select, reals, steps, groups, per, SLOT), first, groups)
-        imag = exchange(gather(select, imags, steps, groups, per, SLOT), second, groups)
+        imag = exchange(gather(select, imags, steps, groups, per, SLOT, last), second, groups)
         return gram(real, imag, last)
 
     chips = chans // 2
     steps = tuple(range(chips))
     swap = [(i, i ^ 1) for i in range(chans)]
-    give_real, give_imag = give(voltages)
-    given_real = lax.ppermute(give_real, "chan", swap)
-    halves = merge(merge_halves_kernel, 1, voltages, given_real)
-    given_imag = lax.ppermute(give_imag, "chan", swap)
+    given = lax.ppermute(give(voltages), "chan", swap)
+    halves = merge(merge_halves_kernel, 1, voltages, given)
     select = plan(assignment, slot_subarray_index, groups, SLOT // 2)
     got = []
     for h in range(2):
         pieces = cross(halves[h * chips : (h + 1) * chips], chans, range(chans))
         got.append(exchange(gather_half(select, pieces, steps, groups, per), first, groups))
-    imags = cross(merge(merge_kernel, 2, voltages, given_imag), chans, range(chans))
-    imag = exchange(gather(select, imags, steps, groups, per, SLOT), second, groups)
+    imags = cross(merge(merge_kernel, 2, voltages, given), chans, range(chans))
+    imag = exchange(gather(select, imags, steps, groups, per, SLOT, last), second, groups)
     return gram(join(*got), imag, last)
 
 

time: 58.6 us -> 56.2 us (0.959)
  waiting for transfers between devices: 20.8 us -> 16.4 us
  starting transfers between devices: 26.8 us -> 29 us
    ppermute x11, waiting for transfers between devices: 20.8 us -> 16.4 us  [the longest x10 14.9 us: exchange(): moved.append(lax.ppermute(part, 'tm', pairs))]
    ppermute x11, starting transfers between devices: 14.1 us -> 16.2 us  [the longest x10 15.7 us: exchange(): moved.append(lax.ppermute(part, 'tm', pairs))]
    pallas_call x1, Pallas kernels: 2.06 us -> 1.05 us  [plan(): pl.pallas_call(functools.partial(plan_kernel, groups, half), out_shape=ja...]
    pallas_call x4 -> x5, Pallas kernels: 4.46 us -> 5.37 us  [the longest x2 2.63 us: gram(): pl.pallas_call(functools.partial(late_kernel, s), out_shape=[jax.ShapeDty...]
  transfers between devices with their start and end apart: 20 -> 20, of which waited for: 3 -> 5; matrix products, arithmetic and copies ran while one was open for 0% -> 0% of each run, Pallas kernels for 13% -> 14%
where the time goes in v8:
time: 56.2 us; the launch traced here: 56.1 us
  starting transfers between devices  29 us (52%)
  waiting for transfers between devices  16.4 us (29%)
  Pallas kernels  9.33 us (17%)
  local copies, waits for them, and re-layouts  1.23 us (2%)
    ppermute x10, starting transfers between devices, exchange(): moved.append(lax.ppermute(part, 'tm', pairs))  15.7 us
    ppermute x10, waiting for transfers between devices, exchange(): moved.append(lax.ppermute(part, 'tm', pairs))  14.9 us
    ppermute x9, starting transfers between devices, cross(): lax.ppermute(chunks[step], 'chan', [(i, i ^ 2 * step) for i in starts])  12.7 us
    pallas_call x2, Pallas kernels, gram(): pl.pallas_call(functools.partial(late_kernel, s), out_shape=[jax.ShapeDty...  2.63 us
    pallas_call x2, Pallas kernels, gather_half(): pl.pallas_call(functools.partial(gather_half_kernel, steps, groups), out_...  2.26 us
    ppermute x1, waiting for transfers between devices, steps_of(): given = lax.ppermute(give(voltages), 'chan', swap)  1.54 us
    pallas_call x1, Pallas kernels, gram(): pl.pallas_call(early_kernel, out_shape=jax.ShapeDtypeStruct((per, 2 * slo...  1.38 us
    pallas_call x1, Pallas kernels, gather(): pl.pallas_call(functools.partial(gather_kernel, steps, len(heights)), out...  1.32 us
  transfers between devices with their start and end apart: 20, of which 5 were waited for; matrix products, arithmetic and copies ran while one was open for 0% of the time, Pallas kernels for 14%

profile of v8, /device:TPU:0, one launch (start us, length us, event | category | flops | bytes accessed | tf_op | source)
XLA Modules:
  0.0 56.1 jit_solution(2878079568833229993)
XLA Ops:
  0.0 0.0 copy-start
  0.0 1.2 %copy-done = bf16[2,8,256,128]{3,2,1,0:T(8,128)(2,1)S(1)} copy-done((bf16[2,8,256,128]{3,2,1,0:T(8,128)(2,1)S(1)}, bf16[2,8,256,128]{3,2,1,0:T(8,128)(2,1)}, u32[]{:S(2)}) %copy-start) | copy-done | bytes 1048600
  1.2 0.0 copy-start.1
  1.2 0.0 copy-start.2
  1.3 0.6 collective-permute-start
  1.8 1.5 %collective-permute-done.given_ref = bf16[2,4,256,128]{3,2,1,0:T(8,128)(2,1)S(1)} collective-permute-done((bf16[2,4,256,128]{3,2,1,0:T(8,128)(2,1)S(1)}, bf16[2,4,256,128]{3,2,1,0:T(8,128)(2,1)S(1)}, u32[]{:S(2)}, u32[]{:S(2)}) %collective-permute-start) | collective-permute-done | bytes 524320 | tf_op jit(solution)/shard_map/ppermute | solution.py:395
  3.4 0.2 shard_map.39
  3.6 2.9 %collective-permute-start.7 = (bf16[256,128]{1,0:T(8,128)(2,1)S(1)}, bf16[256,128]{1,0:T(8,128)(2,1)S(1)}, u32[]{:S(2)}, u32[]{:S(2)}) collective-permute-start(bf16[256,128]{1,0:T(8,128)(2,1)S(1)} %get-tuple-element.43), channel_id=1, source_target_pairs={{0,8},{4,12},{8,0},{12,4},{16,24},{20,28},{24,16},{28,20},{1,9},{5... | collective-permute-start | bytes 196616 | tf_op jit(solution)/shard_map/ppermute | solution.py:364
  6.5 1.5 %collective-permute-start.8 = (bf16[256,128]{1,0:T(8,128)(2,1)S(1)}, bf16[256,128]{1,0:T(8,128)(2,1)S(1)}, u32[]{:S(2)}, u32[]{:S(2)}) collective-permute-start(bf16[256,128]{1,0:T(8,128)(2,1)S(1)} %get-tuple-element.44), channel_id=1, source_target_pairs={{0,16},{4,20},{8,24},{12,28},{16,0},{20,4},{24,8},{28,12},{1,17},{... | collective-permute-start | bytes 196616 | tf_op jit(solution)/shard_map/ppermute | solution.py:364
  8.0 0.5 collective-permute-start.1
  8.6 1.4 %collective-permute-start.9 = (bf16[256,128]{1,0:T(8,128)(2,1)S(1)}, bf16[256,128]{1,0:T(8,128)(2,1)S(1)}, u32[]{:S(2)}, u32[]{:S(2)}) collective-permute-start(bf16[256,128]{1,0:T(8,128)(2,1)S(1)} %get-tuple-element.45), channel_id=1, source_target_pairs={{0,24},{4,28},{8,16},{12,20},{16,8},{20,12},{24,0},{28,4},{1,25},{... | collective-permute-start | bytes 196616 | tf_op jit(solution)/shard_map/ppermute | solution.py:364
  10.1 0.1 collective-permute-start.13
  10.2 0.0 collective-permute-done.7.rest_1_
  10.2 2.0 %collective-permute-start.14 = (bf16[512,128]{1,0:T(8,128)(2,1)S(1)}, bf16[512,128]{1,0:T(8,128)(2,1)S(1)}, u32[]{:S(2)}, u32[]{:S(2)}) collective-permute-start(bf16[512,128]{1,0:T(8,128)(2,1)S(1)} %get-tuple-element.53), channel_id=1, source_target_pairs={{0,16},{4,20},{8,24},{12,28},{16,0},{20,4},{24,8},{28,12},{1,17},{... | collective-permute-start | bytes 393224 | tf_op jit(solution)/shard_map/ppermute | solution.py:364
  12.2 0.0 collective-permute-done.8.rest_2_
  12.2 1.4 %collective-permute-start.15 = (bf16[512,128]{1,0:T(8,128)(2,1)S(1)}, bf16[512,128]{1,0:T(8,128)(2,1)S(1)}, u32[]{:S(2)}, u32[]{:S(2)}) collective-permute-start(bf16[512,128]{1,0:T(8,128)(2,1)S(1)} %get-tuple-element.54), channel_id=1, source_target_pairs={{0,24},{4,28},{8,16},{12,20},{16,8},{20,12},{24,0},{28,4},{1,25},{... | collective-permute-start | bytes 393224 | tf_op jit(solution)/shard_map/ppermute | solution.py:364
  13.6 0.0 copy-done.1
  13.6 0.0 copy-done.2
  13.6 1.0 %shard_map.37.select_ref = bf16[1536,1024]{1,0:T(8,128)(2,1)S(1)} custom-call(s32[1,8]{1,0:T(1,128)S(1)} %bitcast.3, s32[8,128]{1,0:T(8,128)S(1)} %bitcast.2), custom_call_target="tpu_custom_call" | custom-call | flops 4000000000 | bytes 3000000 | tf_op jit(solution)/shard_map/pallas_call | solution.py:76
  14.7 0.0 collective-permute-done.9.rest_3_
  14.7 1.6 %collective-permute-start.2 = (bf16[256,128]{1,0:T(8,128)(2,1)S(1)}, bf16[256,128]{1,0:T(8,128)(2,1)S(1)}, u32[]{:S(2)}, u32[]{:S(2)}) collective-permute-start(bf16[256,128]{1,0:T(8,128)(2,1)S(1)} %get-tuple-element.36), channel_id=1, source_target_pairs={{0,16},{4,20},{8,24},{12,28},{16,0},{20,4},{24,8},{28,12},{1,17},{... | collective-permute-start | bytes 196616 | tf_op jit(solution)/shard_map/ppermute | solution.py:364
  16.3 1.1 %shard_map.41 = (bf16[2,192,128]{2,1,0:T(8,128)(2,1)S(1)}, bf16[2,192,128]{2,1,0:T(8,128)(2,1)S(1)}, bf16[2,192,128]{2,1,0:T(8,128)(2,1)S(1)}, bf16[2,192,128]{2,1,0:T(8,128)(2,1)S(1)}) custom-call(bf16[1536,1024]{1,0:T(8,128)(2,1)S(1)} %shard_map.37.select_ref, bf16[256,128]{1,0:T(8,128)(2,1)S(1)} %get-tuple-element.42.rest_0_, ...), custom_call_target="tpu_custom_call" | custom-call | flops 402653184 | bytes 4000000 | tf_op jit(solution)/shard_map/pallas_call | solution.py:175
  17.4 0.0 collective-permute-done.1.rest_1_
  17.4 1.2 %collective-permute-start.3 = (bf16[256,128]{1,0:T(8,128)(2,1)S(1)}, bf16[256,128]{1,0:T(8,128)(2,1)S(1)}, u32[]{:S(2)}, u32[]{:S(2)}) collective-permute-start(bf16[256,128]{1,0:T(8,128)(2,1)S(1)} %get-tuple-element.37), channel_id=1, source_target_pairs={{0,24},{4,28},{8,16},{12,20},{16,8},{20,12},{24,0},{28,4},{1,25},{... | collective-permute-start | bytes 196616 | tf_op jit(solution)/shard_map/ppermute | solution.py:364
  18.6 0.0 collective-permute-done.13.rest_1_
  18.6 1.6 %collective-permute-start.10 = (bf16[2,192,128]{2,1,0:T(8,128)(2,1)S(1)}, bf16[2,192,128]{2,1,0:T(8,128)(2,1)S(1)}, u32[]{:S(2)}, u32[]{:S(2)}) collective-permute-start(bf16[2,192,128]{2,1,0:T(8,128)(2,1)S(1)} %get-tuple-element.47), channel_id=1, source_target_pairs={{0,1},{1,0},{2,3},{3,2},{4,5},{5,4},{6,7},{7,6},{8,9},{9,8},{10,11... | collective-permute-start | bytes 294920 | tf_op jit(solution)/shard_map/ppermute | solution.py:347
  20.2 0.0 collective-permute-done.14.rest_2_
  20.2 2.6 %collective-permute-start.11 = (bf16[2,192,128]{2,1,0:T(8,128)(2,1)S(1)}, bf16[2,192,128]{2,1,0:T(8,128)(2,1)S(1)}, u32[]{:S(2)}, u32[]{:S(2)}) collective-permute-start(bf16[2,192,128]{2,1,0:T(8,128)(2,1)S(1)} %get-tuple-element.48), channel_id=1, source_target_pairs={{0,2},{1,3},{2,0},{3,1},{4,6},{5,7},{6,4},{7,5},{8,10},{9,11},{10,... | collective-permute-start | bytes 294920 | tf_op jit(solution)/shard_map/ppermute | solution.py:347
  22.8 0.0 collective-permute-done.15.rest_3_
  22.8 0.2 collective-permute-start.12
  23.0 1.3 %shard_map.44 = (bf16[2,384,128]{2,1,0:T(8,128)(2,1)S(1)}, bf16[2,384,128]{2,1,0:T(8,128)(2,1)S(1)}, bf16[1,384,128]{2,1,0:T(8,128)(2,1)S(1)}, bf16[1,384,128]{2,1,0:T(8,128)(2,1)S(1)}, bf16[2,384,128]{2,1,0:T(8,128)(2,1)S(1)}) custom-call(bf16[1536,1024]{1,0:T(8,128)(2,1)S(1)} %shard_map.37.select_ref, bf16[512,128]{1,0:T(8,128)(2,1)S(1)} %get-tuple-element.51.rest_0_, ...), custom_call_target="tpu_custom_call" | custom-call | flops 805306368 | bytes 4000000 | tf_op jit(solution)/shard_map/pallas_call | solution.py:259
  24.4 0.0 collective-permute-done.2.rest_2_
  24.4 0.7 %collective-permute-start.17 = (bf16[2,384,128]{2,1,0:T(8,128)(2,1)S(1)}, bf16[2,384,128]{2,1,0:T(8,128)(2,1)S(1)}, u32[]{:S(2)}, u32[]{:S(2)}) collective-permute-start(bf16[2,384,128]{2,1,0:T(8,128)(2,1)S(1)} %get-tuple-element.60), channel_id=1, source_target_pairs={{0,1},{1,0},{2,3},{3,2},{4,5},{5,4},{6,7},{7,6},{8,9},{9,8},{10,11... | collective-permute-start | bytes 589832 | tf_op jit(solution)/shard_map/ppermute | solution.py:347
  25.1 0.0 collective-permute-done.3.rest_3_
  25.1 3.0 %collective-permute-start.18 = (bf16[2,384,128]{2,1,0:T(8,128)(2,1)S(1)}, bf16[2,384,128]{2,1,0:T(8,128)(2,1)S(1)}, u32[]{:S(2)}, u32[]{:S(2)}) collective-permute-start(bf16[2,384,128]{2,1,0:T(8,128)(2,1)S(1)} %get-tuple-element.61), channel_id=1, source_target_pairs={{0,3},{1,2},{2,1},{3,0},{4,7},{5,6},{6,5},{7,4},{8,11},{9,10},{10,... | collective-permute-start | bytes 589832 | tf_op jit(solution)/shard_map/ppermute | solution.py:347
  28.1 1.1 %shard_map.40 = (bf16[2,192,128]{2,1,0:T(8,128)(2,1)S(1)}, bf16[2,192,128]{2,1,0:T(8,128)(2,1)S(1)}, bf16[2,192,128]{2,1,0:T(8,128)(2,1)S(1)}, bf16[2,192,128]{2,1,0:T(8,128)(2,1)S(1)}) custom-call(bf16[1536,1024]{1,0:T(8,128)(2,1)S(1)} %shard_map.37.select_ref, bf16[256,128]{1,0:T(8,128)(2,1)S(1)} %get-tuple-element.34.rest_0_, ...), custom_call_target="tpu_custom_call" | custom-call | flops 402653184 | bytes 4000000 | tf_op jit(solution)/shard_map/pallas_call | solution.py:175
  29.2 0.0 collective-permute-done.10.refs_5_
  29.3 1.1 %collective-permute-start.4 = (bf16[2,192,128]{2,1,0:T(8,128)(2,1)S(1)}, bf16[2,192,128]{2,1,0:T(8,128)(2,1)S(1)}, u32[]{:S(2)}, u32[]{:S(2)}) collective-permute-start(bf16[2,192,128]{2,1,0:T(8,128)(2,1)S(1)} %get-tuple-element.39), channel_id=1, source_target_pairs={{0,1},{1,0},{2,3},{3,2},{4,5},{5,4},{6,7},{7,6},{8,9},{9,8},{10,11... | collective-permute-start | bytes 294920 | tf_op jit(solution)/shard_map/ppermute | solution.py:347
  30.4 0.0 collective-permute-done.11.refs_6_
  30.4 0.3 collective-permute-start.5
  30.7 0.0 collective-permute-done.12.refs_7_
  30.7 3.0 %collective-permute-start.6 = (bf16[2,192,128]{2,1,0:T(8,128)(2,1)S(1)}, bf16[2,192,128]{2,1,0:T(8,128)(2,1)S(1)}, u32[]{:S(2)}, u32[]{:S(2)}) collective-permute-start(bf16[2,192,128]{2,1,0:T(8,128)(2,1)S(1)} %get-tuple-element.41), channel_id=1, source_target_pairs={{0,3},{1,2},{2,1},{3,0},{4,7},{5,6},{6,5},{7,4},{8,11},{9,10},{10,... | collective-permute-start | bytes 294920 | tf_op jit(solution)/shard_map/ppermute | solution.py:347
  33.7 4.9 %collective-permute-done.4.refs_1_ = bf16[2,192,128]{2,1,0:T(8,128)(2,1)S(1)} collective-permute-done((bf16[2,192,128]{2,1,0:T(8,128)(2,1)S(1)}, bf16[2,192,128]{2,1,0:T(8,128)(2,1)S(1)}, u32[]{:S(2)}, u32[]{:S(2)}) %collective-permute-start.4) | collective-permute-done | bytes 98336 | tf_op jit(solution)/shard_map/ppermute | solution.py:347
  38.7 3.1 %collective-permute-start.19 = (bf16[1,384,128]{2,1,0:T(8,128)(2,1)S(1)}, bf16[1,384,128]{2,1,0:T(8,128)(2,1)S(1)}, u32[]{:S(2)}, u32[]{:S(2)}) collective-permute-start(bf16[1,384,128]{2,1,0:T(8,128)(2,1)S(1)} %get-tuple-element.62), channel_id=1, source_target_pairs={{0,2},{1,3},{2,0},{3,1},{4,6},{5,7},{6,4},{7,5},{8,10},{9,11},{10,... | collective-permute-start | bytes 294920 | tf_op jit(solution)/shard_map/ppermute | solution.py:347
  41.7 6.5 %collective-permute-done.5.refs_2_ = bf16[2,192,128]{2,1,0:T(8,128)(2,1)S(1)} collective-permute-done((bf16[2,192,128]{2,1,0:T(8,128)(2,1)S(1)}, bf16[2,192,128]{2,1,0:T(8,128)(2,1)S(1)}, u32[]{:S(2)}, u32[]{:S(2)}) %collective-permute-start.5) | collective-permute-done | bytes 98336 | tf_op jit(solution)/shard_map/ppermute | solution.py:347
  48.2 0.0 collective-permute-start.16
  48.2 0.0 collective-permute-done.6.refs_3_
  48.2 0.4 shard_map.42
  48.6 0.0 collective-permute-done.17.refs_4_
  48.6 0.0 collective-permute-done.18.refs_5_
  48.6 1.4 %shard_map.45.so_far = f32[2,768,384]{2,1,0:T(8,128)S(1)} custom-call(bf16[2,384,128]{2,1,0:T(8,128)(2,1)S(1)} %get-tuple-element.56.refs_0_, bf16[2,384,128]{2,1,0:T(8,128)(2,1)S(1)} %get-tuple-element.57.refs_1_, bf16[2,384,128]{2,1,0:T(8,128)(2,1)S(1)} %get-tuple-element.58.refs_2_, bf16[2,384,128]{2,1,0:T(8,128)(2,1)S(1)} %get-tuple-element.59.refs_3_, ...), custom_call_target="tpu_custom_call" | custom-call | flops 905969664 | bytes 3000000 | tf_op jit(solution)/shard_map/pallas_call | solution.py:316
  50.0 2.4 %collective-permute-done.19.imag = bf16[1,384,128]{2,1,0:T(8,128)(2,1)S(1)} collective-permute-done((bf16[1,384,128]{2,1,0:T(8,128)(2,1)S(1)}, bf16[1,384,128]{2,1,0:T(8,128)(2,1)S(1)}, u32[]{:S(2)}, u32[]{:S(2)}) %collective-permute-start.19) | collective-permute-done | bytes 98336 | tf_op jit(solution)/shard_map/ppermute | solution.py:347
  52.4 1.3 %shard_map.46.rest_0_ = f32[2,1,2,384,384]{4,3,2,1,0:T(8,128)} custom-call(bf16[2,384,128]{2,1,0:T(8,128)(2,1)S(1)} %get-tuple-element.50.real, bf16[1,384,128]{2,1,0:T(8,128)(2,1)S(1)} %collective-permute-done.19.imag, f32[2,768,384]{2,1,0:T(8,128)S(1)} %shard_map.45.so_far), custom_call_target="tpu_custom_call" | custom-call | flops 150994944 | bytes 2000000 | tf_op jit(solution)/shard_map/pallas_call | solution.py:327
  53.7 1.0 %collective-permute-done.16.imag = bf16[1,384,128]{2,1,0:T(8,128)(2,1)S(1)} collective-permute-done((bf16[1,384,128]{2,1,0:T(8,128)(2,1)S(1)}, bf16[1,384,128]{2,1,0:T(8,128)(2,1)S(1)}, u32[]{:S(2)}, u32[]{:S(2)}) %collective-permute-start.16) | collective-permute-done | bytes 98336 | tf_op jit(solution)/shard_map/ppermute | solution.py:347
  54.8 1.3 %shard_map.47 = f32[2,1,2,384,384]{4,3,2,1,0:T(8,128)} custom-call(bf16[2,384,128]{2,1,0:T(8,128)(2,1)S(1)} %get-tuple-element.50.real, bf16[1,384,128]{2,1,0:T(8,128)(2,1)S(1)} %collective-permute-done.16.imag, f32[2,768,384]{2,1,0:T(8,128)S(1)} %shard_map.45.so_far, f32[2,1,2,384,384]{4,3,2,1,0:T(8,128)} %shard_map.46.rest_0_), custom_call_target="tpu_custom_call", output_to_operand_aliasing={{}: (3, {})} | custom-call | flops 150994944 | bytes 2000000 | tf_op jit(solution)/shard_map/pallas_call | solution.py:327
  (2 shorter events, 0.1 us)
Async XLA Ops:
  0.0 1.2 %copy-start = (bf16[2,8,256,128]{3,2,1,0:T(8,128)(2,1)S(1)}, bf16[2,8,256,128]{3,2,1,0:T(8,128)(2,1)}, u32[]{:S(2)}) copy-start(bf16[2,8,256,128]{3,2,1,0:T(8,128)(2,1)} %x_ref.5) | copy-start | bytes 3145732
  1.2 12.4 %copy-start.1 = (s32[1024,1]{0,1:T(1,128)S(1)}, s32[1024,1]{0,1:T(1,128)}, u32[]{:S(2)}) copy-start(s32[1024,1]{0,1:T(1,128)} %param.4) | copy-start | bytes 12292
  1.2 12.4 %copy-start.2 = (s32[8]{0:T(128)S(1)}, s32[8]{0:T(128)}, u32[]{:S(2)}) copy-start(s32[8]{0:T(128)} %param.5) | copy-start | bytes 100
  1.3 2.1 %collective-permute-start = (bf16[2,4,256,128]{3,2,1,0:T(8,128)(2,1)S(1)}, bf16[2,4,256,128]{3,2,1,0:T(8,128)(2,1)S(1)}, u32[]{:S(2)}, u32[]{:S(2)}) collective-permute-start(bf16[2,4,256,128]{3,2,1,0:T(8,128)(2,1)S(1)} %shard_map.38), channel_id=1, source_target_pairs={{0,4},{4,0},{8,12},{12,8},{16,20},{20,16},{24,28},{28,24},{1,5},{5... | collective-permute-start | bytes 1572872 | tf_op jit(solution)/shard_map/ppermute | solution.py:395
  3.6 6.6 %collective-permute-start.7 = (bf16[256,128]{1,0:T(8,128)(2,1)S(1)}, bf16[256,128]{1,0:T(8,128)(2,1)S(1)}, u32[]{:S(2)}, u32[]{:S(2)}) collective-permute-start(bf16[256,128]{1,0:T(8,128)(2,1)S(1)} %get-tuple-element.43), channel_id=1, source_target_pairs={{0,8},{4,12},{8,0},{12,4},{16,24},{20,28},{24,16},{28,20},{1,9},{5... | collective-permute-start | bytes 196616 | tf_op jit(solution)/shard_map/ppermute | solution.py:364
  6.5 5.7 %collective-permute-start.8 = (bf16[256,128]{1,0:T(8,128)(2,1)S(1)}, bf16[256,128]{1,0:T(8,128)(2,1)S(1)}, u32[]{:S(2)}, u32[]{:S(2)}) collective-permute-start(bf16[256,128]{1,0:T(8,128)(2,1)S(1)} %get-tuple-element.44), channel_id=1, source_target_pairs={{0,16},{4,20},{8,24},{12,28},{16,0},{20,4},{24,8},{28,12},{1,17},{... | collective-permute-start | bytes 196616 | tf_op jit(solution)/shard_map/ppermute | solution.py:364
  8.0 9.4 %collective-permute-start.1 = (bf16[256,128]{1,0:T(8,128)(2,1)S(1)}, bf16[256,128]{1,0:T(8,128)(2,1)S(1)}, u32[]{:S(2)}, u32[]{:S(2)}) collective-permute-start(bf16[256,128]{1,0:T(8,128)(2,1)S(1)} %get-tuple-element.35), channel_id=1, source_target_pairs={{0,8},{4,12},{8,0},{12,4},{16,24},{20,28},{24,16},{28,20},{1,9},{5... | collective-permute-start | bytes 196616 | tf_op jit(solution)/shard_map/ppermute | solution.py:364
  8.6 6.1 %collective-permute-start.9 = (bf16[256,128]{1,0:T(8,128)(2,1)S(1)}, bf16[256,128]{1,0:T(8,128)(2,1)S(1)}, u32[]{:S(2)}, u32[]{:S(2)}) collective-permute-start(bf16[256,128]{1,0:T(8,128)(2,1)S(1)} %get-tuple-element.45), channel_id=1, source_target_pairs={{0,24},{4,28},{8,16},{12,20},{16,8},{20,12},{24,0},{28,4},{1,25},{... | collective-permute-start | bytes 196616 | tf_op jit(solution)/shard_map/ppermute | solution.py:364
  10.1 8.6 %collective-permute-start.13 = (bf16[512,128]{1,0:T(8,128)(2,1)S(1)}, bf16[512,128]{1,0:T(8,128)(2,1)S(1)}, u32[]{:S(2)}, u32[]{:S(2)}) collective-permute-start(bf16[512,128]{1,0:T(8,128)(2,1)S(1)} %get-tuple-element.52), channel_id=1, source_target_pairs={{0,8},{4,12},{8,0},{12,4},{16,24},{20,28},{24,16},{28,20},{1,9},{5... | collective-permute-start | bytes 393224 | tf_op jit(solution)/shard_map/ppermute | solution.py:364
  10.2 10.0 %collective-permute-start.14 = (bf16[512,128]{1,0:T(8,128)(2,1)S(1)}, bf16[512,128]{1,0:T(8,128)(2,1)S(1)}, u32[]{:S(2)}, u32[]{:S(2)}) collective-permute-start(bf16[512,128]{1,0:T(8,128)(2,1)S(1)} %get-tuple-element.53), channel_id=1, source_target_pairs={{0,16},{4,20},{8,24},{12,28},{16,0},{20,4},{24,8},{28,12},{1,17},{... | collective-permute-start | bytes 393224 | tf_op jit(solution)/shard_map/ppermute | solution.py:364
  12.2 10.6 %collective-permute-start.15 = (bf16[512,128]{1,0:T(8,128)(2,1)S(1)}, bf16[512,128]{1,0:T(8,128)(2,1)S(1)}, u32[]{:S(2)}, u32[]{:S(2)}) collective-permute-start(bf16[512,128]{1,0:T(8,128)(2,1)S(1)} %get-tuple-element.54), channel_id=1, source_target_pairs={{0,24},{4,28},{8,16},{12,20},{16,8},{20,12},{24,0},{28,4},{1,25},{... | collective-permute-start | bytes 393224 | tf_op jit(solution)/shard_map/ppermute | solution.py:364
  14.7 9.7 %collective-permute-start.2 = (bf16[256,128]{1,0:T(8,128)(2,1)S(1)}, bf16[256,128]{1,0:T(8,128)(2,1)S(1)}, u32[]{:S(2)}, u32[]{:S(2)}) collective-permute-start(bf16[256,128]{1,0:T(8,128)(2,1)S(1)} %get-tuple-element.36), channel_id=1, source_target_pairs={{0,16},{4,20},{8,24},{12,28},{16,0},{20,4},{24,8},{28,12},{1,17},{... | collective-permute-start | bytes 196616 | tf_op jit(solution)/shard_map/ppermute | solution.py:364
  17.4 7.7 %collective-permute-start.3 = (bf16[256,128]{1,0:T(8,128)(2,1)S(1)}, bf16[256,128]{1,0:T(8,128)(2,1)S(1)}, u32[]{:S(2)}, u32[]{:S(2)}) collective-permute-start(bf16[256,128]{1,0:T(8,128)(2,1)S(1)} %get-tuple-element.37), channel_id=1, source_target_pairs={{0,24},{4,28},{8,16},{12,20},{16,8},{20,12},{24,0},{28,4},{1,25},{... | collective-permute-start | bytes 196616 | tf_op jit(solution)/shard_map/ppermute | solution.py:364
  18.6 10.6 %collective-permute-start.10 = (bf16[2,192,128]{2,1,0:T(8,128)(2,1)S(1)}, bf16[2,192,128]{2,1,0:T(8,128)(2,1)S(1)}, u32[]{:S(2)}, u32[]{:S(2)}) collective-permute-start(bf16[2,192,128]{2,1,0:T(8,128)(2,1)S(1)} %get-tuple-element.47), channel_id=1, source_target_pairs={{0,1},{1,0},{2,3},{3,2},{4,5},{5,4},{6,7},{7,6},{8,9},{9,8},{10,11... | collective-permute-start | bytes 294920 | tf_op jit(solution)/shard_map/ppermute | solution.py:347
  20.2 10.2 %collective-permute-start.11 = (bf16[2,192,128]{2,1,0:T(8,128)(2,1)S(1)}, bf16[2,192,128]{2,1,0:T(8,128)(2,1)S(1)}, u32[]{:S(2)}, u32[]{:S(2)}) collective-permute-start(bf16[2,192,128]{2,1,0:T(8,128)(2,1)S(1)} %get-tuple-element.48), channel_id=1, source_target_pairs={{0,2},{1,3},{2,0},{3,1},{4,6},{5,7},{6,4},{7,5},{8,10},{9,11},{10,... | collective-permute-start | bytes 294920 | tf_op jit(solution)/shard_map/ppermute | solution.py:347
  22.8 7.9 %collective-permute-start.12 = (bf16[2,192,128]{2,1,0:T(8,128)(2,1)S(1)}, bf16[2,192,128]{2,1,0:T(8,128)(2,1)S(1)}, u32[]{:S(2)}, u32[]{:S(2)}) collective-permute-start(bf16[2,192,128]{2,1,0:T(8,128)(2,1)S(1)} %get-tuple-element.49), channel_id=1, source_target_pairs={{0,3},{1,2},{2,1},{3,0},{4,7},{5,6},{6,5},{7,4},{8,11},{9,10},{10,... | collective-permute-start | bytes 294920 | tf_op jit(solution)/shard_map/ppermute | solution.py:347
  24.4 24.2 %collective-permute-start.17 = (bf16[2,384,128]{2,1,0:T(8,128)(2,1)S(1)}, bf16[2,384,128]{2,1,0:T(8,128)(2,1)S(1)}, u32[]{:S(2)}, u32[]{:S(2)}) collective-permute-start(bf16[2,384,128]{2,1,0:T(8,128)(2,1)S(1)} %get-tuple-element.60), channel_id=1, source_target_pairs={{0,1},{1,0},{2,3},{3,2},{4,5},{5,4},{6,7},{7,6},{8,9},{9,8},{10,11... | collective-permute-start | bytes 589832 | tf_op jit(solution)/shard_map/ppermute | solution.py:347
  25.1 23.5 %collective-permute-start.18 = (bf16[2,384,128]{2,1,0:T(8,128)(2,1)S(1)}, bf16[2,384,128]{2,1,0:T(8,128)(2,1)S(1)}, u32[]{:S(2)}, u32[]{:S(2)}) collective-permute-start(bf16[2,384,128]{2,1,0:T(8,128)(2,1)S(1)} %get-tuple-element.61), channel_id=1, source_target_pairs={{0,3},{1,2},{2,1},{3,0},{4,7},{5,6},{6,5},{7,4},{8,11},{9,10},{10,... | collective-permute-start | bytes 589832 | tf_op jit(solution)/shard_map/ppermute | solution.py:347
  29.3 9.4 %collective-permute-start.4 = (bf16[2,192,128]{2,1,0:T(8,128)(2,1)S(1)}, bf16[2,192,128]{2,1,0:T(8,128)(2,1)S(1)}, u32[]{:S(2)}, u32[]{:S(2)}) collective-permute-start(bf16[2,192,128]{2,1,0:T(8,128)(2,1)S(1)} %get-tuple-element.39), channel_id=1, source_target_pairs={{0,1},{1,0},{2,3},{3,2},{4,5},{5,4},{6,7},{7,6},{8,9},{9,8},{10,11... | collective-permute-start | bytes 294920 | tf_op jit(solution)/shard_map/ppermute | solution.py:347
  30.4 17.8 %collective-permute-start.5 = (bf16[2,192,128]{2,1,0:T(8,128)(2,1)S(1)}, bf16[2,192,128]{2,1,0:T(8,128)(2,1)S(1)}, u32[]{:S(2)}, u32[]{:S(2)}) collective-permute-start(bf16[2,192,128]{2,1,0:T(8,128)(2,1)S(1)} %get-tuple-element.40), channel_id=1, source_target_pairs={{0,2},{1,3},{2,0},{3,1},{4,6},{5,7},{6,4},{7,5},{8,10},{9,11},{10,... | collective-permute-start | bytes 294920 | tf_op jit(solution)/shard_map/ppermute | solution.py:347
  30.7 17.5 %collective-permute-start.6 = (bf16[2,192,128]{2,1,0:T(8,128)(2,1)S(1)}, bf16[2,192,128]{2,1,0:T(8,128)(2,1)S(1)}, u32[]{:S(2)}, u32[]{:S(2)}) collective-permute-start(bf16[2,192,128]{2,1,0:T(8,128)(2,1)S(1)} %get-tuple-element.41), channel_id=1, source_target_pairs={{0,3},{1,2},{2,1},{3,0},{4,7},{5,6},{6,5},{7,4},{8,11},{9,10},{10,... | collective-permute-start | bytes 294920 | tf_op jit(solution)/shard_map/ppermute | solution.py:347
  38.7 13.7 %collective-permute-start.19 = (bf16[1,384,128]{2,1,0:T(8,128)(2,1)S(1)}, bf16[1,384,128]{2,1,0:T(8,128)(2,1)S(1)}, u32[]{:S(2)}, u32[]{:S(2)}) collective-permute-start(bf16[1,384,128]{2,1,0:T(8,128)(2,1)S(1)} %get-tuple-element.62), channel_id=1, source_target_pairs={{0,2},{1,3},{2,0},{3,1},{4,6},{5,7},{6,4},{7,5},{8,10},{9,11},{10,... | collective-permute-start | bytes 294920 | tf_op jit(solution)/shard_map/ppermute | solution.py:347
  48.2 6.6 %collective-permute-start.16 = (bf16[1,384,128]{2,1,0:T(8,128)(2,1)S(1)}, bf16[1,384,128]{2,1,0:T(8,128)(2,1)S(1)}, u32[]{:S(2)}, u32[]{:S(2)}) collective-permute-start(bf16[1,384,128]{2,1,0:T(8,128)(2,1)S(1)} %get-tuple-element.55), channel_id=1, source_target_pairs={{0,2},{1,3},{2,0},{3,1},{4,6},{5,7},{6,4},{7,5},{8,10},{9,11},{10,... | collective-permute-start | bytes 294920 | tf_op jit(solution)/shard_map/ppermute | solution.py:347

commit v9 on v8

--- a/solution.py
+++ b/solution.py
@@ -370,8 +370,10 @@
 
 
 def orders(groups):
-    last = 2 if groups == 4 else groups - 1
-    return [2,3,1], [3,1,2], last
+    if groups == 4:
+        return [2, 3, 1], [2, 1, 3], 3
+    rest = list(range(groups - 2, 0, -1))
+    return [groups - 1] + rest, rest + [groups - 1], groups - 1
 
 
 def steps_of(voltages, assignment, slot_subarray_index):

time: 56.2 us -> 56.3 us (level)
  waiting for transfers between devices: 16.4 us -> 12.1 us
  starting transfers between devices: 29 us -> 33.3 us
    ppermute x10, starting transfers between devices: 15.7 us -> 20 us  [exchange(): moved.append(lax.ppermute(part, 'tm', pairs))]
    ppermute x10, waiting for transfers between devices: 14.9 us -> 10.6 us  [exchange(): moved.append(lax.ppermute(part, 'tm', pairs))]
  transfers between devices with their start and end apart: 20 -> 20, of which waited for: 5 -> 3; matrix products, arithmetic and copies ran while one was open for 0% -> 0% of each run, Pallas kernels for 14% -> 14%
where the time goes in v9:
time: 56.3 us; the launch traced here: 56.2 us
  starting transfers between devices  33.3 us (59%)
  waiting for transfers between devices  12.1 us (21%)
  Pallas kernels  9.34 us (17%)
  local copies, waits for them, and re-layouts  1.23 us (2%)
    ppermute x10, starting transfers between devices, exchange(): moved.append(lax.ppermute(part, 'tm', pairs))  20 us
    ppermute x9, starting transfers between devices, cross(): lax.ppermute(chunks[step], 'chan', [(i, i ^ 2 * step) for i in starts])  12.7 us
    ppermute x10, waiting for transfers between devices, exchange(): moved.append(lax.ppermute(part, 'tm', pairs))  10.6 us
    pallas_call x2, Pallas kernels, gram(): pl.pallas_call(functools.partial(late_kernel, s), out_shape=[jax.ShapeDty...  2.64 us
    pallas_call x2, Pallas kernels, gather_half(): pl.pallas_call(functools.partial(gather_half_kernel, steps, groups), out_...  2.26 us
    ppermute x1, waiting for transfers between devices, steps_of(): given = lax.ppermute(give(voltages), 'chan', swap)  1.54 us
    pallas_call x1, Pallas kernels, gram(): pl.pallas_call(early_kernel, out_shape=jax.ShapeDtypeStruct((per, 2 * slo...  1.39 us
    pallas_call x1, Pallas kernels, gather(): pl.pallas_call(functools.partial(gather_kernel, steps, len(heights)), out...  1.32 us
  transfers between devices with their start and end apart: 20, of which 3 were waited for; matrix products, arithmetic and copies ran while one was open for 0% of the time, Pallas kernels for 14%

profile of v9, /device:TPU:0, one launch (start us, length us, event | category | flops | bytes accessed | tf_op | source)
XLA Modules:
  0.0 56.2 jit_solution(6317443284110944085)
XLA Ops:
  0.0 0.0 copy-start
  0.0 1.2 %copy-done = bf16[2,8,256,128]{3,2,1,0:T(8,128)(2,1)S(1)} copy-done((bf16[2,8,256,128]{3,2,1,0:T(8,128)(2,1)S(1)}, bf16[2,8,256,128]{3,2,1,0:T(8,128)(2,1)}, u32[]{:S(2)}) %copy-start) | copy-done | bytes 1048600
  1.2 0.0 copy-start.1
  1.2 0.0 copy-start.2
  1.3 0.6 collective-permute-start
  1.8 1.5 %collective-permute-done.given_ref = bf16[2,4,256,128]{3,2,1,0:T(8,128)(2,1)S(1)} collective-permute-done((bf16[2,4,256,128]{3,2,1,0:T(8,128)(2,1)S(1)}, bf16[2,4,256,128]{3,2,1,0:T(8,128)(2,1)S(1)}, u32[]{:S(2)}, u32[]{:S(2)}) %collective-permute-start) | collective-permute-done | bytes 524320 | tf_op jit(solution)/shard_map/ppermute | solution.py:397
  3.4 0.2 shard_map.39
  3.6 2.9 %collective-permute-start.7 = (bf16[256,128]{1,0:T(8,128)(2,1)S(1)}, bf16[256,128]{1,0:T(8,128)(2,1)S(1)}, u32[]{:S(2)}, u32[]{:S(2)}) collective-permute-start(bf16[256,128]{1,0:T(8,128)(2,1)S(1)} %get-tuple-element.43), channel_id=1, source_target_pairs={{0,8},{4,12},{8,0},{12,4},{16,24},{20,28},{24,16},{28,20},{1,9},{5... | collective-permute-start | bytes 196616 | tf_op jit(solution)/shard_map/ppermute | solution.py:364
  6.5 1.5 %collective-permute-start.8 = (bf16[256,128]{1,0:T(8,128)(2,1)S(1)}, bf16[256,128]{1,0:T(8,128)(2,1)S(1)}, u32[]{:S(2)}, u32[]{:S(2)}) collective-permute-start(bf16[256,128]{1,0:T(8,128)(2,1)S(1)} %get-tuple-element.44), channel_id=1, source_target_pairs={{0,16},{4,20},{8,24},{12,28},{16,0},{20,4},{24,8},{28,12},{1,17},{... | collective-permute-start | bytes 196616 | tf_op jit(solution)/shard_map/ppermute | solution.py:364
  8.0 0.5 collective-permute-start.1
  8.6 1.4 %collective-permute-start.9 = (bf16[256,128]{1,0:T(8,128)(2,1)S(1)}, bf16[256,128]{1,0:T(8,128)(2,1)S(1)}, u32[]{:S(2)}, u32[]{:S(2)}) collective-permute-start(bf16[256,128]{1,0:T(8,128)(2,1)S(1)} %get-tuple-element.45), channel_id=1, source_target_pairs={{0,24},{4,28},{8,16},{12,20},{16,8},{20,12},{24,0},{28,4},{1,25},{... | collective-permute-start | bytes 196616 | tf_op jit(solution)/shard_map/ppermute | solution.py:364
  10.1 0.1 collective-permute-start.13
  10.2 0.0 collective-permute-done.7.rest_1_
  10.2 2.0 %collective-permute-start.14 = (bf16[512,128]{1,0:T(8,128)(2,1)S(1)}, bf16[512,128]{1,0:T(8,128)(2,1)S(1)}, u32[]{:S(2)}, u32[]{:S(2)}) collective-permute-start(bf16[512,128]{1,0:T(8,128)(2,1)S(1)} %get-tuple-element.53), channel_id=1, source_target_pairs={{0,16},{4,20},{8,24},{12,28},{16,0},{20,4},{24,8},{28,12},{1,17},{... | collective-permute-start | bytes 393224 | tf_op jit(solution)/shard_map/ppermute | solution.py:364
  12.2 0.0 collective-permute-done.8.rest_2_
  12.2 1.4 %collective-permute-start.15 = (bf16[512,128]{1,0:T(8,128)(2,1)S(1)}, bf16[512,128]{1,0:T(8,128)(2,1)S(1)}, u32[]{:S(2)}, u32[]{:S(2)}) collective-permute-start(bf16[512,128]{1,0:T(8,128)(2,1)S(1)} %get-tuple-element.54), channel_id=1, source_target_pairs={{0,24},{4,28},{8,16},{12,20},{16,8},{20,12},{24,0},{28,4},{1,25},{... | collective-permute-start | bytes 393224 | tf_op jit(solution)/shard_map/ppermute | solution.py:364
  13.6 0.0 copy-done.1
  13.6 0.0 copy-done.2
  13.6 1.0 %shard_map.37.select_ref = bf16[1536,1024]{1,0:T(8,128)(2,1)S(1)} custom-call(s32[1,8]{1,0:T(1,128)S(1)} %bitcast.3, s32[8,128]{1,0:T(8,128)S(1)} %bitcast.2), custom_call_target="tpu_custom_call" | custom-call | flops 4000000000 | bytes 3000000 | tf_op jit(solution)/shard_map/pallas_call | solution.py:76
  14.7 0.0 collective-permute-done.9.rest_3_
  14.7 1.6 %collective-permute-start.2 = (bf16[256,128]{1,0:T(8,128)(2,1)S(1)}, bf16[256,128]{1,0:T(8,128)(2,1)S(1)}, u32[]{:S(2)}, u32[]{:S(2)}) collective-permute-start(bf16[256,128]{1,0:T(8,128)(2,1)S(1)} %get-tuple-element.36), channel_id=1, source_target_pairs={{0,16},{4,20},{8,24},{12,28},{16,0},{20,4},{24,8},{28,12},{1,17},{... | collective-permute-start | bytes 196616 | tf_op jit(solution)/shard_map/ppermute | solution.py:364
  16.3 1.1 %shard_map.41 = (bf16[2,192,128]{2,1,0:T(8,128)(2,1)S(1)}, bf16[2,192,128]{2,1,0:T(8,128)(2,1)S(1)}, bf16[2,192,128]{2,1,0:T(8,128)(2,1)S(1)}, bf16[2,192,128]{2,1,0:T(8,128)(2,1)S(1)}) custom-call(bf16[1536,1024]{1,0:T(8,128)(2,1)S(1)} %shard_map.37.select_ref, bf16[256,128]{1,0:T(8,128)(2,1)S(1)} %get-tuple-element.42.rest_0_, ...), custom_call_target="tpu_custom_call" | custom-call | flops 402653184 | bytes 4000000 | tf_op jit(solution)/shard_map/pallas_call | solution.py:175
  17.4 0.0 collective-permute-done.1.rest_1_
  17.4 1.2 %collective-permute-start.3 = (bf16[256,128]{1,0:T(8,128)(2,1)S(1)}, bf16[256,128]{1,0:T(8,128)(2,1)S(1)}, u32[]{:S(2)}, u32[]{:S(2)}) collective-permute-start(bf16[256,128]{1,0:T(8,128)(2,1)S(1)} %get-tuple-element.37), channel_id=1, source_target_pairs={{0,24},{4,28},{8,16},{12,20},{16,8},{20,12},{24,0},{28,4},{1,25},{... | collective-permute-start | bytes 196616 | tf_op jit(solution)/shard_map/ppermute | solution.py:364
  18.6 0.0 collective-permute-done.13.rest_1_
  18.6 1.6 %collective-permute-start.10 = (bf16[2,192,128]{2,1,0:T(8,128)(2,1)S(1)}, bf16[2,192,128]{2,1,0:T(8,128)(2,1)S(1)}, u32[]{:S(2)}, u32[]{:S(2)}) collective-permute-start(bf16[2,192,128]{2,1,0:T(8,128)(2,1)S(1)} %get-tuple-element.47), channel_id=1, source_target_pairs={{0,1},{1,0},{2,3},{3,2},{4,5},{5,4},{6,7},{7,6},{8,9},{9,8},{10,11... | collective-permute-start | bytes 294920 | tf_op jit(solution)/shard_map/ppermute | solution.py:347
  20.2 0.0 collective-permute-done.14.rest_2_
  20.2 2.6 %collective-permute-start.11 = (bf16[2,192,128]{2,1,0:T(8,128)(2,1)S(1)}, bf16[2,192,128]{2,1,0:T(8,128)(2,1)S(1)}, u32[]{:S(2)}, u32[]{:S(2)}) collective-permute-start(bf16[2,192,128]{2,1,0:T(8,128)(2,1)S(1)} %get-tuple-element.48), channel_id=1, source_target_pairs={{0,2},{1,3},{2,0},{3,1},{4,6},{5,7},{6,4},{7,5},{8,10},{9,11},{10,... | collective-permute-start | bytes 294920 | tf_op jit(solution)/shard_map/ppermute | solution.py:347
  22.8 0.0 collective-permute-done.15.rest_3_
  22.8 0.2 collective-permute-start.12
  23.0 1.3 %shard_map.44 = (bf16[2,384,128]{2,1,0:T(8,128)(2,1)S(1)}, bf16[2,384,128]{2,1,0:T(8,128)(2,1)S(1)}, bf16[2,384,128]{2,1,0:T(8,128)(2,1)S(1)}, bf16[1,384,128]{2,1,0:T(8,128)(2,1)S(1)}, bf16[1,384,128]{2,1,0:T(8,128)(2,1)S(1)}) custom-call(bf16[1536,1024]{1,0:T(8,128)(2,1)S(1)} %shard_map.37.select_ref, bf16[512,128]{1,0:T(8,128)(2,1)S(1)} %get-tuple-element.51.rest_0_, ...), custom_call_target="tpu_custom_call" | custom-call | flops 805306368 | bytes 4000000 | tf_op jit(solution)/shard_map/pallas_call | solution.py:259
  24.4 0.0 collective-permute-done.2.rest_2_
  24.4 0.7 %collective-permute-start.17 = (bf16[2,384,128]{2,1,0:T(8,128)(2,1)S(1)}, bf16[2,384,128]{2,1,0:T(8,128)(2,1)S(1)}, u32[]{:S(2)}, u32[]{:S(2)}) collective-permute-start(bf16[2,384,128]{2,1,0:T(8,128)(2,1)S(1)} %get-tuple-element.60), channel_id=1, source_target_pairs={{0,1},{1,0},{2,3},{3,2},{4,5},{5,4},{6,7},{7,6},{8,9},{9,8},{10,11... | collective-permute-start | bytes 589832 | tf_op jit(solution)/shard_map/ppermute | solution.py:347
  25.1 0.0 collective-permute-done.3.rest_3_
  25.1 3.5 %collective-permute-start.18 = (bf16[2,384,128]{2,1,0:T(8,128)(2,1)S(1)}, bf16[2,384,128]{2,1,0:T(8,128)(2,1)S(1)}, u32[]{:S(2)}, u32[]{:S(2)}) collective-permute-start(bf16[2,384,128]{2,1,0:T(8,128)(2,1)S(1)} %get-tuple-element.61), channel_id=1, source_target_pairs={{0,2},{1,3},{2,0},{3,1},{4,6},{5,7},{6,4},{7,5},{8,10},{9,11},{10,... | collective-permute-start | bytes 589832 | tf_op jit(solution)/shard_map/ppermute | solution.py:347
  28.6 1.1 %shard_map.40 = (bf16[2,192,128]{2,1,0:T(8,128)(2,1)S(1)}, bf16[2,192,128]{2,1,0:T(8,128)(2,1)S(1)}, bf16[2,192,128]{2,1,0:T(8,128)(2,1)S(1)}, bf16[2,192,128]{2,1,0:T(8,128)(2,1)S(1)}) custom-call(bf16[1536,1024]{1,0:T(8,128)(2,1)S(1)} %shard_map.37.select_ref, bf16[256,128]{1,0:T(8,128)(2,1)S(1)} %get-tuple-element.34.rest_0_, ...), custom_call_target="tpu_custom_call" | custom-call | flops 402653184 | bytes 4000000 | tf_op jit(solution)/shard_map/pallas_call | solution.py:175
  29.7 0.0 collective-permute-done.10.refs_5_
  29.7 0.2 collective-permute-start.4
  29.9 0.0 collective-permute-done.11.refs_6_
  29.9 0.7 %collective-permute-start.5 = (bf16[2,192,128]{2,1,0:T(8,128)(2,1)S(1)}, bf16[2,192,128]{2,1,0:T(8,128)(2,1)S(1)}, u32[]{:S(2)}, u32[]{:S(2)}) collective-permute-start(bf16[2,192,128]{2,1,0:T(8,128)(2,1)S(1)} %get-tuple-element.40), channel_id=1, source_target_pairs={{0,2},{1,3},{2,0},{3,1},{4,6},{5,7},{6,4},{7,5},{8,10},{9,11},{10,... | collective-permute-start | bytes 294920 | tf_op jit(solution)/shard_map/ppermute | solution.py:347
  30.6 0.0 collective-permute-done.12.refs_7_
  30.6 3.6 %collective-permute-start.6 = (bf16[2,192,128]{2,1,0:T(8,128)(2,1)S(1)}, bf16[2,192,128]{2,1,0:T(8,128)(2,1)S(1)}, u32[]{:S(2)}, u32[]{:S(2)}) collective-permute-start(bf16[2,192,128]{2,1,0:T(8,128)(2,1)S(1)} %get-tuple-element.41), channel_id=1, source_target_pairs={{0,3},{1,2},{2,1},{3,0},{4,7},{5,6},{6,5},{7,4},{8,11},{9,10},{10,... | collective-permute-start | bytes 294920 | tf_op jit(solution)/shard_map/ppermute | solution.py:347
  34.2 4.0 %collective-permute-done.4.refs_1_ = bf16[2,192,128]{2,1,0:T(8,128)(2,1)S(1)} collective-permute-done((bf16[2,192,128]{2,1,0:T(8,128)(2,1)S(1)}, bf16[2,192,128]{2,1,0:T(8,128)(2,1)S(1)}, u32[]{:S(2)}, u32[]{:S(2)}) %collective-permute-start.4) | collective-permute-done | bytes 98336 | tf_op jit(solution)/shard_map/ppermute | solution.py:347
  38.2 2.5 %collective-permute-start.19 = (bf16[1,384,128]{2,1,0:T(8,128)(2,1)S(1)}, bf16[1,384,128]{2,1,0:T(8,128)(2,1)S(1)}, u32[]{:S(2)}, u32[]{:S(2)}) collective-permute-start(bf16[1,384,128]{2,1,0:T(8,128)(2,1)S(1)} %get-tuple-element.62), channel_id=1, source_target_pairs={{0,3},{1,2},{2,1},{3,0},{4,7},{5,6},{6,5},{7,4},{8,11},{9,10},{10,... | collective-permute-start | bytes 294920 | tf_op jit(solution)/shard_map/ppermute | solution.py:347
  40.7 6.5 %collective-permute-done.5.refs_2_ = bf16[2,192,128]{2,1,0:T(8,128)(2,1)S(1)} collective-permute-done((bf16[2,192,128]{2,1,0:T(8,128)(2,1)S(1)}, bf16[2,192,128]{2,1,0:T(8,128)(2,1)S(1)}, u32[]{:S(2)}, u32[]{:S(2)}) %collective-permute-start.5) | collective-permute-done | bytes 98336 | tf_op jit(solution)/shard_map/ppermute | solution.py:347
  47.2 4.5 %collective-permute-start.16 = (bf16[1,384,128]{2,1,0:T(8,128)(2,1)S(1)}, bf16[1,384,128]{2,1,0:T(8,128)(2,1)S(1)}, u32[]{:S(2)}, u32[]{:S(2)}) collective-permute-start(bf16[1,384,128]{2,1,0:T(8,128)(2,1)S(1)} %get-tuple-element.55), channel_id=1, source_target_pairs={{0,3},{1,2},{2,1},{3,0},{4,7},{5,6},{6,5},{7,4},{8,11},{9,10},{10,... | collective-permute-start | bytes 294920 | tf_op jit(solution)/shard_map/ppermute | solution.py:347
  51.7 0.0 collective-permute-done.6.refs_3_
  51.7 0.4 shard_map.42
  52.1 0.0 collective-permute-done.17.refs_4_
  52.1 0.0 collective-permute-done.18.refs_5_
  52.1 1.4 %shard_map.45.so_far = f32[2,768,384]{2,1,0:T(8,128)S(1)} custom-call(bf16[2,384,128]{2,1,0:T(8,128)(2,1)S(1)} %get-tuple-element.56.refs_0_, bf16[2,384,128]{2,1,0:T(8,128)(2,1)S(1)} %get-tuple-element.57.refs_1_, bf16[2,384,128]{2,1,0:T(8,128)(2,1)S(1)} %get-tuple-element.58.refs_2_, bf16[2,384,128]{2,1,0:T(8,128)(2,1)S(1)} %get-tuple-element.59.refs_3_, ...), custom_call_target="tpu_custom_call" | custom-call | flops 905969664 | bytes 3000000 | tf_op jit(solution)/shard_map/pallas_call | solution.py:316
  53.5 0.0 collective-permute-done.19.imag
  53.5 1.3 %shard_map.46.rest_0_ = f32[2,1,2,384,384]{4,3,2,1,0:T(8,128)} custom-call(bf16[2,384,128]{2,1,0:T(8,128)(2,1)S(1)} %get-tuple-element.50.real, bf16[1,384,128]{2,1,0:T(8,128)(2,1)S(1)} %collective-permute-done.19.imag, f32[2,768,384]{2,1,0:T(8,128)S(1)} %shard_map.45.so_far), custom_call_target="tpu_custom_call" | custom-call | flops 150994944 | bytes 2000000 | tf_op jit(solution)/shard_map/pallas_call | solution.py:327
  54.9 0.0 collective-permute-done.16.imag
  54.9 1.3 %shard_map.47 = f32[2,1,2,384,384]{4,3,2,1,0:T(8,128)} custom-call(bf16[2,384,128]{2,1,0:T(8,128)(2,1)S(1)} %get-tuple-element.50.real, bf16[1,384,128]{2,1,0:T(8,128)(2,1)S(1)} %collective-permute-done.16.imag, f32[2,768,384]{2,1,0:T(8,128)S(1)} %shard_map.45.so_far, f32[2,1,2,384,384]{4,3,2,1,0:T(8,128)} %shard_map.46.rest_0_), custom_call_target="tpu_custom_call", output_to_operand_aliasing={{}: (3, {})} | custom-call | flops 150994944 | bytes 2000000 | tf_op jit(solution)/shard_map/pallas_call | solution.py:327
  (2 shorter events, 0.1 us)
Async XLA Ops:
  0.0 1.2 %copy-start = (bf16[2,8,256,128]{3,2,1,0:T(8,128)(2,1)S(1)}, bf16[2,8,256,128]{3,2,1,0:T(8,128)(2,1)}, u32[]{:S(2)}) copy-start(bf16[2,8,256,128]{3,2,1,0:T(8,128)(2,1)} %x_ref.5) | copy-start | bytes 3145732
  1.2 12.4 %copy-start.1 = (s32[1024,1]{0,1:T(1,128)S(1)}, s32[1024,1]{0,1:T(1,128)}, u32[]{:S(2)}) copy-start(s32[1024,1]{0,1:T(1,128)} %param.4) | copy-start | bytes 12292
  1.2 12.4 %copy-start.2 = (s32[8]{0:T(128)S(1)}, s32[8]{0:T(128)}, u32[]{:S(2)}) copy-start(s32[8]{0:T(128)} %param.5) | copy-start | bytes 100
  1.3 2.1 %collective-permute-start = (bf16[2,4,256,128]{3,2,1,0:T(8,128)(2,1)S(1)}, bf16[2,4,256,128]{3,2,1,0:T(8,128)(2,1)S(1)}, u32[]{:S(2)}, u32[]{:S(2)}) collective-permute-start(bf16[2,4,256,128]{3,2,1,0:T(8,128)(2,1)S(1)} %shard_map.38), channel_id=1, source_target_pairs={{0,4},{4,0},{8,12},{12,8},{16,20},{20,16},{24,28},{28,24},{1,5},{5... | collective-permute-start | bytes 1572872 | tf_op jit(solution)/shard_map/ppermute | solution.py:397
  3.6 6.6 %collective-permute-start.7 = (bf16[256,128]{1,0:T(8,128)(2,1)S(1)}, bf16[256,128]{1,0:T(8,128)(2,1)S(1)}, u32[]{:S(2)}, u32[]{:S(2)}) collective-permute-start(bf16[256,128]{1,0:T(8,128)(2,1)S(1)} %get-tuple-element.43), channel_id=1, source_target_pairs={{0,8},{4,12},{8,0},{12,4},{16,24},{20,28},{24,16},{28,20},{1,9},{5... | collective-permute-start | bytes 196616 | tf_op jit(solution)/shard_map/ppermute | solution.py:364
  6.5 5.7 %collective-permute-start.8 = (bf16[256,128]{1,0:T(8,128)(2,1)S(1)}, bf16[256,128]{1,0:T(8,128)(2,1)S(1)}, u32[]{:S(2)}, u32[]{:S(2)}) collective-permute-start(bf16[256,128]{1,0:T(8,128)(2,1)S(1)} %get-tuple-element.44), channel_id=1, source_target_pairs={{0,16},{4,20},{8,24},{12,28},{16,0},{20,4},{24,8},{28,12},{1,17},{... | collective-permute-start | bytes 196616 | tf_op jit(solution)/shard_map/ppermute | solution.py:364
  8.0 9.4 %collective-permute-start.1 = (bf16[256,128]{1,0:T(8,128)(2,1)S(1)}, bf16[256,128]{1,0:T(8,128)(2,1)S(1)}, u32[]{:S(2)}, u32[]{:S(2)}) collective-permute-start(bf16[256,128]{1,0:T(8,128)(2,1)S(1)} %get-tuple-element.35), channel_id=1, source_target_pairs={{0,8},{4,12},{8,0},{12,4},{16,24},{20,28},{24,16},{28,20},{1,9},{5... | collective-permute-start | bytes 196616 | tf_op jit(solution)/shard_map/ppermute | solution.py:364
  8.6 6.1 %collective-permute-start.9 = (bf16[256,128]{1,0:T(8,128)(2,1)S(1)}, bf16[256,128]{1,0:T(8,128)(2,1)S(1)}, u32[]{:S(2)}, u32[]{:S(2)}) collective-permute-start(bf16[256,128]{1,0:T(8,128)(2,1)S(1)} %get-tuple-element.45), channel_id=1, source_target_pairs={{0,24},{4,28},{8,16},{12,20},{16,8},{20,12},{24,0},{28,4},{1,25},{... | collective-permute-start | bytes 196616 | tf_op jit(solution)/shard_map/ppermute | solution.py:364
  10.1 8.6 %collective-permute-start.13 = (bf16[512,128]{1,0:T(8,128)(2,1)S(1)}, bf16[512,128]{1,0:T(8,128)(2,1)S(1)}, u32[]{:S(2)}, u32[]{:S(2)}) collective-permute-start(bf16[512,128]{1,0:T(8,128)(2,1)S(1)} %get-tuple-element.52), channel_id=1, source_target_pairs={{0,8},{4,12},{8,0},{12,4},{16,24},{20,28},{24,16},{28,20},{1,9},{5... | collective-permute-start | bytes 393224 | tf_op jit(solution)/shard_map/ppermute | solution.py:364
  10.2 10.0 %collective-permute-start.14 = (bf16[512,128]{1,0:T(8,128)(2,1)S(1)}, bf16[512,128]{1,0:T(8,128)(2,1)S(1)}, u32[]{:S(2)}, u32[]{:S(2)}) collective-permute-start(bf16[512,128]{1,0:T(8,128)(2,1)S(1)} %get-tuple-element.53), channel_id=1, source_target_pairs={{0,16},{4,20},{8,24},{12,28},{16,0},{20,4},{24,8},{28,12},{1,17},{... | collective-permute-start | bytes 393224 | tf_op jit(solution)/shard_map/ppermute | solution.py:364
  12.2 10.6 %collective-permute-start.15 = (bf16[512,128]{1,0:T(8,128)(2,1)S(1)}, bf16[512,128]{1,0:T(8,128)(2,1)S(1)}, u32[]{:S(2)}, u32[]{:S(2)}) collective-permute-start(bf16[512,128]{1,0:T(8,128)(2,1)S(1)} %get-tuple-element.54), channel_id=1, source_target_pairs={{0,24},{4,28},{8,16},{12,20},{16,8},{20,12},{24,0},{28,4},{1,25},{... | collective-permute-start | bytes 393224 | tf_op jit(solution)/shard_map/ppermute | solution.py:364
  14.7 9.7 %collective-permute-start.2 = (bf16[256,128]{1,0:T(8,128)(2,1)S(1)}, bf16[256,128]{1,0:T(8,128)(2,1)S(1)}, u32[]{:S(2)}, u32[]{:S(2)}) collective-permute-start(bf16[256,128]{1,0:T(8,128)(2,1)S(1)} %get-tuple-element.36), channel_id=1, source_target_pairs={{0,16},{4,20},{8,24},{12,28},{16,0},{20,4},{24,8},{28,12},{1,17},{... | collective-permute-start | bytes 196616 | tf_op jit(solution)/shard_map/ppermute | solution.py:364
  17.4 7.7 %collective-permute-start.3 = (bf16[256,128]{1,0:T(8,128)(2,1)S(1)}, bf16[256,128]{1,0:T(8,128)(2,1)S(1)}, u32[]{:S(2)}, u32[]{:S(2)}) collective-permute-start(bf16[256,128]{1,0:T(8,128)(2,1)S(1)} %get-tuple-element.37), channel_id=1, source_target_pairs={{0,24},{4,28},{8,16},{12,20},{16,8},{20,12},{24,0},{28,4},{1,25},{... | collective-permute-start | bytes 196616 | tf_op jit(solution)/shard_map/ppermute | solution.py:364
  18.6 11.1 %collective-permute-start.10 = (bf16[2,192,128]{2,1,0:T(8,128)(2,1)S(1)}, bf16[2,192,128]{2,1,0:T(8,128)(2,1)S(1)}, u32[]{:S(2)}, u32[]{:S(2)}) collective-permute-start(bf16[2,192,128]{2,1,0:T(8,128)(2,1)S(1)} %get-tuple-element.47), channel_id=1, source_target_pairs={{0,1},{1,0},{2,3},{3,2},{4,5},{5,4},{6,7},{7,6},{8,9},{9,8},{10,11... | collective-permute-start | bytes 294920 | tf_op jit(solution)/shard_map/ppermute | solution.py:347
  20.2 9.7 %collective-permute-start.11 = (bf16[2,192,128]{2,1,0:T(8,128)(2,1)S(1)}, bf16[2,192,128]{2,1,0:T(8,128)(2,1)S(1)}, u32[]{:S(2)}, u32[]{:S(2)}) collective-permute-start(bf16[2,192,128]{2,1,0:T(8,128)(2,1)S(1)} %get-tuple-element.48), channel_id=1, source_target_pairs={{0,2},{1,3},{2,0},{3,1},{4,6},{5,7},{6,4},{7,5},{8,10},{9,11},{10,... | collective-permute-start | bytes 294920 | tf_op jit(solution)/shard_map/ppermute | solution.py:347
  22.8 7.8 %collective-permute-start.12 = (bf16[2,192,128]{2,1,0:T(8,128)(2,1)S(1)}, bf16[2,192,128]{2,1,0:T(8,128)(2,1)S(1)}, u32[]{:S(2)}, u32[]{:S(2)}) collective-permute-start(bf16[2,192,128]{2,1,0:T(8,128)(2,1)S(1)} %get-tuple-element.49), channel_id=1, source_target_pairs={{0,3},{1,2},{2,1},{3,0},{4,7},{5,6},{6,5},{7,4},{8,11},{9,10},{10,... | collective-permute-start | bytes 294920 | tf_op jit(solution)/shard_map/ppermute | solution.py:347
  24.4 27.7 %collective-permute-start.17 = (bf16[2,384,128]{2,1,0:T(8,128)(2,1)S(1)}, bf16[2,384,128]{2,1,0:T(8,128)(2,1)S(1)}, u32[]{:S(2)}, u32[]{:S(2)}) collective-permute-start(bf16[2,384,128]{2,1,0:T(8,128)(2,1)S(1)} %get-tuple-element.60), channel_id=1, source_target_pairs={{0,1},{1,0},{2,3},{3,2},{4,5},{5,4},{6,7},{7,6},{8,9},{9,8},{10,11... | collective-permute-start | bytes 589832 | tf_op jit(solution)/shard_map/ppermute | solution.py:347
  25.1 27.0 %collective-permute-start.18 = (bf16[2,384,128]{2,1,0:T(8,128)(2,1)S(1)}, bf16[2,384,128]{2,1,0:T(8,128)(2,1)S(1)}, u32[]{:S(2)}, u32[]{:S(2)}) collective-permute-start(bf16[2,384,128]{2,1,0:T(8,128)(2,1)S(1)} %get-tuple-element.61), channel_id=1, source_target_pairs={{0,2},{1,3},{2,0},{3,1},{4,6},{5,7},{6,4},{7,5},{8,10},{9,11},{10,... | collective-permute-start | bytes 589832 | tf_op jit(solution)/shard_map/ppermute | solution.py:347
  29.7 8.4 %collective-permute-start.4 = (bf16[2,192,128]{2,1,0:T(8,128)(2,1)S(1)}, bf16[2,192,128]{2,1,0:T(8,128)(2,1)S(1)}, u32[]{:S(2)}, u32[]{:S(2)}) collective-permute-start(bf16[2,192,128]{2,1,0:T(8,128)(2,1)S(1)} %get-tuple-element.39), channel_id=1, source_target_pairs={{0,1},{1,0},{2,3},{3,2},{4,5},{5,4},{6,7},{7,6},{8,9},{9,8},{10,11... | collective-permute-start | bytes 294920 | tf_op jit(solution)/shard_map/ppermute | solution.py:347
  29.9 17.3 %collective-permute-start.5 = (bf16[2,192,128]{2,1,0:T(8,128)(2,1)S(1)}, bf16[2,192,128]{2,1,0:T(8,128)(2,1)S(1)}, u32[]{:S(2)}, u32[]{:S(2)}) collective-permute-start(bf16[2,192,128]{2,1,0:T(8,128)(2,1)S(1)} %get-tuple-element.40), channel_id=1, source_target_pairs={{0,2},{1,3},{2,0},{3,1},{4,6},{5,7},{6,4},{7,5},{8,10},{9,11},{10,... | collective-permute-start | bytes 294920 | tf_op jit(solution)/shard_map/ppermute | solution.py:347
  30.6 21.1 %collective-permute-start.6 = (bf16[2,192,128]{2,1,0:T(8,128)(2,1)S(1)}, bf16[2,192,128]{2,1,0:T(8,128)(2,1)S(1)}, u32[]{:S(2)}, u32[]{:S(2)}) collective-permute-start(bf16[2,192,128]{2,1,0:T(8,128)(2,1)S(1)} %get-tuple-element.41), channel_id=1, source_target_pairs={{0,3},{1,2},{2,1},{3,0},{4,7},{5,6},{6,5},{7,4},{8,11},{9,10},{10,... | collective-permute-start | bytes 294920 | tf_op jit(solution)/shard_map/ppermute | solution.py:347
  38.2 15.3 %collective-permute-start.19 = (bf16[1,384,128]{2,1,0:T(8,128)(2,1)S(1)}, bf16[1,384,128]{2,1,0:T(8,128)(2,1)S(1)}, u32[]{:S(2)}, u32[]{:S(2)}) collective-permute-start(bf16[1,384,128]{2,1,0:T(8,128)(2,1)S(1)} %get-tuple-element.62), channel_id=1, source_target_pairs={{0,3},{1,2},{2,1},{3,0},{4,7},{5,6},{6,5},{7,4},{8,11},{9,10},{10,... | collective-permute-start | bytes 294920 | tf_op jit(solution)/shard_map/ppermute | solution.py:347
  47.2 7.6 %collective-permute-start.16 = (bf16[1,384,128]{2,1,0:T(8,128)(2,1)S(1)}, bf16[1,384,128]{2,1,0:T(8,128)(2,1)S(1)}, u32[]{:S(2)}, u32[]{:S(2)}) collective-permute-start(bf16[1,384,128]{2,1,0:T(8,128)(2,1)S(1)} %get-tuple-element.55), channel_id=1, source_target_pairs={{0,3},{1,2},{2,1},{3,0},{4,7},{5,6},{6,5},{7,4},{8,11},{9,10},{10,... | collective-permute-start | bytes 294920 | tf_op jit(solution)/shard_map/ppermute | solution.py:347

commit v10 on v9

--- a/solution.py
+++ b/solution.py
@@ -295,16 +295,18 @@
         out[s] = total
 
 
-def late_kernel(slot, real, imag, so_far, *rest):
-    out, stage, sem = rest[-3:]
+def late_kernel(real, *rest):
+    *imags, so_far, out, stage, sem = rest
     slots = real.shape[1]
-    term = products(real[slot], imag[0])
     copies = []
-    for part in range(2):
-        stage[part] = so_far[slot, part * slots : (part + 1) * slots] + term[part * slots : (part + 1) * slots]
-        copy = pltpu.make_async_copy(stage.at[part], out.at[slot, 0, part], sem.at[part])
-        copy.start()
-        copies.append(copy)
+    for s, imag in enumerate(imags):
+        term = products(real[s], imag[0])
+        for part in range(2):
+            rows = slice(part * slots, (part + 1) * slots)
+            stage[s, part] = so_far[s, rows] + term[rows]
+            copy = pltpu.make_async_copy(stage.at[s, part], out.at[s, 0, part], sem.at[s, part])
+            copy.start()
+            copies.append(copy)
     for copy in copies:
         copy.wait()
 
@@ -321,20 +323,15 @@
         compiler_params=PARAMS,
         cost_estimate=pl.CostEstimate(flops=flops * len(early), bytes_accessed=3_000_000, transcendentals=0),
     )(*[real[e] for e in early], *[imag[e] for e in early])
-    anywhere = pl.BlockSpec(memory_space=pl.ANY)
-    out = ()
-    for s in range(per):
-        out = pl.pallas_call(
-            functools.partial(late_kernel, s),
-            out_shape=[jax.ShapeDtypeStruct((per, 1, 2, slots, slots), jnp.float32)],
-            in_specs=[VMEM] * 3 + [anywhere] * len(out),
-            out_specs=[anywhere],
-            scratch_shapes=[pltpu.VMEM((2, slots, slots), jnp.float32), pltpu.SemaphoreType.DMA((2,))],
-            input_output_aliases={3: 0} if out else {},
-            compiler_params=PARAMS,
-            cost_estimate=pl.CostEstimate(flops=flops // per, bytes_accessed=2_000_000, transcendentals=0),
-        )(real[last], imag[last][s], so_far, *out)
-    return out[0]
+    return pl.pallas_call(
+        late_kernel,
+        out_shape=jax.ShapeDtypeStruct((per, 1, 2, slots, slots), jnp.float32),
+        in_specs=[VMEM] * (2 + per),
+        out_specs=pl.BlockSpec(memory_space=pl.ANY),
+        scratch_shapes=[pltpu.VMEM((per, 2, slots, slots), jnp.float32), pltpu.SemaphoreType.DMA((per, 2))],
+        compiler_params=PARAMS,
+        cost_estimate=pl.CostEstimate(flops=flops, bytes_accessed=3_000_000, transcendentals=0),
+    )(real[last], *imag[last], so_far)
 
 
 def exchange(chunks, order, groups):

time: 56.3 us -> 56.3 us (level)
  Pallas kernels: 9.34 us -> 8.42 us
  waiting for transfers between devices: 12.1 us -> 13 us
    pallas_call x2 -> x1, Pallas kernels: 2.64 us -> 1.72 us  [gram(): pl.pallas_call(late_kernel, out_shape=jax.ShapeDtypeStruct((per, 1, 2, sl...]
    ppermute x10, waiting for transfers between devices: 10.6 us -> 11.5 us  [exchange(): moved.append(lax.ppermute(part, 'tm', pairs))]
  transfers between devices with their start and end apart: 20 -> 20, of which waited for: 3 -> 4; matrix products, arithmetic and copies ran while one was open for 0% -> 0% of each run, Pallas kernels for 14% -> 11%
where the time goes in v10:
time: 56.3 us; the launch traced here: 56.1 us
  starting transfers between devices  33.3 us (59%)
  waiting for transfers between devices  13 us (23%)
  Pallas kernels  8.42 us (15%)
  local copies, waits for them, and re-layouts  1.23 us (2%)
    ppermute x10, starting transfers between devices, exchange(): moved.append(lax.ppermute(part, 'tm', pairs))  20 us
    ppermute x9, starting transfers between devices, cross(): lax.ppermute(chunks[step], 'chan', [(i, i ^ 2 * step) for i in starts])  12.7 us
    ppermute x10, waiting for transfers between devices, exchange(): moved.append(lax.ppermute(part, 'tm', pairs))  11.5 us
    pallas_call x2, Pallas kernels, gather_half(): pl.pallas_call(functools.partial(gather_half_kernel, steps, groups), out_...  2.26 us
    pallas_call x1, Pallas kernels, gram(): pl.pallas_call(late_kernel, out_shape=jax.ShapeDtypeStruct((per, 1, 2, sl...  1.72 us
    ppermute x1, waiting for transfers between devices, steps_of(): given = lax.ppermute(give(voltages), 'chan', swap)  1.54 us
    pallas_call x1, Pallas kernels, gram(): pl.pallas_call(early_kernel, out_shape=jax.ShapeDtypeStruct((per, 2 * slo...  1.39 us
    pallas_call x1, Pallas kernels, gather(): pl.pallas_call(functools.partial(gather_kernel, steps, len(heights)), out...  1.32 us
  transfers between devices with their start and end apart: 20, of which 4 were waited for; matrix products, arithmetic and copies ran while one was open for 0% of the time, Pallas kernels for 11%

profile of v10, /device:TPU:0, one launch (start us, length us, event | category | flops | bytes accessed | tf_op | source)
XLA Modules:
  0.0 56.1 jit_solution(2166181927764141372)
XLA Ops:
  0.0 0.0 copy-start
  0.0 1.2 %copy-done = bf16[2,8,256,128]{3,2,1,0:T(8,128)(2,1)S(1)} copy-done((bf16[2,8,256,128]{3,2,1,0:T(8,128)(2,1)S(1)}, bf16[2,8,256,128]{3,2,1,0:T(8,128)(2,1)}, u32[]{:S(2)}) %copy-start) | copy-done | bytes 1048600
  1.2 0.0 copy-start.1
  1.2 0.0 copy-start.2
  1.3 0.6 collective-permute-start
  1.8 1.5 %collective-permute-done.given_ref = bf16[2,4,256,128]{3,2,1,0:T(8,128)(2,1)S(1)} collective-permute-done((bf16[2,4,256,128]{3,2,1,0:T(8,128)(2,1)S(1)}, bf16[2,4,256,128]{3,2,1,0:T(8,128)(2,1)S(1)}, u32[]{:S(2)}, u32[]{:S(2)}) %collective-permute-start) | collective-permute-done | bytes 524320 | tf_op jit(solution)/shard_map/ppermute | solution.py:394
  3.4 0.2 shard_map.39
  3.6 2.9 %collective-permute-start.7 = (bf16[256,128]{1,0:T(8,128)(2,1)S(1)}, bf16[256,128]{1,0:T(8,128)(2,1)S(1)}, u32[]{:S(2)}, u32[]{:S(2)}) collective-permute-start(bf16[256,128]{1,0:T(8,128)(2,1)S(1)} %get-tuple-element.43), channel_id=1, source_target_pairs={{0,8},{4,12},{8,0},{12,4},{16,24},{20,28},{24,16},{28,20},{1,9},{5... | collective-permute-start | bytes 196616 | tf_op jit(solution)/shard_map/ppermute | solution.py:361
  6.5 1.5 %collective-permute-start.8 = (bf16[256,128]{1,0:T(8,128)(2,1)S(1)}, bf16[256,128]{1,0:T(8,128)(2,1)S(1)}, u32[]{:S(2)}, u32[]{:S(2)}) collective-permute-start(bf16[256,128]{1,0:T(8,128)(2,1)S(1)} %get-tuple-element.44), channel_id=1, source_target_pairs={{0,16},{4,20},{8,24},{12,28},{16,0},{20,4},{24,8},{28,12},{1,17},{... | collective-permute-start | bytes 196616 | tf_op jit(solution)/shard_map/ppermute | solution.py:361
  8.0 0.5 collective-permute-start.1
  8.6 1.4 %collective-permute-start.9 = (bf16[256,128]{1,0:T(8,128)(2,1)S(1)}, bf16[256,128]{1,0:T(8,128)(2,1)S(1)}, u32[]{:S(2)}, u32[]{:S(2)}) collective-permute-start(bf16[256,128]{1,0:T(8,128)(2,1)S(1)} %get-tuple-element.45), channel_id=1, source_target_pairs={{0,24},{4,28},{8,16},{12,20},{16,8},{20,12},{24,0},{28,4},{1,25},{... | collective-permute-start | bytes 196616 | tf_op jit(solution)/shard_map/ppermute | solution.py:361
  10.1 0.1 collective-permute-start.13
  10.2 0.0 collective-permute-done.7.rest_1_
  10.2 2.0 %collective-permute-start.14 = (bf16[512,128]{1,0:T(8,128)(2,1)S(1)}, bf16[512,128]{1,0:T(8,128)(2,1)S(1)}, u32[]{:S(2)}, u32[]{:S(2)}) collective-permute-start(bf16[512,128]{1,0:T(8,128)(2,1)S(1)} %get-tuple-element.53), channel_id=1, source_target_pairs={{0,16},{4,20},{8,24},{12,28},{16,0},{20,4},{24,8},{28,12},{1,17},{... | collective-permute-start | bytes 393224 | tf_op jit(solution)/shard_map/ppermute | solution.py:361
  12.2 0.0 collective-permute-done.8.rest_2_
  12.2 1.4 %collective-permute-start.15 = (bf16[512,128]{1,0:T(8,128)(2,1)S(1)}, bf16[512,128]{1,0:T(8,128)(2,1)S(1)}, u32[]{:S(2)}, u32[]{:S(2)}) collective-permute-start(bf16[512,128]{1,0:T(8,128)(2,1)S(1)} %get-tuple-element.54), channel_id=1, source_target_pairs={{0,24},{4,28},{8,16},{12,20},{16,8},{20,12},{24,0},{28,4},{1,25},{... | collective-permute-start | bytes 393224 | tf_op jit(solution)/shard_map/ppermute | solution.py:361
  13.6 0.0 copy-done.1
  13.6 0.0 copy-done.2
  13.6 1.0 %shard_map.37.select_ref = bf16[1536,1024]{1,0:T(8,128)(2,1)S(1)} custom-call(s32[1,8]{1,0:T(1,128)S(1)} %bitcast.3, s32[8,128]{1,0:T(8,128)S(1)} %bitcast.2), custom_call_target="tpu_custom_call" | custom-call | flops 4000000000 | bytes 3000000 | tf_op jit(solution)/shard_map/pallas_call | solution.py:76
  14.7 0.0 collective-permute-done.9.rest_3_
  14.7 1.6 %collective-permute-start.2 = (bf16[256,128]{1,0:T(8,128)(2,1)S(1)}, bf16[256,128]{1,0:T(8,128)(2,1)S(1)}, u32[]{:S(2)}, u32[]{:S(2)}) collective-permute-start(bf16[256,128]{1,0:T(8,128)(2,1)S(1)} %get-tuple-element.36), channel_id=1, source_target_pairs={{0,16},{4,20},{8,24},{12,28},{16,0},{20,4},{24,8},{28,12},{1,17},{... | collective-permute-start | bytes 196616 | tf_op jit(solution)/shard_map/ppermute | solution.py:361
  16.3 1.1 %shard_map.41 = (bf16[2,192,128]{2,1,0:T(8,128)(2,1)S(1)}, bf16[2,192,128]{2,1,0:T(8,128)(2,1)S(1)}, bf16[2,192,128]{2,1,0:T(8,128)(2,1)S(1)}, bf16[2,192,128]{2,1,0:T(8,128)(2,1)S(1)}) custom-call(bf16[1536,1024]{1,0:T(8,128)(2,1)S(1)} %shard_map.37.select_ref, bf16[256,128]{1,0:T(8,128)(2,1)S(1)} %get-tuple-element.42.rest_0_, ...), custom_call_target="tpu_custom_call" | custom-call | flops 402653184 | bytes 4000000 | tf_op jit(solution)/shard_map/pallas_call | solution.py:175
  17.4 0.0 collective-permute-done.1.rest_1_
  17.4 1.2 %collective-permute-start.3 = (bf16[256,128]{1,0:T(8,128)(2,1)S(1)}, bf16[256,128]{1,0:T(8,128)(2,1)S(1)}, u32[]{:S(2)}, u32[]{:S(2)}) collective-permute-start(bf16[256,128]{1,0:T(8,128)(2,1)S(1)} %get-tuple-element.37), channel_id=1, source_target_pairs={{0,24},{4,28},{8,16},{12,20},{16,8},{20,12},{24,0},{28,4},{1,25},{... | collective-permute-start | bytes 196616 | tf_op jit(solution)/shard_map/ppermute | solution.py:361
  18.6 0.0 collective-permute-done.13.rest_1_
  18.6 1.6 %collective-permute-start.10 = (bf16[2,192,128]{2,1,0:T(8,128)(2,1)S(1)}, bf16[2,192,128]{2,1,0:T(8,128)(2,1)S(1)}, u32[]{:S(2)}, u32[]{:S(2)}) collective-permute-start(bf16[2,192,128]{2,1,0:T(8,128)(2,1)S(1)} %get-tuple-element.47), channel_id=1, source_target_pairs={{0,1},{1,0},{2,3},{3,2},{4,5},{5,4},{6,7},{7,6},{8,9},{9,8},{10,11... | collective-permute-start | bytes 294920 | tf_op jit(solution)/shard_map/ppermute | solution.py:344
  20.2 0.0 collective-permute-done.14.rest_2_
  20.2 2.6 %collective-permute-start.11 = (bf16[2,192,128]{2,1,0:T(8,128)(2,1)S(1)}, bf16[2,192,128]{2,1,0:T(8,128)(2,1)S(1)}, u32[]{:S(2)}, u32[]{:S(2)}) collective-permute-start(bf16[2,192,128]{2,1,0:T(8,128)(2,1)S(1)} %get-tuple-element.48), channel_id=1, source_target_pairs={{0,2},{1,3},{2,0},{3,1},{4,6},{5,7},{6,4},{7,5},{8,10},{9,11},{10,... | collective-permute-start | bytes 294920 | tf_op jit(solution)/shard_map/ppermute | solution.py:344
  22.8 0.0 collective-permute-done.15.rest_3_
  22.8 0.2 collective-permute-start.12
  23.0 1.3 %shard_map.44 = (bf16[2,384,128]{2,1,0:T(8,128)(2,1)S(1)}, bf16[2,384,128]{2,1,0:T(8,128)(2,1)S(1)}, bf16[2,384,128]{2,1,0:T(8,128)(2,1)S(1)}, bf16[1,384,128]{2,1,0:T(8,128)(2,1)S(1)}, bf16[1,384,128]{2,1,0:T(8,128)(2,1)S(1)}) custom-call(bf16[1536,1024]{1,0:T(8,128)(2,1)S(1)} %shard_map.37.select_ref, bf16[512,128]{1,0:T(8,128)(2,1)S(1)} %get-tuple-element.51.rest_0_, ...), custom_call_target="tpu_custom_call" | custom-call | flops 805306368 | bytes 4000000 | tf_op jit(solution)/shard_map/pallas_call | solution.py:259
  24.4 0.0 collective-permute-done.2.rest_2_
  24.4 0.7 %collective-permute-start.18 = (bf16[2,384,128]{2,1,0:T(8,128)(2,1)S(1)}, bf16[2,384,128]{2,1,0:T(8,128)(2,1)S(1)}, u32[]{:S(2)}, u32[]{:S(2)}) collective-permute-start(bf16[2,384,128]{2,1,0:T(8,128)(2,1)S(1)} %get-tuple-element.61), channel_id=1, source_target_pairs={{0,1},{1,0},{2,3},{3,2},{4,5},{5,4},{6,7},{7,6},{8,9},{9,8},{10,11... | collective-permute-start | bytes 589832 | tf_op jit(solution)/shard_map/ppermute | solution.py:344
  25.1 0.0 collective-permute-done.3.rest_3_
  25.1 3.5 %collective-permute-start.19 = (bf16[2,384,128]{2,1,0:T(8,128)(2,1)S(1)}, bf16[2,384,128]{2,1,0:T(8,128)(2,1)S(1)}, u32[]{:S(2)}, u32[]{:S(2)}) collective-permute-start(bf16[2,384,128]{2,1,0:T(8,128)(2,1)S(1)} %get-tuple-element.62), channel_id=1, source_target_pairs={{0,2},{1,3},{2,0},{3,1},{4,6},{5,7},{6,4},{7,5},{8,10},{9,11},{10,... | collective-permute-start | bytes 589832 | tf_op jit(solution)/shard_map/ppermute | solution.py:344
  28.6 1.1 %shard_map.40 = (bf16[2,192,128]{2,1,0:T(8,128)(2,1)S(1)}, bf16[2,192,128]{2,1,0:T(8,128)(2,1)S(1)}, bf16[2,192,128]{2,1,0:T(8,128)(2,1)S(1)}, bf16[2,192,128]{2,1,0:T(8,128)(2,1)S(1)}) custom-call(bf16[1536,1024]{1,0:T(8,128)(2,1)S(1)} %shard_map.37.select_ref, bf16[256,128]{1,0:T(8,128)(2,1)S(1)} %get-tuple-element.34.rest_0_, ...), custom_call_target="tpu_custom_call" | custom-call | flops 402653184 | bytes 4000000 | tf_op jit(solution)/shard_map/pallas_call | solution.py:175
  29.7 0.0 collective-permute-done.10.refs_5_
  29.7 0.2 collective-permute-start.4
  29.9 0.0 collective-permute-done.11.refs_6_
  29.9 0.7 %collective-permute-start.5 = (bf16[2,192,128]{2,1,0:T(8,128)(2,1)S(1)}, bf16[2,192,128]{2,1,0:T(8,128)(2,1)S(1)}, u32[]{:S(2)}, u32[]{:S(2)}) collective-permute-start(bf16[2,192,128]{2,1,0:T(8,128)(2,1)S(1)} %get-tuple-element.40), channel_id=1, source_target_pairs={{0,2},{1,3},{2,0},{3,1},{4,6},{5,7},{6,4},{7,5},{8,10},{9,11},{10,... | collective-permute-start | bytes 294920 | tf_op jit(solution)/shard_map/ppermute | solution.py:344
  30.6 0.0 collective-permute-done.12.refs_7_
  30.6 3.6 %collective-permute-start.6 = (bf16[2,192,128]{2,1,0:T(8,128)(2,1)S(1)}, bf16[2,192,128]{2,1,0:T(8,128)(2,1)S(1)}, u32[]{:S(2)}, u32[]{:S(2)}) collective-permute-start(bf16[2,192,128]{2,1,0:T(8,128)(2,1)S(1)} %get-tuple-element.41), channel_id=1, source_target_pairs={{0,3},{1,2},{2,1},{3,0},{4,7},{5,6},{6,5},{7,4},{8,11},{9,10},{10,... | collective-permute-start | bytes 294920 | tf_op jit(solution)/shard_map/ppermute | solution.py:344
  34.2 4.0 %collective-permute-done.4.refs_1_ = bf16[2,192,128]{2,1,0:T(8,128)(2,1)S(1)} collective-permute-done((bf16[2,192,128]{2,1,0:T(8,128)(2,1)S(1)}, bf16[2,192,128]{2,1,0:T(8,128)(2,1)S(1)}, u32[]{:S(2)}, u32[]{:S(2)}) %collective-permute-start.4) | collective-permute-done | bytes 98336 | tf_op jit(solution)/shard_map/ppermute | solution.py:344
  38.2 2.5 %collective-permute-start.16 = (bf16[1,384,128]{2,1,0:T(8,128)(2,1)S(1)}, bf16[1,384,128]{2,1,0:T(8,128)(2,1)S(1)}, u32[]{:S(2)}, u32[]{:S(2)}) collective-permute-start(bf16[1,384,128]{2,1,0:T(8,128)(2,1)S(1)} %get-tuple-element.55), channel_id=1, source_target_pairs={{0,3},{1,2},{2,1},{3,0},{4,7},{5,6},{6,5},{7,4},{8,11},{9,10},{10,... | collective-permute-start | bytes 294920 | tf_op jit(solution)/shard_map/ppermute | solution.py:344
  40.7 6.5 %collective-permute-done.5.refs_2_ = bf16[2,192,128]{2,1,0:T(8,128)(2,1)S(1)} collective-permute-done((bf16[2,192,128]{2,1,0:T(8,128)(2,1)S(1)}, bf16[2,192,128]{2,1,0:T(8,128)(2,1)S(1)}, u32[]{:S(2)}, u32[]{:S(2)}) %collective-permute-start.5) | collective-permute-done | bytes 98336 | tf_op jit(solution)/shard_map/ppermute | solution.py:344
  47.2 4.5 %collective-permute-start.17 = (bf16[1,384,128]{2,1,0:T(8,128)(2,1)S(1)}, bf16[1,384,128]{2,1,0:T(8,128)(2,1)S(1)}, u32[]{:S(2)}, u32[]{:S(2)}) collective-permute-start(bf16[1,384,128]{2,1,0:T(8,128)(2,1)S(1)} %get-tuple-element.56), channel_id=1, source_target_pairs={{0,3},{1,2},{2,1},{3,0},{4,7},{5,6},{6,5},{7,4},{8,11},{9,10},{10,... | collective-permute-start | bytes 294920 | tf_op jit(solution)/shard_map/ppermute | solution.py:344
  51.7 0.0 collective-permute-done.6.refs_3_
  51.7 0.4 shard_map.42
  52.1 0.0 collective-permute-done.18.refs_4_
  52.1 0.0 collective-permute-done.19.refs_5_
  52.1 1.4 %shard_map.45.rest_2_ = f32[2,768,384]{2,1,0:T(8,128)S(1)} custom-call(bf16[2,384,128]{2,1,0:T(8,128)(2,1)S(1)} %get-tuple-element.57.refs_0_, bf16[2,384,128]{2,1,0:T(8,128)(2,1)S(1)} %get-tuple-element.58.refs_1_, bf16[2,384,128]{2,1,0:T(8,128)(2,1)S(1)} %get-tuple-element.59.refs_2_, bf16[2,384,128]{2,1,0:T(8,128)(2,1)S(1)} %get-tuple-element.60.refs_3_, ...), custom_call_target="tpu_custom_call" | custom-call | flops 905969664 | bytes 3000000 | tf_op jit(solution)/shard_map/pallas_call | solution.py:318
  53.5 0.0 collective-permute-done.16.rest_0_
  53.5 0.9 %collective-permute-done.17.rest_1_ = bf16[1,384,128]{2,1,0:T(8,128)(2,1)S(1)} collective-permute-done((bf16[1,384,128]{2,1,0:T(8,128)(2,1)S(1)}, bf16[1,384,128]{2,1,0:T(8,128)(2,1)S(1)}, u32[]{:S(2)}, u32[]{:S(2)}) %collective-permute-start.17) | collective-permute-done | bytes 98336 | tf_op jit(solution)/shard_map/ppermute | solution.py:344
  54.4 1.7 %shard_map.46 = f32[2,1,2,384,384]{4,3,2,1,0:T(8,128)} custom-call(bf16[2,384,128]{2,1,0:T(8,128)(2,1)S(1)} %get-tuple-element.50.real, bf16[1,384,128]{2,1,0:T(8,128)(2,1)S(1)} %collective-permute-done.16.rest_0_, bf16[1,384,128]{2,1,0:T(8,128)(2,1)S(1)} %collective-permute-done.17.rest_1_, f32[2,768,384]{2,1,0:T(8,128)S(1)} %shard_map.45.rest_2_), custom_call_target="tpu_custom_call" | custom-call | flops 301989888 | bytes 3000000 | tf_op jit(solution)/shard_map/pallas_call | solution.py:326
  (2 shorter events, 0.1 us)
Async XLA Ops:
  0.0 1.2 %copy-start = (bf16[2,8,256,128]{3,2,1,0:T(8,128)(2,1)S(1)}, bf16[2,8,256,128]{3,2,1,0:T(8,128)(2,1)}, u32[]{:S(2)}) copy-start(bf16[2,8,256,128]{3,2,1,0:T(8,128)(2,1)} %x_ref.5) | copy-start | bytes 3145732
  1.2 12.4 %copy-start.1 = (s32[1024,1]{0,1:T(1,128)S(1)}, s32[1024,1]{0,1:T(1,128)}, u32[]{:S(2)}) copy-start(s32[1024,1]{0,1:T(1,128)} %param.4) | copy-start | bytes 12292
  1.2 12.4 %copy-start.2 = (s32[8]{0:T(128)S(1)}, s32[8]{0:T(128)}, u32[]{:S(2)}) copy-start(s32[8]{0:T(128)} %param.5) | copy-start | bytes 100
  1.3 2.1 %collective-permute-start = (bf16[2,4,256,128]{3,2,1,0:T(8,128)(2,1)S(1)}, bf16[2,4,256,128]{3,2,1,0:T(8,128)(2,1)S(1)}, u32[]{:S(2)}, u32[]{:S(2)}) collective-permute-start(bf16[2,4,256,128]{3,2,1,0:T(8,128)(2,1)S(1)} %shard_map.38), channel_id=1, source_target_pairs={{0,4},{4,0},{8,12},{12,8},{16,20},{20,16},{24,28},{28,24},{1,5},{5... | collective-permute-start | bytes 1572872 | tf_op jit(solution)/shard_map/ppermute | solution.py:394
  3.6 6.6 %collective-permute-start.7 = (bf16[256,128]{1,0:T(8,128)(2,1)S(1)}, bf16[256,128]{1,0:T(8,128)(2,1)S(1)}, u32[]{:S(2)}, u32[]{:S(2)}) collective-permute-start(bf16[256,128]{1,0:T(8,128)(2,1)S(1)} %get-tuple-element.43), channel_id=1, source_target_pairs={{0,8},{4,12},{8,0},{12,4},{16,24},{20,28},{24,16},{28,20},{1,9},{5... | collective-permute-start | bytes 196616 | tf_op jit(solution)/shard_map/ppermute | solution.py:361
  6.5 5.7 %collective-permute-start.8 = (bf16[256,128]{1,0:T(8,128)(2,1)S(1)}, bf16[256,128]{1,0:T(8,128)(2,1)S(1)}, u32[]{:S(2)}, u32[]{:S(2)}) collective-permute-start(bf16[256,128]{1,0:T(8,128)(2,1)S(1)} %get-tuple-element.44), channel_id=1, source_target_pairs={{0,16},{4,20},{8,24},{12,28},{16,0},{20,4},{24,8},{28,12},{1,17},{... | collective-permute-start | bytes 196616 | tf_op jit(solution)/shard_map/ppermute | solution.py:361
  8.0 9.4 %collective-permute-start.1 = (bf16[256,128]{1,0:T(8,128)(2,1)S(1)}, bf16[256,128]{1,0:T(8,128)(2,1)S(1)}, u32[]{:S(2)}, u32[]{:S(2)}) collective-permute-start(bf16[256,128]{1,0:T(8,128)(2,1)S(1)} %get-tuple-element.35), channel_id=1, source_target_pairs={{0,8},{4,12},{8,0},{12,4},{16,24},{20,28},{24,16},{28,20},{1,9},{5... | collective-permute-start | bytes 196616 | tf_op jit(solution)/shard_map/ppermute | solution.py:361
  8.6 6.1 %collective-permute-start.9 = (bf16[256,128]{1,0:T(8,128)(2,1)S(1)}, bf16[256,128]{1,0:T(8,128)(2,1)S(1)}, u32[]{:S(2)}, u32[]{:S(2)}) collective-permute-start(bf16[256,128]{1,0:T(8,128)(2,1)S(1)} %get-tuple-element.45), channel_id=1, source_target_pairs={{0,24},{4,28},{8,16},{12,20},{16,8},{20,12},{24,0},{28,4},{1,25},{... | collective-permute-start | bytes 196616 | tf_op jit(solution)/shard_map/ppermute | solution.py:361
  10.1 8.6 %collective-permute-start.13 = (bf16[512,128]{1,0:T(8,128)(2,1)S(1)}, bf16[512,128]{1,0:T(8,128)(2,1)S(1)}, u32[]{:S(2)}, u32[]{:S(2)}) collective-permute-start(bf16[512,128]{1,0:T(8,128)(2,1)S(1)} %get-tuple-element.52), channel_id=1, source_target_pairs={{0,8},{4,12},{8,0},{12,4},{16,24},{20,28},{24,16},{28,20},{1,9},{5... | collective-permute-start | bytes 393224 | tf_op jit(solution)/shard_map/ppermute | solution.py:361
  10.2 10.0 %collective-permute-start.14 = (bf16[512,128]{1,0:T(8,128)(2,1)S(1)}, bf16[512,128]{1,0:T(8,128)(2,1)S(1)}, u32[]{:S(2)}, u32[]{:S(2)}) collective-permute-start(bf16[512,128]{1,0:T(8,128)(2,1)S(1)} %get-tuple-element.53), channel_id=1, source_target_pairs={{0,16},{4,20},{8,24},{12,28},{16,0},{20,4},{24,8},{28,12},{1,17},{... | collective-permute-start | bytes 393224 | tf_op jit(solution)/shard_map/ppermute | solution.py:361
  12.2 10.6 %collective-permute-start.15 = (bf16[512,128]{1,0:T(8,128)(2,1)S(1)}, bf16[512,128]{1,0:T(8,128)(2,1)S(1)}, u32[]{:S(2)}, u32[]{:S(2)}) collective-permute-start(bf16[512,128]{1,0:T(8,128)(2,1)S(1)} %get-tuple-element.54), channel_id=1, source_target_pairs={{0,24},{4,28},{8,16},{12,20},{16,8},{20,12},{24,0},{28,4},{1,25},{... | collective-permute-start | bytes 393224 | tf_op jit(solution)/shard_map/ppermute | solution.py:361
  14.7 9.7 %collective-permute-start.2 = (bf16[256,128]{1,0:T(8,128)(2,1)S(1)}, bf16[256,128]{1,0:T(8,128)(2,1)S(1)}, u32[]{:S(2)}, u32[]{:S(2)}) collective-permute-start(bf16[256,128]{1,0:T(8,128)(2,1)S(1)} %get-tuple-element.36), channel_id=1, source_target_pairs={{0,16},{4,20},{8,24},{12,28},{16,0},{20,4},{24,8},{28,12},{1,17},{... | collective-permute-start | bytes 196616 | tf_op jit(solution)/shard_map/ppermute | solution.py:361
  17.4 7.7 %collective-permute-start.3 = (bf16[256,128]{1,0:T(8,128)(2,1)S(1)}, bf16[256,128]{1,0:T(8,128)(2,1)S(1)}, u32[]{:S(2)}, u32[]{:S(2)}) collective-permute-start(bf16[256,128]{1,0:T(8,128)(2,1)S(1)} %get-tuple-element.37), channel_id=1, source_target_pairs={{0,24},{4,28},{8,16},{12,20},{16,8},{20,12},{24,0},{28,4},{1,25},{... | collective-permute-start | bytes 196616 | tf_op jit(solution)/shard_map/ppermute | solution.py:361
  18.6 11.1 %collective-permute-start.10 = (bf16[2,192,128]{2,1,0:T(8,128)(2,1)S(1)}, bf16[2,192,128]{2,1,0:T(8,128)(2,1)S(1)}, u32[]{:S(2)}, u32[]{:S(2)}) collective-permute-start(bf16[2,192,128]{2,1,0:T(8,128)(2,1)S(1)} %get-tuple-element.47), channel_id=1, source_target_pairs={{0,1},{1,0},{2,3},{3,2},{4,5},{5,4},{6,7},{7,6},{8,9},{9,8},{10,11... | collective-permute-start | bytes 294920 | tf_op jit(solution)/shard_map/ppermute | solution.py:344
  20.2 9.7 %collective-permute-start.11 = (bf16[2,192,128]{2,1,0:T(8,128)(2,1)S(1)}, bf16[2,192,128]{2,1,0:T(8,128)(2,1)S(1)}, u32[]{:S(2)}, u32[]{:S(2)}) collective-permute-start(bf16[2,192,128]{2,1,0:T(8,128)(2,1)S(1)} %get-tuple-element.48), channel_id=1, source_target_pairs={{0,2},{1,3},{2,0},{3,1},{4,6},{5,7},{6,4},{7,5},{8,10},{9,11},{10,... | collective-permute-start | bytes 294920 | tf_op jit(solution)/shard_map/ppermute | solution.py:344
  22.8 7.8 %collective-permute-start.12 = (bf16[2,192,128]{2,1,0:T(8,128)(2,1)S(1)}, bf16[2,192,128]{2,1,0:T(8,128)(2,1)S(1)}, u32[]{:S(2)}, u32[]{:S(2)}) collective-permute-start(bf16[2,192,128]{2,1,0:T(8,128)(2,1)S(1)} %get-tuple-element.49), channel_id=1, source_target_pairs={{0,3},{1,2},{2,1},{3,0},{4,7},{5,6},{6,5},{7,4},{8,11},{9,10},{10,... | collective-permute-start | bytes 294920 | tf_op jit(solution)/shard_map/ppermute | solution.py:344
  24.4 27.7 %collective-permute-start.18 = (bf16[2,384,128]{2,1,0:T(8,128)(2,1)S(1)}, bf16[2,384,128]{2,1,0:T(8,128)(2,1)S(1)}, u32[]{:S(2)}, u32[]{:S(2)}) collective-permute-start(bf16[2,384,128]{2,1,0:T(8,128)(2,1)S(1)} %get-tuple-element.61), channel_id=1, source_target_pairs={{0,1},{1,0},{2,3},{3,2},{4,5},{5,4},{6,7},{7,6},{8,9},{9,8},{10,11... | collective-permute-start | bytes 589832 | tf_op jit(solution)/shard_map/ppermute | solution.py:344
  25.1 27.0 %collective-permute-start.19 = (bf16[2,384,128]{2,1,0:T(8,128)(2,1)S(1)}, bf16[2,384,128]{2,1,0:T(8,128)(2,1)S(1)}, u32[]{:S(2)}, u32[]{:S(2)}) collective-permute-start(bf16[2,384,128]{2,1,0:T(8,128)(2,1)S(1)} %get-tuple-element.62), channel_id=1, source_target_pairs={{0,2},{1,3},{2,0},{3,1},{4,6},{5,7},{6,4},{7,5},{8,10},{9,11},{10,... | collective-permute-start | bytes 589832 | tf_op jit(solution)/shard_map/ppermute | solution.py:344
  29.7 8.4 %collective-permute-start.4 = (bf16[2,192,128]{2,1,0:T(8,128)(2,1)S(1)}, bf16[2,192,128]{2,1,0:T(8,128)(2,1)S(1)}, u32[]{:S(2)}, u32[]{:S(2)}) collective-permute-start(bf16[2,192,128]{2,1,0:T(8,128)(2,1)S(1)} %get-tuple-element.39), channel_id=1, source_target_pairs={{0,1},{1,0},{2,3},{3,2},{4,5},{5,4},{6,7},{7,6},{8,9},{9,8},{10,11... | collective-permute-start | bytes 294920 | tf_op jit(solution)/shard_map/ppermute | solution.py:344
  29.9 17.3 %collective-permute-start.5 = (bf16[2,192,128]{2,1,0:T(8,128)(2,1)S(1)}, bf16[2,192,128]{2,1,0:T(8,128)(2,1)S(1)}, u32[]{:S(2)}, u32[]{:S(2)}) collective-permute-start(bf16[2,192,128]{2,1,0:T(8,128)(2,1)S(1)} %get-tuple-element.40), channel_id=1, source_target_pairs={{0,2},{1,3},{2,0},{3,1},{4,6},{5,7},{6,4},{7,5},{8,10},{9,11},{10,... | collective-permute-start | bytes 294920 | tf_op jit(solution)/shard_map/ppermute | solution.py:344
  30.6 21.1 %collective-permute-start.6 = (bf16[2,192,128]{2,1,0:T(8,128)(2,1)S(1)}, bf16[2,192,128]{2,1,0:T(8,128)(2,1)S(1)}, u32[]{:S(2)}, u32[]{:S(2)}) collective-permute-start(bf16[2,192,128]{2,1,0:T(8,128)(2,1)S(1)} %get-tuple-element.41), channel_id=1, source_target_pairs={{0,3},{1,2},{2,1},{3,0},{4,7},{5,6},{6,5},{7,4},{8,11},{9,10},{10,... | collective-permute-start | bytes 294920 | tf_op jit(solution)/shard_map/ppermute | solution.py:344
  38.2 15.3 %collective-permute-start.16 = (bf16[1,384,128]{2,1,0:T(8,128)(2,1)S(1)}, bf16[1,384,128]{2,1,0:T(8,128)(2,1)S(1)}, u32[]{:S(2)}, u32[]{:S(2)}) collective-permute-start(bf16[1,384,128]{2,1,0:T(8,128)(2,1)S(1)} %get-tuple-element.55), channel_id=1, source_target_pairs={{0,3},{1,2},{2,1},{3,0},{4,7},{5,6},{6,5},{7,4},{8,11},{9,10},{10,... | collective-permute-start | bytes 294920 | tf_op jit(solution)/shard_map/ppermute | solution.py:344
  47.2 7.2 %collective-permute-start.17 = (bf16[1,384,128]{2,1,0:T(8,128)(2,1)S(1)}, bf16[1,384,128]{2,1,0:T(8,128)(2,1)S(1)}, u32[]{:S(2)}, u32[]{:S(2)}) collective-permute-start(bf16[1,384,128]{2,1,0:T(8,128)(2,1)S(1)} %get-tuple-element.56), channel_id=1, source_target_pairs={{0,3},{1,2},{2,1},{3,0},{4,7},{5,6},{6,5},{7,4},{8,11},{9,10},{10,... | collective-permute-start | bytes 294920 | tf_op jit(solution)/shard_map/ppermute | solution.py:344
